TPU v7x, 32 devices: a whole 2x2x4 slice. The times are simulated.
32 devices in a mesh: ctx: 8 (over z, x), fsdp: 4 (over y, core).
Axes of the slice: x: 2, y: 2, z: 4, core: 2. Of those that a mesh axis runs over, the one named last changes fastest.
Arguments:
- tokens: bfloat16 [4, 1024, 1600], P('fsdp', 'ctx'), may hold values from -40 to 40, as said below
- ln1_gain: bfloat16 [1600], P('fsdp'), may hold values from 0.099609375 to 1.8984375
- ln1_shift: bfloat16 [1600], P('fsdp'), may hold values from -3 to 3
- qkv_weight: bfloat16 [1600, 4800], P('fsdp'), may hold values from -0.15625 to 0.15625
- qv_bias: bfloat16 [3200], P('fsdp'), may hold values from -3 to 3
- out_weight: bfloat16 [1600, 1600], P('fsdp'), may hold values from -1.25 to 1.25
- out_bias: bfloat16 [1600], P('fsdp'), may hold values from -3 to 3
- ln2_gain: bfloat16 [1600], P('fsdp'), may hold values from 0.099609375 to 1.8984375
- ln2_shift: bfloat16 [1600], P('fsdp'), may hold values from -3 to 3
- up_weight: bfloat16 [1600, 6400], P('fsdp'), may hold values from -0.15625 to 0.15625
- up_bias: bfloat16 [6400], P('fsdp'), may hold values from -3 to 3
- down_weight: bfloat16 [6400, 1600], P('fsdp'), may hold values from -0.078125 to 0.078125
- down_bias: bfloat16 [1600], P('fsdp'), may hold values from -3 to 3
- block_table: int32 [8], replicated, may hold values from 0 to 7, each once
- cotangent: bfloat16 [4, 1024, 1600], P('fsdp', 'ctx'), may hold values from -6 to 6
Outputs:
- block_out: float32 [4, 1024, 1600], P('fsdp', 'ctx')
- input_grad: float32 [4, 1024, 1600], P('fsdp', 'ctx')
- ln1_gain_grad: float32 [1600], P('fsdp')
- ln1_shift_grad: float32 [1600], P('fsdp')
- qkv_weight_grad: float32 [1600, 4800], P('fsdp')
- qv_bias_grad: float32 [3200], P('fsdp')
- out_weight_grad: float32 [1600, 1600], P('fsdp')
- out_bias_grad: float32 [1600], P('fsdp')
- ln2_gain_grad: float32 [1600], P('fsdp')
- ln2_shift_grad: float32 [1600], P('fsdp')
- up_weight_grad: float32 [1600, 6400], P('fsdp')
- up_bias_grad: float32 [6400], P('fsdp')
- down_weight_grad: float32 [6400, 1600], P('fsdp')
- down_bias_grad: float32 [1600], P('fsdp')
Inputs may be any that keep to these rules, and one draw needn't show every extreme that they name: Device c of ctx holds blocks block_table[c] and 15 - block_table[c] of each of its sequence, in that order; every value appears once. `tokens`: activations of order one.
All inputs are finite; a program needn't handle non-finite values.
Results may differ from a plain program's by a relative error of at most 0.017.
Values may be sent and summed in bfloat16 or wider, within the bound.
A program may use at most 384 MiB of HBM per device.

v0:
```python
import jax
import jax.numpy as jnp
from jax import lax
from jax.sharding import PartitionSpec as P

HEAD_DIM = 64


EPS = 1e-05
SCALE = 0.125


def layer_norm(value, gain, shift):
    centre = value - jnp.mean(value, axis=-1, keepdims=True)
    spread = jnp.mean(centre * centre, axis=-1, keepdims=True)
    return centre * lax.rsqrt(spread + EPS) * gain + shift


def gelu_tanh(value):
    return jax.nn.gelu(value, approximate=True)


def inner_rows(left, right):
    return lax.dot_general(
        left, right, (((0,), (0,)), ((), ())), preferred_element_type=jnp.float32
    )


def times_transpose(left, right):
    return lax.dot_general(
        left, right, (((1,), (1,)), ((), ())), preferred_element_type=jnp.float32
    )


def exponents(query_part, query_place, key_part, key_place):
    raw = jnp.einsum("qhd,khd->hqk", query_part, key_part, preferred_element_type=jnp.float32)
    allowed = key_place[None, None, :] <= query_place[None, :, None]
    return jnp.where(allowed, jnp.exp(raw * SCALE), 0.0)


def score_grads(
    query_part, scaled_part, correction_part, query_place, key_part, value_part, key_place
):
    exponent = exponents(query_part, query_place, key_part, key_place)
    d_expo = jnp.einsum("qhd,khd->hqk", scaled_part, value_part, preferred_element_type=jnp.float32)
    d_raw = (exponent * (d_expo - correction_part.T[:, :, None])).astype(jnp.bfloat16) * SCALE
    return (exponent, d_raw)


def on_device(
    tokens,
    ln1_gain,
    ln1_shift,
    qkv_weight,
    qv_bias,
    out_weight,
    out_bias,
    ln2_gain,
    ln2_shift,
    up_weight,
    up_bias,
    down_weight,
    down_bias,
    block_table,
    cotangent,
):
    rows = tokens.shape[1]
    width = tokens.shape[2]
    heads = width // HEAD_DIM
    half = rows // 2
    count = lax.axis_size("ctx")
    within = jnp.arange(rows, dtype=jnp.int32)
    block_of = jnp.where(
        within[None, :] < half, block_table[:, None], 2 * count - 1 - block_table[:, None]
    )
    place = block_of * half + within[None, :] % half
    device = lax.axis_index("ctx")
    query_place = jnp.sum(
        jnp.where(jnp.arange(count, dtype=jnp.int32)[:, None] == device, place, 0), axis=0
    )
    key_place = place.reshape(-1)
    kblock = 4 * rows
    nblock = key_place.shape[0] // kblock
    place_blocks = key_place.reshape(nblock, kblock)
    attn_parts = (
        lax.all_gather(ln1_gain, "fsdp", axis=0, tiled=True),
        lax.all_gather(ln1_shift, "fsdp", axis=0, tiled=True),
        lax.all_gather(qkv_weight, "fsdp", axis=0, tiled=True),
        lax.all_gather(qv_bias, "fsdp", axis=0, tiled=True),
        lax.all_gather(out_weight, "fsdp", axis=0, tiled=True),
        lax.all_gather(out_bias, "fsdp", axis=0, tiled=True),
    )
    gain1 = attn_parts[0].astype(jnp.float32)
    shift1 = attn_parts[1].astype(jnp.float32)
    w_qkv = attn_parts[2]
    b_qv = attn_parts[3].astype(jnp.float32)
    w_out = attn_parts[4]
    b_out = attn_parts[5].astype(jnp.float32)
    inputs = tokens[0].astype(jnp.float32)
    normed1, ln1_back = jax.vjp(layer_norm, inputs, gain1, shift1)
    act1 = normed1.astype(jnp.bfloat16)
    projected = jnp.dot(act1, w_qkv, preferred_element_type=jnp.float32)
    query = (projected[:, :width] + b_qv[:width]).astype(jnp.bfloat16)
    keys = projected[:, width : 2 * width].astype(jnp.bfloat16)
    values = (projected[:, 2 * width :] + b_qv[width:]).astype(jnp.bfloat16)
    keys_all, values_all = (
        lax.all_gather(keys, "ctx", axis=0, tiled=True),
        lax.all_gather(values, "ctx", axis=0, tiled=True),
    )
    key_blocks = keys_all.reshape(nblock, kblock, heads, HEAD_DIM)
    value_blocks = values_all.reshape(nblock, kblock, heads, HEAD_DIM)
    query3 = query.reshape(rows, heads, HEAD_DIM)

    def forward_step(carry, parts):
        total, numerator = carry
        key_part, value_part, part_place = parts
        exponent = exponents(query3, query_place, key_part, part_place)
        total = total + jnp.sum(exponent, axis=2)
        numerator = numerator + jnp.einsum(
            "hqk,khd->qhd",
            exponent.astype(jnp.bfloat16),
            value_part,
            preferred_element_type=jnp.float32,
        )
        return ((total, numerator), None)

    begin = (jnp.zeros((heads, rows), jnp.float32), jnp.zeros((rows, heads, HEAD_DIM), jnp.float32))
    (total, numerator), _ = lax.scan(forward_step, begin, (key_blocks, value_blocks, place_blocks))
    totals_rows = total.T
    attended = numerator / totals_rows[:, :, None]
    attn = attended.reshape(rows, width).astype(jnp.bfloat16)
    mid = inputs + jnp.dot(attn, w_out, preferred_element_type=jnp.float32) + b_out
    mlp_parts = (
        lax.all_gather(ln2_gain, "fsdp", axis=0, tiled=True),
        lax.all_gather(ln2_shift, "fsdp", axis=0, tiled=True),
        lax.all_gather(up_weight, "fsdp", axis=0, tiled=True),
        lax.all_gather(up_bias, "fsdp", axis=0, tiled=True),
        lax.all_gather(down_weight, "fsdp", axis=0, tiled=True),
        lax.all_gather(down_bias, "fsdp", axis=0, tiled=True),
    )
    gain2 = mlp_parts[0].astype(jnp.float32)
    shift2 = mlp_parts[1].astype(jnp.float32)
    w_up = mlp_parts[2]
    b_up = mlp_parts[3].astype(jnp.float32)
    w_down = mlp_parts[4]
    b_down = mlp_parts[5].astype(jnp.float32)
    normed2, ln2_back = jax.vjp(layer_norm, mid, gain2, shift2)
    act2 = normed2.astype(jnp.bfloat16)
    hidden_in = jnp.dot(act2, w_up, preferred_element_type=jnp.float32) + b_up
    activated, gelu_back = jax.vjp(gelu_tanh, hidden_in)
    hidden = activated.astype(jnp.bfloat16)
    result = mid + jnp.dot(hidden, w_down, preferred_element_type=jnp.float32) + b_down
    grad_out = cotangent[0].astype(jnp.float32)
    grad_branch2 = grad_out.astype(jnp.bfloat16)
    d_down = inner_rows(hidden, grad_branch2)
    d_down_bias = jnp.sum(grad_branch2.astype(jnp.float32), axis=0)
    d_hidden = times_transpose(grad_branch2, w_down)
    d_hidden_in = gelu_back(d_hidden)[0].astype(jnp.bfloat16)
    d_up = inner_rows(act2, d_hidden_in)
    d_up_bias = jnp.sum(d_hidden_in.astype(jnp.float32), axis=0)
    d_act2 = times_transpose(d_hidden_in, w_up)
    d_mid_norm, d_gain2, d_shift2 = ln2_back(d_act2)
    mlp_owned = (
        lax.psum_scatter(d_gain2, "fsdp", scatter_dimension=0, tiled=True),
        lax.psum_scatter(d_shift2, "fsdp", scatter_dimension=0, tiled=True),
        lax.psum_scatter(d_up, "fsdp", scatter_dimension=0, tiled=True),
        lax.psum_scatter(d_up_bias, "fsdp", scatter_dimension=0, tiled=True),
        lax.psum_scatter(d_down, "fsdp", scatter_dimension=0, tiled=True),
        lax.psum_scatter(d_down_bias, "fsdp", scatter_dimension=0, tiled=True),
    )
    mlp_total = lax.psum(
        (mlp_owned[0], mlp_owned[1], mlp_owned[2], mlp_owned[3], mlp_owned[4], mlp_owned[5]), "ctx"
    )
    d_mid = grad_out + d_mid_norm
    grad_branch1 = d_mid.astype(jnp.bfloat16)
    d_out = inner_rows(attn, grad_branch1)
    d_out_bias = jnp.sum(grad_branch1.astype(jnp.float32), axis=0)
    d_attn = times_transpose(grad_branch1, w_out).reshape(rows, heads, HEAD_DIM)
    scaled = (d_attn / totals_rows[:, :, None]).astype(jnp.bfloat16)
    correction = jnp.sum(d_attn * attended, axis=2) / totals_rows
    zero_rows = jnp.zeros((rows, heads, HEAD_DIM), jnp.float32)

    def back_step(d_query, parts):
        key_part, value_part, part_place = parts
        exponent, d_raw = score_grads(
            query3, scaled, correction, query_place, key_part, value_part, part_place
        )
        d_query = d_query + jnp.einsum(
            "hqk,khd->qhd", d_raw, key_part, preferred_element_type=jnp.float32
        )
        d_key = jnp.einsum("hqk,qhd->khd", d_raw, query3, preferred_element_type=jnp.float32)
        d_value = jnp.einsum(
            "hqk,qhd->khd",
            exponent.astype(jnp.bfloat16),
            scaled,
            preferred_element_type=jnp.float32,
        )
        return (d_query, (d_key, d_value))

    d_query, (key_terms, value_terms) = lax.scan(
        back_step, zero_rows, (key_blocks, value_blocks, place_blocks)
    )
    d_keys, d_values = (
        lax.psum_scatter(key_terms.reshape(-1, width), "ctx", scatter_dimension=0, tiled=True),
        lax.psum_scatter(value_terms.reshape(-1, width), "ctx", scatter_dimension=0, tiled=True),
    )
    grad_query = d_query.reshape(rows, width).astype(jnp.bfloat16)
    grad_keys = d_keys.astype(jnp.bfloat16)
    grad_values = d_values.astype(jnp.bfloat16)
    grad_qkv = jnp.concatenate([grad_query, grad_keys, grad_values], axis=1)
    d_qkv = inner_rows(act1, grad_qkv)
    d_qv_bias = jnp.concatenate(
        [
            jnp.sum(grad_query.astype(jnp.float32), axis=0),
            jnp.sum(grad_values.astype(jnp.float32), axis=0),
        ]
    )
    d_act1 = times_transpose(grad_qkv, w_qkv)
    d_input_norm, d_gain1, d_shift1 = ln1_back(d_act1)
    input_grad = d_mid + d_input_norm
    attn_owned = (
        lax.psum_scatter(d_gain1, "fsdp", scatter_dimension=0, tiled=True),
        lax.psum_scatter(d_shift1, "fsdp", scatter_dimension=0, tiled=True),
        lax.psum_scatter(d_qkv, "fsdp", scatter_dimension=0, tiled=True),
        lax.psum_scatter(d_qv_bias, "fsdp", scatter_dimension=0, tiled=True),
        lax.psum_scatter(d_out, "fsdp", scatter_dimension=0, tiled=True),
        lax.psum_scatter(d_out_bias, "fsdp", scatter_dimension=0, tiled=True),
    )
    attn_total = lax.psum(
        (attn_owned[0], attn_owned[1], attn_owned[2], attn_owned[3], attn_owned[4], attn_owned[5]),
        "ctx",
    )
    return (
        result[None],
        input_grad[None],
        attn_total[0],
        attn_total[1],
        attn_total[2],
        attn_total[3],
        attn_total[4],
        attn_total[5],
        mlp_total[0],
        mlp_total[1],
        mlp_total[2],
        mlp_total[3],
        mlp_total[4],
        mlp_total[5],
    )


def solution(mesh):
    return jax.shard_map(
        on_device,
        mesh=mesh,
        in_specs=(
            P("fsdp", "ctx", None),
            P("fsdp"),
            P("fsdp"),
            P("fsdp", None),
            P("fsdp"),
            P("fsdp", None),
            P("fsdp"),
            P("fsdp"),
            P("fsdp"),
            P("fsdp", None),
            P("fsdp"),
            P("fsdp", None),
            P("fsdp"),
            P(),
            P("fsdp", "ctx", None),
        ),
        out_specs=(
            P("fsdp", "ctx", None),
            P("fsdp", "ctx", None),
            P("fsdp"),
            P("fsdp"),
            P("fsdp", None),
            P("fsdp"),
            P("fsdp", None),
            P("fsdp"),
            P("fsdp"),
            P("fsdp"),
            P("fsdp", None),
            P("fsdp"),
            P("fsdp", None),
            P("fsdp"),
        ),
        check_vma=False,
    )
```

profile of v0, /device:TPU:0, one launch (start us, length us, event | category | flops | bytes accessed | tf_op | source)
XLA Modules:
  0.0 3008.3 jit_solution(12149930245180257995)
XLA Ops:
  12.7 13.7 all-reduce.19
  27.1 84.4 %all-gather.7.cloned.1.call-done = bf16[1600,4800]{1,0:T(8,128)(2,1)} async-done(((bf16[400,4800]{1,0:T(8,128)(2,1)}), bf16[1600,4800]{1,0:T(8,128)(2,1)}) %all-gather.7.cloned.1.call-update) | async-done | bytes 15360016 | tf_op jit(solution)/shard_map/all_gather | solution.py:88
  111.4 10.6 fusion.98
  125.0 1.9 slice.33
  129.4 60.0 %all-gather.11.cloned.1.call-done = bf16[1024,1600]{0,1:T(8,128)(2,1)} async-done(((bf16[128,1600]{0,1:T(8,128)(2,1)}), bf16[1024,1600]{0,1:T(8,128)(2,1)}) %all-gather.11.cloned.1.call-update) | async-done | bytes 3276816 | tf_op jit(solution)/shard_map/all_gather | solution.py:108
  189.3 8.5 reshape.231
  197.8 4.4 copy.62
  202.3 52.1 %all-gather.9.cloned.1.call-done = bf16[1024,1600]{0,1:T(8,128)(2,1)} async-done(((bf16[128,1600]{0,1:T(8,128)(2,1)}), bf16[1024,1600]{0,1:T(8,128)(2,1)}) %all-gather.9.cloned.1.call-update) | async-done | bytes 3276816 | tf_op jit(solution)/shard_map/all_gather | solution.py:107
  254.3 8.5 reshape.229
  262.9 4.9 copy.61
  267.8 12.9 while.28
  267.9 3.3 fusion.152
  271.3 2.9 fusion.153
  274.3 3.3 fusion.152
  277.6 2.9 fusion.153
  280.8 14.0 all-gather.13.cloned.1.call-done
  294.8 4.8 fusion.106
  299.9 125.3 %all-gather.15.cloned.1.call-done = bf16[1600,6400]{1,0:T(8,128)(2,1)} async-done(((bf16[400,6400]{1,0:T(8,128)(2,1)}), bf16[1600,6400]{1,0:T(8,128)(2,1)}) %all-gather.15.cloned.1.call-update) | async-done | bytes 20480016 | tf_op jit(solution)/shard_map/all_gather | solution.py:136
  425.2 12.2 convolution_add_fusion
  437.4 122.6 %all-gather.17.cloned.1.call-done = bf16[6400,1600]{1,0:T(8,128)(2,1)} async-done(((bf16[1600,1600]{1,0:T(8,128)(2,1)}), bf16[6400,1600]{1,0:T(8,128)(2,1)}) %all-gather.17.cloned.1.call-update) | async-done | bytes 20480016 | tf_op jit(solution)/shard_map/all_gather | solution.py:138
  560.0 11.9 convert_reduce_fusion
  572.0 12.7 multiply_reduce_fusion
  586.0 1.6 fusion.108
  588.6 281.8 %while.29 = (s32[]{:T(128)}, f32[128,25,64]{0,2,1:T(8,128)}, f32[2,512,25,64]{1,0,3,2:T(2,128)}, f32[2,512,25,64]{1,0,3,2:T(2,128)}, bf16[2,512,25,64]{1,3,2,0:T...) while((s32[]{:T(128)}, f32[128,25,64]{0,2,1:T(8,128)}, ...), condition=%wide.region_12.13_spmd.clone, body=%wide.region_11.12_spmd.clone.sunk | while | flops 1063796736 | bytes 77221088 | solution.py:200
  589.2 2.6 fusion.164
  591.8 4.0 fusion.165
  595.8 2.3 fusion.167
  598.1 3.4 copy.102
  601.6 2.6 fusion.166
  604.2 2.5 convolution_bitcast_fusion.2
  606.8 5.1 copy.101
  611.9 59.0 %dynamic_update_slice.11 = f32[2,512,25,64]{1,0,3,2:T(2,128)} dynamic-update-slice(f32[2,512,25,64]{1,0,3,2:T(2,128)} %get-tuple-element.526, f32[1,512,25,64]{1,0,3,2:T(1,128)} %copy.101, s32[]{:T(128)S(6)} %copy.126, s32[]{:T(128)} %constant.73.clone.1..sunk.1, s32[]{:T(128)} %constant.73.clone.1..sunk.1, s32[]{:T(128)} %constant.73.clone.1..sunk.1) | dynamic-update-slice | bytes 6553604 | tf_op jit(solution)/shard_map/while/body/jit(dynamic_update_index_in_dim)/dynamic_update_slice | solution.py:200
  670.9 58.8 %dynamic_update_slice.12 = f32[2,512,25,64]{1,0,3,2:T(2,128)} dynamic-update-slice(f32[2,512,25,64]{1,0,3,2:T(2,128)} %get-tuple-element.527, f32[1,512,25,64]{1,0,3,2:T(1,128)S(1)} %copy.102, s32[]{:T(128)S(6)} %copy.126, s32[]{:T(128)} %constant.73.clone.1..sunk.1, s32[]{:T(128)} %constant.73.clone.1..sunk.1, s32[]{:T(128)} %constant.73.clone.1..sunk.1) | dynamic-update-slice | bytes 6553604 | tf_op jit(solution)/shard_map/while/body/jit(dynamic_update_index_in_dim)/dynamic_update_slice | solution.py:200
  729.8 2.6 fusion.164
  732.4 4.0 fusion.165
  736.4 2.3 fusion.167
  738.7 3.4 copy.102
  742.2 2.6 fusion.166
  744.8 2.5 convolution_bitcast_fusion.2
  747.4 5.1 copy.101
  752.5 59.0 %dynamic_update_slice.11 = f32[2,512,25,64]{1,0,3,2:T(2,128)} dynamic-update-slice(f32[2,512,25,64]{1,0,3,2:T(2,128)} %get-tuple-element.526, f32[1,512,25,64]{1,0,3,2:T(1,128)} %copy.101, s32[]{:T(128)S(6)} %copy.126, s32[]{:T(128)} %constant.73.clone.1..sunk.1, s32[]{:T(128)} %constant.73.clone.1..sunk.1, s32[]{:T(128)} %constant.73.clone.1..sunk.1) | dynamic-update-slice | bytes 6553604 | tf_op jit(solution)/shard_map/while/body/jit(dynamic_update_index_in_dim)/dynamic_update_slice | solution.py:200
  811.5 58.8 %dynamic_update_slice.12 = f32[2,512,25,64]{1,0,3,2:T(2,128)} dynamic-update-slice(f32[2,512,25,64]{1,0,3,2:T(2,128)} %get-tuple-element.527, f32[1,512,25,64]{1,0,3,2:T(1,128)S(1)} %copy.102, s32[]{:T(128)S(6)} %copy.126, s32[]{:T(128)} %constant.73.clone.1..sunk.1, s32[]{:T(128)} %constant.73.clone.1..sunk.1, s32[]{:T(128)} %constant.73.clone.1..sunk.1) | dynamic-update-slice | bytes 6553604 | tf_op jit(solution)/shard_map/while/body/jit(dynamic_update_index_in_dim)/dynamic_update_slice | solution.py:200
  870.4 7.2 copy.95
  877.7 7.3 copy.96
  886.2 5.7 fusion.107
  893.3 106.7 %reduce-scatter.7.cloned.1.call-done = f32[128,1600]{0,1:T(8,128)} async-done(((f32[1024,1600]{0,1:T(8,128)}), f32[128,1600]{0,1:T(8,128)}) %reduce-scatter.7.cloned.1.call-update) | async-done | bytes 819216 | tf_op jit(solution)/shard_map/reduce_scatter | solution.py:204
  1001.2 124.4 %reduce-scatter.9.cloned.1.call-done = f32[128,1600]{0,1:T(8,128)} async-done(((f32[1024,1600]{0,1:T(8,128)}), f32[128,1600]{0,1:T(8,128)}) %reduce-scatter.9.cloned.1.call-update) | async-done | bytes 819216 | tf_op jit(solution)/shard_map/reduce_scatter | solution.py:205
  1127.1 17.7 fusion.81
  1146.6 17.3 fusion.100
  1164.9 18.8 fusion.83
  1184.8 9.8 fusion.101
  1195.8 1.9 convert_reduce_fusion.1
  1197.8 15.6 reduce-scatter.13.cloned.1.call-done
  1213.5 224.2 %reduce-scatter.11.cloned.1.call-done = f32[400,4800]{1,0:T(8,128)} async-done(((f32[1600,4800]{1,0:T(8,128)}), f32[400,4800]{1,0:T(8,128)}) %reduce-scatter.11.cloned.1.call-update) | async-done | bytes 7680016 | tf_op jit(solution)/shard_map/reduce_scatter | solution.py:224
  1437.6 295.6 %reduce-scatter.15.cloned.1.call-done = f32[400,6400]{1,0:T(8,128)} async-done(((f32[1600,6400]{1,0:T(8,128)}), f32[400,6400]{1,0:T(8,128)}) %reduce-scatter.15.cloned.1.call-update) | async-done | bytes 10240016 | tf_op jit(solution)/shard_map/reduce_scatter | solution.py:166
  1733.3 289.2 %reduce-scatter.17.cloned.1.call-done = f32[1600,1600]{1,0:T(8,128)} async-done(((f32[6400,1600]{1,0:T(8,128)}), f32[1600,1600]{1,0:T(8,128)}) %reduce-scatter.17.cloned.1.call-update) | async-done | bytes 10240016 | tf_op jit(solution)/shard_map/reduce_scatter | solution.py:168
  2024.4 14.6 fusion.65
  2039.0 19.7 all-reduce.25.cloned.1.call-done
  2065.0 39.9 %all-reduce.16 = (f32[400]{0:T(512)}, f32[400]{0:T(512)}, f32[800]{0:T(1024)}, f32[400]{0:T(512)}, f32[400]{0:T(512)}, /*index=5*/f32[400]{0:T(512)}, f32[1600]{0:T(1024)}, f32[400]{0:T(512)}) all-reduce(f32[400]{0:T(512)S(1)} %dynamic-slice.9, f32[400]{0:T(512)S(1)} %dynamic-slice.11, ...), channel_id=1, replica_groups=mesh['ctx'=8,'fsdp'=4] {'ctx'}, use_global_device_ids=true, to_apply=%region_19.20 | all-reduce | flops 4800 | bytes 38400 | tf_op jit(solution)/shard_map/psum | solution.py:229
  2104.9 874.7 %all-reduce.23.cloned.1.call-done = (f32[400,4800]{1,0:T(8,128)}, f32[400,1600]{1,0:T(8,128)}, f32[400,6400]{1,0:T(8,128)}, f32[1600,1600]{1,0:T(8,128)}) async-done(((f32[400,4800]{1,0:T(8,128)}, f32[400,1600]{1,0:T(8,128)}, f32[400,6400]{1,0:T(8,128)}, f32[1600,1600]{1,0:T(8,128)}), (f32[400,4800]{1,0:T(8,128)}, f32[400,1600]{1,0:T(8,128)}, f32[400,6400]{1,0:T(8,128)}, ...) | async-done | bytes 30720016 | tf_op jit(solution)/shard_map/psum | solution.py:229
  2979.6 7.1 copy.146
  2986.6 1.5 copy.147
  2988.1 9.3 copy.148
  2997.4 4.1 copy.149
  (222 shorter events, 29.0 us)
Async XLA Ops:
  7.2 3.4 copy-start.39
  7.2 3.7 copy-start.40
  7.2 3.9 copy-start.41
  7.2 4.2 copy-start.42
  7.2 4.4 copy-start.43
  7.2 4.7 copy-start.44
  7.3 4.9 copy-start.38
  7.3 5.2 copy-start.34
  7.3 19.2 copy-start.5
  7.3 104.1 %all-gather.7.cloned.1.call-start = ((), (), s32[]{:S(2)}) async-start(), calls=%async_computation.6 | async-start | bytes 19456000 | tf_op jit(solution)/shard_map/all_gather | solution.py:88
  8.0 181.3 %all-gather.11.cloned.1.call-start = ((), (), s32[]{:S(2)}) async-start(), calls=%async_computation.8 | async-start | bytes 3686400 | tf_op jit(solution)/shard_map/all_gather | solution.py:108
  26.5 95.6 %copy-start.25 = (f32[1600]{0:T(1024)}, f32[1600]{0:T(1024)S(1)}, u32[]{:S(2)}) copy-start(f32[1600]{0:T(1024)S(1)} %convert_element_type.104) | copy-start | bytes 19204
  26.5 95.6 %copy-start.23 = (f32[1600]{0:T(1024)}, f32[1600]{0:T(1024)S(1)}, u32[]{:S(2)}) copy-start(f32[1600]{0:T(1024)S(1)} %convert_element_type.103) | copy-start | bytes 19204
  26.7 95.3 %copy-start.29 = (f32[128]{0:T(128)}, f32[128]{0:T(128)S(1)}, u32[]{:S(2)}) copy-start(f32[128]{0:T(128)S(1)} %broadcast_multiply_fusion.1) | copy-start | bytes 1540
  27.0 95.1 %copy-start.45 = (f32[128]{0:T(128)}, f32[128]{0:T(128)S(1)}, u32[]{:S(2)}) copy-start(f32[128]{0:T(128)S(1)} %fusion.76) | copy-start | bytes 1540
  27.0 95.1 %copy-start.31 = (f32[128]{0:T(128)}, f32[128]{0:T(128)S(1)}, u32[]{:S(2)}) copy-start(f32[128]{0:T(128)S(1)} %fusion.93) | copy-start | bytes 1540
  122.1 1.4 copy-start.9
  124.9 129.4 %all-gather.9.cloned.1.call-start = ((), (), s32[]{:S(2)}) async-start(), calls=%async_computation.7 | async-start | bytes 3686400 | tf_op jit(solution)/shard_map/all_gather | solution.py:107
  126.9 167.9 %all-gather.13.cloned.1.call-start = ((), (), s32[]{:S(2)}) async-start(), calls=%async_computation.9 | async-start | bytes 6656000 | tf_op jit(solution)/shard_map/all_gather | solution.py:90
  127.5 297.7 %all-gather.15.cloned.1.call-start = ((), (), s32[]{:S(2)}) async-start(), calls=%async_computation.10 | async-start | bytes 25600000 | tf_op jit(solution)/shard_map/all_gather | solution.py:136
  128.1 431.9 %all-gather.17.cloned.1.call-start = ((), (), s32[]{:S(2)}) async-start(), calls=%async_computation.11 | async-start | bytes 26624000 | tf_op jit(solution)/shard_map/all_gather | solution.py:138
  128.7 871.3 %reduce-scatter.7.cloned.1.call-start = ((), (), s32[]{:S(2)}) async-start(), calls=%async_computation.12 | async-start | bytes 7372800 | tf_op jit(solution)/shard_map/reduce_scatter | solution.py:204
  129.1 296.0 %copy-start.27 = (f32[1600]{0:T(1024)}, f32[1600]{0:T(1024)S(1)}, u32[]{:S(2)}) copy-start(f32[1600]{0:T(1024)S(1)} %convert_element_type.113) | copy-start | bytes 19204
  280.8 18.8 copy-start.12
  299.6 285.1 %copy-start = (f32[128,1600]{0,1:T(8,128)}, f32[128,1600]{0,1:T(8,128)S(1)}, u32[]{:S(2)}) copy-start(f32[128,1600]{0,1:T(8,128)S(1)} %get-tuple-element.354) | copy-start | bytes 2457604
  299.9 260.2 %copy-start.14 = (bf16[1,128,1600]{1,2,0:T(8,128)(2,1)S(1)}, bf16[1,128,1600]{1,2,0:T(8,128)(2,1)}, u32[]{:S(2)}) copy-start(bf16[1,128,1600]{1,2,0:T(8,128)(2,1)} %param.33) | copy-start | bytes 1228804
  572.0 12.7 copy-start.7
  572.0 14.0 slice-start
  572.0 14.0 slice-start.1
  585.0 2.5 copy-start.10
  585.1 2.5 copy-start.35
  586.0 1.6 copy-start.16
  598.1 3.4 copy-start.2
  604.2 2.6 copy-start.3
  738.7 3.4 copy-start.2
  744.8 2.6 copy-start.3
  877.7 247.9 %reduce-scatter.9.cloned.1.call-start = ((), (), s32[]{:S(2)}) async-start(), calls=%async_computation.13 | async-start | bytes 7372800 | tf_op jit(solution)/shard_map/reduce_scatter | solution.py:205
  885.0 1.2 copy-start.17
  885.0 328.4 %reduce-scatter.13.cloned.1.call-start = ((), (), s32[]{:S(2)}) async-start(), calls=%async_computation.15 | async-start | bytes 13312000 | tf_op jit(solution)/shard_map/reduce_scatter | solution.py:226
  891.9 1.2 copy-start.4
  891.9 235.2 %copy-start.6 = (bf16[1,128,1600]{1,2,0:T(8,128)(2,1)S(1)}, bf16[1,128,1600]{1,2,0:T(8,128)(2,1)}, u32[]{:S(2)}) copy-start(bf16[1,128,1600]{1,2,0:T(8,128)(2,1)} %param.19) | copy-start | bytes 1228804
  891.9 235.2 %copy-start.24 = (f32[1600]{0:T(1024)S(1)}, f32[1600]{0:T(1024)}, u32[]{:S(2)}) copy-start(f32[1600]{0:T(1024)} %copy-done.23) | copy-start | bytes 19204
  891.9 235.2 %copy-start.26 = (f32[1600]{0:T(1024)S(1)}, f32[1600]{0:T(1024)}, u32[]{:S(2)}) copy-start(f32[1600]{0:T(1024)} %copy-done.25) | copy-start | bytes 19204
  891.9 235.2 %copy-start.30 = (f32[128]{0:T(128)S(1)}, f32[128]{0:T(128)}, u32[]{:S(2)}) copy-start(f32[128]{0:T(128)} %copy-done.29) | copy-start | bytes 1540
  891.9 235.2 %copy-start.32 = (f32[128]{0:T(128)S(1)}, f32[128]{0:T(128)}, u32[]{:S(2)}) copy-start(f32[128]{0:T(128)} %copy-done.31) | copy-start | bytes 1540
  891.9 545.7 %reduce-scatter.11.cloned.1.call-start = ((), (), s32[]{:S(2)}) async-start(), calls=%async_computation.14 | async-start | bytes 38912000 | tf_op jit(solution)/shard_map/reduce_scatter | solution.py:224
  1001.2 143.6 %copy-start.19 = (bf16[128,1600]{0,1:T(8,128)(2,1)}, bf16[128,1600]{0,1:T(8,128)(2,1)S(1)}, u32[]{:S(2)}) copy-start(bf16[128,1600]{0,1:T(8,128)(2,1)S(1)} %convert_element_type.124) | copy-start | bytes 1228804
  1127.1 17.7 copy-start.21
  1144.8 1.2 copy-start.1
  1144.8 1.8 copy-start.8
  1144.8 1.8 copy-start.28
  1144.9 588.4 %reduce-scatter.15.cloned.1.call-start = ((), (), s32[]{:S(2)}) async-start(), calls=%async_computation.16 | async-start | bytes 51200000 | tf_op jit(solution)/shard_map/reduce_scatter | solution.py:166
  1163.9 858.6 %reduce-scatter.17.cloned.1.call-start = ((), (), s32[]{:S(2)}) async-start(), calls=%async_computation.17 | async-start | bytes 53248000 | tf_op jit(solution)/shard_map/reduce_scatter | solution.py:168
  1183.7 1.1 copy-start.22
  1183.7 875.1 %all-reduce.25.cloned.1.call-start = ((), (), s32[]{:S(2)}) async-start(), calls=%async_computation.19 | async-start | bytes 188416
  1184.8 9.8 copy-start.46
  1184.8 11.0 copy-start.11
  1184.8 11.0 copy-start.36
  1197.8 1781.8 %all-reduce.23.cloned.1.call-start = ((), (), s32[]{:S(2)}) async-start(), calls=%async_computation.18 | async-start | bytes 62668800 | tf_op jit(solution)/shard_map/psum | solution.py:229
  2022.4 2.0 copy-start.33
  2979.6 7.1 copy-start.18
  2986.6 10.8 slice-start.2
  2988.1 9.3 slice-start.3
  2988.1 9.3 slice-start.4
  (5 other events, 4.8 us)
Sparse Core Ops, SparseCore 0:
  9.7 101.7 all-gather.6
  125.0 64.2 all-gather.10
  192.0 62.3 all-gather.8
  255.7 39.0 all-gather.12
  296.3 128.8 all-gather.14
  426.6 133.3 all-gather.16
  877.8 122.1 reduce-scatter.6
  1004.2 121.3 reduce-scatter.8
  1128.8 84.6 reduce-scatter.12
  1215.9 221.6 reduce-scatter.10
  1440.3 292.9 reduce-scatter.14
  1735.7 286.6 reduce-scatter.16
  2026.4 32.3 all-reduce.24
  2063.5 916.0 all-reduce.22
where the time goes:
time: 3030 us; the launch traced here: 3010 us
  waiting for transfers between devices  2410 us (80%)
  local copies, waits for them, and re-layouts  333 us (11%)
  matrix products  178 us (6%)
  blocking collectives  53.7 us (2%)
    psum x1, waiting for transfers between devices, on_device(): lax.psum((attn_owned[0], attn_owned[1], attn_owned[2], attn_owned[3], att...  875 us
    reduce_scatter x1, waiting for transfers between devices, on_device(): lax.psum_scatter(d_up, 'fsdp', scatter_dimension=0, tiled=True)  296 us
    reduce_scatter x1, waiting for transfers between devices, on_device(): lax.psum_scatter(d_down, 'fsdp', scatter_dimension=0, tiled=True)  289 us
    dynamic_update_slice x8, local copies, waits for them, and re-layouts, on_device(): lax.scan(back_step, zero_rows, (key_blocks, value_blocks, place_blocks))  253 us
    reduce_scatter x1, waiting for transfers between devices, on_device(): lax.psum_scatter(d_qkv, 'fsdp', scatter_dimension=0, tiled=True)  224 us
    all_gather x1, waiting for transfers between devices, on_device(): lax.all_gather(up_weight, 'fsdp', axis=0, tiled=True)  125 us
    reduce_scatter x1, waiting for transfers between devices, on_device(): lax.psum_scatter(value_terms.reshape(-1, width), 'ctx', scatter_dimension...  124 us
    all_gather x1, waiting for transfers between devices, on_device(): lax.all_gather(down_weight, 'fsdp', axis=0, tiled=True)  123 us
  transfers between devices with their start and end apart: 14, of which 14 were waited for; matrix products, arithmetic and copies ran while one was open for 6% of the time, Pallas kernels for 0%

commit v1 on v0

v1 whole, which is shorter than its diff:
```python
import functools

import jax
import jax.numpy as jnp
from jax import lax
from jax.experimental import pallas as pl
from jax.experimental.pallas import tpu as pltpu
from jax.sharding import PartitionSpec as P

HEAD_DIM = 64
EPS = 1e-05
SCALE = 0.125
F32 = jnp.float32
BF16 = jnp.bfloat16


def dot(left, right):
    return jnp.dot(left, right, preferred_element_type=F32)


def dot_t(left, right):
    return lax.dot_general(left, right, (((1,), (1,)), ((), ())), preferred_element_type=F32)


def t_dot(left, right):
    return lax.dot_general(left, right, (((0,), (0,)), ((), ())), preferred_element_type=F32)


def ln_stats(value):
    centre = value - jnp.mean(value, axis=-1, keepdims=True)
    spread = jnp.mean(centre * centre, axis=-1, keepdims=True)
    rstd = lax.rsqrt(spread + EPS)
    return centre * rstd, rstd


def ln_back(grad, normed, rstd, gain):
    dn = grad * gain
    first = jnp.mean(dn, axis=-1, keepdims=True)
    second = jnp.mean(dn * normed, axis=-1, keepdims=True)
    return (dn - first - normed * second) * rstd


def attn_fwd_body(slots, qp_ref, kp_ref, q_ref, k_ref, v_ref, attn_ref, o_ref, l_ref):
    allowed = kp_ref[...] <= qp_ref[...]
    for h in range(slots):
        cols = slice(h * HEAD_DIM, (h + 1) * HEAD_DIM)
        raw = dot_t(q_ref[:, cols], k_ref[:, cols])
        e = jnp.where(allowed, jnp.exp(raw * SCALE), 0.0)
        total = jnp.sum(e, axis=1, keepdims=True)
        numer = dot(e.astype(BF16), v_ref[:, cols])
        o = numer / total
        o_ref[:, cols] = o
        attn_ref[:, cols] = o.astype(BF16)
        l_ref[:, h : h + 1] = total


def attn_bwd_body(
    slots, qp_ref, kp_ref, q_ref, k_ref, v_ref, do_ref, o_ref, l_ref, dq_ref, dk_ref, dv_ref, dk_acc, dv_acc
):
    step = pl.program_id(0)

    @pl.when(step == 0)
    def _():
        dk_acc[...] = jnp.zeros_like(dk_acc)
        dv_acc[...] = jnp.zeros_like(dv_acc)

    allowed = kp_ref[...] <= qp_ref[...]
    for h in range(slots):
        cols = slice(h * HEAD_DIM, (h + 1) * HEAD_DIM)
        q = q_ref[:, cols]
        k = k_ref[:, cols]
        v = v_ref[:, cols]
        do = do_ref[:, cols]
        total = l_ref[:, h : h + 1]
        w = (do / total).astype(BF16)
        corr = jnp.sum(do * o_ref[:, cols], axis=1, keepdims=True) / total
        e = jnp.where(allowed, jnp.exp(dot_t(q, k) * SCALE), 0.0)
        de = dot_t(w, v)
        ds = (e * (de - corr)).astype(BF16)
        dq_ref[:, cols] = (dot(ds, k) * SCALE).astype(BF16)
        dk_acc[:, cols] += t_dot(ds, q)
        dv_acc[:, cols] += t_dot(e.astype(BF16), w)

    @pl.when(step == pl.num_programs(0) - 1)
    def _():
        dk_ref[...] = (dk_acc[...] * SCALE).astype(BF16)
        dv_ref[...] = dv_acc[...].astype(BF16)


def attn_specs(rows, wide, slots):
    qb = 256 if rows <= 1024 else 128
    q_spec = pl.BlockSpec((qb, wide), lambda i: (i, 0))
    l_spec = pl.BlockSpec((qb, slots), lambda i: (i, 0))
    all_spec = pl.BlockSpec((rows, wide), lambda i: (0, 0))
    qp_spec = pl.BlockSpec((qb, 1), lambda i: (i, 0))
    kp_spec = pl.BlockSpec((1, rows), lambda i: (0, 0))
    return rows // qb, q_spec, l_spec, all_spec, qp_spec, kp_spec


def attention_fwd(place, q, k, v, slots):
    rows, wide = q.shape
    steps, q_spec, l_spec, all_spec, qp_spec, kp_spec = attn_specs(rows, wide, slots)
    return pl.pallas_call(
        functools.partial(attn_fwd_body, slots),
        grid=(steps,),
        in_specs=[qp_spec, kp_spec, q_spec, all_spec, all_spec],
        out_specs=[q_spec, q_spec, l_spec],
        out_shape=[
            jax.ShapeDtypeStruct((rows, wide), BF16),
            jax.ShapeDtypeStruct((rows, wide), F32),
            jax.ShapeDtypeStruct((rows, slots), F32),
        ],
        name="attn_fwd",
        cost_estimate=pl.CostEstimate(
            flops=4 * rows * rows * wide, bytes_accessed=16 * rows * wide, transcendentals=rows * rows * slots
        ),
        compiler_params=pltpu.CompilerParams(vmem_limit_bytes=60 * 2**20),
    )(place.reshape(rows, 1), place.reshape(1, rows), q, k, v)


def attention_bwd(place, q, k, v, do, o, total, slots):
    rows, wide = q.shape
    steps, q_spec, l_spec, all_spec, qp_spec, kp_spec = attn_specs(rows, wide, slots)
    shape = jax.ShapeDtypeStruct((rows, wide), BF16)
    return pl.pallas_call(
        functools.partial(attn_bwd_body, slots),
        grid=(steps,),
        in_specs=[qp_spec, kp_spec, q_spec, all_spec, all_spec, q_spec, q_spec, l_spec],
        out_specs=[q_spec, all_spec, all_spec],
        out_shape=[shape, shape, shape],
        scratch_shapes=[pltpu.VMEM((rows, wide), F32), pltpu.VMEM((rows, wide), F32)],
        name="attn_bwd",
        cost_estimate=pl.CostEstimate(
            flops=10 * rows * rows * wide, bytes_accessed=24 * rows * wide, transcendentals=rows * rows * slots
        ),
        compiler_params=pltpu.CompilerParams(vmem_limit_bytes=60 * 2**20),
    )(place.reshape(rows, 1), place.reshape(1, rows), q, k, v, do, o, total)


def ag_ctx(value):
    return lax.all_gather(value, "ctx", axis=0, tiled=True)


def rs_ctx(value):
    return lax.psum_scatter(value.astype(BF16), "ctx", scatter_dimension=0, tiled=True)


def ag_fsdp(value):
    return lax.all_gather(value, "fsdp", axis=0, tiled=True)


def rs_fsdp(value):
    return lax.psum_scatter(value.astype(BF16), "fsdp", scatter_dimension=0, tiled=True)


def head_columns(value, width, c, n):
    heads = width // HEAD_DIM
    base, rest = divmod(heads, n)
    parts = []
    if base:
        parts.append(lax.dynamic_slice_in_dim(value, c * base * HEAD_DIM, base * HEAD_DIM, axis=-1))
    if rest:
        start = jnp.minimum(base * n + c, heads - 1) * HEAD_DIM
        extra = lax.dynamic_slice_in_dim(value, start, HEAD_DIM, axis=-1)
        parts.append(jnp.where(c < rest, extra, jnp.zeros_like(extra)))
    return jnp.concatenate(parts, axis=-1)


def spread_heads(value, heads, n):
    base, rest = divmod(heads, n)
    rows = value.shape[1]
    parts = []
    if base:
        body = value[:, :, : base * HEAD_DIM]
        parts.append(jnp.transpose(body, (1, 0, 2)).reshape(rows, n * base * HEAD_DIM))
    if rest:
        tail = value[:rest, :, base * HEAD_DIM :]
        parts.append(jnp.transpose(tail, (1, 0, 2)).reshape(rows, rest * HEAD_DIM))
    return jnp.concatenate(parts, axis=1)


def place_heads(value, heads, c, n):
    base, rest = divmod(heads, n)
    out = jnp.zeros((heads * HEAD_DIM,), value.dtype)
    if rest:
        start = jnp.minimum(base * n + c, heads - 1) * HEAD_DIM
        extra = jnp.where(c < rest, value[base * HEAD_DIM :], 0.0)
        out = lax.dynamic_update_slice(out, extra, (start,))
    if base:
        out = lax.dynamic_update_slice(out, value[: base * HEAD_DIM], (c * base * HEAD_DIM,))
    return out


def head_rows(value, heads, c, f, n):
    base, rest = divmod(heads, n)
    local, width = value.shape
    pad = max(base, 1) * HEAD_DIM
    padded = jnp.pad(value, ((pad, pad), (0, 0)))
    parts = []
    if base:
        start = jnp.clip(c * base * HEAD_DIM - f * local + pad, 0, local + 2 * pad - base * HEAD_DIM)
        parts.append(lax.dynamic_slice_in_dim(padded, start, base * HEAD_DIM, axis=0))
    if rest:
        start = jnp.clip((base * n + c) * HEAD_DIM - f * local + pad, 0, local + 2 * pad - HEAD_DIM)
        extra = lax.dynamic_slice_in_dim(padded, start, HEAD_DIM, axis=0)
        parts.append(jnp.where(c < rest, extra, jnp.zeros_like(extra)))
    return jnp.concatenate(parts, axis=0)


def on_device(
    tokens,
    ln1_gain,
    ln1_shift,
    qkv_weight,
    qv_bias,
    out_weight,
    out_bias,
    ln2_gain,
    ln2_shift,
    up_weight,
    up_bias,
    down_weight,
    down_bias,
    block_table,
    cotangent,
):
    rows, width = tokens.shape[1:]
    heads = width // HEAD_DIM
    n = lax.axis_size("ctx")
    nf = lax.axis_size("fsdp")
    c = lax.axis_index("ctx")
    f = lax.axis_index("fsdp")
    slots = -(-heads // n)
    wide = slots * HEAD_DIM
    half = rows // 2
    local = width // nf
    ff = up_weight.shape[1]
    ff_local = ff // nf
    ff_part = ff_local // n

    within = jnp.arange(rows, dtype=jnp.int32)
    block_of = jnp.where(within[None, :] < half, block_table[:, None], 2 * n - 1 - block_table[:, None])
    place = (block_of * half + within[None, :] % half).reshape(-1)

    vectors = (ln1_gain, ln1_shift, qv_bias, out_bias, ln2_gain, ln2_shift, up_bias, down_bias)
    packed = lax.all_gather(jnp.concatenate(vectors), "fsdp", axis=0, tiled=False)
    full, at = [], 0
    for vector in vectors:
        size = vector.shape[0]
        full.append(packed[:, at : at + size].reshape(-1).astype(F32))
        at += size
    gain1, shift1, b_qv, b_out, gain2, shift2, b_up, b_down = full

    x_all = ag_ctx(tokens[0])
    q_w = head_columns(qkv_weight[:, :width], width, c, n)
    k_w = head_columns(qkv_weight[:, width : 2 * width], width, c, n)
    v_w = head_columns(qkv_weight[:, 2 * width :], width, c, n)
    w_qkv = ag_fsdp(jnp.concatenate([q_w, k_w, v_w], axis=1))
    w_out = lax.psum(head_rows(out_weight, heads, c, f, n), "fsdp")
    g2_all = ag_ctx(cotangent[0])
    up_mine = lax.dynamic_slice_in_dim(up_weight.reshape(local, nf, n, ff_part), c, 1, axis=2)
    w_up = ag_fsdp(up_mine.reshape(local, nf * ff_part))
    w_down = ag_fsdp(lax.dynamic_slice_in_dim(down_weight, c * ff_part, ff_part, axis=0))
    b_up_mine = lax.dynamic_slice_in_dim(b_up.reshape(nf, n, ff_part), c, 1, axis=1).reshape(-1)
    bq = head_columns(b_qv[:width], width, c, n)
    bv = head_columns(b_qv[width:], width, c, n)

    n1_all, _ = ln_stats(x_all.astype(F32))
    act1 = (n1_all * gain1 + shift1).astype(BF16)
    proj = dot(act1, w_qkv)
    q = (proj[:, :wide] + bq).astype(BF16)
    k = proj[:, wide : 2 * wide].astype(BF16)
    v = (proj[:, 2 * wide :] + bv).astype(BF16)
    attn, o, total = attention_fwd(place, q, k, v, slots)
    x = tokens[0].astype(F32)
    mid = x + rs_ctx(dot(attn, w_out)).astype(F32) + b_out
    attn_all = spread_heads(lax.all_gather(attn, "ctx", axis=0, tiled=False), heads, n)

    n2, rstd2 = ln_stats(mid)
    act2 = ag_ctx((n2 * gain2 + shift2).astype(BF16))
    u = dot(act2, w_up) + b_up_mine
    activated, gelu_back = jax.vjp(lambda t: jax.nn.gelu(t, approximate=True), u)
    hidden = activated.astype(BF16)
    dh = dot_t(g2_all, w_down)
    du = gelu_back(dh)[0].astype(BF16)
    da2 = rs_ctx(dot_t(du, w_up)).astype(F32)
    result = mid + rs_ctx(dot(hidden, w_down)).astype(F32) + b_down
    d_down = rs_fsdp(t_dot(hidden, g2_all))
    d_up = rs_fsdp(t_dot(act2, du))
    d_up_bias = jnp.sum(du.astype(F32), axis=0)
    grad_out = cotangent[0].astype(F32)
    d_down_bias = jnp.sum(grad_out, axis=0)
    d_down = lax.all_gather(d_down, "ctx", axis=0, tiled=True)
    d_up = lax.all_gather(d_up, "ctx", axis=0, tiled=False)

    d_gain2 = jnp.sum(da2 * n2, axis=0)
    d_shift2 = jnp.sum(da2, axis=0)
    d_mid = grad_out + ln_back(da2, n2, rstd2, gain2)
    g1 = d_mid.astype(BF16)
    d_out_bias = jnp.sum(g1.astype(F32), axis=0)
    g1_all = ag_ctx(g1)
    d_attn = dot_t(g1_all, w_out)
    gq, gk, gv = attention_bwd(place, q, k, v, d_attn, o, total, slots)
    g_qkv = jnp.concatenate([gq, gk, gv], axis=1)
    da1 = rs_ctx(dot_t(g_qkv, w_qkv)).astype(F32)
    d_qkv = rs_fsdp(t_dot(act1, g_qkv))
    out_part = width // n
    g1_mine = lax.dynamic_slice_in_dim(g1_all, c * out_part, out_part, axis=1)
    d_out = rs_fsdp(t_dot(attn_all, g1_mine))
    gathered = lax.all_gather(jnp.concatenate([d_qkv, d_out], axis=1), "ctx", axis=0, tiled=False)
    d_qkv_full = jnp.concatenate(
        [spread_heads(gathered[:, :, i * wide : (i + 1) * wide], heads, n) for i in range(3)], axis=1
    ).astype(F32)
    d_out_full = jnp.transpose(gathered[:, :, 3 * wide :], (1, 0, 2)).reshape(local, width).astype(F32)
    d_up_full = jnp.transpose(d_up.reshape(n, local, nf, ff_part), (1, 2, 0, 3)).reshape(local, ff).astype(F32)
    d_down_full = d_down.astype(F32)

    n1, rstd1 = ln_stats(x)
    d_gain1 = jnp.sum(da1 * n1, axis=0)
    d_shift1 = jnp.sum(da1, axis=0)
    input_grad = d_mid + ln_back(da1, n1, rstd1, gain1)

    dq_bias = place_heads(jnp.sum(gq.astype(F32), axis=0), heads, c, n)
    dv_bias = place_heads(jnp.sum(gv.astype(F32), axis=0), heads, c, n)
    up_placed = lax.dynamic_update_slice(
        jnp.zeros((nf, n, ff_part), F32), d_up_bias.reshape(nf, 1, ff_part), (0, c, 0)
    )
    smalls = (
        d_gain1,
        d_shift1,
        jnp.concatenate([dq_bias, dv_bias]),
        d_out_bias,
        d_gain2,
        d_shift2,
        up_placed.reshape(-1),
        d_down_bias,
    )
    packed = jnp.concatenate([s.reshape(nf, -1) for s in smalls], axis=1)
    summed = lax.psum(packed, ("ctx", "fsdp"))
    mine = lax.dynamic_slice_in_dim(summed, f, 1, axis=0)[0]
    out, at = [], 0
    for s in smalls:
        size = s.size // nf
        out.append(mine[at : at + size])
        at += size
    return (
        result[None],
        input_grad[None],
        out[0],
        out[1],
        d_qkv_full,
        out[2],
        d_out_full,
        out[3],
        out[4],
        out[5],
        d_up_full,
        out[6],
        d_down_full,
        out[7],
    )


def solution(mesh):
    rows, one, two = P("fsdp", "ctx", None), P("fsdp"), P("fsdp", None)
    return jax.shard_map(
        on_device,
        mesh=mesh,
        in_specs=(rows, one, one, two, one, two, one, one, one, two, one, two, one, P(), rows),
        out_specs=(rows, rows, one, one, two, one, two, one, one, one, two, one, two, one),
        check_vma=False,
    )
```

time: 3030 us -> 1430 us (0.47)
  waiting for transfers between devices: 2410 us -> 1060 us
  local copies, waits for them, and re-layouts: 333 us -> 185 us
  matrix products: 178 us -> 74.8 us
  blocking collectives: 53.7 us -> 13.6 us
    reduce_scatter x6 -> x3, waiting for transfers between devices: 1060 us -> 61.6 us  [rs_fsdp(): lax.psum_scatter(value.astype(BF16), 'fsdp', scatter_dimension=0, tiled=T...]
    psum x1 -> x2, waiting for transfers between devices: 875 us -> 136 us  [the longest x1 115 us: on_device(): summed = lax.psum(packed, ('ctx', 'fsdp'))]
    unnamed x15 -> x26, waiting for transfers between devices: 22.2 us -> 323 us
    dynamic_update_slice x8 -> x3, local copies, waits for them, and re-layouts: 253 us -> 0.23 us  [the longest x2 0.18 us: place_heads(): lax.dynamic_update_slice(out, value[:base * HEAD_DIM], (c * base * HEAD_D...]
    dot_general x26 -> x12, matrix products: 178 us -> 74.8 us  [the longest x4 27.7 us: t_dot(): lax.dot_general(left, right, (((0,), (0,)), ((), ())), preferred_element_...]
    all_gather x6 -> x11, waiting for transfers between devices: 458 us -> 545 us  [the longest x4 224 us: ag_ctx(): return lax.all_gather(value, 'ctx', axis=0, tiled=True)]
    convert_element_type x0 -> x12, local copies, waits for them, and re-layouts: none -> 58.1 us  [the longest x3 49.1 us: on_device(): jnp.transpose(d_up.reshape(n, local, nf, ff_part), (1, 2, 0, 3))]
    psum x1 -> x0, blocking collectives: 39.9 us -> none  [on_device(): lax.psum((attn_owned[0], attn_owned[1], attn_owned[2], attn_owned[3], att...]
  transfers between devices with their start and end apart: 14 -> 21, of which waited for: 14 -> 21; matrix products, arithmetic and copies ran while one was open for 6% -> 15% of each run, Pallas kernels for 0% -> 2%
where the time goes in v1:
time: 1430 us; the launch traced here: 1420 us
  waiting for transfers between devices  1060 us (74%)
  local copies, waits for them, and re-layouts  185 us (13%)
  matrix products  74.8 us (5%)
  other arithmetic  32.5 us (2%)
  Pallas kernels  27.3 us (2%)
  between operations  15.7 us (1%)
    unnamed x26, waiting for transfers between devices  323 us
    all_gather x4, waiting for transfers between devices, ag_ctx(): return lax.all_gather(value, 'ctx', axis=0, tiled=True)  224 us
    psum x1, waiting for transfers between devices, on_device(): summed = lax.psum(packed, ('ctx', 'fsdp'))  115 us
    all_gather x1, waiting for transfers between devices, on_device(): lax.all_gather(jnp.concatenate([d_qkv, d_out], axis=1), 'ctx', axis=0, ti...  102 us
    all_gather x1, waiting for transfers between devices, on_device(): d_up = lax.all_gather(d_up, 'ctx', axis=0, tiled=False)  92 us
    reduce_scatter x3, waiting for transfers between devices, rs_fsdp(): lax.psum_scatter(value.astype(BF16), 'fsdp', scatter_dimension=0, tiled=T...  61.6 us
    all_gather x3, waiting for transfers between devices, ag_fsdp(): return lax.all_gather(value, 'fsdp', axis=0, tiled=True)  60.5 us
    convert_element_type x3, local copies, waits for them, and re-layouts, on_device(): jnp.transpose(d_up.reshape(n, local, nf, ff_part), (1, 2, 0, 3))  49.1 us
  transfers between devices with their start and end apart: 21, of which 21 were waited for; matrix products, arithmetic and copies ran while one was open for 15% of the time, Pallas kernels for 2%

profile of v1, /device:TPU:0, one launch (start us, length us, event | category | flops | bytes accessed | tf_op | source)
XLA Modules:
  0.0 1416.1 jit_solution(10775627566787645909)
XLA Ops:
  8.0 2.8 fusion.67
  16.0 13.6 all-reduce.1
  31.7 45.2 %all-gather.30.cloned.1.call-done = bf16[1,1024,1600]{1,2,0:T(8,128)(2,1)} async-done(((bf16[1,128,1600]{1,2,0:T(8,128)(2,1)}), bf16[1,1024,1600]{1,2,0:T(8,128)(2,1)}) %all-gather.30.cloned.1.call-update) | async-done | bytes 3276816 | tf_op jit(solution)/shard_map/all_gather | solution.py:141
  76.9 2.7 convert_reduce_fusion
  80.8 21.1 %all-gather.18.cloned.1.call-done = bf16[1600,768]{1,0:T(8,128)(2,1)} async-done(((bf16[400,768]{1,0:T(8,128)(2,1)}), bf16[1600,768]{1,0:T(8,128)(2,1)}) %all-gather.18.cloned.1.call-update) | async-done | bytes 2457616 | tf_op jit(solution)/shard_map/all_gather | solution.py:149
  101.9 5.3 fusion.64
  109.3 9.8 attn_fwd.1
  119.0 21.2 %all-reduce.6.cloned.1.call-done = bf16[256,1600]{1,0:T(8,128)(2,1)} async-done(((bf16[256,1600]{1,0:T(8,128)(2,1)}), bf16[256,1600]{1,0:T(8,128)(2,1)}) %all-reduce.6.cloned.1.call-update) | async-done | bytes 819216 | tf_op jit(solution)/shard_map/psum | solution.py:259
  140.2 2.4 convolution_convert_fusion.3
  142.6 3.5 copy.86
  146.5 21.4 %reshape.320 = bf16[400,4,8,200]{3,2,1,0:T(8,128)(2,1)} reshape(bf16[400,6400]{1,0:T(8,128)(2,1)} %param.24) | data formatting | bytes 10240000 | tf_op jit(solution)/shard_map/reshape | solution.py:261
  167.8 8.6 dynamic-slice_reduce_fusion
  178.2 46.0 %reduce-scatter.25.cloned.1.call-done = bf16[128,1600]{1,0:T(8,128)(2,1)} async-done(((bf16[1024,1600]{1,0:T(8,128)(2,1)}), bf16[128,1600]{1,0:T(8,128)(2,1)}) %reduce-scatter.25.cloned.1.call-update) | async-done | bytes 409616
  227.9 2.0 constant_dynamic-slice_fusion.1
  231.6 20.9 %all-gather.22.cloned.1.call-done = bf16[1600,800]{1,0:T(8,128)(2,1)} async-done(((bf16[400,800]{1,0:T(8,128)(2,1)}), bf16[1600,800]{1,0:T(8,128)(2,1)}) %all-gather.22.cloned.1.call-update) | async-done | bytes 2560016 | tf_op jit(solution)/shard_map/all_gather | solution.py:149
  252.5 66.7 %all-gather.20.cloned.1.call-done = bf16[1024,1600]{0,1:T(8,128)(2,1)} async-done(((bf16[128,1600]{0,1:T(8,128)(2,1)}), bf16[1024,1600]{0,1:T(8,128)(2,1)}) %all-gather.20.cloned.1.call-update) | async-done | bytes 3276816 | tf_op jit(solution)/shard_map/all_gather | solution.py:141
  319.1 7.7 fusion.70
  326.8 18.4 %all-gather.24.cloned.1.call-done = bf16[800,1600]{1,0:T(8,128)(2,1)} async-done(((bf16[200,1600]{1,0:T(8,128)(2,1)}), bf16[800,1600]{1,0:T(8,128)(2,1)}) %all-gather.24.cloned.1.call-update) | async-done | bytes 2560016 | tf_op jit(solution)/shard_map/all_gather | solution.py:149
  345.2 66.2 %all-gather.32.cloned.1.call-done = bf16[1,1024,1600]{1,2,0:T(8,128)(2,1)} async-done(((bf16[1,128,1600]{1,2,0:T(8,128)(2,1)}), bf16[1,1024,1600]{1,2,0:T(8,128)(2,1)}) %all-gather.32.cloned.1.call-update) | async-done | bytes 3276816 | tf_op jit(solution)/shard_map/all_gather | solution.py:141
  411.5 8.2 convert_reduce_fusion.1
  419.7 4.9 convolution_convert_fusion
  424.7 5.4 copy.90
  430.4 76.0 %reduce-scatter.29.cloned.1.call-done = bf16[128,1600]{1,0:T(8,128)(2,1)} async-done(((bf16[1024,1600]{1,0:T(8,128)(2,1)}), bf16[128,1600]{1,0:T(8,128)(2,1)}) %reduce-scatter.29.cloned.1.call-update) | async-done | bytes 409616
  510.8 7.6 convolution_convert_fusion.4
  518.5 8.4 convolution_convert_fusion.5
  527.2 46.3 %all-gather.26.cloned.1.call-done = bf16[1024,1600]{0,1:T(8,128)(2,1)} async-done(((bf16[128,1600]{0,1:T(8,128)(2,1)}), bf16[1024,1600]{0,1:T(8,128)(2,1)}) %all-gather.26.cloned.1.call-update) | async-done | bytes 3276816 | tf_op jit(solution)/shard_map/all_gather | solution.py:141
  573.5 4.1 fusion.71.do_ref
  577.5 17.5 %attn_bwd.1 = (bf16[1024,256]{1,0:T(8,128)(2,1)}, bf16[1024,256]{1,0:T(8,128)(2,1)}, bf16[1024,256]{1,0:T(8,128)(2,1)}) custom-call(s32[1024,1]{1,0:T(8,128)} %copy.73.qp_ref, s32[1,1024]{1,0:T(1,128)} %bitcast.169, bf16[1024,256]{1,0:T(8,128)(2,1)} %get-tuple-element.47.q_ref, bf16[1024,256]{1,0:T(8,128)(2,1)} %slice.246.k_ref, ...), custom_call_target="tpu_custom_call" | custom-call | flops 2684354560 | bytes 6291456 | tf_op jit(solution)/shard_map/attn_bwd/pallas_call | solution.py:125
  599.4 5.8 convolution_convert_fusion.1
  605.2 5.5 copy.92
  610.8 35.8 %all-gather.34.cloned.1.call-done = bf16[8192,256]{1,0:T(8,128)(2,1)} async-done(((bf16[1024,256]{1,0:T(8,128)(2,1)}), bf16[8192,256]{1,0:T(8,128)(2,1)}) %all-gather.34.cloned.1.call-update) | async-done | bytes 4194320 | tf_op jit(solution)/shard_map/all_gather | solution.py:277
  647.8 6.2 copy.97
  654.1 4.5 fusion.24
  658.7 7.1 convolution_convert_fusion.6
  666.1 8.7 convolution_convert_fusion.2
  674.8 5.4 copy.88
  680.3 3.4 reduce-scatter.33.cloned.1.call-done
  683.7 38.6 %reduce-scatter.35.cloned.1.call-done = bf16[200,1600]{1,0:T(8,128)(2,1)} async-done(((bf16[800,1600]{1,0:T(8,128)(2,1)}), bf16[200,1600]{1,0:T(8,128)(2,1)}) %reduce-scatter.35.cloned.1.call-update) | async-done | bytes 640016
  724.3 79.9 %reduce-scatter.31.cloned.1.call-done = bf16[128,1600]{1,0:T(8,128)(2,1)} async-done(((bf16[1024,1600]{1,0:T(8,128)(2,1)}), bf16[128,1600]{1,0:T(8,128)(2,1)}) %reduce-scatter.31.cloned.1.call-update) | async-done | bytes 409616
  807.6 22.3 %reduce-scatter.23.cloned.1.call-done = bf16[400,200]{1,0:T(8,128)(2,1)} async-done(((bf16[1600,200]{1,0:T(8,128)(2,1)}), bf16[400,200]{1,0:T(8,128)(2,1)}) %reduce-scatter.23.cloned.1.call-update) | async-done | bytes 160016 | tf_op jit(solution)/shard_map/reduce_scatter | solution.py:153
  829.9 35.9 %reduce-scatter.21.cloned.1.call-done = bf16[400,768]{1,0:T(8,128)(2,1)} async-done(((bf16[1600,768]{1,0:T(8,128)(2,1)}), bf16[400,768]{1,0:T(8,128)(2,1)}) %reduce-scatter.21.cloned.1.call-update) | async-done | bytes 614416 | tf_op jit(solution)/shard_map/reduce_scatter | solution.py:153
  865.8 2.2 pad_maximum_fusion.1
  868.1 79.6 %reduce-scatter.27.cloned.1.call-done = bf16[128,1600]{1,0:T(8,128)(2,1)} async-done(((bf16[1024,1600]{1,0:T(8,128)(2,1)}), bf16[128,1600]{1,0:T(8,128)(2,1)}) %reduce-scatter.27.cloned.1.call-update) | async-done | bytes 409616
  949.0 92.0 %all-gather.38.cloned.1.call-done = bf16[3200,800]{1,0:T(8,128)(2,1)} async-done(((bf16[400,800]{1,0:T(8,128)(2,1)}), bf16[3200,800]{1,0:T(8,128)(2,1)}) %all-gather.38.cloned.1.call-update) | async-done | bytes 5120016 | tf_op jit(solution)/shard_map/all_gather | solution.py:294
  1041.0 8.5 copy.84
  1049.5 17.2 %reshape.342 = f32[8,400,4,200]{1,0,3,2:T(8,128)} reshape(bf16[3200,800]{0,1:T(8,128)(2,1)} %copy.84) | data formatting | bytes 15360000 | tf_op jit(solution)/shard_map/convert_element_type | solution.py:315
  1066.7 17.9 %copy.85 = f32[400,4,8,200]{3,2,1,0:T(8,128)} copy(f32[400,4,8,200]{0,2,3,1:T(8,128)} %bitcast.159) | data formatting | bytes 20480000 | tf_op jit(solution)/shard_map/convert_element_type | solution.py:315
  1084.6 14.0 reshape.341
  1098.7 29.7 %all-gather.28.cloned.1.call-done = bf16[1600,1600]{1,0:T(8,128)(2,1)} async-done(((bf16[200,1600]{1,0:T(8,128)(2,1)}), bf16[1600,1600]{1,0:T(8,128)(2,1)}) %all-gather.28.cloned.1.call-update) | async-done | bytes 5120016 | tf_op jit(solution)/shard_map/all_gather | solution.py:293
  1128.3 7.3 convert_element_type.228
  1135.7 2.5 fusion.45
  1138.2 114.6 %all-reduce.8.cloned.1.call-done = f32[4,4800]{1,0:T(4,128)} async-done(((f32[4,4800]{1,0:T(4,128)}), f32[4,4800]{1,0:T(4,128)}) %all-reduce.8.cloned.1.call-update) | async-done | bytes 76816 | tf_op jit(solution)/shard_map/psum | solution.py:339
  1257.1 102.5 %all-gather.36.cloned.1.call-done = bf16[3200,968]{1,0:T(8,128)(2,1)} async-done(((bf16[400,968]{1,0:T(8,128)(2,1)}), bf16[3200,968]{1,0:T(8,128)(2,1)}) %all-gather.36.cloned.1.call-update) | async-done | bytes 6195216 | tf_op jit(solution)/shard_map/all_gather | solution.py:310
  1359.6 4.5 slice_bitcast_fusion
  1364.1 1.8 slice_bitcast_fusion.3
  1369.3 3.9 reshape.330
  1373.2 3.2 copy.79
  1376.3 3.8 reshape.331
  1380.2 3.1 copy.80
  1383.3 3.8 reshape.332
  1387.2 7.7 concatenate.50
  1394.9 5.8 convert_element_type.218
  1400.7 3.6 copy.81
  1404.3 4.8 reshape.340
  (180 shorter events, 43.1 us)
Async XLA Ops:
  7.2 69.8 %all-gather.30.cloned.1.call-start = ((), (), s32[]{:S(2)}) async-start(), calls=%async_computation.18 | async-start | bytes 3686400 | tf_op jit(solution)/shard_map/all_gather | solution.py:141
  7.9 94.0 %all-gather.18.cloned.1.call-start = ((), (), s32[]{:S(2)}) async-start(), calls=%async_computation.8 | async-start | bytes 3072000 | tf_op jit(solution)/shard_map/all_gather | solution.py:149
  10.8 1.9 copy-start.3
  12.5 1.6 copy-start.19
  12.5 2.9 copy-start.9
  12.5 2.9 copy-start.10
  12.5 2.9 copy-start.11
  12.5 2.9 copy-start.12
  12.5 2.9 copy-start.13
  12.6 2.9 copy-start.14
  12.6 2.9 copy-start.15
  12.6 2.9 copy-start.16
  12.6 17.6 %copy-start.17 = (s32[8]{0:T(128)S(1)}, s32[8]{0:T(128)}, u32[]{:S(2)}) copy-start(s32[8]{0:T(128)} %param.28) | copy-start | bytes 100
  12.6 127.6 %all-reduce.6.cloned.1.call-start = ((), (), s32[]{:S(2)}) async-start(), calls=%async_computation.9 | async-start | bytes 1703936 | tf_op jit(solution)/shard_map/psum | solution.py:259
  14.1 210.2 %reduce-scatter.25.cloned.1.call-start = ((), (), s32[]{:S(2)}) async-start(), calls=%async_computation.23 | async-start | bytes 3833856
  30.3 50.4 %copy-start.8 = (s32[8,128]{1,0:T(8,128)}, s32[8,128]{1,0:T(8,128)S(1)}, u32[]{:S(2)}) copy-start(s32[8,128]{1,0:T(8,128)S(1)} %multiply_add_fusion) | copy-start | bytes 12292
  76.9 2.9 copy-start.1
  146.1 106.3 %all-gather.22.cloned.1.call-start = ((), (), s32[]{:S(2)}) async-start(), calls=%async_computation.11 | async-start | bytes 3584000 | tf_op jit(solution)/shard_map/all_gather | solution.py:149
  167.8 57.6 %copy-start = (bf16[1,128,1600]{1,2,0:T(8,128)(2,1)S(1)}, bf16[1,128,1600]{1,2,0:T(8,128)(2,1)}, u32[]{:S(2)}) copy-start(bf16[1,128,1600]{1,2,0:T(8,128)(2,1)} %param.15) | copy-start | bytes 1228804
  177.9 141.2 %all-gather.20.cloned.1.call-start = ((), (), s32[]{:S(2)}) async-start(), calls=%async_computation.10 | async-start | bytes 3686400 | tf_op jit(solution)/shard_map/all_gather | solution.py:141
  227.9 117.4 %all-gather.24.cloned.1.call-start = ((), (), s32[]{:S(2)}) async-start(), calls=%async_computation.12 | async-start | bytes 3328000 | tf_op jit(solution)/shard_map/all_gather | solution.py:149
  230.0 181.5 %all-gather.32.cloned.1.call-start = ((), (), s32[]{:S(2)}) async-start(), calls=%async_computation.19 | async-start | bytes 3686400 | tf_op jit(solution)/shard_map/all_gather | solution.py:141
  230.7 275.7 %reduce-scatter.29.cloned.1.call-start = ((), (), s32[]{:S(2)}) async-start(), calls=%async_computation.25 | async-start | bytes 3833856
  411.5 8.3 copy-start.18
  419.7 4.9 copy-start.20
  430.1 78.5 %copy-start.2 = (bf16[1,128,1600]{1,2,0:T(8,128)(2,1)S(1)}, bf16[1,128,1600]{1,2,0:T(8,128)(2,1)}, u32[]{:S(2)}) copy-start(bf16[1,128,1600]{1,2,0:T(8,128)(2,1)} %param.29) | copy-start | bytes 1228804
  430.1 143.4 %all-gather.26.cloned.1.call-start = ((), (), s32[]{:S(2)}) async-start(), calls=%async_computation.13 | async-start | bytes 3686400 | tf_op jit(solution)/shard_map/all_gather | solution.py:141
  509.9 136.7 %all-gather.34.cloned.1.call-start = ((), (), s32[]{:S(2)}) async-start(), calls=%async_computation.20 | async-start | bytes 4718592 | tf_op jit(solution)/shard_map/all_gather | solution.py:277
  510.6 173.1 %reduce-scatter.33.cloned.1.call-start = ((), (), s32[]{:S(2)}) async-start(), calls=%async_computation.27 | async-start | bytes 3584000 | tf_op jit(solution)/shard_map/reduce_scatter | solution.py:153
  518.4 55.0 %copy-start.6 = (bf16[256,1600]{1,0:T(8,128)(2,1)S(1)}, bf16[256,1600]{1,0:T(8,128)(2,1)}, u32[]{:S(2)}) copy-start(bf16[256,1600]{1,0:T(8,128)(2,1)} %all-reduce.6.cloned.1.call-done) | copy-start | bytes 2457604
  518.4 203.9 %reduce-scatter.35.cloned.1.call-start = ((), (), s32[]{:S(2)}) async-start(), calls=%async_computation.28 | async-start | bytes 3328000
  526.9 277.3 %reduce-scatter.31.cloned.1.call-start = ((), (), s32[]{:S(2)}) async-start(), calls=%async_computation.26 | async-start | bytes 3833856
  598.3 1.1 copy-start.7
  610.7 219.2 %reduce-scatter.23.cloned.1.call-start = ((), (), s32[]{:S(2)}) async-start(), calls=%async_computation.16 | async-start | bytes 1024000 | tf_op jit(solution)/shard_map/reduce_scatter | solution.py:153
  658.6 207.2 %reduce-scatter.21.cloned.1.call-start = ((), (), s32[]{:S(2)}) async-start(), calls=%async_computation.15 | async-start | bytes 3072000 | tf_op jit(solution)/shard_map/reduce_scatter | solution.py:153
  665.8 281.9 %reduce-scatter.27.cloned.1.call-start = ((), (), s32[]{:S(2)}) async-start(), calls=%async_computation.24 | async-start | bytes 3833856
  680.2 43.0 %copy-start.5 = (bf16[1024,256]{1,0:T(8,128)(2,1)S(1)}, bf16[1024,256]{1,0:T(8,128)(2,1)}, u32[]{:S(2)}) copy-start(bf16[1024,256]{1,0:T(8,128)(2,1)} %get-tuple-element.25) | copy-start | bytes 1572868
  680.2 43.6 %copy-start.4 = (bf16[1024,256]{1,0:T(8,128)(2,1)S(1)}, bf16[1024,256]{1,0:T(8,128)(2,1)}, u32[]{:S(2)}) copy-start(bf16[1024,256]{1,0:T(8,128)(2,1)} %get-tuple-element.23) | copy-start | bytes 1572868
  680.2 360.8 %all-gather.38.cloned.1.call-start = ((), (), s32[]{:S(2)}) async-start(), calls=%async_computation.22 | async-start | bytes 6451200 | tf_op jit(solution)/shard_map/all_gather | solution.py:294
  683.7 444.6 %all-gather.28.cloned.1.call-start = ((), (), s32[]{:S(2)}) async-start(), calls=%async_computation.17 | async-start | bytes 5990400 | tf_op jit(solution)/shard_map/all_gather | solution.py:293
  722.4 530.4 %all-reduce.8.cloned.1.call-start = ((), (), s32[]{:S(2)}) async-start(), calls=%async_computation.14 | async-start | bytes 155648 | tf_op jit(solution)/shard_map/psum | solution.py:339
  807.1 552.5 %all-gather.36.cloned.1.call-start = ((), (), s32[]{:S(2)}) async-start(), calls=%async_computation.21 | async-start | bytes 7372800 | tf_op jit(solution)/shard_map/all_gather | solution.py:310
Sparse Core Ops, SparseCore 0:
  10.0 66.8 all-gather.29
  79.1 22.7 all-gather.17
  104.9 35.3 all-reduce.5
  146.3 77.9 reduce-scatter.24
  226.2 26.2 all-gather.21
  254.9 64.1 all-gather.19
  321.3 23.9 all-gather.23
  347.3 64.1 all-gather.31
  430.2 76.1 reduce-scatter.28
  510.0 63.4 all-gather.25
  575.6 70.9 all-gather.33
  649.0 34.6 reduce-scatter.32
  686.8 35.5 reduce-scatter.34
  726.4 77.7 reduce-scatter.30
  807.2 22.6 reduce-scatter.22
  832.4 33.4 reduce-scatter.20
  869.9 77.8 reduce-scatter.26
  949.8 91.1 all-gather.37
  1043.2 85.0 all-gather.27
  1133.8 119.0 all-reduce.7
  1255.6 103.9 all-gather.35

commit v2 on v1

--- a/solution.py
+++ b/solution.py
@@ -12,6 +12,7 @@
 SCALE = 0.125
 F32 = jnp.float32
 BF16 = jnp.bfloat16
+MESH = pl.DeviceIdType.MESH
 
 
 def dot(left, right):
@@ -137,6 +138,306 @@
     )(place.reshape(rows, 1), place.reshape(1, rows), q, k, v, do, o, total)
 
 
+def split_axis(n):
+    across = 2 if n <= 8 else 4
+    return n // across, across
+
+
+def line_neighbours(me, lines, across):
+    a, b = lax.div(me, across), lax.rem(me, across)
+    return a, b, [
+        (a < lines - 1, me + across),
+        (a > 0, me - across),
+        (b < across - 1, me + 1),
+        (b > 0, me - 1),
+    ]
+
+
+def exchange_body(n, nf, counts, *refs):
+    n_ctx, n_fsdp, n_red = counts
+    total = n_ctx + n_fsdp + n_red
+    ctx_in = refs[:n_ctx]
+    fsdp_in = refs[n_ctx : n_ctx + n_fsdp]
+    red_in = refs[n_ctx + n_fsdp : total]
+    ctx_out = refs[total : total + n_ctx]
+    fsdp_out = refs[total + n_ctx : total + n_ctx + n_fsdp]
+    red_out = refs[total + n_ctx + n_fsdp : 2 * total]
+    scratch = refs[2 * total :]
+    land = scratch[:n_red]
+    sums = scratch[n_red : 2 * n_red]
+    copy_sem, send_sem, recv_sem, fs_send, fs_recv = scratch[2 * n_red :]
+
+    lines, across = split_axis(n)
+    me = lax.axis_index("ctx")
+    f = lax.axis_index("fsdp")
+    a, b, near = line_neighbours(me, lines, across)
+    peers = [lax.rem(f + k, nf) for k in range(1, nf)] if n_fsdp + n_red else []
+    barrier = pltpu.get_barrier_semaphore()
+    if n_ctx + n_red:
+        for exists, target in near:
+
+            @pl.when(exists)
+            def _(target=target):
+                pl.semaphore_signal(barrier, inc=1, device_id={"ctx": target}, device_id_type=MESH)
+
+    for peer in peers:
+        pl.semaphore_signal(barrier, inc=1, device_id={"fsdp": peer}, device_id_type=MESH)
+    waits = len(peers)
+    if n_ctx + n_red:
+        waits = waits + sum(exists.astype(jnp.int32) for exists, _ in near)
+    pl.semaphore_wait(barrier, waits)
+
+    gathered = list(zip(ctx_in, ctx_out)) + list(zip(sums, red_out))
+
+    def hop(i, block, way, own=False):
+        source, out = gathered[i]
+        return pltpu.make_async_remote_copy(
+            src_ref=source if own else out.at[block],
+            dst_ref=out.at[block],
+            send_sem=send_sem.at[i, way, block],
+            recv_sem=recv_sem.at[i, way, block],
+            device_id={"ctx": me + (across, -across, 1, -1)[way]},
+            device_id_type=MESH,
+        )
+
+    def fs_hop(i, peer, source):
+        if i < n_fsdp:
+            src, dst = fsdp_in[i], fsdp_out[i].at[source]
+        else:
+            src, dst = red_in[i - n_fsdp].at[peer], land[i - n_fsdp].at[source]
+        return pltpu.make_async_remote_copy(
+            src_ref=src,
+            dst_ref=dst,
+            send_sem=fs_send.at[i, peer],
+            recv_sem=fs_recv.at[i, source],
+            device_id={"fsdp": peer},
+            device_id_type=MESH,
+        )
+
+    keeps = []
+    for i in range(n_fsdp + n_red):
+        for peer in peers:
+            fs_hop(i, peer, f).start()
+
+    def begin(i):
+        for way in range(4):
+            pl.when(near[way][0])(lambda way=way: hop(i, me, way, True).start())
+        keep = pltpu.make_async_copy(gathered[i][0], gathered[i][1].at[me], copy_sem.at[i])
+        keep.start()
+        keeps.append(keep)
+
+    for i in range(n_ctx):
+        begin(i)
+    for i in range(n_fsdp):
+        keep = pltpu.make_async_copy(fsdp_in[i], fsdp_out[i].at[f], copy_sem.at[n_ctx + n_red + i])
+        keep.start()
+        keeps.append(keep)
+    for i in range(n_red):
+        value = red_in[i][f].astype(F32)
+        for peer in peers:
+            fs_hop(n_fsdp + i, peer, peer).wait_recv()
+            value = value + land[i][peer].astype(F32)
+        sums[i][...] = value.astype(sums[i].dtype)
+        begin(n_ctx + i)
+
+    for i in range(len(gathered)):
+        for d in range(1, lines):
+            for way, there, source in ((0, a >= d, me - d * across), (1, a + d < lines, me + d * across)):
+
+                @pl.when(there)
+                def _(i=i, source=source, way=way):
+                    hop(i, source, way).wait_recv()
+                    for on in (way, 2, 3):
+                        pl.when(near[on][0])(lambda on=on: hop(i, source, on).start())
+
+    for i in range(len(gathered)):
+        for d in range(1, across):
+            for step in range(lines):
+                for sign in (1, -1) if step else (1,):
+                    for way, there, shift in ((2, b >= d, -d), (3, b + d < across, d)):
+                        other = a + sign * step
+
+                        @pl.when(there & (other >= 0) & (other < lines))
+                        def _(i=i, source=other * across + b + shift, way=way):
+                            hop(i, source, way).wait_recv()
+                            if d < across - 1:
+                                pl.when(near[way][0])(lambda: hop(i, source, way).start())
+
+    for i in range(n_fsdp):
+        for peer in peers:
+            fs_hop(i, peer, peer).wait_recv()
+
+    for keep in keeps:
+        keep.wait()
+    for i in range(n_fsdp + n_red):
+        for peer in peers:
+            fs_hop(i, peer, f).wait_send()
+    for i in range(len(gathered)):
+        for way in range(4):
+            pl.when(near[way][0])(lambda i=i, way=way: hop(i, me, way, True).wait_send())
+        for d in range(1, lines):
+            for way, there, source in ((0, a >= d, me - d * across), (1, a + d < lines, me + d * across)):
+
+                @pl.when(there)
+                def _(i=i, source=source, way=way):
+                    for on in (way, 2, 3):
+                        pl.when(near[on][0])(lambda on=on: hop(i, source, on).wait_send())
+
+        for d in range(1, across - 1):
+            for line in range(lines):
+                for way, there, shift in ((2, b >= d, -d), (3, b + d < across, d)):
+
+                    @pl.when(there & near[way][0])
+                    def _(i=i, source=line * across + b + shift, way=way):
+                        hop(i, source, way).wait_send()
+
+
+def exchange(call, n, nf, ctx=(), fsdp=(), red=()):
+    shape = jax.ShapeDtypeStruct
+    gathered = len(ctx) + len(red)
+    outs = [shape((n, *x.shape), x.dtype) for x in ctx]
+    outs += [shape((nf, *x.shape), x.dtype) for x in fsdp]
+    outs += [shape((n, *x.shape[1:]), x.dtype) for x in red]
+    sent = max(len(fsdp) + len(red), 1)
+    return pl.pallas_call(
+        functools.partial(exchange_body, n, nf, (len(ctx), len(fsdp), len(red))),
+        in_specs=[pl.BlockSpec(memory_space=pltpu.VMEM)] * len(outs),
+        out_specs=[pl.BlockSpec(memory_space=pl.ANY)] * len(outs),
+        out_shape=outs,
+        scratch_shapes=[pltpu.VMEM(x.shape, x.dtype) for x in red]
+        + [pltpu.VMEM(x.shape[1:], x.dtype) for x in red]
+        + [
+            pltpu.SemaphoreType.DMA((len(outs),)),
+            pltpu.SemaphoreType.DMA((max(gathered, 1), 4, n)),
+            pltpu.SemaphoreType.DMA((max(gathered, 1), 4, n)),
+            pltpu.SemaphoreType.DMA((sent, nf)),
+            pltpu.SemaphoreType.DMA((sent, nf)),
+        ],
+        name=f"exchange_{call}",
+        compiler_params=pltpu.CompilerParams(collective_id=call, has_side_effects=True, vmem_limit_bytes=60 * 2**20),
+    )(*ctx, *fsdp, *red)
+
+
+def scatter_body(n, p_ref, out_ref, across_in, sums, line_in, a_send, a_recv, l_send, l_recv):
+    lines, across = split_axis(n)
+    me = lax.axis_index("ctx")
+    a, b, near = line_neighbours(me, lines, across)
+    peers = [me - b + lax.rem(b + k, across) for k in range(1, across)]
+    barrier = pltpu.get_barrier_semaphore()
+    for peer in peers:
+        pl.semaphore_signal(barrier, inc=1, device_id={"ctx": peer}, device_id_type=MESH)
+    for exists, target in near[:2]:
+
+        @pl.when(exists)
+        def _(target=target):
+            pl.semaphore_signal(barrier, inc=1, device_id={"ctx": target}, device_id_type=MESH)
+
+    pl.semaphore_wait(barrier, len(peers) + sum(exists.astype(jnp.int32) for exists, _ in near[:2]))
+
+    def over(line, k):
+        return pltpu.make_async_remote_copy(
+            src_ref=p_ref.at[line * across + lax.rem(b + k, across)],
+            dst_ref=across_in.at[k - 1, line],
+            send_sem=a_send.at[k - 1, line],
+            recv_sem=a_recv.at[k - 1, line],
+            device_id={"ctx": peers[k - 1]},
+            device_id_type=MESH,
+        )
+
+    def along(line, way):
+        return pltpu.make_async_remote_copy(
+            src_ref=sums.at[line],
+            dst_ref=line_in.at[way, line],
+            send_sem=l_send.at[way, line],
+            recv_sem=l_recv.at[way, line],
+            device_id={"ctx": me + (across, -across)[way]},
+            device_id_type=MESH,
+        )
+
+    for av in range(lines):
+
+        @pl.when(a == av)
+        def _(av=av):
+            order = sorted(range(lines), key=lambda j: (-abs(j - av), j))
+            for line in order:
+                for k in range(1, across):
+                    over(line, k).start()
+            for line in order:
+                value = p_ref[line * across + b].astype(F32)
+                for k in range(1, across):
+                    over(line, k).wait_recv()
+                    value = value + across_in[k - 1, line].astype(F32)
+                if line != av:
+                    way = 0 if line > av else 1
+                    if av > 0 if way == 0 else av < lines - 1:
+                        along(line, way).wait_recv()
+                        value = value + line_in[way, line].astype(F32)
+                    sums[line] = value.astype(BF16)
+                    along(line, way).start()
+                else:
+                    for way, there in ((0, av > 0), (1, av < lines - 1)):
+                        if there:
+                            along(line, way).wait_recv()
+                            value = value + line_in[way, line].astype(F32)
+                    out_ref[...] = value
+            for line in order:
+                for k in range(1, across):
+                    over(line, k).wait_send()
+                if line != av:
+                    along(line, 0 if line > av else 1).wait_send()
+
+
+def scatter(p, n, call):
+    rows, width = p.shape[0] // n, p.shape[1]
+    lines, across = split_axis(n)
+    return pl.pallas_call(
+        functools.partial(scatter_body, n),
+        in_specs=[pl.BlockSpec(memory_space=pltpu.VMEM)],
+        out_specs=pl.BlockSpec(memory_space=pltpu.VMEM),
+        out_shape=jax.ShapeDtypeStruct((rows, width), F32),
+        scratch_shapes=[
+            pltpu.VMEM((across - 1, lines, rows, width), BF16),
+            pltpu.VMEM((lines, rows, width), BF16),
+            pltpu.VMEM((2, lines, rows, width), BF16),
+            pltpu.SemaphoreType.DMA((across - 1, lines)),
+            pltpu.SemaphoreType.DMA((across - 1, lines)),
+            pltpu.SemaphoreType.DMA((2, lines)),
+            pltpu.SemaphoreType.DMA((2, lines)),
+        ],
+        name=f"scatter_{call}",
+        compiler_params=pltpu.CompilerParams(collective_id=call, has_side_effects=True, vmem_limit_bytes=60 * 2**20),
+    )(p.astype(BF16).reshape(n, rows, width))
+
+
+def columns_body(moves, in_ref, out_ref):
+    for block, start, goal, size in moves:
+        out_ref[:, goal : goal + size] = in_ref[block, :, start : start + size].astype(F32)
+
+
+def place_columns(value, moves, width):
+    n, rows, part = value.shape
+    step = next(s for s in (80, 16, rows) if rows % s == 0)
+    return pl.pallas_call(
+        functools.partial(columns_body, tuple(moves)),
+        grid=(rows // step,),
+        in_specs=[pl.BlockSpec((n, step, part), lambda i: (0, i, 0))],
+        out_specs=pl.BlockSpec((step, width), lambda i: (i, 0)),
+        out_shape=jax.ShapeDtypeStruct((rows, width), F32),
+        name="place_columns",
+        cost_estimate=pl.CostEstimate(flops=0, bytes_accessed=6 * rows * width, transcendentals=0),
+        compiler_params=pltpu.CompilerParams(vmem_limit_bytes=48 * 2**20),
+    )(value)
+
+
+def head_moves(n, heads, offset, goal):
+    base, rest = divmod(heads, n)
+    moves = [(c, offset, goal + c * base * HEAD_DIM, base * HEAD_DIM) for c in range(n) if base]
+    moves += [
+        (c, offset + base * HEAD_DIM, goal + (base * n + c) * HEAD_DIM, HEAD_DIM) for c in range(rest)
+    ]
+    return moves
+
+
 def ag_ctx(value):
     return lax.all_gather(value, "ctx", axis=0, tiled=True)
 
@@ -147,10 +448,6 @@
 
 def ag_fsdp(value):
     return lax.all_gather(value, "fsdp", axis=0, tiled=True)
-
-
-def rs_fsdp(value):
-    return lax.psum_scatter(value.astype(BF16), "fsdp", scatter_dimension=0, tiled=True)
 
 
 def head_columns(value, width, c, n):
@@ -243,7 +540,15 @@
     place = (block_of * half + within[None, :] % half).reshape(-1)
 
     vectors = (ln1_gain, ln1_shift, qv_bias, out_bias, ln2_gain, ln2_shift, up_bias, down_bias)
-    packed = lax.all_gather(jnp.concatenate(vectors), "fsdp", axis=0, tiled=False)
+    flat = jnp.concatenate(vectors)
+    flat = jnp.pad(flat, (0, -flat.shape[0] % 2048)).reshape(-1, 128)
+    q_w = head_columns(qkv_weight[:, :width], width, c, n)
+    k_w = head_columns(qkv_weight[:, width : 2 * width], width, c, n)
+    v_w = head_columns(qkv_weight[:, 2 * width :], width, c, n)
+    x_all, packed, w_qkv = exchange(0, n, nf, ctx=[tokens[0]], fsdp=[flat, jnp.concatenate([q_w, k_w, v_w], axis=1)])
+    x_all = x_all.reshape(n * rows, width)
+    w_qkv = w_qkv.reshape(width, 3 * wide)
+    packed = packed.reshape(nf, -1)
     full, at = [], 0
     for vector in vectors:
         size = vector.shape[0]
@@ -251,15 +556,10 @@
         at += size
     gain1, shift1, b_qv, b_out, gain2, shift2, b_up, b_down = full
 
-    x_all = ag_ctx(tokens[0])
-    q_w = head_columns(qkv_weight[:, :width], width, c, n)
-    k_w = head_columns(qkv_weight[:, width : 2 * width], width, c, n)
-    v_w = head_columns(qkv_weight[:, 2 * width :], width, c, n)
-    w_qkv = ag_fsdp(jnp.concatenate([q_w, k_w, v_w], axis=1))
     w_out = lax.psum(head_rows(out_weight, heads, c, f, n), "fsdp")
     g2_all = ag_ctx(cotangent[0])
-    up_mine = lax.dynamic_slice_in_dim(up_weight.reshape(local, nf, n, ff_part), c, 1, axis=2)
-    w_up = ag_fsdp(up_mine.reshape(local, nf * ff_part))
+    up_mine = [lax.dynamic_slice_in_dim(up_weight, i * ff_local + c * ff_part, ff_part, axis=1) for i in range(nf)]
+    w_up = ag_fsdp(jnp.concatenate(up_mine, axis=1))
     w_down = ag_fsdp(lax.dynamic_slice_in_dim(down_weight, c * ff_part, ff_part, axis=0))
     b_up_mine = lax.dynamic_slice_in_dim(b_up.reshape(nf, n, ff_part), c, 1, axis=1).reshape(-1)
     bq = head_columns(b_qv[:width], width, c, n)
@@ -273,47 +573,40 @@
     v = (proj[:, 2 * wide :] + bv).astype(BF16)
     attn, o, total = attention_fwd(place, q, k, v, slots)
     x = tokens[0].astype(F32)
-    mid = x + rs_ctx(dot(attn, w_out)).astype(F32) + b_out
+    mid = x + scatter(dot(attn, w_out), n, 1) + b_out
     attn_all = spread_heads(lax.all_gather(attn, "ctx", axis=0, tiled=False), heads, n)
 
     n2, rstd2 = ln_stats(mid)
-    act2 = ag_ctx((n2 * gain2 + shift2).astype(BF16))
+    (act2,) = exchange(2, n, nf, ctx=[(n2 * gain2 + shift2).astype(BF16)])
+    act2 = act2.reshape(n * rows, width)
     u = dot(act2, w_up) + b_up_mine
     activated, gelu_back = jax.vjp(lambda t: jax.nn.gelu(t, approximate=True), u)
     hidden = activated.astype(BF16)
     dh = dot_t(g2_all, w_down)
     du = gelu_back(dh)[0].astype(BF16)
-    da2 = rs_ctx(dot_t(du, w_up)).astype(F32)
+    da2 = scatter(dot_t(du, w_up), n, 3)
     result = mid + rs_ctx(dot(hidden, w_down)).astype(F32) + b_down
-    d_down = rs_fsdp(t_dot(hidden, g2_all))
-    d_up = rs_fsdp(t_dot(act2, du))
+    d_down = t_dot(hidden, g2_all).astype(BF16).reshape(nf, ff_part, width)
+    d_up = t_dot(act2, du).astype(BF16).reshape(nf, local, nf * ff_part)
     d_up_bias = jnp.sum(du.astype(F32), axis=0)
     grad_out = cotangent[0].astype(F32)
     d_down_bias = jnp.sum(grad_out, axis=0)
-    d_down = lax.all_gather(d_down, "ctx", axis=0, tiled=True)
-    d_up = lax.all_gather(d_up, "ctx", axis=0, tiled=False)
 
     d_gain2 = jnp.sum(da2 * n2, axis=0)
     d_shift2 = jnp.sum(da2, axis=0)
     d_mid = grad_out + ln_back(da2, n2, rstd2, gain2)
     g1 = d_mid.astype(BF16)
     d_out_bias = jnp.sum(g1.astype(F32), axis=0)
-    g1_all = ag_ctx(g1)
+    (g1_all,) = exchange(4, n, nf, ctx=[g1])
+    g1_all = g1_all.reshape(n * rows, width)
     d_attn = dot_t(g1_all, w_out)
     gq, gk, gv = attention_bwd(place, q, k, v, d_attn, o, total, slots)
     g_qkv = jnp.concatenate([gq, gk, gv], axis=1)
-    da1 = rs_ctx(dot_t(g_qkv, w_qkv)).astype(F32)
-    d_qkv = rs_fsdp(t_dot(act1, g_qkv))
+    da1 = scatter(dot_t(g_qkv, w_qkv), n, 5)
+    d_qkv = t_dot(act1, g_qkv).astype(BF16).reshape(nf, local, 3 * wide)
     out_part = width // n
     g1_mine = lax.dynamic_slice_in_dim(g1_all, c * out_part, out_part, axis=1)
-    d_out = rs_fsdp(t_dot(attn_all, g1_mine))
-    gathered = lax.all_gather(jnp.concatenate([d_qkv, d_out], axis=1), "ctx", axis=0, tiled=False)
-    d_qkv_full = jnp.concatenate(
-        [spread_heads(gathered[:, :, i * wide : (i + 1) * wide], heads, n) for i in range(3)], axis=1
-    ).astype(F32)
-    d_out_full = jnp.transpose(gathered[:, :, 3 * wide :], (1, 0, 2)).reshape(local, width).astype(F32)
-    d_up_full = jnp.transpose(d_up.reshape(n, local, nf, ff_part), (1, 2, 0, 3)).reshape(local, ff).astype(F32)
-    d_down_full = d_down.astype(F32)
+    d_out = t_dot(attn_all, g1_mine).astype(BF16).reshape(nf, local, out_part)
 
     n1, rstd1 = ln_stats(x)
     d_gain1 = jnp.sum(da1 * n1, axis=0)
@@ -336,8 +629,18 @@
         d_down_bias,
     )
     packed = jnp.concatenate([s.reshape(nf, -1) for s in smalls], axis=1)
-    summed = lax.psum(packed, ("ctx", "fsdp"))
-    mine = lax.dynamic_slice_in_dim(summed, f, 1, axis=0)[0]
+    packed = jnp.pad(packed, ((0, 0), (0, -packed.shape[1] % 1024))).reshape(nf, -1, 128)
+    d_up, d_down, d_out, d_qkv, packed = exchange(6, n, nf, red=[d_up, d_down, d_out, d_qkv, packed])
+    mine = jnp.sum(packed, axis=0).reshape(-1)
+    d_up_full = place_columns(
+        d_up,
+        [(i, j * ff_part, j * ff_local + i * ff_part, ff_part) for i in range(n) for j in range(nf)],
+        ff,
+    )
+    d_down_full = d_down.reshape(ff_local, width).astype(F32)
+    d_out_full = place_columns(d_out, [(i, 0, i * out_part, out_part) for i in range(n)], width)
+    moves = [m for i in range(3) for m in head_moves(n, heads, i * wide, i * width)]
+    d_qkv_full = place_columns(d_qkv, moves, 3 * width)
     out, at = [], 0
     for s in smalls:
         size = s.size // nf

time: 1430 us -> 818 us (0.57)
  the two profiles are of different devices: /device:TPU:0 before, /device:TPU:3 now
where the time goes in v2:
time: 818 us; the launch traced here: 807 us
  Pallas kernels  604 us (74%)
  local copies, waits for them, and re-layouts  76.4 us (9%)
  matrix products  69.9 us (9%)
  other arithmetic  34.6 us (4%)
  between operations  15 us (2%)
    pallas_call x4, Pallas kernels, exchange(): pl.pallas_call(functools.partial(exchange_body, n, nf, (len(ctx), len(fsd...  420 us
    pallas_call x3, Pallas kernels, scatter(): pl.pallas_call(functools.partial(scatter_body, n), in_specs=[pl.BlockSpec...  145 us
    dot_general x4, matrix products, dot_t(): lax.dot_general(left, right, (((1,), (1,)), ((), ())), preferred_element_...  24.4 us
    dot_general x4, matrix products, dot(): return jnp.dot(left, right, preferred_element_type=F32)  23.6 us
    unnamed x73, local copies, waits for them, and re-layouts  23 us
    dot_general x4, matrix products, t_dot(): lax.dot_general(left, right, (((0,), (0,)), ((), ())), preferred_element_...  21.9 us
    pallas_call x1, Pallas kernels, attention_bwd(): pl.pallas_call(functools.partial(attn_bwd_body, slots), grid=(steps,), in...  17.7 us
  transfers between devices with their start and end apart: 6, of which 1 were waited for; matrix products, arithmetic and copies ran while one was open for 15% of the time, Pallas kernels for 29%

profile of v2, /device:TPU:3, one launch (start us, length us, event | category | flops | bytes accessed | tf_op | source)
XLA Modules:
  0.0 807.1 jit_solution(13472447660736992646)
XLA Ops:
  7.2 1.0 pad_dynamic-slice_fusion.1
  9.4 1.7 constant_dynamic-slice_fusion.4
  11.1 1.2 pad_maximum_fusion.1
  12.4 2.0 constant_dynamic-slice_fusion
  16.1 1.0 copy.54.qp_ref
  17.1 3.0 fusion.53
  20.8 1.1 concatenate.36.refs_2_
  22.7 44.8 %exchange_0.1 = (bf16[8,128,1600]{2,1,0:T(8,128)(2,1)}, bf16[4,48,128]{2,1,0:T(8,128)(2,1)}, bf16[4,400,768]{2,1,0:T(8,128)(2,1)}) custom-call(bf16[128,1600]{1,0:T(8,128)(2,1)} %bitcast.107, bf16[48,128]{1,0:T(8,128)(2,1)} %pad_bitcast_fusion.1.refs_1_, bf16[400,768]{1,0:T(8,128)(2,1)} %concatenate.36.refs_2_), custom_call_target="tpu_custom_call" | custom-call | tf_op jit(solution)/shard_map/exchange_0/pallas_call | solution.py:302
  69.2 2.5 convert_reduce_fusion
  71.7 1.0 multiply_reduce_fusion
  72.8 1.5 add_convert_fusion
  74.5 3.0 fusion.56
  78.7 1.2 fusion.26
  79.9 9.6 %attn_fwd.1 = (bf16[1024,256]{1,0:T(8,128)(2,1)}, f32[1024,256]{1,0:T(8,128)}, f32[1024,4]{1,0:T(8,128)}) custom-call(s32[1024,1]{1,0:T(8,128)} %copy.54.qp_ref, s32[1,1024]{1,0:T(1,128)} %bitcast.135, bf16[1024,256]{1,0:T(8,128)(2,1)} %get-tuple-element.105.q_ref, bf16[1024,256]{1,0:T(8,128)(2,1)} %slice.171.k_ref, bf16[1024,256]{1,0:T(8,128)(2,1)} %get-tuple-element.104.v_ref), custom_call_target="tpu_custom_call" | custom-call | flops 1073741824 | bytes 4194304 | tf_op jit(solution)/shard_map/attn_fwd/pallas_call | solution.py:104
  90.4 1.2 convert_reduce_fusion.2
  91.6 4.2 convolution_convert_fusion.3
  95.8 5.4 copy.55
  101.2 51.5 %scatter_1.1 = f32[128,1600]{1,0:T(8,128)} custom-call(bf16[8,128,1600]{2,1,0:T(8,128)(2,1)} %bitcast.108), custom_call_target="tpu_custom_call" | custom-call | tf_op jit(solution)/shard_map/scatter_1/pallas_call | solution.py:393
  152.7 1.5 fusion.51
  155.2 1.0 add_convert_fusion.1.refs_0_
  156.2 70.4 %exchange_2.1 = bf16[8,128,1600]{2,1,0:T(8,128)(2,1)} custom-call(bf16[128,1600]{1,0:T(8,128)(2,1)} %add_convert_fusion.1.refs_0_), custom_call_target="tpu_custom_call" | custom-call | tf_op jit(solution)/shard_map/exchange_2/pallas_call | solution.py:302
  226.6 7.7 fusion.57
  234.3 8.7 %convolution_convert_fusion.2 = bf16[1024,1600]{0,1:T(8,128)(2,1)} fusion(bf16[800,1600]{1,0:T(8,128)(2,1)} %all-gather.9.cloned.1.call-done, f32[1024,800]{0,1:T(8,128)} %fusion.57, f32[800]{0:T(1024)S(1)} %add.253), kind=kOutput, calls=%fused_computation.13 | convolution fusion | flops 2631270400 | bytes 9116800 | tf_op jit(solution)/shard_map/dot_general | solution.py:19
  243.0 14.6 %copy.56 = bf16[1024,1600]{1,0:T(8,128)(2,1)} copy(bf16[1024,1600]{0,1:T(8,128)(2,1)} %convolution_convert_fusion.2) | data formatting | bytes 6553600 | tf_op jit(solution)/shard_map/convert_element_type | solution.py:446
  257.5 2.0 copy.57
  259.5 1.1 convert_reduce_fusion.3
  260.8 2.7 fusion.3
  263.5 9.3 %convert_reduce_fusion.1 = (f32[800]{0:T(1024)S(1)}, bf16[1024,800]{0,1:T(8,128)(2,1)}) fusion(f32[1024,800]{0,1:T(8,128)} %fusion.57, f32[800]{0:T(1024)S(1)} %add.253, bf16[800,1600]{1,0:T(8,128)(2,1)} %all-gather.9.cloned.1.call-done, bf16[1,1024,1600]{1,2,0:T(8,128)(2,1)} %all-gather.11.cloned.1.call-done), kind=kOutput, calls=%fused_computation.37 | convolution fusion | flops 2640280832 | bytes 10758400 | tf_op jit(solution)/shard_map/dot_general | solution.py:23
  273.1 6.1 convolution_convert_fusion.4
  279.2 5.2 copy.61
  284.4 5.9 convolution_convert_fusion
  290.3 3.5 copy.58
  293.8 54.0 %scatter_3.1 = f32[128,1600]{1,0:T(8,128)} custom-call(bf16[8,128,1600]{2,1,0:T(8,128)(2,1)} %bitcast.109), custom_call_target="tpu_custom_call" | custom-call | tf_op jit(solution)/shard_map/scatter_3/pallas_call | solution.py:393
  347.8 1.5 multiply_reduce_fusion.1
  349.5 8.4 %convolution_convert_fusion.5 = bf16[800,1600]{1,0:T(8,128)(2,1)} fusion(bf16[1,1024,1600]{1,2,0:T(8,128)(2,1)} %all-gather.11.cloned.1.call-done, f32[1024,800]{0,1:T(8,128)} %fusion.57, f32[800]{0:T(1024)S(1)} %add.253), kind=kOutput, calls=%fused_computation.16 | convolution fusion | flops 2630912000 | bytes 9116800 | tf_op jit(solution)/shard_map/dot_general | solution.py:27
  357.8 1.1 slice.143
  359.1 6.3 copy.67
  365.4 5.9 reduce-scatter.2.cloned.1.call-done
  371.3 2.8 convert_reduce_fusion.6
  374.1 40.1 %exchange_4.1 = bf16[8,128,1600]{2,1,0:T(8,128)(2,1)} custom-call(bf16[128,1600]{1,0:T(8,128)(2,1)} %get-tuple-element.93.refs_0_), custom_call_target="tpu_custom_call" | custom-call | tf_op jit(solution)/shard_map/exchange_4/pallas_call | solution.py:302
  414.3 4.1 fusion.58.do_ref
  418.4 17.7 %attn_bwd.1 = (bf16[1024,256]{1,0:T(8,128)(2,1)}, bf16[1024,256]{1,0:T(8,128)(2,1)}, bf16[1024,256]{1,0:T(8,128)(2,1)}) custom-call(s32[1024,1]{1,0:T(8,128)} %copy.54.qp_ref, s32[1,1024]{1,0:T(1,128)} %bitcast.136, bf16[1024,256]{1,0:T(8,128)(2,1)} %get-tuple-element.105.q_ref, bf16[1024,256]{1,0:T(8,128)(2,1)} %slice.171.k_ref, ...), custom_call_target="tpu_custom_call" | custom-call | flops 2684354560 | bytes 6291456 | tf_op jit(solution)/shard_map/attn_bwd/pallas_call | solution.py:126
  436.0 1.2 convert_reduce_fusion.5
  437.2 1.9 constant_dynamic-update-slice_fusion.2
  439.7 1.2 convert_reduce_fusion.4
  441.2 3.2 fusion.21
  444.4 2.3 copy.64
  446.7 1.9 constant_dynamic-update-slice_fusion.1
  448.6 1.9 constant_dynamic-update-slice_fusion
  450.4 5.1 convolution_convert_fusion.1
  455.5 4.3 convolution_convert_fusion.6
  459.8 3.5 copy.60
  463.3 39.1 %scatter_5.1 = f32[128,1600]{1,0:T(8,128)} custom-call(bf16[8,128,1600]{2,1,0:T(8,128)(2,1)} %bitcast.110), custom_call_target="tpu_custom_call" | custom-call | tf_op jit(solution)/shard_map/scatter_5/pallas_call | solution.py:393
  502.5 1.6 fusion.38
  505.0 264.2 %exchange_6.1 = (bf16[8,400,800]{2,1,0:T(8,128)(2,1)}, bf16[8,200,1600]{2,1,0:T(8,128)(2,1)}, bf16[8,400,200]{2,1,0:T(8,128)(2,1)}, bf16[8,400,768]{2,1,0:T(8,128)(2,1)}, f32[8,40,128]{2,1,0:T(8,128)}) custom-call(bf16[4,400,800]{2,1,0:T(8,128)(2,1)} %bitcast.111, bf16[4,200,1600]{2,1,0:T(8,128)(2,1)} %bitcast.123, bf16[4,400,200]{2,1,0:T(8,128)(2,1)} %bitcast.121, ...), custom_call_target="tpu_custom_call" | custom-call | tf_op jit(solution)/shard_map/exchange_6/pallas_call | solution.py:302
  769.3 1.1 reduce_sum.199
  772.3 2.3 copy.65
  774.7 2.4 fusion.37
  777.1 2.3 copy.66
  779.5 2.9 place_columns.4
  782.4 2.5 copy-done
  784.9 4.2 place_columns.3
  789.2 5.6 place_columns.5
  794.8 5.2 bitcast_convert_fusion
  (153 shorter events, 13.8 us)
Async XLA Ops:
  7.2 84.4 %all-reduce.5.cloned.1.call-start = ((), (), s32[]{:S(2)}) async-start(), calls=%async_computation.1 | async-start | bytes 1703936 | tf_op jit(solution)/shard_map/psum | solution.py:559
  9.3 5.7 copy-start.14
  9.3 217.2 %all-gather.7.cloned.1.call-start = ((), (), s32[]{:S(2)}) async-start(), calls=%async_computation.2 | async-start | bytes 3584000 | tf_op jit(solution)/shard_map/all_gather | solution.py:450
  9.4 6.6 copy-start.25
  12.3 221.9 %all-gather.9.cloned.1.call-start = ((), (), s32[]{:S(2)}) async-start(), calls=%async_computation.3 | async-start | bytes 3328000 | tf_op jit(solution)/shard_map/all_gather | solution.py:450
  14.4 249.1 %all-gather.11.cloned.1.call-start = ((), (), s32[]{:S(2)}) async-start(), calls=%async_computation.5 | async-start | bytes 3686400 | tf_op jit(solution)/shard_map/all_gather | solution.py:442
  15.0 342.9 %all-gather.13.cloned.1.call-start = ((), (), s32[]{:S(2)}) async-start(), calls=%async_computation.6 | async-start | bytes 4718592 | tf_op jit(solution)/shard_map/all_gather | solution.py:577
  16.1 4.0 copy-start.16
  20.1 1.8 copy-start.17
  20.2 1.8 copy-start.18
  20.2 1.8 copy-start.19
  20.2 1.8 copy-start.20
  20.2 1.8 copy-start.21
  20.2 1.8 copy-start.22
  20.2 1.8 copy-start.23
  20.2 1.8 copy-start.24
  67.5 4.2 copy-start.2
  72.8 1.7 copy-start.26
  89.5 281.7 %reduce-scatter.2.cloned.1.call-start = ((), (), s32[]{:S(2)}) async-start(), calls=%async_computation.4 | async-start | bytes 3833856 | tf_op jit(solution)/shard_map/reduce_scatter | solution.py:446
  101.2 51.5 %copy-start.5 = (bf16[1,128,1600]{2,1,0:T(8,128)(2,1)S(1)}, bf16[1,128,1600]{2,1,0:T(8,128)(2,1)}, u32[]{:S(2)}) copy-start(bf16[1,128,1600]{2,1,0:T(8,128)(2,1)} %copy.53) | copy-start | bytes 1228804
  154.2 1.0 copy-start.3
  263.5 9.6 %copy-start.11 = (bf16[8,128,1600]{2,1,0:T(8,128)(2,1)S(1)}, bf16[8,128,1600]{2,1,0:T(8,128)(2,1)}, u32[]{:S(2)}) copy-start(bf16[8,128,1600]{2,1,0:T(8,128)(2,1)} %exchange_2.1) | copy-start | bytes 9830404
  293.8 54.0 %copy-start.4 = (f32[128,1600]{1,0:T(8,128)S(1)}, f32[128,1600]{1,0:T(8,128)}, u32[]{:S(2)}) copy-start(f32[128,1600]{1,0:T(8,128)} %copy-done.3) | copy-start | bytes 2457604
  359.1 12.2 %copy-start.8 = (f32[128,1600]{1,0:T(8,128)S(1)}, f32[128,1600]{1,0:T(8,128)}, u32[]{:S(2)}) copy-start(f32[128,1600]{1,0:T(8,128)} %scatter_3.1) | copy-start | bytes 2457604
  359.1 12.2 %copy-start.9 = (bf16[1,128,1600]{2,1,0:T(8,128)(2,1)S(1)}, bf16[1,128,1600]{2,1,0:T(8,128)(2,1)}, u32[]{:S(2)}) copy-start(bf16[1,128,1600]{2,1,0:T(8,128)(2,1)} %copy.57) | copy-start | bytes 1228804
  365.4 48.9 %copy-start.13 = (bf16[256,1600]{1,0:T(8,128)(2,1)S(1)}, bf16[256,1600]{1,0:T(8,128)(2,1)}, u32[]{:S(2)}) copy-start(bf16[256,1600]{1,0:T(8,128)(2,1)} %all-reduce.5.cloned.1.call-done) | copy-start | bytes 2457604
  418.3 22.9 %copy-start.12 = (bf16[8,1024,192]{1,2,0:T(8,128)(2,1)S(1)}, bf16[8,1024,192]{1,2,0:T(8,128)(2,1)}, u32[]{:S(2)}) copy-start(bf16[8,1024,192]{1,2,0:T(8,128)(2,1)} %copy.67) | copy-start | bytes 9437188
  450.4 5.1 copy-start.10
  450.4 5.1 copy-start.15
  463.3 39.1 %copy-start.6 = (bf16[1,128,1600]{2,1,0:T(8,128)(2,1)S(1)}, bf16[1,128,1600]{2,1,0:T(8,128)(2,1)}, u32[]{:S(2)}) copy-start(bf16[1,128,1600]{2,1,0:T(8,128)(2,1)} %copy.53) | copy-start | bytes 1228804
  505.0 269.7 %copy-start.7 = (f32[128,1600]{1,0:T(8,128)S(1)}, f32[128,1600]{1,0:T(8,128)}, u32[]{:S(2)}) copy-start(f32[128,1600]{1,0:T(8,128)} %scatter_5.1) | copy-start | bytes 2457604
  769.3 10.2 %copy-start.1 = (bf16[8,400,200]{2,1,0:T(8,128)(2,1)S(1)}, bf16[8,400,200]{2,1,0:T(8,128)(2,1)}, u32[]{:S(2)}) copy-start(bf16[8,400,200]{2,1,0:T(8,128)(2,1)} %get-tuple-element.39.in_ref) | copy-start | bytes 3840004
  782.4 6.8 slice-start
  782.4 2.5 copy-start
  784.9 4.2 slice-start.1
  784.9 9.9 %slice-start.2 = ((s8[5324800]{0:T(1024)(128)(4,1)}), s8[1130496]{0:T(1024)(128)(4,1)S(1)}, s32[]{:S(2)}) async-start(s8[5324800]{0:T(1024)(128)(4,1)} %bitcast.112), calls=%async_computation.9 | async-start | bytes 2260992
  789.2 5.6 slice-start.3
Sparse Core Ops, SparseCore 0:
  10.9 42.2 all-reduce.4
  55.3 27.3 all-gather.6
  84.8 25.7 all-gather.8
  112.5 88.1 all-gather.10
  202.7 73.1 all-gather.12
  279.9 91.3 reduce-scatter.1

commit v3 on v1

--- a/solution.py
+++ b/solution.py
@@ -12,6 +12,7 @@
 SCALE = 0.125
 F32 = jnp.float32
 BF16 = jnp.bfloat16
+MESH = pl.DeviceIdType.MESH
 
 
 def dot(left, right):
@@ -137,6 +138,477 @@
     )(place.reshape(rows, 1), place.reshape(1, rows), q, k, v, do, o, total)
 
 
+def split_axis(n):
+    across = 2 if n <= 8 else 4
+    return n // across, across
+
+
+def place_of(me, lines, across):
+    a, b = lax.div(me, across), lax.rem(me, across)
+    near = [(a < lines - 1, me + across), (a > 0, me - across), (b < across - 1, me + 1), (b > 0, me - 1)]
+    return a, b, near
+
+
+def turned_rows(rows, dtype, across):
+    tile = 16 if dtype == BF16 else 8
+    return rows // 6 // tile * tile if across == 2 else 0
+
+
+def meet(near, peers):
+    barrier = pltpu.get_barrier_semaphore()
+    for exists, target in near:
+
+        @pl.when(exists)
+        def _(target=target):
+            pl.semaphore_signal(barrier, inc=1, device_id={"ctx": target}, device_id_type=MESH)
+
+    for axis, peer in peers:
+        pl.semaphore_signal(barrier, inc=1, device_id={axis: peer}, device_id_type=MESH)
+    pl.semaphore_wait(barrier, len(peers) + sum(exists.astype(jnp.int32) for exists, _ in near))
+
+
+class Fsdp:
+    def __init__(self, nf, gather_in, gather_out, red_in, red_out, scratch):
+        self.gather_in, self.gather_out, self.red_in, self.red_out = gather_in, gather_out, red_in, red_out
+        n_gather, n_red = len(gather_in), len(red_in)
+        self.near_in, self.stage, self.far_in = scratch[:n_red], scratch[n_red : 2 * n_red], scratch[2 * n_red : 3 * n_red]
+        self.keep_sem, self.g_send, self.g_recv, self.r_send, self.r_recv = scratch[3 * n_red : 3 * n_red + 5]
+        self.f = lax.axis_index("fsdp")
+        self.core = lax.rem(self.f, 2)
+        self.mate = self.f + 1 - 2 * self.core
+        self.pairs = nf // 2
+        self.pair = lax.div(self.f, 2)
+        self.other = [lax.rem(self.pair + k, self.pairs) for k in range(1, self.pairs)]
+        self.peers = [self.mate] + [2 * y + self.core for y in self.other] if n_gather + n_red else []
+
+    @staticmethod
+    def scratch(nf, gather, red):
+        pairs = nf // 2
+        dma = pltpu.SemaphoreType.DMA
+        out = []
+        for _ in range(3):
+            out += [pltpu.VMEM((pairs, *x.shape[1:]), x.dtype) for x in red]
+        g, r = max(len(gather), 1), max(len(red), 1)
+        return out + [dma((g,)), dma((g, 2, nf)), dma((g, nf)), dma((r, 2, pairs)), dma((r, 2, pairs))]
+
+    def copy(self, src, dst, send, recv, target):
+        return pltpu.make_async_remote_copy(
+            src_ref=src, dst_ref=dst, send_sem=send, recv_sem=recv, device_id={"fsdp": target}, device_id_type=MESH
+        )
+
+    def spread(self, i, source, target, own):
+        out = self.gather_out[i].at[source]
+        send = self.g_send.at[i, 0, target] if own else self.g_send.at[i, 1, source]
+        return self.copy(self.gather_in[i] if own else out, out, send, self.g_recv.at[i, source], target)
+
+    def keep(self, i):
+        return pltpu.make_async_copy(self.gather_in[i], self.gather_out[i].at[self.f], self.keep_sem.at[i])
+
+    def to_mate(self, j, y):
+        src = self.red_in[j].at[2 * y + 1 - self.core]
+        return self.copy(src, self.near_in[j].at[y], self.r_send.at[j, 0, y], self.r_recv.at[j, 0, y], self.mate)
+
+    def to_far(self, j, y, source):
+        send, recv = self.r_send.at[j, 1, y], self.r_recv.at[j, 1, source]
+        return self.copy(self.stage[j].at[y], self.far_in[j].at[source], send, recv, 2 * y + self.core)
+
+    def start(self):
+        for j in range(len(self.red_in)):
+            for y in range(self.pairs):
+                self.to_mate(j, y).start()
+        for i in range(len(self.gather_in)):
+            for target in self.peers[1:] + self.peers[:1]:
+                self.spread(i, self.f, target, True).start()
+            self.keep(i).start()
+
+    def middle(self):
+        for j in range(len(self.red_in)):
+            for y in range(self.pairs):
+                self.to_mate(j, y).wait_recv()
+            for y in self.other:
+                value = self.red_in[j][2 * y + self.core].astype(F32) + self.near_in[j][y].astype(F32)
+                self.stage[j][y] = value.astype(self.stage[j].dtype)
+                self.to_far(j, y, self.pair).start()
+
+    def end(self):
+        for j in range(len(self.red_in)):
+            value = self.red_in[j][self.f].astype(F32) + self.near_in[j][self.pair].astype(F32)
+            for y in self.other:
+                self.to_far(j, y, y).wait_recv()
+                value = value + self.far_in[j][y].astype(F32)
+            self.red_out[j][...] = value.astype(self.red_out[j].dtype)
+        for i in range(len(self.gather_in)):
+            for y in self.other:
+                source = 2 * y + self.core
+                self.spread(i, source, self.mate, False).wait_recv()
+                self.spread(i, source, self.mate, False).start()
+
+    def finish(self):
+        for i in range(len(self.gather_in)):
+            self.spread(i, self.mate, self.mate, False).wait_recv()
+            for y in self.other:
+                self.spread(i, 2 * y + 1 - self.core, self.mate, False).wait_recv()
+            self.keep(i).wait()
+            for target in self.peers:
+                self.spread(i, self.f, target, True).wait_send()
+            for y in self.other:
+                self.spread(i, 2 * y + self.core, self.mate, False).wait_send()
+        for j in range(len(self.red_in)):
+            for y in range(self.pairs):
+                self.to_mate(j, y).wait_send()
+            for y in self.other:
+                self.to_far(j, y, self.pair).wait_send()
+
+
+def exchange_body(n, nf, counts, *refs):
+    n_ctx, n_fsdp, n_red = counts
+    total = n_ctx + n_fsdp + n_red
+    ctx_in, fsdp_in, red_in = refs[:n_ctx], refs[n_ctx : n_ctx + n_fsdp], refs[n_ctx + n_fsdp : total]
+    outs = refs[total : 2 * total]
+    ctx_out, fsdp_out, red_out = outs[:n_ctx], outs[n_ctx : n_ctx + n_fsdp], outs[n_ctx + n_fsdp :]
+    scratch = refs[2 * total :]
+    sums = scratch[:n_red]
+    copy_sem, send_sem, recv_sem = scratch[n_red : n_red + 3]
+    fs = Fsdp(nf, fsdp_in, fsdp_out, red_in, sums, scratch[n_red + 3 :])
+
+    lines, across = split_axis(n)
+    me = lax.axis_index("ctx")
+    a, b, near = place_of(me, lines, across)
+    gathered = list(zip(ctx_in, ctx_out)) + list(zip(sums, red_out))
+    meet(near if gathered else [], [("fsdp", peer) for peer in fs.peers])
+    fs.start()
+
+    def part(i, turned):
+        rows = gathered[i][1].shape[1]
+        last = turned_rows(rows, gathered[i][1].dtype, across)
+        return pl.ds(rows - last, last) if turned else pl.ds(0, rows - last)
+
+    def turns(i):
+        return bool(turned_rows(gathered[i][1].shape[1], gathered[i][1].dtype, across))
+
+    def hop(i, block, way, turned=False, own=False):
+        source, out = gathered[i]
+        rows = part(i, turned)
+        return pltpu.make_async_remote_copy(
+            src_ref=source.at[rows] if own else out.at[block, rows],
+            dst_ref=out.at[block, rows],
+            send_sem=send_sem.at[i, way, block, int(turned)],
+            recv_sem=recv_sem.at[i, way, block, int(turned)],
+            device_id={"ctx": me + (across, -across, 1, -1)[way]},
+            device_id_type=MESH,
+        )
+
+    def keep(i):
+        return pltpu.make_async_copy(gathered[i][0], gathered[i][1].at[me], copy_sem.at[i])
+
+    def each_own(i, act):
+        for turned in (True, False) if turns(i) else (False,):
+            for way in (2, 3, 0, 1):
+                pl.when(near[way][0])(lambda way=way: act(hop(i, me, way, turned, True)))
+
+    def each_twin(i, wait, act):
+        if turns(i):
+            twin = me + 1 - 2 * b
+            for way in (2, 3):
+
+                @pl.when(near[5 - way][0])
+                def _(way=way):
+                    if wait:
+                        hop(i, twin, way, True).wait_recv()
+                    for on in (0, 1):
+                        pl.when(near[on][0])(lambda on=on: act(hop(i, twin, on, True)))
+
+    def each_relay(i, d, wait, act):
+        for way, there, shift in ((0, a >= d, -d * across), (1, a + d < lines, d * across)):
+
+            @pl.when(there)
+            def _(way=way, shift=shift):
+                for turned, block in [(False, me + shift)] + (
+                    [(True, me + shift), (True, me + 1 - 2 * b + shift)] if turns(i) else []
+                ):
+                    if wait:
+                        hop(i, block, way, turned).wait_recv()
+                    for on in (way,) if turned else (2, 3, way):
+                        pl.when(near[on][0])(lambda on=on: act(hop(i, block, on, turned)))
+
+    def start(copy):
+        copy.start()
+
+    def wait_send(copy):
+        copy.wait_send()
+
+    for i in range(n_ctx):
+        each_own(i, start)
+        keep(i).start()
+    fs.middle()
+    for i in range(len(gathered)):
+        if i == n_ctx:
+            fs.end()
+            for j in range(n_ctx, len(gathered)):
+                each_own(j, start)
+                keep(j).start()
+        each_twin(i, True, start)
+        for d in range(1, lines):
+            each_relay(i, d, True, start)
+
+    for i in range(len(gathered)):
+        for d in range(1, across):
+            for step in range(lines):
+                for sign in (1, -1) if step else (1,):
+                    for way, there, shift in ((2, b >= d, -d), (3, b + d < across, d)):
+                        other = a + sign * step
+
+                        @pl.when(there & (other >= 0) & (other < lines))
+                        def _(i=i, source=other * across + b + shift, way=way):
+                            hop(i, source, way).wait_recv()
+                            if d < across - 1:
+                                pl.when(near[way][0])(lambda: hop(i, source, way).start())
+
+    if not n_red:
+        fs.end()
+
+    for i in range(len(gathered)):
+        keep(i).wait()
+        each_own(i, wait_send)
+        each_twin(i, False, wait_send)
+        for d in range(1, lines):
+            each_relay(i, d, False, wait_send)
+        for d in range(1, across - 1):
+            for line in range(lines):
+                for way, there, shift in ((2, b >= d, -d), (3, b + d < across, d)):
+
+                    @pl.when(there & near[way][0])
+                    def _(i=i, source=line * across + b + shift, way=way):
+                        hop(i, source, way).wait_send()
+
+    fs.finish()
+
+
+def exchange(call, n, nf, ctx=(), fsdp=(), red=()):
+    shape = jax.ShapeDtypeStruct
+    gathered = max(len(ctx) + len(red), 1)
+    outs = [shape((n, *x.shape), x.dtype) for x in ctx]
+    outs += [shape((nf, *x.shape), x.dtype) for x in fsdp]
+    outs += [shape((n, *x.shape[1:]), x.dtype) for x in red]
+    return pl.pallas_call(
+        functools.partial(exchange_body, n, nf, (len(ctx), len(fsdp), len(red))),
+        in_specs=[pl.BlockSpec(memory_space=pltpu.VMEM)] * len(outs),
+        out_specs=[pl.BlockSpec(memory_space=pl.ANY)] * len(outs),
+        out_shape=outs,
+        scratch_shapes=[pltpu.VMEM(x.shape[1:], x.dtype) for x in red]
+        + [
+            pltpu.SemaphoreType.DMA((gathered,)),
+            pltpu.SemaphoreType.DMA((gathered, 4, n, 2)),
+            pltpu.SemaphoreType.DMA((gathered, 4, n, 2)),
+        ]
+        + Fsdp.scratch(nf, fsdp, red),
+        name=f"exchange_{call}",
+        compiler_params=pltpu.CompilerParams(collective_id=call, has_side_effects=True, vmem_limit_bytes=60 * 2**20),
+    )(*ctx, *fsdp, *red)
+
+
+def product_body(n, nf, counts, transposed, *refs):
+    n_fsdp, n_red = counts
+    left, right = refs[:2]
+    more = n_fsdp + n_red
+    fsdp_in, red_in = refs[2 : 2 + n_fsdp], refs[2 + n_fsdp : 2 + more]
+    out = refs[2 + more]
+    fsdp_out, red_out = refs[3 + more : 3 + more + n_fsdp], refs[3 + more + n_fsdp : 3 + 2 * more]
+    part, acc, acc_t, over_in, sums, sums_t, line_in, line_in_t, twin_in = refs[3 + 2 * more : 12 + 2 * more]
+    o_send, o_recv, l_send, l_recv, t_send, t_recv, w_send, w_recv = refs[12 + 2 * more : 20 + 2 * more]
+    fs = Fsdp(nf, fsdp_in, fsdp_out, red_in, red_out, refs[20 + 2 * more :])
+
+    lines, across = split_axis(n)
+    me = lax.axis_index("ctx")
+    a, b, near = place_of(me, lines, across)
+    rows = out.shape[0]
+    last = turned_rows(rows, BF16, across)
+    head, tail = pl.ds(0, rows - last), pl.ds(rows - last, last)
+    peers = [me - b + lax.rem(b + k, across) for k in range(1, across)]
+    meet(near[:2], [("ctx", peer) for peer in peers] + [("fsdp", peer) for peer in fs.peers])
+    fs.start()
+
+    def copy(src, dst, send, recv, target):
+        return pltpu.make_async_remote_copy(
+            src_ref=src, dst_ref=dst, send_sem=send, recv_sem=recv, device_id={"ctx": target}, device_id_type=MESH
+        )
+
+    def over(line, k):
+        src = part.at[line, lax.rem(b + k, across), head]
+        return copy(src, over_in.at[k - 1, line], o_send.at[k - 1, line], o_recv.at[k - 1, line], peers[k - 1])
+
+    def along(line, way):
+        target = me + (across, -across)[way]
+        return copy(sums.at[line], line_in.at[way, line], l_send.at[way, line], l_recv.at[way, line], target)
+
+    def along_t(line, way):
+        target = me + (across, -across)[way]
+        return copy(sums_t.at[line], line_in_t.at[way, line], t_send.at[way, line], t_recv.at[way, line], target)
+
+    def twin():
+        return copy(sums_t.at[a, 1 - b], twin_in, w_send, w_recv, peers[0])
+
+    order = []
+    for k in range(lines):
+        line = jnp.int32(0)
+        for av in range(lines):
+            line = jnp.where(a == av, sorted(range(lines), key=lambda j: (-abs(j - av), j))[k], line)
+        order.append(line)
+
+    for line in order:
+        lhs = left[pl.ds(pl.multiple_of(line * across * rows, across * rows), across * rows), :]
+        value = dot_t(lhs, right[...]) if transposed else dot(lhs, right[...])
+        part[line] = value.astype(BF16).reshape(across, rows, value.shape[1])
+        for k in range(1, across):
+            over(line, k).start()
+    fs.middle()
+    for line in order[:-1]:
+        up, down = line > a, line < a
+        if last:
+            acc_t[...] = part[line, :, tail].astype(F32)
+            for way, there in ((0, up & (a > 0)), (1, down & (a < lines - 1))):
+
+                @pl.when(there)
+                def _(way=way, line=line):
+                    along_t(line, way).wait_recv()
+                    acc_t[...] += line_in_t[way, line].astype(F32)
+
+            sums_t[line] = acc_t[...].astype(BF16)
+            pl.when(up)(lambda line=line: along_t(line, 0).start())
+            pl.when(down)(lambda line=line: along_t(line, 1).start())
+        value = part[line, b, head].astype(F32)
+        for k in range(1, across):
+            over(line, k).wait_recv()
+            value = value + over_in[k - 1, line].astype(F32)
+        acc[...] = value
+        for way, there in ((0, up & (a > 0)), (1, down & (a < lines - 1))):
+
+            @pl.when(there)
+            def _(way=way, line=line):
+                along(line, way).wait_recv()
+                acc[...] += line_in[way, line].astype(F32)
+
+        sums[line] = acc[...].astype(BF16)
+        pl.when(up)(lambda line=line: along(line, 0).start())
+        pl.when(down)(lambda line=line: along(line, 1).start())
+
+    if last:
+        acc_t[...] = part[a, :, tail].astype(F32)
+        for way in range(2):
+
+            @pl.when(near[1 - way][0])
+            def _(way=way):
+                along_t(a, way).wait_recv()
+                acc_t[...] += line_in_t[way, a].astype(F32)
+
+        sums_t[a] = acc_t[...].astype(BF16)
+        twin().start()
+    value = part[a, b, head].astype(F32)
+    for k in range(1, across):
+        over(a, k).wait_recv()
+        value = value + over_in[k - 1, a].astype(F32)
+    acc[...] = value
+    for way in range(2):
+
+        @pl.when(near[1 - way][0])
+        def _(way=way):
+            along(a, way).wait_recv()
+            acc[...] += line_in[way, a].astype(F32)
+
+    out[head, :] = acc[...]
+    fs.end()
+    if last:
+        twin().wait_recv()
+        out[tail, :] = acc_t[b] + twin_in[...].astype(F32)
+
+    for line in order:
+        for k in range(1, across):
+            over(line, k).wait_send()
+    for line in order[:-1]:
+        for way, there in ((0, line > a), (1, line < a)):
+
+            @pl.when(there)
+            def _(way=way, line=line):
+                along(line, way).wait_send()
+                if last:
+                    along_t(line, way).wait_send()
+
+    if last:
+        twin().wait_send()
+    fs.finish()
+
+
+def product(call, n, nf, left, right, transposed=False, fsdp=(), red=()):
+    rows, width = left.shape[0] // n, right.shape[0 if transposed else 1]
+    lines, across = split_axis(n)
+    last = turned_rows(rows, BF16, across)
+    some = max(last, 16)
+    shape = jax.ShapeDtypeStruct
+    vmem, dma = pltpu.VMEM, pltpu.SemaphoreType.DMA
+    outs = [shape((rows, width), F32)]
+    outs += [shape((nf, *x.shape), x.dtype) for x in fsdp]
+    outs += [shape(x.shape[1:], x.dtype) for x in red]
+    return pl.pallas_call(
+        functools.partial(product_body, n, nf, (len(fsdp), len(red)), transposed),
+        in_specs=[pl.BlockSpec(memory_space=vmem)] * (2 + len(fsdp) + len(red)),
+        out_specs=[pl.BlockSpec(memory_space=vmem)]
+        + [pl.BlockSpec(memory_space=pl.ANY)] * len(fsdp)
+        + [pl.BlockSpec(memory_space=vmem)] * len(red),
+        out_shape=outs,
+        scratch_shapes=[
+            vmem((lines, across, rows, width), BF16),
+            vmem((rows - last, width), F32),
+            vmem((across, some, width), F32),
+            vmem((across - 1, lines, rows - last, width), BF16),
+            vmem((lines, rows - last, width), BF16),
+            vmem((lines, across, some, width), BF16),
+            vmem((2, lines, rows - last, width), BF16),
+            vmem((2, lines, across, some, width), BF16),
+            vmem((some, width), BF16),
+            dma((across - 1, lines)),
+            dma((across - 1, lines)),
+            dma((2, lines)),
+            dma((2, lines)),
+            dma((2, lines)),
+            dma((2, lines)),
+            dma,
+            dma,
+        ]
+        + Fsdp.scratch(nf, fsdp, red),
+        name=f"product_{call}",
+        compiler_params=pltpu.CompilerParams(collective_id=call, has_side_effects=True, vmem_limit_bytes=63 * 2**20),
+    )(left, right, *fsdp, *red)
+
+
+def columns_body(moves, in_ref, out_ref):
+    for block, start, goal, size in moves:
+        out_ref[:, goal : goal + size] = in_ref[block, :, start : start + size].astype(F32)
+
+
+def place_columns(value, moves, width):
+    n, rows, part = value.shape
+    step = next(s for s in (80, 16, rows) if rows % s == 0)
+    return pl.pallas_call(
+        functools.partial(columns_body, tuple(moves)),
+        grid=(rows // step,),
+        in_specs=[pl.BlockSpec((n, step, part), lambda i: (0, i, 0))],
+        out_specs=pl.BlockSpec((step, width), lambda i: (i, 0)),
+        out_shape=jax.ShapeDtypeStruct((rows, width), F32),
+        name="place_columns",
+        cost_estimate=pl.CostEstimate(flops=0, bytes_accessed=6 * rows * width, transcendentals=0),
+        compiler_params=pltpu.CompilerParams(vmem_limit_bytes=48 * 2**20),
+    )(value)
+
+
+def head_moves(n, heads, offset, goal):
+    base, rest = divmod(heads, n)
+    moves = [(c, offset, goal + c * base * HEAD_DIM, base * HEAD_DIM) for c in range(n) if base]
+    moves += [
+        (c, offset + base * HEAD_DIM, goal + (base * n + c) * HEAD_DIM, HEAD_DIM) for c in range(rest)
+    ]
+    return moves
+
+
 def ag_ctx(value):
     return lax.all_gather(value, "ctx", axis=0, tiled=True)
 
@@ -147,10 +619,6 @@
 
 def ag_fsdp(value):
     return lax.all_gather(value, "fsdp", axis=0, tiled=True)
-
-
-def rs_fsdp(value):
-    return lax.psum_scatter(value.astype(BF16), "fsdp", scatter_dimension=0, tiled=True)
 
 
 def head_columns(value, width, c, n):
@@ -243,7 +711,16 @@
     place = (block_of * half + within[None, :] % half).reshape(-1)
 
     vectors = (ln1_gain, ln1_shift, qv_bias, out_bias, ln2_gain, ln2_shift, up_bias, down_bias)
-    packed = lax.all_gather(jnp.concatenate(vectors), "fsdp", axis=0, tiled=False)
+    flat = jnp.concatenate(vectors)
+    flat = jnp.pad(flat, (0, -flat.shape[0] % 2048)).reshape(-1, 128)
+    q_w = head_columns(qkv_weight[:, :width], width, c, n)
+    k_w = head_columns(qkv_weight[:, width : 2 * width], width, c, n)
+    v_w = head_columns(qkv_weight[:, 2 * width :], width, c, n)
+    x_all, packed, w_qkv = exchange(0, n, nf, ctx=[tokens[0]], fsdp=[flat, jnp.concatenate([q_w, k_w, v_w], axis=1)])
+    x_all = x_all.reshape(n * rows, width)
+    w_qkv = w_qkv.reshape(width, 3 * wide)
+    up_weight, down_weight, cotangent, packed = lax.optimization_barrier((up_weight, down_weight, cotangent, packed))
+    packed = packed.reshape(nf, -1)
     full, at = [], 0
     for vector in vectors:
         size = vector.shape[0]
@@ -251,15 +728,10 @@
         at += size
     gain1, shift1, b_qv, b_out, gain2, shift2, b_up, b_down = full
 
-    x_all = ag_ctx(tokens[0])
-    q_w = head_columns(qkv_weight[:, :width], width, c, n)
-    k_w = head_columns(qkv_weight[:, width : 2 * width], width, c, n)
-    v_w = head_columns(qkv_weight[:, 2 * width :], width, c, n)
-    w_qkv = ag_fsdp(jnp.concatenate([q_w, k_w, v_w], axis=1))
     w_out = lax.psum(head_rows(out_weight, heads, c, f, n), "fsdp")
     g2_all = ag_ctx(cotangent[0])
-    up_mine = lax.dynamic_slice_in_dim(up_weight.reshape(local, nf, n, ff_part), c, 1, axis=2)
-    w_up = ag_fsdp(up_mine.reshape(local, nf * ff_part))
+    up_mine = [lax.dynamic_slice_in_dim(up_weight, i * ff_local + c * ff_part, ff_part, axis=1) for i in range(nf)]
+    w_up = ag_fsdp(jnp.concatenate(up_mine, axis=1))
     w_down = ag_fsdp(lax.dynamic_slice_in_dim(down_weight, c * ff_part, ff_part, axis=0))
     b_up_mine = lax.dynamic_slice_in_dim(b_up.reshape(nf, n, ff_part), c, 1, axis=1).reshape(-1)
     bq = head_columns(b_qv[:width], width, c, n)
@@ -273,47 +745,41 @@
     v = (proj[:, 2 * wide :] + bv).astype(BF16)
     attn, o, total = attention_fwd(place, q, k, v, slots)
     x = tokens[0].astype(F32)
-    mid = x + rs_ctx(dot(attn, w_out)).astype(F32) + b_out
+    (mixed,) = product(1, n, nf, attn, w_out)
+    mid = x + mixed + b_out
     attn_all = spread_heads(lax.all_gather(attn, "ctx", axis=0, tiled=False), heads, n)
 
     n2, rstd2 = ln_stats(mid)
-    act2 = ag_ctx((n2 * gain2 + shift2).astype(BF16))
+    (act2,) = exchange(2, n, nf, ctx=[(n2 * gain2 + shift2).astype(BF16)])
+    act2 = act2.reshape(n * rows, width)
     u = dot(act2, w_up) + b_up_mine
     activated, gelu_back = jax.vjp(lambda t: jax.nn.gelu(t, approximate=True), u)
     hidden = activated.astype(BF16)
     dh = dot_t(g2_all, w_down)
     du = gelu_back(dh)[0].astype(BF16)
-    da2 = rs_ctx(dot_t(du, w_up)).astype(F32)
     result = mid + rs_ctx(dot(hidden, w_down)).astype(F32) + b_down
-    d_down = rs_fsdp(t_dot(hidden, g2_all))
-    d_up = rs_fsdp(t_dot(act2, du))
+    d_down = t_dot(hidden, g2_all).astype(BF16).reshape(nf, ff_part, width)
+    d_up = t_dot(act2, du).astype(BF16).reshape(nf, local, nf * ff_part)
+    da2, d_up, d_down = product(3, n, nf, du, w_up, True, red=[d_up, d_down])
     d_up_bias = jnp.sum(du.astype(F32), axis=0)
     grad_out = cotangent[0].astype(F32)
     d_down_bias = jnp.sum(grad_out, axis=0)
-    d_down = lax.all_gather(d_down, "ctx", axis=0, tiled=True)
-    d_up = lax.all_gather(d_up, "ctx", axis=0, tiled=False)
 
     d_gain2 = jnp.sum(da2 * n2, axis=0)
     d_shift2 = jnp.sum(da2, axis=0)
     d_mid = grad_out + ln_back(da2, n2, rstd2, gain2)
     g1 = d_mid.astype(BF16)
     d_out_bias = jnp.sum(g1.astype(F32), axis=0)
-    g1_all = ag_ctx(g1)
+    (g1_all,) = exchange(4, n, nf, ctx=[g1])
+    g1_all = g1_all.reshape(n * rows, width)
     d_attn = dot_t(g1_all, w_out)
     gq, gk, gv = attention_bwd(place, q, k, v, d_attn, o, total, slots)
     g_qkv = jnp.concatenate([gq, gk, gv], axis=1)
-    da1 = rs_ctx(dot_t(g_qkv, w_qkv)).astype(F32)
-    d_qkv = rs_fsdp(t_dot(act1, g_qkv))
+    d_qkv = t_dot(act1, g_qkv).astype(BF16).reshape(nf, local, 3 * wide)
     out_part = width // n
     g1_mine = lax.dynamic_slice_in_dim(g1_all, c * out_part, out_part, axis=1)
-    d_out = rs_fsdp(t_dot(attn_all, g1_mine))
-    gathered = lax.all_gather(jnp.concatenate([d_qkv, d_out], axis=1), "ctx", axis=0, tiled=False)
-    d_qkv_full = jnp.concatenate(
-        [spread_heads(gathered[:, :, i * wide : (i + 1) * wide], heads, n) for i in range(3)], axis=1
-    ).astype(F32)
-    d_out_full = jnp.transpose(gathered[:, :, 3 * wide :], (1, 0, 2)).reshape(local, width).astype(F32)
-    d_up_full = jnp.transpose(d_up.reshape(n, local, nf, ff_part), (1, 2, 0, 3)).reshape(local, ff).astype(F32)
-    d_down_full = d_down.astype(F32)
+    d_out = t_dot(attn_all, g1_mine).astype(BF16).reshape(nf, local, out_part)
+    da1, d_qkv, d_out = product(5, n, nf, g_qkv, w_qkv, True, red=[d_qkv, d_out])
 
     n1, rstd1 = ln_stats(x)
     d_gain1 = jnp.sum(da1 * n1, axis=0)
@@ -336,8 +802,20 @@
         d_down_bias,
     )
     packed = jnp.concatenate([s.reshape(nf, -1) for s in smalls], axis=1)
-    summed = lax.psum(packed, ("ctx", "fsdp"))
-    mine = lax.dynamic_slice_in_dim(summed, f, 1, axis=0)[0]
+    packed = jnp.pad(packed, ((0, 0), (0, -packed.shape[1] % 1024))).reshape(nf, -1, 128)
+    d_up, d_down, d_out, d_qkv, packed = exchange(
+        6, n, nf, ctx=[d_up, d_down, d_out, d_qkv], red=[packed]
+    )
+    mine = jnp.sum(packed, axis=0).reshape(-1)
+    d_up_full = place_columns(
+        d_up,
+        [(i, j * ff_part, j * ff_local + i * ff_part, ff_part) for i in range(n) for j in range(nf)],
+        ff,
+    )
+    d_down_full = d_down.reshape(ff_local, width).astype(F32)
+    d_out_full = place_columns(d_out, [(i, 0, i * out_part, out_part) for i in range(n)], width)
+    moves = [m for i in range(3) for m in head_moves(n, heads, i * wide, i * width)]
+    d_qkv_full = place_columns(d_qkv, moves, 3 * width)
     out, at = [], 0
     for s in smalls:
         size = s.size // nf

time: 1430 us -> 756 us (0.53)
  waiting for transfers between devices: 1060 us -> 50 us
  Pallas kernels: 27.3 us -> 536 us
  local copies, waits for them, and re-layouts: 185 us -> 55.2 us
  matrix products: 74.8 us -> 56.8 us
    pallas_call x0 -> x10, Pallas kernels: none -> 509 us  [the longest x4 347 us: exchange(): pl.pallas_call(functools.partial(exchange_body, n, nf, (len(ctx), len(fsd...]
    unnamed x26 -> x6, waiting for transfers between devices: 323 us -> 0.61 us
    all_gather x4 -> x1, waiting for transfers between devices: 224 us -> 0.01 us  [ag_ctx(): return lax.all_gather(value, 'ctx', axis=0, tiled=True)]
    all_gather x3 -> x0, waiting for transfers between devices: 224 us -> none  [the longest x1 102 us: on_device(): lax.all_gather(jnp.concatenate([d_qkv, d_out], axis=1), 'ctx', axis=0, ti...]
    psum x1 -> x0, waiting for transfers between devices: 115 us -> none  [on_device(): summed = lax.psum(packed, ('ctx', 'fsdp'))]
    all_gather x3 -> x2, waiting for transfers between devices: 60.5 us -> 0.02 us  [ag_fsdp(): return lax.all_gather(value, 'fsdp', axis=0, tiled=True)]
    convert_element_type x5 -> x3, local copies, waits for them, and re-layouts: 57.5 us -> 12 us  [the longest x1 5.84 us: on_device(): d_up = t_dot(act2, du).astype(BF16).reshape(nf, local, nf * ff_part)]
    all_gather x1, waiting for transfers between devices: 35.8 us -> 0.02 us  [on_device(): lax.all_gather(attn, 'ctx', axis=0, tiled=False)]
  transfers between devices with their start and end apart: 21 -> 6, of which waited for: 21 -> 1; matrix products, arithmetic and copies ran while one was open for 15% -> 13% of each run, Pallas kernels for 2% -> 31%
where the time goes in v3:
time: 756 us; the launch traced here: 745 us
  Pallas kernels  536 us (71%)
  matrix products  56.8 us (8%)
  local copies, waits for them, and re-layouts  55.2 us (7%)
  waiting for transfers between devices  50 us (7%)
  other arithmetic  31.9 us (4%)
  between operations  15.2 us (2%)
    pallas_call x4, Pallas kernels, exchange(): pl.pallas_call(functools.partial(exchange_body, n, nf, (len(ctx), len(fsd...  347 us
    pallas_call x3, Pallas kernels, product(): pl.pallas_call(functools.partial(product_body, n, nf, (len(fsdp), len(red...  149 us
    reduce_scatter x1, waiting for transfers between devices, rs_ctx(): lax.psum_scatter(value.astype(BF16), 'ctx', scatter_dimension=0, tiled=True)  49.3 us
    dot_general x4, matrix products, t_dot(): lax.dot_general(left, right, (((0,), (0,)), ((), ())), preferred_element_...  23.3 us
    unnamed x76, local copies, waits for them, and re-layouts  19.9 us
    dot_general x3, matrix products, dot(): return jnp.dot(left, right, preferred_element_type=F32)  18.3 us
    pallas_call x1, Pallas kernels, attention_bwd(): pl.pallas_call(functools.partial(attn_bwd_body, slots), grid=(steps,), in...  17.7 us
    dot_general x2, matrix products, dot_t(): lax.dot_general(left, right, (((1,), (1,)), ((), ())), preferred_element_...  15.2 us
  transfers between devices with their start and end apart: 6, of which 1 were waited for; matrix products, arithmetic and copies ran while one was open for 13% of the time, Pallas kernels for 31%

profile of v3, /device:TPU:0, one launch (start us, length us, event | category | flops | bytes accessed | tf_op | source)
XLA Modules:
  0.0 745.2 jit_solution(7419346737738827477)
XLA Ops:
  7.2 1.3 pad_dynamic-slice_fusion.1
  8.7 1.0 pad_maximum_fusion
  9.7 3.8 fusion.50
  13.8 1.2 constant_dynamic-slice_fusion.5
  14.9 1.0 dynamic-slice_select_fusion
  16.1 2.0 copy.53
  18.0 1.1 concatenate.36.refs_2_
  19.9 48.9 %exchange_0.1 = (bf16[8,128,1600]{2,1,0:T(8,128)(2,1)}, bf16[4,48,128]{2,1,0:T(8,128)(2,1)}, bf16[4,400,768]{2,1,0:T(8,128)(2,1)}) custom-call(bf16[128,1600]{1,0:T(8,128)(2,1)} %bitcast.85, bf16[48,128]{1,0:T(8,128)(2,1)} %pad_bitcast_fusion.1.refs_1_, bf16[400,768]{1,0:T(8,128)(2,1)} %concatenate.36.refs_2_), custom_call_target="tpu_custom_call" | custom-call | tf_op jit(solution)/shard_map/exchange_0/pallas_call | solution.py:393
  68.8 1.8 constant_dynamic-slice_fusion.4
  70.5 1.2 pad_maximum_fusion.1
  71.9 2.0 constant_dynamic-slice_fusion
  74.6 1.0 copy.54.qp_ref
  76.9 1.0 multiply_reduce_fusion
  78.0 1.5 add_convert_fusion
  80.1 3.0 fusion.53
  83.1 0.9 slice.171.k_ref
  84.3 1.2 fusion.23
  85.4 9.7 %attn_fwd.1 = (bf16[1024,256]{1,0:T(8,128)(2,1)}, f32[1024,256]{1,0:T(8,128)}, f32[1024,4]{1,0:T(8,128)}) custom-call(s32[1024,1]{1,0:T(8,128)} %copy.54.qp_ref, s32[1,1024]{1,0:T(1,128)} %bitcast.112, bf16[1024,256]{1,0:T(8,128)(2,1)} %get-tuple-element.125.q_ref, bf16[1024,256]{1,0:T(8,128)(2,1)} %slice.171.k_ref, bf16[1024,256]{1,0:T(8,128)(2,1)} %get-tuple-element.124.v_ref), custom_call_target="tpu_custom_call" | custom-call | flops 1073741824 | bytes 4194304 | tf_op jit(solution)/shard_map/attn_fwd/pallas_call | solution.py:104
  95.9 45.3 %product_1.1 = f32[128,1600]{1,0:T(8,128)} custom-call(bf16[1024,256]{1,0:T(8,128)(2,1)} %get-tuple-element.42.refs_0_, bf16[256,1600]{1,0:T(8,128)(2,1)} %all-reduce.5.cloned.1.call-done.refs_1_), custom_call_target="tpu_custom_call" | custom-call | tf_op jit(solution)/shard_map/product_1/pallas_call | solution.py:551
  141.3 1.5 fusion.48
  143.7 1.0 add_convert_fusion.1.refs_0_
  144.6 66.4 %exchange_2.1 = bf16[8,128,1600]{2,1,0:T(8,128)(2,1)} custom-call(bf16[128,1600]{1,0:T(8,128)(2,1)} %add_convert_fusion.1.refs_0_), custom_call_target="tpu_custom_call" | custom-call | tf_op jit(solution)/shard_map/exchange_2/pallas_call | solution.py:393
  211.0 8.5 %fusion.54 = f32[1024,800]{1,0:T(8,128)} fusion(bf16[1024,1600]{1,0:T(8,128)(2,1)} %bitcast.91, bf16[1600,800]{1,0:T(8,128)(2,1)} %all-gather.7.cloned.1.call-done.refs_1_), kind=kOutput, calls=%fused_computation.134 | convolution fusion | flops 2621440000 | bytes 9113600 | tf_op jit(solution)/shard_map/dot_general | solution.py:19
  219.6 6.8 convolution_convert_fusion
  226.4 3.7 copy.56
  230.1 2.1 copy.57
  232.3 1.1 convert_reduce_fusion.3
  233.5 2.8 fusion.3
  236.3 11.1 %convert_reduce_fusion.1 = (f32[800]{0:T(1024)S(1)}, bf16[1024,800]{1,0:T(8,128)(2,1)}) fusion(f32[1024,800]{1,0:T(8,128)} %fusion.54, f32[800]{0:T(1024)S(1)} %add.253, bf16[800,1600]{1,0:T(8,128)(2,1)} %all-gather.9.cloned.1.call-done, bf16[1,1024,1600]{1,2,0:T(8,128)(2,1)} %all-gather.11.cloned.1.call-done), kind=kOutput, calls=%fused_computation.19 | convolution fusion | flops 2640280832 | bytes 10758400 | tf_op jit(solution)/shard_map/dot_general | solution.py:23
  247.6 6.6 convolution_convert_fusion.2
  254.2 5.8 copy.60
  260.0 7.9 %convolution_convert_fusion.1 = bf16[800,1600]{1,0:T(8,128)(2,1)} fusion(bf16[1,1024,1600]{1,2,0:T(8,128)(2,1)S(1)} %copy-done.28, f32[1024,800]{1,0:T(8,128)} %fusion.54, f32[800]{0:T(1024)S(1)} %add.253), kind=kOutput, calls=%fused_computation.21 | convolution fusion | flops 2630912000 | bytes 9116800 | tf_op jit(solution)/shard_map/dot_general | solution.py:27
  267.9 60.2 %product_3.1 = (f32[128,1600]{1,0:T(8,128)}, bf16[400,800]{1,0:T(8,128)(2,1)}, bf16[200,1600]{1,0:T(8,128)(2,1)}) custom-call(bf16[1024,800]{1,0:T(8,128)(2,1)} %get-tuple-element.147.refs_0_, bf16[1600,800]{1,0:T(8,128)(2,1)} %all-gather.7.cloned.1.call-done.refs_1_, bf16[4,400,800]{2,1,0:T(8,128)(2,1)} %bitcast.86, bf16[4,200,1600]{2,1,0:T(8,128)(2,1)} %bitcast.98), custom_call_target="tpu_custom_call" | custom-call | tf_op jit(solution)/shard_map/product_3/pallas_call | solution.py:551
  328.1 1.6 multiply_reduce_fusion.1
  329.9 1.1 slice.143
  331.0 0.8 copy.70
  331.8 6.4 copy.69
  338.3 49.3 %reduce-scatter.2.cloned.1.call-done = bf16[128,1600]{1,0:T(8,128)(2,1)} async-done(((bf16[1024,1600]{1,0:T(8,128)(2,1)}), bf16[128,1600]{1,0:T(8,128)(2,1)}) %reduce-scatter.2.cloned.1.call-update) | async-done | bytes 409616 | tf_op jit(solution)/shard_map/reduce_scatter | solution.py:617
  387.5 2.8 convert_reduce_fusion.6
  390.3 41.9 %exchange_4.1 = bf16[8,128,1600]{2,1,0:T(8,128)(2,1)} custom-call(bf16[128,1600]{1,0:T(8,128)(2,1)} %get-tuple-element.113.refs_0_), custom_call_target="tpu_custom_call" | custom-call | tf_op jit(solution)/shard_map/exchange_4/pallas_call | solution.py:393
  432.3 4.1 fusion.55.do_ref
  436.4 17.7 %attn_bwd.1 = (bf16[1024,256]{1,0:T(8,128)(2,1)}, bf16[1024,256]{1,0:T(8,128)(2,1)}, bf16[1024,256]{1,0:T(8,128)(2,1)}) custom-call(s32[1024,1]{1,0:T(8,128)} %copy.54.qp_ref, s32[1,1024]{1,0:T(1,128)} %bitcast.113, bf16[1024,256]{1,0:T(8,128)(2,1)} %get-tuple-element.125.q_ref, bf16[1024,256]{1,0:T(8,128)(2,1)} %slice.171.k_ref, ...), custom_call_target="tpu_custom_call" | custom-call | flops 2684354560 | bytes 6291456 | tf_op jit(solution)/shard_map/attn_bwd/pallas_call | solution.py:126
  454.1 1.2 convert_reduce_fusion.5
  455.3 1.9 constant_dynamic-update-slice_fusion.2
  457.6 1.2 convert_reduce_fusion.4
  459.3 3.2 fusion.20
  462.6 2.4 copy.64
  465.0 1.9 constant_dynamic-update-slice_fusion.1
  466.8 1.9 constant_dynamic-update-slice_fusion.refs_0_
  468.7 5.6 convolution_convert_fusion.3
  474.3 43.4 %product_5.1 = (f32[128,1600]{1,0:T(8,128)}, bf16[400,768]{1,0:T(8,128)(2,1)}, bf16[400,200]{1,0:T(8,128)(2,1)}) custom-call(bf16[1024,768]{1,0:T(8,128)(2,1)} %constant_dynamic-update-slice_fusion.refs_0_, bf16[1600,768]{1,0:T(8,128)(2,1)} %bitcast.99, bf16[4,400,768]{2,1,0:T(8,128)(2,1)} %bitcast.101, bf16[4,400,200]{2,1,0:T(8,128)(2,1)} %bitcast.96), custom_call_target="tpu_custom_call" | custom-call | tf_op jit(solution)/shard_map/product_5/pallas_call | solution.py:551
  517.8 1.6 fusion.35
  520.4 189.7 %exchange_6.1 = (bf16[8,400,800]{2,1,0:T(8,128)(2,1)}, bf16[8,200,1600]{2,1,0:T(8,128)(2,1)}, bf16[8,400,200]{2,1,0:T(8,128)(2,1)}, bf16[8,400,768]{2,1,0:T(8,128)(2,1)}, f32[8,40,128]{2,1,0:T(8,128)}) custom-call(bf16[400,800]{1,0:T(8,128)(2,1)} %get-tuple-element.53.refs_0_, bf16[200,1600]{1,0:T(8,128)(2,1)} %get-tuple-element.54.refs_1_, ...), custom_call_target="tpu_custom_call" | custom-call | tf_op jit(solution)/shard_map/exchange_6/pallas_call | solution.py:393
  710.1 1.1 reduce_sum.199
  711.9 0.7 slice.150
  712.5 0.7 fusion.51
  713.2 1.2 copy.65
  714.4 1.8 fusion.34
  716.2 1.2 copy.66
  717.4 2.9 place_columns.4
  720.3 2.5 copy-done
  722.8 4.2 place_columns.3
  727.1 5.6 place_columns.5
  732.7 5.2 bitcast_convert_fusion
  (151 shorter events, 9.0 us)
Async XLA Ops:
  7.2 88.8 %all-reduce.5.cloned.1.call-start = ((), (), s32[]{:S(2)}) async-start(), calls=%async_computation.1 | async-start | bytes 1703936 | tf_op jit(solution)/shard_map/psum | solution.py:731
  9.7 201.3 %all-gather.7.cloned.1.call-start = ((), (), s32[]{:S(2)}) async-start(), calls=%async_computation.2 | async-start | bytes 3584000 | tf_op jit(solution)/shard_map/all_gather | solution.py:621
  13.5 5.6 copy-start.19
  13.5 5.6 copy-start.20
  13.6 5.6 copy-start.21
  13.6 5.6 copy-start.22
  13.6 5.6 copy-start.23
  13.6 5.6 copy-start.24
  13.6 5.6 copy-start.25
  13.6 5.6 copy-start.26
  68.7 5.8 copy-start.27
  68.7 6.9 copy-start.17
  68.8 7.6 %copy-start.2 = (bf16[8,128,1600]{2,1,0:T(8,128)(2,1)S(1)}, bf16[8,128,1600]{2,1,0:T(8,128)(2,1)}, u32[]{:S(2)}) copy-start(bf16[8,128,1600]{2,1,0:T(8,128)(2,1)} %get-tuple-element.38) | copy-start | bytes 9830404
  71.8 147.8 %all-gather.9.cloned.1.call-start = ((), (), s32[]{:S(2)}) async-start(), calls=%async_computation.3 | async-start | bytes 3328000 | tf_op jit(solution)/shard_map/all_gather | solution.py:621
  73.9 162.4 %all-gather.11.cloned.1.call-start = ((), (), s32[]{:S(2)}) async-start(), calls=%async_computation.5 | async-start | bytes 3686400 | tf_op jit(solution)/shard_map/all_gather | solution.py:613
  74.5 255.5 %all-gather.13.cloned.1.call-start = ((), (), s32[]{:S(2)}) async-start(), calls=%async_computation.6 | async-start | bytes 4718592 | tf_op jit(solution)/shard_map/all_gather | solution.py:750
  74.6 3.3 copy-start.18
  78.0 2.1 copy-start.14
  85.4 10.3 %copy-start.6 = (bf16[1,128,1600]{2,1,0:T(8,128)(2,1)S(1)}, bf16[1,128,1600]{2,1,0:T(8,128)(2,1)}, u32[]{:S(2)}) copy-start(bf16[1,128,1600]{2,1,0:T(8,128)(2,1)} %copy.53) | copy-start | bytes 1228804
  95.2 292.3 %reduce-scatter.2.cloned.1.call-start = ((), (), s32[]{:S(2)}) async-start(), calls=%async_computation.4 | async-start | bytes 3833856 | tf_op jit(solution)/shard_map/reduce_scatter | solution.py:617
  142.8 0.9 copy-start.4
  230.1 3.4 copy-start.3
  236.2 11.3 %copy-start.11 = (bf16[8,128,1600]{2,1,0:T(8,128)(2,1)S(1)}, bf16[8,128,1600]{2,1,0:T(8,128)(2,1)}, u32[]{:S(2)}) copy-start(bf16[8,128,1600]{2,1,0:T(8,128)(2,1)} %exchange_2.1) | copy-start | bytes 9830404
  254.2 5.8 copy-start.28
  267.9 60.2 %copy-start.5 = (f32[128,1600]{1,0:T(8,128)S(1)}, f32[128,1600]{1,0:T(8,128)}, u32[]{:S(2)}) copy-start(f32[128,1600]{1,0:T(8,128)} %copy-done.4) | copy-start | bytes 2457604
  331.8 55.7 %copy-start.8 = (bf16[1,128,1600]{2,1,0:T(8,128)(2,1)S(1)}, bf16[1,128,1600]{2,1,0:T(8,128)(2,1)}, u32[]{:S(2)}) copy-start(bf16[1,128,1600]{2,1,0:T(8,128)(2,1)} %copy.57) | copy-start | bytes 1228804
  331.8 55.7 %copy-start.12 = (f32[128,1600]{1,0:T(8,128)S(1)}, f32[128,1600]{1,0:T(8,128)}, u32[]{:S(2)}) copy-start(f32[128,1600]{1,0:T(8,128)} %get-tuple-element.46) | copy-start | bytes 2457604
  338.3 94.0 %copy-start.15 = (bf16[256,1600]{1,0:T(8,128)(2,1)S(1)}, bf16[256,1600]{1,0:T(8,128)(2,1)}, u32[]{:S(2)}) copy-start(bf16[256,1600]{1,0:T(8,128)(2,1)} %all-reduce.5.cloned.1.call-done.refs_1_) | copy-start | bytes 2457604
  436.4 22.9 %copy-start.13 = (bf16[8,1024,192]{1,2,0:T(8,128)(2,1)S(1)}, bf16[8,1024,192]{1,2,0:T(8,128)(2,1)}, u32[]{:S(2)}) copy-start(bf16[8,1024,192]{1,2,0:T(8,128)(2,1)} %copy.69) | copy-start | bytes 9437188
  436.4 22.9 %copy-start.16 = (bf16[1,1024,64]{1,2,0:T(8,128)(2,1)S(1)}, bf16[1,1024,64]{1,2,0:T(8,128)(2,1)}, u32[]{:S(2)}) copy-start(bf16[1,1024,64]{1,2,0:T(8,128)(2,1)} %copy.70) | copy-start | bytes 393220
  462.6 6.2 copy-start.10
  474.3 43.4 %copy-start.7 = (bf16[1,128,1600]{2,1,0:T(8,128)(2,1)S(1)}, bf16[1,128,1600]{2,1,0:T(8,128)(2,1)}, u32[]{:S(2)}) copy-start(bf16[1,128,1600]{2,1,0:T(8,128)(2,1)} %copy.53) | copy-start | bytes 1228804
  517.8 195.5 %copy-start.9 = (f32[1,128,1600]{2,1,0:T(8,128)S(1)}, f32[1,128,1600]{2,1,0:T(8,128)}, u32[]{:S(2)}) copy-start(f32[1,128,1600]{2,1,0:T(8,128)} %get-tuple-element.126) | copy-start | bytes 2457604
  710.1 7.2 copy-start.1
  720.3 6.8 slice-start
  720.3 2.5 copy-start
  722.8 4.2 slice-start.1
  722.8 9.9 %slice-start.2 = ((s8[5324800]{0:T(1024)(128)(4,1)}), s8[4194304]{0:T(1024)(128)(4,1)S(1)}, s32[]{:S(2)}) async-start(s8[5324800]{0:T(1024)(128)(4,1)} %bitcast.87), calls=%async_computation.9 | async-start | bytes 8388608
  727.1 5.6 slice-start.3
Sparse Core Ops, SparseCore 0:
  10.9 40.6 all-reduce.4
  71.9 25.5 all-gather.6
  99.7 25.7 all-gather.8
  127.4 86.8 all-gather.10
  216.2 74.3 all-gather.12
  294.7 92.7 reduce-scatter.1

commit v4 on v3

--- a/solution.py
+++ b/solution.py
@@ -151,7 +151,8 @@
 
 def turned_rows(rows, dtype, across):
     tile = 16 if dtype == BF16 else 8
-    return rows // 6 // tile * tile if across == 2 else 0
+    share = 4 if rows <= 128 else 5
+    return rows // share // tile * tile if across == 2 else 0
 
 
 def meet(near, peers):
@@ -212,6 +213,10 @@
         send, recv = self.r_send.at[j, 1, y], self.r_recv.at[j, 1, source]
         return self.copy(self.stage[j].at[y], self.far_in[j].at[source], send, recv, 2 * y + self.core)
 
+    def write(self, j, value):
+        out, first = self.red_out[j]
+        out[:, first : first + value.shape[1]] = value.astype(out.dtype)
+
     def start(self):
         for j in range(len(self.red_in)):
             for y in range(self.pairs):
@@ -236,7 +241,7 @@
             for y in self.other:
                 self.to_far(j, y, y).wait_recv()
                 value = value + self.far_in[j][y].astype(F32)
-            self.red_out[j][...] = value.astype(self.red_out[j].dtype)
+            self.write(j, value)
         for i in range(len(self.gather_in)):
             for y in self.other:
                 source = 2 * y + self.core
@@ -260,16 +265,23 @@
                 self.to_far(j, y, self.pair).wait_send()
 
 
-def exchange_body(n, nf, counts, *refs):
-    n_ctx, n_fsdp, n_red = counts
-    total = n_ctx + n_fsdp + n_red
-    ctx_in, fsdp_in, red_in = refs[:n_ctx], refs[n_ctx : n_ctx + n_fsdp], refs[n_ctx + n_fsdp : total]
-    outs = refs[total : 2 * total]
-    ctx_out, fsdp_out, red_out = outs[:n_ctx], outs[n_ctx : n_ctx + n_fsdp], outs[n_ctx + n_fsdp :]
-    scratch = refs[2 * total :]
-    sums = scratch[:n_red]
-    copy_sem, send_sem, recv_sem = scratch[n_red : n_red + 3]
-    fs = Fsdp(nf, fsdp_in, fsdp_out, red_in, sums, scratch[n_red + 3 :])
+def exchange_body(n, nf, counts, firsts, *refs):
+    n_ctx, n_fsdp, n_own, n_red, n_pack = counts
+    bounds = [0]
+    for size in counts:
+        bounds.append(bounds[-1] + size)
+    ctx_in, fsdp_in, own_in, red_in, pack_in = (refs[i:j] for i, j in zip(bounds, bounds[1:]))
+    refs = refs[bounds[-1] :]
+    n_joint = len(firsts) - n_pack
+    n_sums = n_red - n_joint + (1 if n_pack else 0)
+    ctx_out, fsdp_out, own_out = refs[:n_ctx], refs[n_ctx : n_ctx + n_fsdp], refs[n_ctx + n_fsdp : n_ctx + n_fsdp + n_own]
+    refs = refs[n_ctx + n_fsdp + n_own :]
+    red_out, sums, scratch = refs[:n_sums], refs[n_sums : 2 * n_sums], refs[2 * n_sums :]
+    copy_sem, send_sem, recv_sem = scratch[:3]
+    goals = [(out, 0) for out in own_out]
+    goals += [(sums[0], firsts[j]) for j in range(n_joint)]
+    goals += [(out, 0) for out in sums[1 if n_pack else 0 :]]
+    fs = Fsdp(nf, fsdp_in, fsdp_out, own_in + red_in, goals, scratch[3:])
 
     lines, across = split_axis(n)
     me = lax.axis_index("ctx")
@@ -341,6 +353,9 @@
         each_own(i, start)
         keep(i).start()
     fs.middle()
+    for j in range(n_pack):
+        first = firsts[n_joint + j]
+        sums[0][:, first : first + pack_in[j].shape[1]] = pack_in[j][...]
     for i in range(len(gathered)):
         if i == n_ctx:
             fs.end()
@@ -364,7 +379,7 @@
                             if d < across - 1:
                                 pl.when(near[way][0])(lambda: hop(i, source, way).start())
 
-    if not n_red:
+    if len(gathered) == n_ctx:
         fs.end()
 
     for i in range(len(gathered)):
@@ -384,39 +399,43 @@
     fs.finish()
 
 
-def exchange(call, n, nf, ctx=(), fsdp=(), red=()):
+def exchange(call, n, nf, ctx=(), fsdp=(), own=(), red=(), pack=(), firsts=()):
     shape = jax.ShapeDtypeStruct
-    gathered = max(len(ctx) + len(red), 1)
+    sums = [shape(x.shape[1:], x.dtype) for x in red]
+    if pack:
+        joint = len(firsts) - len(pack)
+        width = sum(x.shape[1] for x in [*sums[:joint], *pack])
+        sums = [shape((pack[0].shape[0], width), pack[0].dtype)] + sums[joint:]
     outs = [shape((n, *x.shape), x.dtype) for x in ctx]
     outs += [shape((nf, *x.shape), x.dtype) for x in fsdp]
-    outs += [shape((n, *x.shape[1:]), x.dtype) for x in red]
+    outs += [shape(x.shape[1:], x.dtype) for x in own]
+    outs += [shape((n, *x.shape), x.dtype) for x in sums]
+    gathered = max(len(ctx) + len(sums), 1)
+    any_spec, vmem_spec = pl.BlockSpec(memory_space=pl.ANY), pl.BlockSpec(memory_space=pltpu.VMEM)
+    inputs = (*ctx, *fsdp, *own, *red, *pack)
     return pl.pallas_call(
-        functools.partial(exchange_body, n, nf, (len(ctx), len(fsdp), len(red))),
-        in_specs=[pl.BlockSpec(memory_space=pltpu.VMEM)] * len(outs),
-        out_specs=[pl.BlockSpec(memory_space=pl.ANY)] * len(outs),
+        functools.partial(exchange_body, n, nf, (len(ctx), len(fsdp), len(own), len(red), len(pack)), firsts),
+        in_specs=[vmem_spec] * len(inputs),
+        out_specs=[any_spec] * (len(ctx) + len(fsdp)) + [vmem_spec] * len(own) + [any_spec] * len(sums),
         out_shape=outs,
-        scratch_shapes=[pltpu.VMEM(x.shape[1:], x.dtype) for x in red]
+        scratch_shapes=[pltpu.VMEM(x.shape, x.dtype) for x in sums]
         + [
             pltpu.SemaphoreType.DMA((gathered,)),
             pltpu.SemaphoreType.DMA((gathered, 4, n, 2)),
             pltpu.SemaphoreType.DMA((gathered, 4, n, 2)),
         ]
-        + Fsdp.scratch(nf, fsdp, red),
+        + Fsdp.scratch(nf, fsdp, [*own, *red]),
         name=f"exchange_{call}",
         compiler_params=pltpu.CompilerParams(collective_id=call, has_side_effects=True, vmem_limit_bytes=60 * 2**20),
-    )(*ctx, *fsdp, *red)
-
-
-def product_body(n, nf, counts, transposed, *refs):
-    n_fsdp, n_red = counts
+    )(*inputs)
+
+
+def product_body(n, n_sides, transposed, *refs):
     left, right = refs[:2]
-    more = n_fsdp + n_red
-    fsdp_in, red_in = refs[2 : 2 + n_fsdp], refs[2 + n_fsdp : 2 + more]
-    out = refs[2 + more]
-    fsdp_out, red_out = refs[3 + more : 3 + more + n_fsdp], refs[3 + more + n_fsdp : 3 + 2 * more]
-    part, acc, acc_t, over_in, sums, sums_t, line_in, line_in_t, twin_in = refs[3 + 2 * more : 12 + 2 * more]
-    o_send, o_recv, l_send, l_recv, t_send, t_recv, w_send, w_recv = refs[12 + 2 * more : 20 + 2 * more]
-    fs = Fsdp(nf, fsdp_in, fsdp_out, red_in, red_out, refs[20 + 2 * more :])
+    side_in, refs = refs[2 : 2 + 2 * n_sides], refs[2 + 2 * n_sides :]
+    out, side_out, refs = refs[0], refs[1 : 1 + n_sides], refs[1 + n_sides :]
+    part, acc, acc_t, over_in, sums, sums_t, line_in, line_in_t, twin_in = refs[:9]
+    o_send, o_recv, l_send, l_recv, t_send, t_recv, w_send, w_recv = refs[9:]
 
     lines, across = split_axis(n)
     me = lax.axis_index("ctx")
@@ -425,8 +444,7 @@
     last = turned_rows(rows, BF16, across)
     head, tail = pl.ds(0, rows - last), pl.ds(rows - last, last)
     peers = [me - b + lax.rem(b + k, across) for k in range(1, across)]
-    meet(near[:2], [("ctx", peer) for peer in peers] + [("fsdp", peer) for peer in fs.peers])
-    fs.start()
+    meet(near[:2], [("ctx", peer) for peer in peers])
 
     def copy(src, dst, send, recv, target):
         return pltpu.make_async_remote_copy(
@@ -461,8 +479,9 @@
         part[line] = value.astype(BF16).reshape(across, rows, value.shape[1])
         for k in range(1, across):
             over(line, k).start()
-    fs.middle()
-    for line in order[:-1]:
+    for step, line in enumerate(order[:-1]):
+        for j in range(step * n_sides // (lines - 1), (step + 1) * n_sides // (lines - 1)):
+            side_out[j][...] = t_dot(side_in[2 * j][...], side_in[2 * j + 1][...]).astype(BF16)
         up, down = line > a, line < a
         if last:
             acc_t[...] = part[line, :, tail].astype(F32)
@@ -516,7 +535,6 @@
             acc[...] += line_in[way, a].astype(F32)
 
     out[head, :] = acc[...]
-    fs.end()
     if last:
         twin().wait_recv()
         out[tail, :] = acc_t[b] + twin_in[...].astype(F32)
@@ -535,10 +553,12 @@
 
     if last:
         twin().wait_send()
-    fs.finish()
-
-
-def product(call, n, nf, left, right, transposed=False, fsdp=(), red=()):
+
+
+def product(call, n, left, right, transposed=False, sides=()):
+    if sides and left.shape[0] > 1024:
+        (total,) = product(call, n, left, right, transposed)
+        return [total] + [t_dot(x, y).astype(BF16) for x, y in sides]
     rows, width = left.shape[0] // n, right.shape[0 if transposed else 1]
     lines, across = split_axis(n)
     last = turned_rows(rows, BF16, across)
@@ -546,14 +566,11 @@
     shape = jax.ShapeDtypeStruct
     vmem, dma = pltpu.VMEM, pltpu.SemaphoreType.DMA
     outs = [shape((rows, width), F32)]
-    outs += [shape((nf, *x.shape), x.dtype) for x in fsdp]
-    outs += [shape(x.shape[1:], x.dtype) for x in red]
+    outs += [shape((x.shape[1], y.shape[1]), BF16) for x, y in sides]
     return pl.pallas_call(
-        functools.partial(product_body, n, nf, (len(fsdp), len(red)), transposed),
-        in_specs=[pl.BlockSpec(memory_space=vmem)] * (2 + len(fsdp) + len(red)),
-        out_specs=[pl.BlockSpec(memory_space=vmem)]
-        + [pl.BlockSpec(memory_space=pl.ANY)] * len(fsdp)
-        + [pl.BlockSpec(memory_space=vmem)] * len(red),
+        functools.partial(product_body, n, len(sides), transposed),
+        in_specs=[pl.BlockSpec(memory_space=vmem)] * (2 + 2 * len(sides)),
+        out_specs=[pl.BlockSpec(memory_space=vmem)] * len(outs),
         out_shape=outs,
         scratch_shapes=[
             vmem((lines, across, rows, width), BF16),
@@ -573,11 +590,10 @@
             dma((2, lines)),
             dma,
             dma,
-        ]
-        + Fsdp.scratch(nf, fsdp, red),
+        ],
         name=f"product_{call}",
         compiler_params=pltpu.CompilerParams(collective_id=call, has_side_effects=True, vmem_limit_bytes=63 * 2**20),
-    )(left, right, *fsdp, *red)
+    )(left, right, *[z for pair in sides for z in pair])
 
 
 def columns_body(moves, in_ref, out_ref):
@@ -719,7 +735,7 @@
     x_all, packed, w_qkv = exchange(0, n, nf, ctx=[tokens[0]], fsdp=[flat, jnp.concatenate([q_w, k_w, v_w], axis=1)])
     x_all = x_all.reshape(n * rows, width)
     w_qkv = w_qkv.reshape(width, 3 * wide)
-    up_weight, down_weight, cotangent, packed = lax.optimization_barrier((up_weight, down_weight, cotangent, packed))
+    cotangent, packed = lax.optimization_barrier((cotangent, packed))
     packed = packed.reshape(nf, -1)
     full, at = [], 0
     for vector in vectors:
@@ -730,9 +746,6 @@
 
     w_out = lax.psum(head_rows(out_weight, heads, c, f, n), "fsdp")
     g2_all = ag_ctx(cotangent[0])
-    up_mine = [lax.dynamic_slice_in_dim(up_weight, i * ff_local + c * ff_part, ff_part, axis=1) for i in range(nf)]
-    w_up = ag_fsdp(jnp.concatenate(up_mine, axis=1))
-    w_down = ag_fsdp(lax.dynamic_slice_in_dim(down_weight, c * ff_part, ff_part, axis=0))
     b_up_mine = lax.dynamic_slice_in_dim(b_up.reshape(nf, n, ff_part), c, 1, axis=1).reshape(-1)
     bq = head_columns(b_qv[:width], width, c, n)
     bv = head_columns(b_qv[width:], width, c, n)
@@ -744,8 +757,12 @@
     k = proj[:, wide : 2 * wide].astype(BF16)
     v = (proj[:, 2 * wide :] + bv).astype(BF16)
     attn, o, total = attention_fwd(place, q, k, v, slots)
+    up_weight, down_weight, attn = lax.optimization_barrier((up_weight, down_weight, attn))
+    up_mine = [lax.dynamic_slice_in_dim(up_weight, i * ff_local + c * ff_part, ff_part, axis=1) for i in range(nf)]
+    w_up = ag_fsdp(jnp.concatenate(up_mine, axis=1))
+    w_down = ag_fsdp(lax.dynamic_slice_in_dim(down_weight, c * ff_part, ff_part, axis=0))
     x = tokens[0].astype(F32)
-    (mixed,) = product(1, n, nf, attn, w_out)
+    (mixed,) = product(1, n, attn, w_out)
     mid = x + mixed + b_out
     attn_all = spread_heads(lax.all_gather(attn, "ctx", axis=0, tiled=False), heads, n)
 
@@ -757,10 +774,9 @@
     hidden = activated.astype(BF16)
     dh = dot_t(g2_all, w_down)
     du = gelu_back(dh)[0].astype(BF16)
-    result = mid + rs_ctx(dot(hidden, w_down)).astype(F32) + b_down
-    d_down = t_dot(hidden, g2_all).astype(BF16).reshape(nf, ff_part, width)
-    d_up = t_dot(act2, du).astype(BF16).reshape(nf, local, nf * ff_part)
-    da2, d_up, d_down = product(3, n, nf, du, w_up, True, red=[d_up, d_down])
+    da2, d_up, d_down = product(3, n, du, w_up, True, sides=[(act2, du), (hidden, g2_all)])
+    d_up = d_up.reshape(nf, local, nf * ff_part)
+    d_down = d_down.reshape(nf, ff_part, width)
     d_up_bias = jnp.sum(du.astype(F32), axis=0)
     grad_out = cotangent[0].astype(F32)
     d_down_bias = jnp.sum(grad_out, axis=0)
@@ -770,16 +786,18 @@
     d_mid = grad_out + ln_back(da2, n2, rstd2, gain2)
     g1 = d_mid.astype(BF16)
     d_out_bias = jnp.sum(g1.astype(F32), axis=0)
-    (g1_all,) = exchange(4, n, nf, ctx=[g1])
+    g1_all, d_up, d_down = exchange(4, n, nf, ctx=[g1], own=[d_up, d_down])
     g1_all = g1_all.reshape(n * rows, width)
+    hidden, g1_all = lax.optimization_barrier((hidden, g1_all))
+    result = mid + rs_ctx(dot(hidden, w_down)).astype(F32) + b_down
     d_attn = dot_t(g1_all, w_out)
     gq, gk, gv = attention_bwd(place, q, k, v, d_attn, o, total, slots)
     g_qkv = jnp.concatenate([gq, gk, gv], axis=1)
-    d_qkv = t_dot(act1, g_qkv).astype(BF16).reshape(nf, local, 3 * wide)
     out_part = width // n
     g1_mine = lax.dynamic_slice_in_dim(g1_all, c * out_part, out_part, axis=1)
-    d_out = t_dot(attn_all, g1_mine).astype(BF16).reshape(nf, local, out_part)
-    da1, d_qkv, d_out = product(5, n, nf, g_qkv, w_qkv, True, red=[d_qkv, d_out])
+    da1, d_qkv, d_out = product(5, n, g_qkv, w_qkv, True, sides=[(act1, g_qkv), (attn_all, g1_mine)])
+    d_qkv = d_qkv.reshape(nf, local, 3 * wide)
+    d_out = d_out.reshape(nf, local, out_part)
 
     n1, rstd1 = ln_stats(x)
     d_gain1 = jnp.sum(da1 * n1, axis=0)
@@ -803,19 +821,20 @@
     )
     packed = jnp.concatenate([s.reshape(nf, -1) for s in smalls], axis=1)
     packed = jnp.pad(packed, ((0, 0), (0, -packed.shape[1] % 1024))).reshape(nf, -1, 128)
-    d_up, d_down, d_out, d_qkv, packed = exchange(
-        6, n, nf, ctx=[d_up, d_down, d_out, d_qkv], red=[packed]
+    at_up, at_out = 3 * wide, 3 * wide + nf * ff_part
+    d_down, joint, packed = exchange(
+        6, n, nf, ctx=[d_down], red=[d_qkv, d_out, packed], pack=[d_up], firsts=(0, at_out, at_up)
     )
     mine = jnp.sum(packed, axis=0).reshape(-1)
     d_up_full = place_columns(
-        d_up,
-        [(i, j * ff_part, j * ff_local + i * ff_part, ff_part) for i in range(n) for j in range(nf)],
+        joint,
+        [(i, at_up + j * ff_part, j * ff_local + i * ff_part, ff_part) for i in range(n) for j in range(nf)],
         ff,
     )
     d_down_full = d_down.reshape(ff_local, width).astype(F32)
-    d_out_full = place_columns(d_out, [(i, 0, i * out_part, out_part) for i in range(n)], width)
+    d_out_full = place_columns(joint, [(i, at_out, i * out_part, out_part) for i in range(n)], width)
     moves = [m for i in range(3) for m in head_moves(n, heads, i * wide, i * width)]
-    d_qkv_full = place_columns(d_qkv, moves, 3 * width)
+    d_qkv_full = place_columns(joint, moves, 3 * width)
     out, at = [], 0
     for s in smalls:
         size = s.size // nf

time: 756 us -> 754 us (level)
  Pallas kernels: 536 us -> 594 us
  waiting for transfers between devices: 50 us -> 0.64 us
  matrix products: 56.8 us -> 34.5 us
  other arithmetic: 31.9 us -> 44.4 us
    reduce_scatter x1, waiting for transfers between devices: 49.3 us -> 0.01 us  [rs_ctx(): lax.psum_scatter(value.astype(BF16), 'ctx', scatter_dimension=0, tiled=True)]
    pallas_call x3, Pallas kernels: 149 us -> 177 us  [product(): pl.pallas_call(functools.partial(product_body, n, len(sides), transposed)...]
    dot_general x4 -> x0, matrix products: 23.3 us -> none  [t_dot(): lax.dot_general(left, right, (((0,), (0,)), ((), ())), preferred_element_...]
    pallas_call x4, Pallas kernels: 347 us -> 363 us  [exchange(): pl.pallas_call(functools.partial(exchange_body, n, nf, (len(ctx), len(fsd...]
    pallas_call x3, Pallas kernels: 12.8 us -> 27.3 us  [place_columns(): pl.pallas_call(functools.partial(columns_body, tuple(moves)), grid=(rows...]
    unnamed x76 -> x50, local copies, waits for them, and re-layouts: 19.9 us -> 8.39 us
    transpose x0 -> x2, local copies, waits for them, and re-layouts: none -> 10.7 us  [spread_heads(): jnp.transpose(body, (1, 0, 2)).reshape(rows, n * base * HEAD_DIM)]
    convert_element_type x2 -> x0, local copies, waits for them, and re-layouts: 8.26 us -> none  [the longest x1 5.84 us: on_device(): d_up = t_dot(act2, du).astype(BF16).reshape(nf, local, nf * ff_part)]
  transfers between devices with their start and end apart: 6 -> 6, of which waited for: 1 -> 0; matrix products, arithmetic and copies ran while one was open for 13% -> 17% of each run, Pallas kernels for 31% -> 80%
where the time goes in v4:
time: 754 us; the launch traced here: 744 us
  Pallas kernels  594 us (79%)
  local copies, waits for them, and re-layouts  54.5 us (7%)
  other arithmetic  44.4 us (6%)
  matrix products  34.5 us (5%)
  between operations  14.8 us (2%)
    pallas_call x4, Pallas kernels, exchange(): pl.pallas_call(functools.partial(exchange_body, n, nf, (len(ctx), len(fsd...  363 us
    pallas_call x3, Pallas kernels, product(): pl.pallas_call(functools.partial(product_body, n, len(sides), transposed)...  177 us
    pallas_call x3, Pallas kernels, place_columns(): pl.pallas_call(functools.partial(columns_body, tuple(moves)), grid=(rows...  27.3 us
    dot_general x3, matrix products, dot(): return jnp.dot(left, right, preferred_element_type=F32)  19.5 us
    pallas_call x1, Pallas kernels, attention_bwd(): pl.pallas_call(functools.partial(attn_bwd_body, slots), grid=(steps,), in...  17.5 us
  transfers between devices with their start and end apart: 6, of which 0 were waited for; matrix products, arithmetic and copies ran while one was open for 17% of the time, Pallas kernels for 80%

profile of v4, /device:TPU:0, one launch (start us, length us, event | category | flops | bytes accessed | tf_op | source)
XLA Modules:
  0.0 743.7 jit_solution(5735731667773804965)
XLA Ops:
  7.2 1.3 pad_dynamic-slice_fusion.1
  8.7 1.0 pad_maximum_fusion.2
  10.8 4.0 fusion.39
  14.8 1.0 dynamic-slice_select_fusion.2
  15.8 1.1 constant_dynamic-slice_fusion.8
  16.9 0.8 dynamic-slice_select_fusion
  18.0 0.6 pad_bitcast_fusion.1.refs_1_
  18.6 2.0 copy.51
  20.6 1.8 concatenate.36.refs_2_
  22.5 48.9 %exchange_0.1 = (bf16[8,128,1600]{2,1,0:T(8,128)(2,1)}, bf16[4,48,128]{2,1,0:T(8,128)(2,1)}, bf16[4,400,768]{2,1,0:T(8,128)(2,1)}) custom-call(bf16[128,1600]{1,0:T(8,128)(2,1)} %bitcast.78, bf16[48,128]{1,0:T(8,128)(2,1)} %pad_bitcast_fusion.1.refs_1_, bf16[400,768]{1,0:T(8,128)(2,1)} %concatenate.36.refs_2_), custom_call_target="tpu_custom_call" | custom-call | tf_op jit(solution)/shard_map/exchange_0/pallas_call | solution.py:416
  71.4 1.0 copy.71
  73.5 2.5 convert_reduce_fusion
  76.0 1.0 multiply_reduce_fusion
  77.4 1.5 add_convert_fusion
  79.1 3.0 fusion.42
  82.1 1.7 copy-done.6
  83.8 1.2 fusion.11
  85.1 2.1 slice.173.k_ref
  87.2 1.0 copy.52.qp_ref
  88.3 9.7 %attn_fwd.1 = (bf16[1024,256]{1,0:T(8,128)(2,1)}, f32[1024,256]{1,0:T(8,128)}, f32[1024,4]{1,0:T(8,128)}) custom-call(s32[1024,1]{1,0:T(8,128)} %copy.52.qp_ref, s32[1,1024]{1,0:T(1,128)} %bitcast.103, bf16[1024,256]{1,0:T(8,128)(2,1)} %get-tuple-element.133.q_ref, bf16[1024,256]{1,0:T(8,128)(2,1)} %slice.173.k_ref, bf16[1024,256]{1,0:T(8,128)(2,1)} %get-tuple-element.132.v_ref), custom_call_target="tpu_custom_call" | custom-call | flops 1073741824 | bytes 4194304 | tf_op jit(solution)/shard_map/attn_fwd/pallas_call | solution.py:104
  97.9 1.6 constant_dynamic-slice_fusion.5
  99.5 1.2 pad_maximum_fusion.3
  100.8 2.0 constant_dynamic-slice_fusion.1
  102.9 2.0 copy.54
  106.6 1.2 convert_reduce_fusion.2
  107.8 2.8 fusion.3.refs_2_
  110.5 42.7 %product_1.1 = f32[128,1600]{1,0:T(8,128)} custom-call(bf16[1024,256]{1,0:T(8,128)(2,1)} %get-tuple-element.47.refs_0_, bf16[256,1600]{1,0:T(8,128)(2,1)} %all-reduce.5.cloned.1.call-done.refs_1_), custom_call_target="tpu_custom_call" | custom-call | tf_op jit(solution)/shard_map/product_1/pallas_call | solution.py:570
  153.2 1.6 fusion.37
  155.1 1.0 add_convert_fusion.1.refs_0_
  156.1 81.3 %exchange_2.1 = bf16[8,128,1600]{2,1,0:T(8,128)(2,1)} custom-call(bf16[128,1600]{1,0:T(8,128)(2,1)} %add_convert_fusion.1.refs_0_), custom_call_target="tpu_custom_call" | custom-call | tf_op jit(solution)/shard_map/exchange_2/pallas_call | solution.py:416
  237.4 9.7 %multiply_convert_fusion = (bf16[1024,800]{1,0:T(8,128)(2,1)}, f32[1024,800]{1,0:T(8,128)}) fusion(f32[800]{0:T(1024)S(1)} %add.253, bf16[1024,1600]{1,0:T(8,128)(2,1)} %bitcast.79, bf16[1600,800]{1,0:T(8,128)(2,1)} %all-gather.7.cloned.1.call-done.refs_1_), kind=kOutput, calls=%fused_computation.21 | convolution fusion | flops 2629632000 | bytes 10755200 | tf_op jit(solution)/shard_map/dot_general | solution.py:19
  247.1 10.9 %convert_reduce_fusion.1 = (f32[800]{0:T(1024)S(1)}, bf16[1024,800]{1,0:T(8,128)(2,1)}) fusion(f32[1024,800]{1,0:T(8,128)} %get-tuple-element.154, f32[800]{0:T(1024)S(1)} %add.253, bf16[800,1600]{1,0:T(8,128)(2,1)} %all-gather.9.cloned.1.call-done, bf16[1,1024,1600]{2,1,0:T(8,128)(2,1)} %all-gather.11.cloned.1.call-done), kind=kOutput, calls=%fused_computation.20 | convolution fusion | flops 2640280832 | bytes 10758400 | tf_op jit(solution)/shard_map/dot_general | solution.py:23
  258.1 77.9 %product_3.1 = (f32[128,1600]{1,0:T(8,128)}, bf16[1600,800]{1,0:T(8,128)(2,1)}, bf16[800,1600]{1,0:T(8,128)(2,1)}) custom-call(bf16[1024,800]{1,0:T(8,128)(2,1)} %get-tuple-element.156.refs_0_.refs_3_, bf16[1600,800]{1,0:T(8,128)(2,1)} %all-gather.7.cloned.1.call-done.refs_1_, bf16[1024,1600]{1,0:T(8,128)(2,1)} %bitcast.80, ...), custom_call_target="tpu_custom_call" | custom-call | tf_op jit(solution)/shard_map/product_3/pallas_call | solution.py:570
  336.0 1.5 multiply_reduce_fusion.1
  337.5 2.7 convert_reduce_fusion.6
  340.3 48.8 %exchange_4.1 = (bf16[8,128,1600]{2,1,0:T(8,128)(2,1)}, bf16[400,800]{1,0:T(8,128)(2,1)}, bf16[200,1600]{1,0:T(8,128)(2,1)}) custom-call(bf16[128,1600]{1,0:T(8,128)(2,1)} %get-tuple-element.121.refs_0_, bf16[4,400,800]{2,1,0:T(8,128)(2,1)} %bitcast.86, bf16[4,200,1600]{2,1,0:T(8,128)(2,1)} %bitcast.87), custom_call_target="tpu_custom_call" | custom-call | tf_op jit(solution)/shard_map/exchange_4/pallas_call | solution.py:416
  389.1 6.8 convolution_convert_fusion
  395.9 5.5 copy.58
  402.6 4.1 fusion.43.do_ref
  406.6 17.5 %attn_bwd.1 = (bf16[1024,256]{1,0:T(8,128)(2,1)}, bf16[1024,256]{1,0:T(8,128)(2,1)}, bf16[1024,256]{1,0:T(8,128)(2,1)}) custom-call(s32[1024,1]{1,0:T(8,128)} %copy.52.qp_ref, s32[1,1024]{1,0:T(1,128)} %bitcast.104, bf16[1024,256]{1,0:T(8,128)(2,1)} %get-tuple-element.133.q_ref, bf16[1024,256]{1,0:T(8,128)(2,1)} %slice.173.k_ref, ...), custom_call_target="tpu_custom_call" | custom-call | flops 2684354560 | bytes 6291456 | tf_op jit(solution)/shard_map/attn_bwd/pallas_call | solution.py:126
  424.2 1.2 convert_reduce_fusion.5
  425.7 1.2 convert_reduce_fusion.4
  427.3 2.2 constant_dynamic-slice_fusion.refs_5_
  429.5 2.6 pad_maximum_fusion.1.refs_0_.refs_3_
  432.1 4.5 slice_bitcast_fusion
  436.6 6.2 copy.60
  442.8 4.7 copy.61
  447.5 1.1 slice_bitcast_fusion.1
  448.5 3.9 pad_maximum_fusion.refs_4_
  452.4 56.4 %product_5.1 = (f32[128,1600]{1,0:T(8,128)}, bf16[1600,768]{1,0:T(8,128)(2,1)}, bf16[1600,200]{1,0:T(8,128)(2,1)}) custom-call(bf16[1024,768]{1,0:T(8,128)(2,1)} %pad_maximum_fusion.1.refs_0_.refs_3_, bf16[1600,768]{1,0:T(8,128)(2,1)} %bitcast.89, bf16[1024,1600]{1,0:T(8,128)(2,1)} %fusion.3.refs_2_, bf16[1024,768]{1,0:T(8,128)(2,1)} %pad_maximum_fusion.1.refs_0_.refs_3_, ...), custom_call_target="tpu_custom_call" | custom-call | tf_op jit(solution)/shard_map/product_5/pallas_call | solution.py:570
  508.8 1.7 fusion.23
  510.8 0.6 copy.70
  511.5 183.6 %exchange_6.1 = (bf16[8,200,1600]{2,1,0:T(8,128)(2,1)}, bf16[8,400,1768]{2,1,0:T(8,128)(2,1)}, f32[8,40,128]{2,1,0:T(8,128)}) custom-call(bf16[200,1600]{1,0:T(8,128)(2,1)} %get-tuple-element.63.refs_0_, bf16[4,400,768]{2,1,0:T(8,128)(2,1)} %bitcast.88, bf16[4,400,200]{2,1,0:T(8,128)(2,1)} %bitcast.91, f32[4,40,128]{2,1,0:T(8,128)} %bitcast.92, ...), custom_call_target="tpu_custom_call" | custom-call | tf_op jit(solution)/shard_map/exchange_6/pallas_call | solution.py:416
  695.1 0.9 reduce_sum.199
  696.1 0.7 slice.146
  696.7 0.7 slice.150
  697.4 7.2 place_columns.4
  704.6 9.2 %place_columns.3 = f32[400,4800]{1,0:T(8,128)} custom-call(bf16[8,400,1768]{2,1,0:T(8,128)(2,1)} %get-tuple-element.68.in_ref), custom_call_target="tpu_custom_call" | custom-call | bytes 11520000 | tf_op jit(solution)/shard_map/place_columns/pallas_call | solution.py:607
  713.8 10.9 %place_columns.5 = f32[400,6400]{1,0:T(8,128)} custom-call(bf16[8,400,1768]{2,1,0:T(8,128)(2,1)} %get-tuple-element.68.in_ref), custom_call_target="tpu_custom_call" | custom-call | bytes 15360000 | tf_op jit(solution)/shard_map/place_columns/pallas_call | solution.py:607
  725.2 1.2 copy.63
  726.3 0.7 fusion.40
  727.0 7.3 bitcast_convert_fusion
  734.4 1.1 add_bitcast_fusion
  735.5 1.2 copy.62
  (123 shorter events, 8.0 us)
Async XLA Ops:
  7.2 103.4 %all-reduce.5.cloned.1.call-start = ((), (), s32[]{:S(2)}) async-start(), calls=%async_computation.1 | async-start | bytes 1703936 | tf_op jit(solution)/shard_map/psum | solution.py:747
  9.7 227.8 %all-gather.7.cloned.1.call-start = ((), (), s32[]{:S(2)}) async-start(), calls=%async_computation.2 | async-start | bytes 3584000 | tf_op jit(solution)/shard_map/all_gather | solution.py:637
  10.7 7.1 copy-start.10
  10.8 7.1 copy-start.11
  10.8 7.1 copy-start.12
  10.8 7.1 copy-start.13
  10.8 7.1 copy-start.14
  10.8 7.1 copy-start.15
  10.8 7.1 copy-start.16
  10.8 7.1 copy-start.17
  14.8 58.2 %copy-start.18 = (s32[8]{0:T(128)S(1)}, s32[8]{0:T(128)}, u32[]{:S(2)}) copy-start(s32[8]{0:T(128)} %param.28) | copy-start | bytes 100
  71.4 4.7 copy-start
  77.4 1.7 copy-start.5
  79.1 5.9 copy-start.19
  79.1 5.9 copy-start.20
  79.1 5.9 copy-start.21
  82.1 1.7 copy-start.6
  85.1 3.1 copy-start.9
  100.8 146.3 %all-gather.9.cloned.1.call-start = ((), (), s32[]{:S(2)}) async-start(), calls=%async_computation.3 | async-start | bytes 3328000 | tf_op jit(solution)/shard_map/all_gather | solution.py:637
  102.8 144.3 %all-gather.11.cloned.1.call-start = ((), (), s32[]{:S(2)}) async-start(), calls=%async_computation.5 | async-start | bytes 3833856 | tf_op jit(solution)/shard_map/all_gather | solution.py:629
  104.9 327.2 %all-gather.13.cloned.1.call-start = ((), (), s32[]{:S(2)}) async-start(), calls=%async_computation.6 | async-start | bytes 4718592 | tf_op jit(solution)/shard_map/all_gather | solution.py:767
  105.5 628.9 %reduce-scatter.2.cloned.1.call-start = ((), (), s32[]{:S(2)}) async-start(), calls=%async_computation.4 | async-start | bytes 3833856 | tf_op jit(solution)/shard_map/reduce_scatter | solution.py:633
  340.3 48.8 %copy-start.7 = (bf16[1024,800]{1,0:T(8,128)(2,1)S(1)}, bf16[1024,800]{1,0:T(8,128)(2,1)}, u32[]{:S(2)}) copy-start(bf16[1024,800]{1,0:T(8,128)(2,1)} %get-tuple-element.55.refs_4_) | copy-start | bytes 4915204
  395.9 5.6 copy-start.2
  401.4 1.2 copy-start.8
  713.8 10.9 %copy-start.1 = (bf16[1,128,1600]{2,1,0:T(8,128)(2,1)S(1)}, bf16[1,128,1600]{2,1,0:T(8,128)(2,1)}, u32[]{:S(2)}) copy-start(bf16[1,128,1600]{2,1,0:T(8,128)(2,1)} %copy.51) | copy-start | bytes 1228804
  713.8 10.9 %copy-start.3 = (f32[128,1600]{1,0:T(8,128)S(1)}, f32[128,1600]{1,0:T(8,128)}, u32[]{:S(2)}) copy-start(f32[128,1600]{1,0:T(8,128)} %get-tuple-element.62) | copy-start | bytes 2457604
  713.8 10.9 %copy-start.4 = (f32[128,1600]{1,0:T(8,128)S(1)}, f32[128,1600]{1,0:T(8,128)}, u32[]{:S(2)}) copy-start(f32[128,1600]{1,0:T(8,128)} %get-tuple-element.122) | copy-start | bytes 2457604
Sparse Core Ops, SparseCore 0:
  10.9 40.1 all-reduce.4
  100.9 25.1 all-gather.6
  128.3 25.7 all-gather.8
  156.1 79.4 all-gather.10
  237.6 95.3 all-gather.12
  401.6 83.3 reduce-scatter.1

commit v5 on v4

--- a/solution.py
+++ b/solution.py
@@ -356,15 +356,23 @@
     for j in range(n_pack):
         first = firsts[n_joint + j]
         sums[0][:, first : first + pack_in[j].shape[1]] = pack_in[j][...]
+    begun = n_ctx
     for i in range(len(gathered)):
-        if i == n_ctx:
+        if i == begun:
             fs.end()
-            for j in range(n_ctx, len(gathered)):
+            for j in range(begun, len(gathered)):
                 each_own(j, start)
                 keep(j).start()
+            begun = len(gathered)
         each_twin(i, True, start)
         for d in range(1, lines):
             each_relay(i, d, True, start)
+            if i == 0 and d == 1 and n_sums:
+                fs.end()
+                for j in range(begun, len(gathered)):
+                    each_own(j, start)
+                    keep(j).start()
+                begun = len(gathered)
 
     for i in range(len(gathered)):
         for d in range(1, across):
@@ -430,149 +438,38 @@
     )(*inputs)
 
 
-def product_body(n, n_sides, transposed, *refs):
-    left, right = refs[:2]
-    side_in, refs = refs[2 : 2 + 2 * n_sides], refs[2 + 2 * n_sides :]
-    out, side_out, refs = refs[0], refs[1 : 1 + n_sides], refs[1 + n_sides :]
-    part, acc, acc_t, over_in, sums, sums_t, line_in, line_in_t, twin_in = refs[:9]
-    o_send, o_recv, l_send, l_recv, t_send, t_recv, w_send, w_recv = refs[9:]
-
-    lines, across = split_axis(n)
-    me = lax.axis_index("ctx")
-    a, b, near = place_of(me, lines, across)
-    rows = out.shape[0]
-    last = turned_rows(rows, BF16, across)
-    head, tail = pl.ds(0, rows - last), pl.ds(rows - last, last)
-    peers = [me - b + lax.rem(b + k, across) for k in range(1, across)]
-    meet(near[:2], [("ctx", peer) for peer in peers])
-
-    def copy(src, dst, send, recv, target):
-        return pltpu.make_async_remote_copy(
-            src_ref=src, dst_ref=dst, send_sem=send, recv_sem=recv, device_id={"ctx": target}, device_id_type=MESH
-        )
-
-    def over(line, k):
-        src = part.at[line, lax.rem(b + k, across), head]
-        return copy(src, over_in.at[k - 1, line], o_send.at[k - 1, line], o_recv.at[k - 1, line], peers[k - 1])
-
-    def along(line, way):
-        target = me + (across, -across)[way]
-        return copy(sums.at[line], line_in.at[way, line], l_send.at[way, line], l_recv.at[way, line], target)
-
-    def along_t(line, way):
-        target = me + (across, -across)[way]
-        return copy(sums_t.at[line], line_in_t.at[way, line], t_send.at[way, line], t_recv.at[way, line], target)
-
-    def twin():
-        return copy(sums_t.at[a, 1 - b], twin_in, w_send, w_recv, peers[0])
-
-    order = []
-    for k in range(lines):
-        line = jnp.int32(0)
-        for av in range(lines):
-            line = jnp.where(a == av, sorted(range(lines), key=lambda j: (-abs(j - av), j))[k], line)
-        order.append(line)
-
-    for line in order:
-        lhs = left[pl.ds(pl.multiple_of(line * across * rows, across * rows), across * rows), :]
-        value = dot_t(lhs, right[...]) if transposed else dot(lhs, right[...])
-        part[line] = value.astype(BF16).reshape(across, rows, value.shape[1])
-        for k in range(1, across):
-            over(line, k).start()
-    for step, line in enumerate(order[:-1]):
-        for j in range(step * n_sides // (lines - 1), (step + 1) * n_sides // (lines - 1)):
-            side_out[j][...] = t_dot(side_in[2 * j][...], side_in[2 * j + 1][...]).astype(BF16)
-        up, down = line > a, line < a
-        if last:
-            acc_t[...] = part[line, :, tail].astype(F32)
-            for way, there in ((0, up & (a > 0)), (1, down & (a < lines - 1))):
-
-                @pl.when(there)
-                def _(way=way, line=line):
-                    along_t(line, way).wait_recv()
-                    acc_t[...] += line_in_t[way, line].astype(F32)
-
-            sums_t[line] = acc_t[...].astype(BF16)
-            pl.when(up)(lambda line=line: along_t(line, 0).start())
-            pl.when(down)(lambda line=line: along_t(line, 1).start())
-        value = part[line, b, head].astype(F32)
-        for k in range(1, across):
-            over(line, k).wait_recv()
-            value = value + over_in[k - 1, line].astype(F32)
-        acc[...] = value
-        for way, there in ((0, up & (a > 0)), (1, down & (a < lines - 1))):
-
-            @pl.when(there)
-            def _(way=way, line=line):
-                along(line, way).wait_recv()
-                acc[...] += line_in[way, line].astype(F32)
-
-        sums[line] = acc[...].astype(BF16)
-        pl.when(up)(lambda line=line: along(line, 0).start())
-        pl.when(down)(lambda line=line: along(line, 1).start())
-
-    if last:
-        acc_t[...] = part[a, :, tail].astype(F32)
-        for way in range(2):
-
-            @pl.when(near[1 - way][0])
-            def _(way=way):
-                along_t(a, way).wait_recv()
-                acc_t[...] += line_in_t[way, a].astype(F32)
-
-        sums_t[a] = acc_t[...].astype(BF16)
-        twin().start()
-    value = part[a, b, head].astype(F32)
-    for k in range(1, across):
-        over(a, k).wait_recv()
-        value = value + over_in[k - 1, a].astype(F32)
-    acc[...] = value
-    for way in range(2):
-
-        @pl.when(near[1 - way][0])
-        def _(way=way):
-            along(a, way).wait_recv()
-            acc[...] += line_in[way, a].astype(F32)
-
-    out[head, :] = acc[...]
-    if last:
-        twin().wait_recv()
-        out[tail, :] = acc_t[b] + twin_in[...].astype(F32)
-
-    for line in order:
-        for k in range(1, across):
-            over(line, k).wait_send()
-    for line in order[:-1]:
-        for way, there in ((0, line > a), (1, line < a)):
-
-            @pl.when(there)
-            def _(way=way, line=line):
-                along(line, way).wait_send()
-                if last:
-                    along_t(line, way).wait_send()
-
-    if last:
-        twin().wait_send()
-
-
-def product(call, n, left, right, transposed=False, sides=()):
-    if sides and left.shape[0] > 1024:
-        (total,) = product(call, n, left, right, transposed)
-        return [total] + [t_dot(x, y).astype(BF16) for x, y in sides]
-    rows, width = left.shape[0] // n, right.shape[0 if transposed else 1]
-    lines, across = split_axis(n)
-    last = turned_rows(rows, BF16, across)
-    some = max(last, 16)
-    shape = jax.ShapeDtypeStruct
-    vmem, dma = pltpu.VMEM, pltpu.SemaphoreType.DMA
-    outs = [shape((rows, width), F32)]
-    outs += [shape((x.shape[1], y.shape[1]), BF16) for x, y in sides]
-    return pl.pallas_call(
-        functools.partial(product_body, n, len(sides), transposed),
-        in_specs=[pl.BlockSpec(memory_space=vmem)] * (2 + 2 * len(sides)),
-        out_specs=[pl.BlockSpec(memory_space=vmem)] * len(outs),
-        out_shape=outs,
-        scratch_shapes=[
+def side_product(x, y, out, moves):
+    if moves is None:
+        out[...] = t_dot(x[...], y[...]).astype(BF16)
+        return
+    for block in sorted({move[0] for move in moves}):
+        value = t_dot(x[block], y[...]).astype(BF16)
+        for _, start, goal, size in [move for move in moves if move[0] == block]:
+            out[goal : goal + size, :] = value[start : start + size]
+
+
+class Scatter:
+    def __init__(self, n, transposed, left, right, out, scratch):
+        self.left, self.right, self.out, self.transposed = left, right, out, transposed
+        self.part, self.acc, self.acc_t, self.over_in, self.sums, self.sums_t = scratch[:6]
+        self.line_in, self.line_in_t, self.twin_in = scratch[6:9]
+        self.o_send, self.o_recv, self.l_send, self.l_recv, self.t_send, self.t_recv = scratch[9:15]
+        self.w_send, self.w_recv = scratch[15:17]
+        self.lines, self.across = split_axis(n)
+        self.me = lax.axis_index("ctx")
+        self.a, self.b, self.near = place_of(self.me, self.lines, self.across)
+        self.rows = out.shape[0]
+        self.last = turned_rows(self.rows, BF16, self.across)
+        self.head, self.tail = pl.ds(0, self.rows - self.last), pl.ds(self.rows - self.last, self.last)
+        self.peers = [self.me - self.b + lax.rem(self.b + k, self.across) for k in range(1, self.across)]
+
+    @staticmethod
+    def scratch(n, rows, width):
+        lines, across = split_axis(n)
+        last = turned_rows(rows, BF16, across)
+        some = max(last, 16)
+        vmem, dma = pltpu.VMEM, pltpu.SemaphoreType.DMA
+        return [
             vmem((lines, across, rows, width), BF16),
             vmem((rows - last, width), F32),
             vmem((across, some, width), F32),
@@ -590,30 +487,214 @@
             dma((2, lines)),
             dma,
             dma,
-        ],
+        ]
+
+    def copy(self, src, dst, send, recv, target):
+        return pltpu.make_async_remote_copy(
+            src_ref=src, dst_ref=dst, send_sem=send, recv_sem=recv, device_id={"ctx": target}, device_id_type=MESH
+        )
+
+    def over(self, line, k):
+        src = self.part.at[line, lax.rem(self.b + k, self.across), self.head]
+        send, recv = self.o_send.at[k - 1, line], self.o_recv.at[k - 1, line]
+        return self.copy(src, self.over_in.at[k - 1, line], send, recv, self.peers[k - 1])
+
+    def along(self, line, way):
+        target = self.me + (self.across, -self.across)[way]
+        send, recv = self.l_send.at[way, line], self.l_recv.at[way, line]
+        return self.copy(self.sums.at[line], self.line_in.at[way, line], send, recv, target)
+
+    def along_t(self, line, way):
+        target = self.me + (self.across, -self.across)[way]
+        send, recv = self.t_send.at[way, line], self.t_recv.at[way, line]
+        return self.copy(self.sums_t.at[line], self.line_in_t.at[way, line], send, recv, target)
+
+    def twin(self):
+        return self.copy(self.sums_t.at[self.a, 1 - self.b], self.twin_in, self.w_send, self.w_recv, self.peers[0])
+
+    def compute(self, line):
+        size = self.across * self.rows
+        lhs = self.left[pl.ds(pl.multiple_of(line * size, size), size), :]
+        value = dot_t(lhs, self.right[...]) if self.transposed else dot(lhs, self.right[...])
+        self.part[line] = value.astype(BF16).reshape(self.across, self.rows, value.shape[1])
+        for k in range(1, self.across):
+            self.over(line, k).start()
+
+    def collect(self, line, acc, landed, hop, ways):
+        for way, there in ways:
+
+            @pl.when(there)
+            def _(way=way):
+                hop(line, way).wait_recv()
+                acc[...] += landed[way, line].astype(F32)
+
+    def across_sum(self, line):
+        value = self.part[line, self.b, self.head].astype(F32)
+        for k in range(1, self.across):
+            self.over(line, k).wait_recv()
+            value = value + self.over_in[k - 1, line].astype(F32)
+        self.acc[...] = value
+
+    def pass_on(self, line):
+        up, down = line > self.a, line < self.a
+        ways = ((0, up & (self.a > 0)), (1, down & (self.a < self.lines - 1)))
+        if self.last:
+            self.acc_t[...] = self.part[line, :, self.tail].astype(F32)
+            self.collect(line, self.acc_t, self.line_in_t, self.along_t, ways)
+            self.sums_t[line] = self.acc_t[...].astype(BF16)
+            pl.when(up)(lambda: self.along_t(line, 0).start())
+            pl.when(down)(lambda: self.along_t(line, 1).start())
+        self.across_sum(line)
+        self.collect(line, self.acc, self.line_in, self.along, ways)
+        self.sums[line] = self.acc[...].astype(BF16)
+        pl.when(up)(lambda: self.along(line, 0).start())
+        pl.when(down)(lambda: self.along(line, 1).start())
+
+    def own(self):
+        ways = ((0, self.near[1][0]), (1, self.near[0][0]))
+        if self.last:
+            self.acc_t[...] = self.part[self.a, :, self.tail].astype(F32)
+            self.collect(self.a, self.acc_t, self.line_in_t, self.along_t, ways)
+            self.sums_t[self.a] = self.acc_t[...].astype(BF16)
+            self.twin().start()
+        self.across_sum(self.a)
+        self.collect(self.a, self.acc, self.line_in, self.along, ways)
+        self.out[self.head, :] = self.acc[...]
+        if self.last:
+            self.twin().wait_recv()
+            self.out[self.tail, :] = self.acc_t[self.b] + self.twin_in[...].astype(F32)
+
+    def sent(self, order):
+        for line in order:
+            for k in range(1, self.across):
+                self.over(line, k).wait_send()
+        for line in order[:-1]:
+            for way, there in ((0, line > self.a), (1, line < self.a)):
+
+                @pl.when(there)
+                def _(way=way, line=line):
+                    self.along(line, way).wait_send()
+                    if self.last:
+                        self.along_t(line, way).wait_send()
+
+        if self.last:
+            self.twin().wait_send()
+
+
+def product_body(n, nf, counts, transposed, moves, *refs):
+    n_prod, n_sides, n_fsdp = counts
+    pairs, refs = refs[: 2 * n_prod], refs[2 * n_prod :]
+    side_in, refs = refs[: 2 * n_sides], refs[2 * n_sides :]
+    fsdp_in, refs = refs[:n_fsdp], refs[n_fsdp:]
+    outs, side_out, fsdp_out = refs[:n_prod], refs[n_prod : n_prod + n_sides], refs[n_prod + n_sides : n_prod + n_sides + n_fsdp]
+    scratch = refs[n_prod + n_sides + n_fsdp :]
+    each = 17
+    jobs = [
+        Scatter(n, transposed[p], pairs[2 * p], pairs[2 * p + 1], outs[p], scratch[each * p : each * (p + 1)])
+        for p in range(n_prod)
+    ]
+    fs = Fsdp(nf, fsdp_in, fsdp_out, [], [], scratch[each * n_prod :])
+    a, lines = jobs[0].a, jobs[0].lines
+    meet(jobs[0].near[:2], [("ctx", peer) for peer in jobs[0].peers] + [("fsdp", peer) for peer in fs.peers])
+
+    order = []
+    for k in range(lines):
+        line = jnp.int32(0)
+        for av in range(lines):
+            line = jnp.where(a == av, sorted(range(lines), key=lambda j: (-abs(j - av), j))[k], line)
+        order.append(line)
+
+    for job in jobs:
+        for line in order:
+            job.compute(line)
+    fs.start()
+    steps = [(job, line) for job in jobs for line in order[:-1]]
+    for step, (job, line) in enumerate(steps):
+        job.pass_on(line)
+        for j in range(step * n_sides // len(steps), (step + 1) * n_sides // len(steps)):
+            side_product(side_in[2 * j], side_in[2 * j + 1], side_out[j], moves[j])
+        if step == len(order) - 2:
+            fs.end()
+    for job in jobs:
+        job.own()
+    for job in jobs:
+        job.sent(order)
+    fs.finish()
+
+
+def product(call, n, nf, products, sides=(), fsdp=()):
+    length = products[0][0].shape[0]
+    if length > 1024 and (sides or len(products) > 1):
+        sums = []
+        for i, one in enumerate(products):
+            total, *gathered = product(call if i == 0 else call + 10, n, nf, [one], fsdp=fsdp if i == 0 else ())
+            sums.append(total)
+            fsdp_out = gathered if i == 0 else fsdp_out
+        others = []
+        for x, y, moves in sides:
+            if moves is None:
+                others.append(t_dot(x, y).astype(BF16))
+            else:
+                ordered = sorted(moves, key=lambda move: move[2])
+                x = jnp.concatenate([x[block, :, start : start + size] for block, start, _, size in ordered], axis=1)
+                others.append(t_dot(x, y).astype(BF16))
+        return [*sums, *others, *fsdp_out]
+    rows = length // n
+    shape = jax.ShapeDtypeStruct
+    widths = [right.shape[0 if turned else 1] for _, right, turned in products]
+    outs = [shape((rows, width), F32) for width in widths]
+    for x, y, moves in sides:
+        outs.append(shape((x.shape[1] if moves is None else sum(m[3] for m in moves), y.shape[1]), BF16))
+    outs += [shape((nf, *x.shape), x.dtype) for x in fsdp]
+    inputs = [z for left, right, _ in products for z in (left, right)] + [z for x, y, _ in sides for z in (x, y)]
+    vmem_spec, any_spec = pl.BlockSpec(memory_space=pltpu.VMEM), pl.BlockSpec(memory_space=pl.ANY)
+    return pl.pallas_call(
+        functools.partial(
+            product_body,
+            n,
+            nf,
+            (len(products), len(sides), len(fsdp)),
+            tuple(turned for _, _, turned in products),
+            tuple(moves for _, _, moves in sides),
+        ),
+        in_specs=[vmem_spec] * (len(inputs) + len(fsdp)),
+        out_specs=[vmem_spec] * (len(outs) - len(fsdp)) + [any_spec] * len(fsdp),
+        out_shape=outs,
+        scratch_shapes=[s for width in widths for s in Scatter.scratch(n, rows, width)] + Fsdp.scratch(nf, fsdp, ()),
         name=f"product_{call}",
         compiler_params=pltpu.CompilerParams(collective_id=call, has_side_effects=True, vmem_limit_bytes=63 * 2**20),
-    )(left, right, *[z for pair in sides for z in pair])
-
-
-def columns_body(moves, in_ref, out_ref):
-    for block, start, goal, size in moves:
-        out_ref[:, goal : goal + size] = in_ref[block, :, start : start + size].astype(F32)
-
-
-def place_columns(value, moves, width):
-    n, rows, part = value.shape
+    )(*inputs, *fsdp)
+
+
+def layout_body(moves, joint_ref, down_ref, down_out, *outs):
+    for out_ref, per_out in zip(outs, moves):
+        for block, start, goal, size in per_out:
+            out_ref[:, goal : goal + size] = joint_ref[block, :, start : start + size].astype(F32)
+    down_out[...] = down_ref[...].astype(F32)
+
+
+def lay_out(joint, down, widths, moves):
+    n, rows, part = joint.shape
     step = next(s for s in (80, 16, rows) if rows % s == 0)
+    grid = rows // step
+    tall, wide = down.shape
     return pl.pallas_call(
-        functools.partial(columns_body, tuple(moves)),
-        grid=(rows // step,),
-        in_specs=[pl.BlockSpec((n, step, part), lambda i: (0, i, 0))],
-        out_specs=pl.BlockSpec((step, width), lambda i: (i, 0)),
-        out_shape=jax.ShapeDtypeStruct((rows, width), F32),
-        name="place_columns",
-        cost_estimate=pl.CostEstimate(flops=0, bytes_accessed=6 * rows * width, transcendentals=0),
-        compiler_params=pltpu.CompilerParams(vmem_limit_bytes=48 * 2**20),
-    )(value)
+        functools.partial(layout_body, tuple(tuple(m) for m in moves)),
+        grid=(grid,),
+        in_specs=[
+            pl.BlockSpec((n, step, part), lambda i: (0, i, 0)),
+            pl.BlockSpec((tall // grid, wide), lambda i: (i, 0)),
+        ],
+        out_specs=[pl.BlockSpec((tall // grid, wide), lambda i: (i, 0))]
+        + [pl.BlockSpec((step, width), lambda i: (i, 0)) for width in widths],
+        out_shape=[jax.ShapeDtypeStruct(down.shape, F32)]
+        + [jax.ShapeDtypeStruct((rows, width), F32) for width in widths],
+        name="lay_out",
+        cost_estimate=pl.CostEstimate(
+            flops=0, bytes_accessed=6 * (rows * sum(widths) + tall * wide), transcendentals=0
+        ),
+        compiler_params=pltpu.CompilerParams(vmem_limit_bytes=60 * 2**20),
+    )(joint, down)
 
 
 def head_moves(n, heads, offset, goal):
@@ -623,18 +704,6 @@
         (c, offset + base * HEAD_DIM, goal + (base * n + c) * HEAD_DIM, HEAD_DIM) for c in range(rest)
     ]
     return moves
-
-
-def ag_ctx(value):
-    return lax.all_gather(value, "ctx", axis=0, tiled=True)
-
-
-def rs_ctx(value):
-    return lax.psum_scatter(value.astype(BF16), "ctx", scatter_dimension=0, tiled=True)
-
-
-def ag_fsdp(value):
-    return lax.all_gather(value, "fsdp", axis=0, tiled=True)
 
 
 def head_columns(value, width, c, n):
@@ -648,19 +717,6 @@
         extra = lax.dynamic_slice_in_dim(value, start, HEAD_DIM, axis=-1)
         parts.append(jnp.where(c < rest, extra, jnp.zeros_like(extra)))
     return jnp.concatenate(parts, axis=-1)
-
-
-def spread_heads(value, heads, n):
-    base, rest = divmod(heads, n)
-    rows = value.shape[1]
-    parts = []
-    if base:
-        body = value[:, :, : base * HEAD_DIM]
-        parts.append(jnp.transpose(body, (1, 0, 2)).reshape(rows, n * base * HEAD_DIM))
-    if rest:
-        tail = value[:rest, :, base * HEAD_DIM :]
-        parts.append(jnp.transpose(tail, (1, 0, 2)).reshape(rows, rest * HEAD_DIM))
-    return jnp.concatenate(parts, axis=1)
 
 
 def place_heads(value, heads, c, n):
@@ -732,10 +788,13 @@
     q_w = head_columns(qkv_weight[:, :width], width, c, n)
     k_w = head_columns(qkv_weight[:, width : 2 * width], width, c, n)
     v_w = head_columns(qkv_weight[:, 2 * width :], width, c, n)
-    x_all, packed, w_qkv = exchange(0, n, nf, ctx=[tokens[0]], fsdp=[flat, jnp.concatenate([q_w, k_w, v_w], axis=1)])
+    w_mine = jnp.concatenate([q_w, k_w, v_w], axis=1)
+    out_mine = head_rows(out_weight, heads, c, f, n)
+    x_all, packed, w_qkv, w_out = exchange(0, n, nf, ctx=[tokens[0]], fsdp=[flat, w_mine, out_mine])
+    up_weight, down_weight, packed = lax.optimization_barrier((up_weight, down_weight, packed))
+    w_out = jnp.sum(w_out.astype(F32), axis=0).astype(BF16)
     x_all = x_all.reshape(n * rows, width)
     w_qkv = w_qkv.reshape(width, 3 * wide)
-    cotangent, packed = lax.optimization_barrier((cotangent, packed))
     packed = packed.reshape(nf, -1)
     full, at = [], 0
     for vector in vectors:
@@ -744,8 +803,6 @@
         at += size
     gain1, shift1, b_qv, b_out, gain2, shift2, b_up, b_down = full
 
-    w_out = lax.psum(head_rows(out_weight, heads, c, f, n), "fsdp")
-    g2_all = ag_ctx(cotangent[0])
     b_up_mine = lax.dynamic_slice_in_dim(b_up.reshape(nf, n, ff_part), c, 1, axis=1).reshape(-1)
     bq = head_columns(b_qv[:width], width, c, n)
     bv = head_columns(b_qv[width:], width, c, n)
@@ -757,24 +814,32 @@
     k = proj[:, wide : 2 * wide].astype(BF16)
     v = (proj[:, 2 * wide :] + bv).astype(BF16)
     attn, o, total = attention_fwd(place, q, k, v, slots)
-    up_weight, down_weight, attn = lax.optimization_barrier((up_weight, down_weight, attn))
     up_mine = [lax.dynamic_slice_in_dim(up_weight, i * ff_local + c * ff_part, ff_part, axis=1) for i in range(nf)]
-    w_up = ag_fsdp(jnp.concatenate(up_mine, axis=1))
-    w_down = ag_fsdp(lax.dynamic_slice_in_dim(down_weight, c * ff_part, ff_part, axis=0))
+    mixed, w_up = product(1, n, nf, [(attn, w_out, False)], fsdp=[jnp.concatenate(up_mine, axis=1)])
+    w_up = w_up.reshape(width, nf * ff_part)
     x = tokens[0].astype(F32)
-    (mixed,) = product(1, n, attn, w_out)
     mid = x + mixed + b_out
-    attn_all = spread_heads(lax.all_gather(attn, "ctx", axis=0, tiled=False), heads, n)
 
     n2, rstd2 = ln_stats(mid)
-    (act2,) = exchange(2, n, nf, ctx=[(n2 * gain2 + shift2).astype(BF16)])
+    act2, g2_all, attn_all, w_down = exchange(
+        2,
+        n,
+        nf,
+        ctx=[(n2 * gain2 + shift2).astype(BF16), cotangent[0], attn],
+        fsdp=[lax.dynamic_slice_in_dim(down_weight, c * ff_part, ff_part, axis=0)],
+    )
     act2 = act2.reshape(n * rows, width)
+    g2_all = g2_all.reshape(n * rows, width)
+    w_down = w_down.reshape(nf * ff_part, width)
     u = dot(act2, w_up) + b_up_mine
     activated, gelu_back = jax.vjp(lambda t: jax.nn.gelu(t, approximate=True), u)
     hidden = activated.astype(BF16)
     dh = dot_t(g2_all, w_down)
     du = gelu_back(dh)[0].astype(BF16)
-    da2, d_up, d_down = product(3, n, du, w_up, True, sides=[(act2, du), (hidden, g2_all)])
+    da2, fed, d_up, d_down = product(
+        3, n, nf, [(du, w_up, True), (hidden, w_down, False)], sides=[(act2, du, None), (hidden, g2_all, None)]
+    )
+    result = mid + fed + b_down
     d_up = d_up.reshape(nf, local, nf * ff_part)
     d_down = d_down.reshape(nf, ff_part, width)
     d_up_bias = jnp.sum(du.astype(F32), axis=0)
@@ -788,14 +853,18 @@
     d_out_bias = jnp.sum(g1.astype(F32), axis=0)
     g1_all, d_up, d_down = exchange(4, n, nf, ctx=[g1], own=[d_up, d_down])
     g1_all = g1_all.reshape(n * rows, width)
-    hidden, g1_all = lax.optimization_barrier((hidden, g1_all))
-    result = mid + rs_ctx(dot(hidden, w_down)).astype(F32) + b_down
     d_attn = dot_t(g1_all, w_out)
     gq, gk, gv = attention_bwd(place, q, k, v, d_attn, o, total, slots)
     g_qkv = jnp.concatenate([gq, gk, gv], axis=1)
     out_part = width // n
     g1_mine = lax.dynamic_slice_in_dim(g1_all, c * out_part, out_part, axis=1)
-    da1, d_qkv, d_out = product(5, n, g_qkv, w_qkv, True, sides=[(act1, g_qkv), (attn_all, g1_mine)])
+    da1, d_qkv, d_out = product(
+        5,
+        n,
+        nf,
+        [(g_qkv, w_qkv, True)],
+        sides=[(act1, g_qkv, None), (attn_all, g1_mine, head_moves(n, heads, 0, 0))],
+    )
     d_qkv = d_qkv.reshape(nf, local, 3 * wide)
     d_out = d_out.reshape(nf, local, out_part)
 
@@ -826,15 +895,12 @@
         6, n, nf, ctx=[d_down], red=[d_qkv, d_out, packed], pack=[d_up], firsts=(0, at_out, at_up)
     )
     mine = jnp.sum(packed, axis=0).reshape(-1)
-    d_up_full = place_columns(
-        joint,
-        [(i, at_up + j * ff_part, j * ff_local + i * ff_part, ff_part) for i in range(n) for j in range(nf)],
-        ff,
+    up_moves = [(i, at_up + j * ff_part, j * ff_local + i * ff_part, ff_part) for i in range(n) for j in range(nf)]
+    out_moves = [(i, at_out, i * out_part, out_part) for i in range(n)]
+    qkv_moves = [m for i in range(3) for m in head_moves(n, heads, i * wide, i * width)]
+    d_down_full, d_up_full, d_out_full, d_qkv_full = lay_out(
+        joint, d_down.reshape(ff_local, width), (ff, width, 3 * width), (up_moves, out_moves, qkv_moves)
     )
-    d_down_full = d_down.reshape(ff_local, width).astype(F32)
-    d_out_full = place_columns(joint, [(i, at_out, i * out_part, out_part) for i in range(n)], width)
-    moves = [m for i in range(3) for m in head_moves(n, heads, i * wide, i * width)]
-    d_qkv_full = place_columns(joint, moves, 3 * width)
     out, at = [], 0
     for s in smalls:
         size = s.size // nf

time: 754 us -> 727 us (0.964)
  Pallas kernels: 594 us -> 633 us
  local copies, waits for them, and re-layouts: 54.5 us -> 30.5 us
  matrix products: 34.5 us -> 20.3 us
  between operations: 14.8 us -> 1.28 us
    pallas_call x4, Pallas kernels: 363 us -> 411 us  [exchange(): pl.pallas_call(functools.partial(exchange_body, n, nf, (len(ctx), len(fsd...]
    transpose x2 -> x0, local copies, waits for them, and re-layouts: 10.7 us -> none  [spread_heads(): jnp.transpose(body, (1, 0, 2)).reshape(rows, n * base * HEAD_DIM)]
    dot_general x3 -> x2, matrix products: 19.5 us -> 8.97 us  [dot(): return jnp.dot(left, right, preferred_element_type=F32)]
    pallas_call x6 -> x4, Pallas kernels: 204 us -> 194 us  [the longest x3 177 us: product(): pl.pallas_call(functools.partial(product_body, n, nf, (len(products), len...]
  transfers between devices with their start and end apart: 6 -> 0, of which waited for: 0 -> 0; matrix products, arithmetic and copies ran while one was open for 17% -> 0% of each run, Pallas kernels for 80% -> 0%
where the time goes in v5:
time: 727 us; the launch traced here: 722 us
  Pallas kernels  633 us (87%)
  other arithmetic  37.3 us (5%)
  local copies, waits for them, and re-layouts  30.5 us (4%)
  matrix products  20.3 us (3%)
    pallas_call x4, Pallas kernels, exchange(): pl.pallas_call(functools.partial(exchange_body, n, nf, (len(ctx), len(fsd...  411 us
    pallas_call x3, Pallas kernels, product(): pl.pallas_call(functools.partial(product_body, n, nf, (len(products), len...  177 us
    pallas_call x1, Pallas kernels, attention_bwd(): pl.pallas_call(functools.partial(attn_bwd_body, slots), grid=(steps,), in...  17.5 us
    pallas_call x1, Pallas kernels, lay_out(): pl.pallas_call(functools.partial(layout_body, tuple((tuple(m) for m in mo...  17.3 us

profile of v5, /device:TPU:0, one launch (start us, length us, event | category | flops | bytes accessed | tf_op | source)
XLA Modules:
  0.0 721.9 jit_solution(16499394397248277500)
XLA Ops:
  0.7 0.8 broadcast_subtract_fusion
  1.4 0.7 multiply_add_fusion
  2.2 5.6 concatenate.32
  7.8 0.6 pad_bitcast_fusion.1.refs_1_
  8.5 1.2 copy.45
  9.9 0.5 broadcast_multiply_fusion.2
  10.4 2.0 copy.47
  12.4 1.0 copy.46.qp_ref
  13.4 0.3 pad_dynamic-slice_fusion.1
  13.7 1.0 pad_maximum_fusion.1.refs_3_
  14.7 2.8 fusion.34
  17.9 0.2 constant_dynamic-slice_fusion.6
  18.1 1.1 concatenate.33.refs_2_
  19.2 50.2 %exchange_0.1 = (bf16[8,128,1600]{2,1,0:T(8,128)(2,1)}, bf16[4,48,128]{2,1,0:T(8,128)(2,1)}, bf16[4,400,768]{2,1,0:T(8,128)(2,1)}, bf16[4,256,1600]{2,1,0:T(8,128)(2,1)}) custom-call(bf16[128,1600]{1,0:T(8,128)(2,1)} %bitcast.64, bf16[48,128]{1,0:T(8,128)(2,1)} %pad_bitcast_fusion.1.refs_1_, bf16[400,768]{1,0:T(8,128)(2,1)} %concatenate.33.refs_2_, ...), custom_call_target="tpu_custom_call" | custom-call | tf_op jit(solution)/shard_map/exchange_0/pallas_call | solution.py:424
  69.5 1.0 copy.62
  70.4 2.6 convert_reduce_fusion
  73.0 1.0 multiply_reduce_fusion
  74.1 0.6 fusion.30
  75.0 0.6 pad_maximum_fusion.5
  75.9 0.6 pad_maximum_fusion.4
  77.4 2.0 constant_dynamic-slice_fusion.1.refs_3_
  79.4 1.6 constant_dynamic-slice_fusion.5
  81.0 1.2 pad_maximum_fusion.2.refs_2_
  82.2 3.7 reduce_sum.194.refs_1_
  85.9 2.7 fusion.3.refs_2_
  88.6 1.5 add_convert_fusion
  90.1 0.2 copy-done.9
  90.3 3.0 fusion.37
  93.3 0.8 slice.161.k_ref
  94.1 1.2 fusion.11
  95.3 9.6 %attn_fwd.1 = (bf16[1024,256]{1,0:T(8,128)(2,1)}, f32[1024,256]{1,0:T(8,128)}, f32[1024,4]{1,0:T(8,128)}) custom-call(s32[1024,1]{1,0:T(8,128)} %copy.46.qp_ref, s32[1,1024]{1,0:T(1,128)} %bitcast.93, bf16[1024,256]{1,0:T(8,128)(2,1)} %get-tuple-element.152.q_ref, bf16[1024,256]{1,0:T(8,128)(2,1)} %slice.161.k_ref, bf16[1024,256]{1,0:T(8,128)(2,1)} %get-tuple-element.151.v_ref), custom_call_target="tpu_custom_call" | custom-call | flops 1073741824 | bytes 4194304 | tf_op jit(solution)/shard_map/attn_fwd/pallas_call | solution.py:104
  105.0 44.6 %product_1.1 = (f32[128,1600]{1,0:T(8,128)}, bf16[4,400,800]{2,1,0:T(8,128)(2,1)}) custom-call(bf16[1024,256]{1,0:T(8,128)(2,1)} %get-tuple-element.54.refs_0_.refs_2_, bf16[256,1600]{1,0:T(8,128)(2,1)} %reduce_sum.194.refs_1_, bf16[400,800]{1,0:T(8,128)(2,1)} %pad_maximum_fusion.2.refs_2_), custom_call_target="tpu_custom_call" | custom-call | tf_op jit(solution)/shard_map/product_1/pallas_call | solution.py:651
  149.6 1.8 fusion.32
  151.3 0.2 multiply_reduce_fusion.3
  151.6 1.0 add_convert_fusion.1.refs_0_
  152.6 127.4 %exchange_2.1 = (bf16[8,128,1600]{2,1,0:T(8,128)(2,1)}, bf16[8,128,1600]{2,1,0:T(8,128)(2,1)}, bf16[8,1024,256]{2,1,0:T(8,128)(2,1)}, bf16[4,200,1600]{2,1,0:T(8,128)(2,1)}) custom-call(bf16[128,1600]{1,0:T(8,128)(2,1)} %add_convert_fusion.1.refs_0_, bf16[128,1600]{1,0:T(8,128)(2,1)} %bitcast.66, bf16[1024,256]{1,0:T(8,128)(2,1)} %get-tuple-element.54.refs_0_.refs_2_, ...), custom_call_target="tpu_custom_call" | custom-call | tf_op jit(solution)/shard_map/exchange_2/pallas_call | solution.py:424
  280.0 6.0 fusion.38
  286.0 7.2 convert_reduce_fusion.1
  293.2 90.2 %product_3.1 = (f32[128,1600]{1,0:T(8,128)}, f32[128,1600]{1,0:T(8,128)}, bf16[1600,800]{1,0:T(8,128)(2,1)}, bf16[800,1600]{1,0:T(8,128)(2,1)}) custom-call(bf16[1024,800]{1,0:T(8,128)(2,1)} %get-tuple-element.137.refs_0_.refs_5_, bf16[1600,800]{1,0:T(8,128)(2,1)} %bitcast.73, bf16[1024,800]{1,0:T(8,128)(2,1)} %get-tuple-element.150.refs_2_.refs_6_, ...), custom_call_target="tpu_custom_call" | custom-call | tf_op jit(solution)/shard_map/product_3/pallas_call | solution.py:651
  383.7 1.5 multiply_reduce_fusion.1
  385.3 3.5 convert_reduce_fusion.6
  388.8 49.4 %exchange_4.1 = (bf16[8,128,1600]{2,1,0:T(8,128)(2,1)}, bf16[400,800]{1,0:T(8,128)(2,1)}, bf16[200,1600]{1,0:T(8,128)(2,1)}) custom-call(bf16[128,1600]{1,0:T(8,128)(2,1)} %get-tuple-element.139.refs_0_, bf16[4,400,800]{2,1,0:T(8,128)(2,1)} %bitcast.72, bf16[4,200,1600]{2,1,0:T(8,128)(2,1)} %bitcast.75), custom_call_target="tpu_custom_call" | custom-call | tf_op jit(solution)/shard_map/exchange_4/pallas_call | solution.py:424
  438.4 4.1 fusion.39.do_ref
  442.5 17.5 %attn_bwd.1 = (bf16[1024,256]{1,0:T(8,128)(2,1)}, bf16[1024,256]{1,0:T(8,128)(2,1)}, bf16[1024,256]{1,0:T(8,128)(2,1)}) custom-call(s32[1024,1]{1,0:T(8,128)} %copy.46.qp_ref, s32[1,1024]{1,0:T(1,128)} %bitcast.94, bf16[1024,256]{1,0:T(8,128)(2,1)} %get-tuple-element.152.q_ref, bf16[1024,256]{1,0:T(8,128)(2,1)} %slice.161.k_ref, ...), custom_call_target="tpu_custom_call" | custom-call | flops 2684354560 | bytes 6291456 | tf_op jit(solution)/shard_map/attn_bwd/pallas_call | solution.py:126
  460.0 2.2 constant_dynamic-slice_fusion.refs_5_
  462.2 1.2 convert_reduce_fusion.5
  463.4 0.2 fusion.27
  463.6 0.5 slice_dynamic-update-slice_fusion.1
  464.2 1.2 convert_reduce_fusion.4
  465.4 0.2 fusion.28
  465.7 2.6 pad_maximum_fusion.refs_0_.refs_3_
  468.3 42.4 %product_5.1 = (f32[128,1600]{1,0:T(8,128)}, bf16[1600,768]{1,0:T(8,128)(2,1)}, bf16[1600,200]{1,0:T(8,128)(2,1)}) custom-call(bf16[1024,768]{1,0:T(8,128)(2,1)} %pad_maximum_fusion.refs_0_.refs_3_, bf16[1600,768]{1,0:T(8,128)(2,1)} %bitcast.79, bf16[1024,1600]{1,0:T(8,128)(2,1)} %fusion.3.refs_2_, bf16[1024,768]{1,0:T(8,128)(2,1)} %pad_maximum_fusion.refs_0_.refs_3_, ...), custom_call_target="tpu_custom_call" | custom-call | tf_op jit(solution)/shard_map/product_5/pallas_call | solution.py:651
  510.7 1.6 fusion.23
  512.5 1.8 fusion.22
  514.3 1.2 copy.54
  515.5 0.2 concatenate.42
  515.7 0.6 copy.61
  516.4 1.2 copy.53
  517.5 183.9 %exchange_6.1 = (bf16[8,200,1600]{2,1,0:T(8,128)(2,1)}, bf16[8,400,1768]{2,1,0:T(8,128)(2,1)}, f32[8,40,128]{2,1,0:T(8,128)}) custom-call(bf16[200,1600]{1,0:T(8,128)(2,1)} %get-tuple-element.75.refs_0_, bf16[4,400,768]{2,1,0:T(8,128)(2,1)} %bitcast.78, bf16[4,400,200]{2,1,0:T(8,128)(2,1)} %bitcast.81, f32[4,40,128]{2,1,0:T(8,128)} %bitcast.82, ...), custom_call_target="tpu_custom_call" | custom-call | tf_op jit(solution)/shard_map/exchange_6/pallas_call | solution.py:424
  701.4 0.9 reduce_sum.212
  702.4 0.7 slice.136
  703.0 0.7 slice.140
  703.7 0.7 fusion.35
  704.4 17.3 %lay_out.1 = (f32[1600,1600]{1,0:T(8,128)}, f32[400,6400]{1,0:T(8,128)}, f32[400,1600]{1,0:T(8,128)}, f32[400,4800]{1,0:T(8,128)}) custom-call(bf16[8,400,1768]{2,1,0:T(8,128)(2,1)} %get-tuple-element.80.joint_ref, bf16[1600,1600]{1,0:T(8,128)(2,1)} %bitcast.65), custom_call_target="tpu_custom_call" | custom-call | bytes 46080000 | tf_op jit(solution)/shard_map/lay_out/pallas_call | solution.py:681
  (80 shorter events, 3.1 us)
Async XLA Ops:
  0.6 12.8 %copy-start.3 = (bf16[400,1600]{1,0:T(8,128)(2,1)S(1)}, bf16[400,1600]{1,0:T(8,128)(2,1)}, u32[]{:S(2)}) copy-start(bf16[400,1600]{1,0:T(8,128)(2,1)} %param.20) | copy-start | bytes 3840004
  2.2 12.5 %copy-start.10 = (s32[8,128]{1,0:T(8,128)}, s32[8,128]{1,0:T(8,128)S(1)}, u32[]{:S(2)}) copy-start(s32[8,128]{1,0:T(8,128)S(1)} %multiply_add_fusion) | copy-start | bytes 12292
  9.7 7.8 %copy-start.1 = (bf16[1,128,1600]{2,1,0:T(8,128)(2,1)}, bf16[1,128,1600]{2,1,0:T(8,128)(2,1)S(1)}, u32[]{:S(2)}) copy-start(bf16[1,128,1600]{2,1,0:T(8,128)(2,1)S(1)} %copy.45) | copy-start | bytes 1228804
  69.5 3.6 copy-start
  79.4 6.5 copy-start.11
  88.6 1.7 copy-start.9
  90.3 3.8 copy-start.13
  90.3 3.8 copy-start.14
  95.3 54.2 %copy-start.12 = (f32[128]{0:T(128)S(1)}, f32[128]{0:T(128)}, u32[]{:S(2)}) copy-start(f32[128]{0:T(128)} %broadcast_multiply_fusion.2) | copy-start | bytes 1540
  149.5 130.5 %copy-start.7 = (bf16[4,400,800]{2,1,0:T(8,128)(2,1)S(1)}, bf16[4,400,800]{2,1,0:T(8,128)(2,1)}, u32[]{:S(2)}) copy-start(bf16[4,400,800]{2,1,0:T(8,128)(2,1)} %get-tuple-element.62) | copy-start | bytes 7680004
  280.0 6.0 copy-start.5
  280.0 6.0 copy-start.8
  388.8 49.7 %copy-start.6 = (bf16[256,1600]{1,0:T(8,128)(2,1)S(1)}, bf16[256,1600]{1,0:T(8,128)(2,1)}, u32[]{:S(2)}) copy-start(bf16[256,1600]{1,0:T(8,128)(2,1)} %reduce_sum.194.refs_1_) | copy-start | bytes 2457604
  468.3 42.4 %copy-start.2 = (bf16[1,128,1600]{2,1,0:T(8,128)(2,1)S(1)}, bf16[1,128,1600]{2,1,0:T(8,128)(2,1)}, u32[]{:S(2)}) copy-start(bf16[1,128,1600]{2,1,0:T(8,128)(2,1)} %copy-done.1) | copy-start | bytes 1228804
  510.7 5.6 copy-start.4

commit v6 on v5

--- a/solution.py
+++ b/solution.py
@@ -265,7 +265,7 @@
                 self.to_far(j, y, self.pair).wait_send()
 
 
-def exchange_body(n, nf, counts, firsts, *refs):
+def exchange_body(n, nf, counts, firsts, moves, *refs):
     n_ctx, n_fsdp, n_own, n_red, n_pack = counts
     bounds = [0]
     for size in counts:
@@ -276,31 +276,34 @@
     n_sums = n_red - n_joint + (1 if n_pack else 0)
     ctx_out, fsdp_out, own_out = refs[:n_ctx], refs[n_ctx : n_ctx + n_fsdp], refs[n_ctx + n_fsdp : n_ctx + n_fsdp + n_own]
     refs = refs[n_ctx + n_fsdp + n_own :]
-    red_out, sums, scratch = refs[:n_sums], refs[n_sums : 2 * n_sums], refs[2 * n_sums :]
-    copy_sem, send_sem, recv_sem = scratch[:3]
+    red_out, refs = refs[:n_sums], refs[n_sums:]
+    if moves:
+        placed, refs = refs[0], refs[1:]
+    sums, scratch = refs[:n_sums], refs[n_sums:]
+    copy_sem, send_sem, recv_sem, place_send, place_recv = scratch[:5]
     goals = [(out, 0) for out in own_out]
     goals += [(sums[0], firsts[j]) for j in range(n_joint)]
     goals += [(out, 0) for out in sums[1 if n_pack else 0 :]]
-    fs = Fsdp(nf, fsdp_in, fsdp_out, own_in + red_in, goals, scratch[3:])
+    fs = Fsdp(nf, fsdp_in, fsdp_out, own_in + red_in, goals, scratch[5:])
 
     lines, across = split_axis(n)
     me = lax.axis_index("ctx")
     a, b, near = place_of(me, lines, across)
-    gathered = list(zip(ctx_in, ctx_out)) + list(zip(sums, red_out))
-    meet(near if gathered else [], [("fsdp", peer) for peer in fs.peers])
+    pieces = [(src, out, 0, out.shape[1]) for src, out in zip(ctx_in, ctx_out)]
+    late = len(pieces)
+    for src, out in reversed(list(zip(sums, red_out))):
+        pieces += [(src, out, first, rows) for first, rows in cut(out.shape[1])]
+    peers = [lax.rem(fs.f + k, nf) for k in range(1, nf)] if moves else fs.peers
+    meet(near if pieces else [], [("fsdp", peer) for peer in peers])
     fs.start()
 
-    def part(i, turned):
-        rows = gathered[i][1].shape[1]
-        last = turned_rows(rows, gathered[i][1].dtype, across)
-        return pl.ds(rows - last, last) if turned else pl.ds(0, rows - last)
-
-    def turns(i):
-        return bool(turned_rows(gathered[i][1].shape[1], gathered[i][1].dtype, across))
+    def turned_part(i):
+        return turned_rows(pieces[i][3], pieces[i][1].dtype, across)
 
     def hop(i, block, way, turned=False, own=False):
-        source, out = gathered[i]
-        rows = part(i, turned)
+        source, out, first, size = pieces[i]
+        last = turned_part(i)
+        rows = pl.ds(first + size - last, last) if turned else pl.ds(first, size - last)
         return pltpu.make_async_remote_copy(
             src_ref=source.at[rows] if own else out.at[block, rows],
             dst_ref=out.at[block, rows],
@@ -311,15 +314,17 @@
         )
 
     def keep(i):
-        return pltpu.make_async_copy(gathered[i][0], gathered[i][1].at[me], copy_sem.at[i])
+        source, out, first, size = pieces[i]
+        rows = pl.ds(first, size)
+        return pltpu.make_async_copy(source.at[rows], out.at[me, rows], copy_sem.at[i])
 
     def each_own(i, act):
-        for turned in (True, False) if turns(i) else (False,):
+        for turned in (True, False) if turned_part(i) else (False,):
             for way in (2, 3, 0, 1):
                 pl.when(near[way][0])(lambda way=way: act(hop(i, me, way, turned, True)))
 
     def each_twin(i, wait, act):
-        if turns(i):
+        if turned_part(i):
             twin = me + 1 - 2 * b
             for way in (2, 3):
 
@@ -336,7 +341,7 @@
             @pl.when(there)
             def _(way=way, shift=shift):
                 for turned, block in [(False, me + shift)] + (
-                    [(True, me + shift), (True, me + 1 - 2 * b + shift)] if turns(i) else []
+                    [(True, me + shift), (True, me + 1 - 2 * b + shift)] if turned_part(i) else []
                 ):
                     if wait:
                         hop(i, block, way, turned).wait_recv()
@@ -349,32 +354,31 @@
     def wait_send(copy):
         copy.wait_send()
 
-    for i in range(n_ctx):
-        each_own(i, start)
-        keep(i).start()
+    def begin(these):
+        for i in these:
+            each_own(i, start)
+            keep(i).start()
+
+    begin(range(late))
     fs.middle()
     for j in range(n_pack):
         first = firsts[n_joint + j]
         sums[0][:, first : first + pack_in[j].shape[1]] = pack_in[j][...]
-    begun = n_ctx
-    for i in range(len(gathered)):
-        if i == begun:
-            fs.end()
-            for j in range(begun, len(gathered)):
-                each_own(j, start)
-                keep(j).start()
-            begun = len(gathered)
-        each_twin(i, True, start)
-        for d in range(1, lines):
+    if n_sums:
+        if late:
+            each_twin(0, True, start)
+            each_relay(0, 1, True, start)
+        fs.end()
+        begin(range(late, len(pieces)))
+    for d in range(1, lines):
+        for i in range(len(pieces)):
+            if d == 1:
+                if i == 0 and late and n_sums:
+                    continue
+                each_twin(i, True, start)
             each_relay(i, d, True, start)
-            if i == 0 and d == 1 and n_sums:
-                fs.end()
-                for j in range(begun, len(gathered)):
-                    each_own(j, start)
-                    keep(j).start()
-                begun = len(gathered)
-
-    for i in range(len(gathered)):
+
+    def crossed(i):
         for d in range(1, across):
             for step in range(lines):
                 for sign in (1, -1) if step else (1,):
@@ -382,16 +386,51 @@
                         other = a + sign * step
 
                         @pl.when(there & (other >= 0) & (other < lines))
-                        def _(i=i, source=other * across + b + shift, way=way):
+                        def _(source=other * across + b + shift, way=way):
                             hop(i, source, way).wait_recv()
                             if d < across - 1:
                                 pl.when(near[way][0])(lambda: hop(i, source, way).start())
 
-    if len(gathered) == n_ctx:
+    def place(k, act_local, act_send):
+        block, row, src, dst, goal, size = moves[k]
+        source, goal = red_out[1].at[block, pl.ds(row, size)], placed.at[pl.ds(goal, size)]
+        if src == dst:
+            pl.when(fs.f == src)(lambda: act_local(pltpu.make_async_copy(source, goal, place_send.at[k])))
+            return
+        remote = pltpu.make_async_remote_copy(
+            src_ref=source,
+            dst_ref=goal,
+            send_sem=place_send.at[k],
+            recv_sem=place_recv.at[k],
+            device_id={"fsdp": jnp.int32(dst)},
+            device_id_type=MESH,
+        )
+        pl.when(fs.f == src)(lambda: act_send(remote))
+        if act_local is wait_copy:
+            pl.when(fs.f == dst)(remote.wait_recv)
+
+    def wait_copy(copy):
+        copy.wait()
+
+    if moves:
+        ready = [i for i in range(len(pieces)) if pieces[i][1] is red_out[1]]
+        for i in ready:
+            crossed(i)
+            keep(i).wait()
+        for k in range(len(moves)):
+            place(k, start, start)
+    else:
+        ready = []
+    for i in range(len(pieces)):
+        if i not in ready:
+            crossed(i)
+            keep(i).wait()
+    for k in range(len(moves)):
+        place(k, wait_copy, wait_send)
+    if not n_sums:
         fs.end()
 
-    for i in range(len(gathered)):
-        keep(i).wait()
+    for i in range(len(pieces)):
         each_own(i, wait_send)
         each_twin(i, False, wait_send)
         for d in range(1, lines):
@@ -407,7 +446,14 @@
     fs.finish()
 
 
-def exchange(call, n, nf, ctx=(), fsdp=(), own=(), red=(), pack=(), firsts=()):
+def cut(rows):
+    if rows < 400:
+        return [(0, rows)]
+    half = rows // 32 * 16
+    return [(0, rows - half), (rows - half, half)]
+
+
+def exchange(call, n, nf, ctx=(), fsdp=(), own=(), red=(), pack=(), firsts=(), moves=(), kept=0):
     shape = jax.ShapeDtypeStruct
     sums = [shape(x.shape[1:], x.dtype) for x in red]
     if pack:
@@ -418,34 +464,27 @@
     outs += [shape((nf, *x.shape), x.dtype) for x in fsdp]
     outs += [shape(x.shape[1:], x.dtype) for x in own]
     outs += [shape((n, *x.shape), x.dtype) for x in sums]
-    gathered = max(len(ctx) + len(sums), 1)
+    outs += [shape((kept, sums[1].shape[1]), sums[1].dtype)] if moves else []
+    gathered = max(len(ctx) + sum(len(cut(x.shape[0])) for x in sums), 1)
     any_spec, vmem_spec = pl.BlockSpec(memory_space=pl.ANY), pl.BlockSpec(memory_space=pltpu.VMEM)
     inputs = (*ctx, *fsdp, *own, *red, *pack)
+    dma = pltpu.SemaphoreType.DMA
     return pl.pallas_call(
-        functools.partial(exchange_body, n, nf, (len(ctx), len(fsdp), len(own), len(red), len(pack)), firsts),
+        functools.partial(
+            exchange_body, n, nf, (len(ctx), len(fsdp), len(own), len(red), len(pack)), tuple(firsts), tuple(moves)
+        ),
         in_specs=[vmem_spec] * len(inputs),
-        out_specs=[any_spec] * (len(ctx) + len(fsdp)) + [vmem_spec] * len(own) + [any_spec] * len(sums),
+        out_specs=[any_spec] * (len(ctx) + len(fsdp))
+        + [vmem_spec] * len(own)
+        + [any_spec] * (len(sums) + (1 if moves else 0)),
         out_shape=outs,
         scratch_shapes=[pltpu.VMEM(x.shape, x.dtype) for x in sums]
-        + [
-            pltpu.SemaphoreType.DMA((gathered,)),
-            pltpu.SemaphoreType.DMA((gathered, 4, n, 2)),
-            pltpu.SemaphoreType.DMA((gathered, 4, n, 2)),
-        ]
+        + [dma((gathered,)), dma((gathered, 4, n, 2)), dma((gathered, 4, n, 2))]
+        + [dma((max(len(moves), 1),))] * 2
         + Fsdp.scratch(nf, fsdp, [*own, *red]),
         name=f"exchange_{call}",
         compiler_params=pltpu.CompilerParams(collective_id=call, has_side_effects=True, vmem_limit_bytes=60 * 2**20),
     )(*inputs)
-
-
-def side_product(x, y, out, moves):
-    if moves is None:
-        out[...] = t_dot(x[...], y[...]).astype(BF16)
-        return
-    for block in sorted({move[0] for move in moves}):
-        value = t_dot(x[block], y[...]).astype(BF16)
-        for _, start, goal, size in [move for move in moves if move[0] == block]:
-            out[goal : goal + size, :] = value[start : start + size]
 
 
 class Scatter:
@@ -581,7 +620,7 @@
             self.twin().wait_send()
 
 
-def product_body(n, nf, counts, transposed, moves, *refs):
+def product_body(n, nf, counts, transposed, *refs):
     n_prod, n_sides, n_fsdp = counts
     pairs, refs = refs[: 2 * n_prod], refs[2 * n_prod :]
     side_in, refs = refs[: 2 * n_sides], refs[2 * n_sides :]
@@ -612,7 +651,7 @@
     for step, (job, line) in enumerate(steps):
         job.pass_on(line)
         for j in range(step * n_sides // len(steps), (step + 1) * n_sides // len(steps)):
-            side_product(side_in[2 * j], side_in[2 * j + 1], side_out[j], moves[j])
+            side_out[j][...] = t_dot(side_in[2 * j][...], side_in[2 * j + 1][...]).astype(BF16)
         if step == len(order) - 2:
             fs.end()
     for job in jobs:
@@ -630,23 +669,14 @@
             total, *gathered = product(call if i == 0 else call + 10, n, nf, [one], fsdp=fsdp if i == 0 else ())
             sums.append(total)
             fsdp_out = gathered if i == 0 else fsdp_out
-        others = []
-        for x, y, moves in sides:
-            if moves is None:
-                others.append(t_dot(x, y).astype(BF16))
-            else:
-                ordered = sorted(moves, key=lambda move: move[2])
-                x = jnp.concatenate([x[block, :, start : start + size] for block, start, _, size in ordered], axis=1)
-                others.append(t_dot(x, y).astype(BF16))
-        return [*sums, *others, *fsdp_out]
+        return [*sums, *[t_dot(x, y).astype(BF16) for x, y in sides], *fsdp_out]
     rows = length // n
     shape = jax.ShapeDtypeStruct
     widths = [right.shape[0 if turned else 1] for _, right, turned in products]
     outs = [shape((rows, width), F32) for width in widths]
-    for x, y, moves in sides:
-        outs.append(shape((x.shape[1] if moves is None else sum(m[3] for m in moves), y.shape[1]), BF16))
+    outs += [shape((x.shape[1], y.shape[1]), BF16) for x, y in sides]
     outs += [shape((nf, *x.shape), x.dtype) for x in fsdp]
-    inputs = [z for left, right, _ in products for z in (left, right)] + [z for x, y, _ in sides for z in (x, y)]
+    inputs = [z for left, right, _ in products for z in (left, right)] + [z for side in sides for z in side]
     vmem_spec, any_spec = pl.BlockSpec(memory_space=pltpu.VMEM), pl.BlockSpec(memory_space=pl.ANY)
     return pl.pallas_call(
         functools.partial(
@@ -655,7 +685,6 @@
             nf,
             (len(products), len(sides), len(fsdp)),
             tuple(turned for _, _, turned in products),
-            tuple(moves for _, _, moves in sides),
         ),
         in_specs=[vmem_spec] * (len(inputs) + len(fsdp)),
         out_specs=[vmem_spec] * (len(outs) - len(fsdp)) + [any_spec] * len(fsdp),
@@ -666,35 +695,45 @@
     )(*inputs, *fsdp)
 
 
-def layout_body(moves, joint_ref, down_ref, down_out, *outs):
-    for out_ref, per_out in zip(outs, moves):
+def row_moves(n, nf, heads):
+    part, local = -(-heads // n) * HEAD_DIM // nf, heads * HEAD_DIM // nf
+    moves = []
+    for block, start, goal, size in head_moves(n, heads, 0, 0):
+        done = 0
+        while done < size:
+            here, there = start + done, goal + done
+            rows = min(size - done, part - here % part, local - there % local)
+            moves.append((block, here % part, here // part, there // local, there % local, rows))
+            done += rows
+    return moves
+
+
+def layout_body(moves, joint_ref, down_ref, out_ref, down_out, out_out, *outs):
+    for ref, per_out in zip(outs, moves):
         for block, start, goal, size in per_out:
-            out_ref[:, goal : goal + size] = joint_ref[block, :, start : start + size].astype(F32)
+            ref[:, goal : goal + size] = joint_ref[block, :, start : start + size].astype(F32)
     down_out[...] = down_ref[...].astype(F32)
-
-
-def lay_out(joint, down, widths, moves):
+    out_out[...] = out_ref[...].astype(F32)
+
+
+def lay_out(joint, down, out, widths, moves):
     n, rows, part = joint.shape
     step = next(s for s in (80, 16, rows) if rows % s == 0)
     grid = rows // step
-    tall, wide = down.shape
+    plain = [pl.BlockSpec((x.shape[0] // grid, x.shape[1]), lambda i: (i, 0)) for x in (down, out)]
     return pl.pallas_call(
         functools.partial(layout_body, tuple(tuple(m) for m in moves)),
         grid=(grid,),
-        in_specs=[
-            pl.BlockSpec((n, step, part), lambda i: (0, i, 0)),
-            pl.BlockSpec((tall // grid, wide), lambda i: (i, 0)),
-        ],
-        out_specs=[pl.BlockSpec((tall // grid, wide), lambda i: (i, 0))]
-        + [pl.BlockSpec((step, width), lambda i: (i, 0)) for width in widths],
-        out_shape=[jax.ShapeDtypeStruct(down.shape, F32)]
+        in_specs=[pl.BlockSpec((n, step, part), lambda i: (0, i, 0)), *plain],
+        out_specs=plain + [pl.BlockSpec((step, width), lambda i: (i, 0)) for width in widths],
+        out_shape=[jax.ShapeDtypeStruct(x.shape, F32) for x in (down, out)]
         + [jax.ShapeDtypeStruct((rows, width), F32) for width in widths],
         name="lay_out",
         cost_estimate=pl.CostEstimate(
-            flops=0, bytes_accessed=6 * (rows * sum(widths) + tall * wide), transcendentals=0
+            flops=0, bytes_accessed=6 * (rows * sum(widths) + down.size + out.size), transcendentals=0
         ),
         compiler_params=pltpu.CompilerParams(vmem_limit_bytes=60 * 2**20),
-    )(joint, down)
+    )(joint, down, out)
 
 
 def head_moves(n, heads, offset, goal):
@@ -783,8 +822,8 @@
     place = (block_of * half + within[None, :] % half).reshape(-1)
 
     vectors = (ln1_gain, ln1_shift, qv_bias, out_bias, ln2_gain, ln2_shift, up_bias, down_bias)
-    flat = jnp.concatenate(vectors)
-    flat = jnp.pad(flat, (0, -flat.shape[0] % 2048)).reshape(-1, 128)
+    longest = max(v.shape[0] for v in vectors)
+    flat = jnp.stack([jnp.pad(v, (0, longest - v.shape[0])) for v in vectors] * (-(-16 // len(vectors))))
     q_w = head_columns(qkv_weight[:, :width], width, c, n)
     k_w = head_columns(qkv_weight[:, width : 2 * width], width, c, n)
     v_w = head_columns(qkv_weight[:, 2 * width :], width, c, n)
@@ -795,12 +834,7 @@
     w_out = jnp.sum(w_out.astype(F32), axis=0).astype(BF16)
     x_all = x_all.reshape(n * rows, width)
     w_qkv = w_qkv.reshape(width, 3 * wide)
-    packed = packed.reshape(nf, -1)
-    full, at = [], 0
-    for vector in vectors:
-        size = vector.shape[0]
-        full.append(packed[:, at : at + size].reshape(-1).astype(F32))
-        at += size
+    full = [packed[:, i, : v.shape[0]].reshape(-1).astype(F32) for i, v in enumerate(vectors)]
     gain1, shift1, b_qv, b_out, gain2, shift2, b_up, b_down = full
 
     b_up_mine = lax.dynamic_slice_in_dim(b_up.reshape(nf, n, ff_part), c, 1, axis=1).reshape(-1)
@@ -821,11 +855,11 @@
     mid = x + mixed + b_out
 
     n2, rstd2 = ln_stats(mid)
-    act2, g2_all, attn_all, w_down = exchange(
+    act2, g2_all, w_down = exchange(
         2,
         n,
         nf,
-        ctx=[(n2 * gain2 + shift2).astype(BF16), cotangent[0], attn],
+        ctx=[(n2 * gain2 + shift2).astype(BF16), cotangent[0]],
         fsdp=[lax.dynamic_slice_in_dim(down_weight, c * ff_part, ff_part, axis=0)],
     )
     act2 = act2.reshape(n * rows, width)
@@ -837,7 +871,7 @@
     dh = dot_t(g2_all, w_down)
     du = gelu_back(dh)[0].astype(BF16)
     da2, fed, d_up, d_down = product(
-        3, n, nf, [(du, w_up, True), (hidden, w_down, False)], sides=[(act2, du, None), (hidden, g2_all, None)]
+        3, n, nf, [(du, w_up, True), (hidden, w_down, False)], sides=[(act2, du), (hidden, g2_all)]
     )
     result = mid + fed + b_down
     d_up = d_up.reshape(nf, local, nf * ff_part)
@@ -856,17 +890,9 @@
     d_attn = dot_t(g1_all, w_out)
     gq, gk, gv = attention_bwd(place, q, k, v, d_attn, o, total, slots)
     g_qkv = jnp.concatenate([gq, gk, gv], axis=1)
-    out_part = width // n
-    g1_mine = lax.dynamic_slice_in_dim(g1_all, c * out_part, out_part, axis=1)
-    da1, d_qkv, d_out = product(
-        5,
-        n,
-        nf,
-        [(g_qkv, w_qkv, True)],
-        sides=[(act1, g_qkv, None), (attn_all, g1_mine, head_moves(n, heads, 0, 0))],
-    )
+    da1, d_qkv, d_out = product(5, n, nf, [(g_qkv, w_qkv, True)], sides=[(act1, g_qkv), (attn, g1_all)])
     d_qkv = d_qkv.reshape(nf, local, 3 * wide)
-    d_out = d_out.reshape(nf, local, out_part)
+    d_out = d_out.reshape(nf, wide // nf, width)
 
     n1, rstd1 = ln_stats(x)
     d_gain1 = jnp.sum(da1 * n1, axis=0)
@@ -890,16 +916,23 @@
     )
     packed = jnp.concatenate([s.reshape(nf, -1) for s in smalls], axis=1)
     packed = jnp.pad(packed, ((0, 0), (0, -packed.shape[1] % 1024))).reshape(nf, -1, 128)
-    at_up, at_out = 3 * wide, 3 * wide + nf * ff_part
-    d_down, joint, packed = exchange(
-        6, n, nf, ctx=[d_down], red=[d_qkv, d_out, packed], pack=[d_up], firsts=(0, at_out, at_up)
+    at_up = 3 * wide
+    d_down, joint, _, packed, d_out = exchange(
+        6,
+        n,
+        nf,
+        ctx=[d_down],
+        red=[d_qkv, d_out, packed],
+        pack=[d_up],
+        firsts=(0, at_up),
+        moves=row_moves(n, nf, heads),
+        kept=local,
     )
     mine = jnp.sum(packed, axis=0).reshape(-1)
     up_moves = [(i, at_up + j * ff_part, j * ff_local + i * ff_part, ff_part) for i in range(n) for j in range(nf)]
-    out_moves = [(i, at_out, i * out_part, out_part) for i in range(n)]
     qkv_moves = [m for i in range(3) for m in head_moves(n, heads, i * wide, i * width)]
-    d_down_full, d_up_full, d_out_full, d_qkv_full = lay_out(
-        joint, d_down.reshape(ff_local, width), (ff, width, 3 * width), (up_moves, out_moves, qkv_moves)
+    d_down_full, d_out_full, d_up_full, d_qkv_full = lay_out(
+        joint, d_down.reshape(ff_local, width), d_out, (ff, 3 * width), (up_moves, qkv_moves)
     )
     out, at = [], 0
     for s in smalls:

time: 727 us -> 697 us (0.959)
  Pallas kernels: 633 us -> 606 us
    pallas_call x4, Pallas kernels: 411 us -> 385 us  [exchange(): pl.pallas_call(functools.partial(exchange_body, n, nf, (len(ctx), len(fsd...]
where the time goes in v6:
time: 697 us; the launch traced here: 693 us
  Pallas kernels  606 us (87%)
  other arithmetic  38.1 us (5%)
  local copies, waits for them, and re-layouts  27.4 us (4%)
  matrix products  20.3 us (3%)
    pallas_call x4, Pallas kernels, exchange(): pl.pallas_call(functools.partial(exchange_body, n, nf, (len(ctx), len(fsd...  385 us
    pallas_call x3, Pallas kernels, product(): pl.pallas_call(functools.partial(product_body, n, nf, (len(products), len...  176 us
    pallas_call x1, Pallas kernels, attention_bwd(): pl.pallas_call(functools.partial(attn_bwd_body, slots), grid=(steps,), in...  17.5 us
    pallas_call x1, Pallas kernels, lay_out(): pl.pallas_call(functools.partial(layout_body, tuple((tuple(m) for m in mo...  17.5 us

profile of v6, /device:TPU:0, one launch (start us, length us, event | category | flops | bytes accessed | tf_op | source)
XLA Modules:
  0.0 692.9 jit_solution(4907043809901827988)
XLA Ops:
  0.7 0.8 broadcast_subtract_fusion
  1.5 0.7 multiply_add_fusion
  2.2 0.7 pad.31
  2.9 0.7 pad.32
  3.6 0.7 pad.33
  4.3 0.7 pad.34
  5.0 0.7 pad.35
  5.7 0.7 pad.36
  6.4 0.7 pad.37
  7.1 0.7 stack.41
  7.8 1.4 stack.43.refs_1_
  9.3 1.2 copy.45
  10.7 1.0 copy.47
  11.7 1.0 copy.46.qp_ref
  12.7 0.3 pad_dynamic-slice_fusion.1
  13.0 1.0 pad_maximum_fusion.1.refs_3_
  14.0 2.8 fusion.34
  17.4 1.1 concatenate.29.refs_2_
  18.5 50.3 %exchange_0.1 = (bf16[8,128,1600]{2,1,0:T(8,128)(2,1)}, bf16[4,16,1600]{2,1,0:T(8,128)(2,1)}, bf16[4,400,768]{2,1,0:T(8,128)(2,1)}, bf16[4,256,1600]{2,1,0:T(8,128)(2,1)}) custom-call(bf16[128,1600]{1,0:T(8,128)(2,1)} %bitcast.58, bf16[16,1600]{1,0:T(8,128)(2,1)} %stack.43.refs_1_, bf16[400,768]{1,0:T(8,128)(2,1)} %concatenate.29.refs_2_, ...), custom_call_target="tpu_custom_call" | custom-call | tf_op jit(solution)/shard_map/exchange_0/pallas_call | solution.py:472
  68.8 2.6 convert_reduce_fusion
  71.5 0.3 copy-done
  71.8 1.0 multiply_reduce_fusion
  72.9 0.8 slice_convert_fusion.1
  74.4 1.0 convert_reduce_fusion.7
  75.4 1.2 convert_reduce_fusion.8
  77.3 2.0 constant_dynamic-slice_fusion.refs_2_
  79.3 1.6 constant_dynamic-slice_fusion.4
  80.9 1.2 pad_maximum_fusion.2.refs_2_
  82.2 3.6 reduce_sum.194.refs_1_
  85.8 2.7 fusion.3.refs_2_
  88.5 1.5 add_convert_fusion
  90.2 3.0 fusion.36
  93.2 0.8 slice.155.k_ref
  94.1 1.3 fusion.11
  95.3 9.6 %attn_fwd.1 = (bf16[1024,256]{1,0:T(8,128)(2,1)}, f32[1024,256]{1,0:T(8,128)}, f32[1024,4]{1,0:T(8,128)}) custom-call(s32[1024,1]{1,0:T(8,128)} %copy.46.qp_ref, s32[1,1024]{1,0:T(1,128)} %bitcast.83, bf16[1024,256]{1,0:T(8,128)(2,1)} %get-tuple-element.160.q_ref, bf16[1024,256]{1,0:T(8,128)(2,1)} %slice.155.k_ref, bf16[1024,256]{1,0:T(8,128)(2,1)} %get-tuple-element.159.v_ref), custom_call_target="tpu_custom_call" | custom-call | flops 1073741824 | bytes 4194304 | tf_op jit(solution)/shard_map/attn_fwd/pallas_call | solution.py:104
  104.9 44.1 %product_1.1 = (f32[128,1600]{1,0:T(8,128)}, bf16[4,400,800]{2,1,0:T(8,128)(2,1)}) custom-call(bf16[1024,256]{1,0:T(8,128)(2,1)} %get-tuple-element.54.refs_0_.refs_4_, bf16[256,1600]{1,0:T(8,128)(2,1)} %reduce_sum.194.refs_1_, bf16[400,800]{1,0:T(8,128)(2,1)} %pad_maximum_fusion.2.refs_2_), custom_call_target="tpu_custom_call" | custom-call | tf_op jit(solution)/shard_map/product_1/pallas_call | solution.py:681
  149.0 1.8 fusion.32
  150.8 0.2 multiply_reduce_fusion.3
  151.0 1.0 add_convert_fusion.1.refs_0_
  152.0 82.5 %exchange_2.1 = (bf16[8,128,1600]{2,1,0:T(8,128)(2,1)}, bf16[8,128,1600]{2,1,0:T(8,128)(2,1)}, bf16[4,200,1600]{2,1,0:T(8,128)(2,1)}) custom-call(bf16[128,1600]{1,0:T(8,128)(2,1)} %add_convert_fusion.1.refs_0_, bf16[128,1600]{1,0:T(8,128)(2,1)} %bitcast.60, bf16[200,1600]{1,0:T(8,128)(2,1)} %constant_dynamic-slice_fusion.refs_2_), custom_call_target="tpu_custom_call" | custom-call | tf_op jit(solution)/shard_map/exchange_2/pallas_call | solution.py:472
  234.5 6.0 fusion.37
  240.5 7.2 %convert_reduce_fusion.1 = (f32[800]{0:T(1024)S(1)}, bf16[1024,800]{1,0:T(8,128)(2,1)}, bf16[1024,800]{1,0:T(8,128)(2,1)}) fusion(f32[1024,800]{1,0:T(8,128)S(1)} %fusion.37, f32[800]{0:T(1024)S(1)} %add.260, bf16[1024,1600]{1,0:T(8,128)(2,1)S(1)} %bitcast.66, bf16[800,1600]{1,0:T(8,128)(2,1)S(1)} %bitcast.73), kind=kOutput, calls=%fused_computation.17 | convolution fusion | flops 2641919232 | bytes 12396800 | tf_op jit(solution)/shard_map/dot_general | solution.py:23
  247.8 89.7 %product_3.1 = (f32[128,1600]{1,0:T(8,128)}, f32[128,1600]{1,0:T(8,128)}, bf16[1600,800]{1,0:T(8,128)(2,1)}, bf16[800,1600]{1,0:T(8,128)(2,1)}) custom-call(bf16[1024,800]{1,0:T(8,128)(2,1)} %get-tuple-element.145.refs_0_.refs_5_, bf16[1600,800]{1,0:T(8,128)(2,1)} %bitcast.69, bf16[1024,800]{1,0:T(8,128)(2,1)} %get-tuple-element.158.refs_2_.refs_6_, ...), custom_call_target="tpu_custom_call" | custom-call | tf_op jit(solution)/shard_map/product_3/pallas_call | solution.py:681
  337.7 1.5 multiply_reduce_fusion.1
  339.4 3.5 convert_reduce_fusion.6
  342.9 49.5 %exchange_4.1 = (bf16[8,128,1600]{2,1,0:T(8,128)(2,1)}, bf16[400,800]{1,0:T(8,128)(2,1)}, bf16[200,1600]{1,0:T(8,128)(2,1)}) custom-call(bf16[128,1600]{1,0:T(8,128)(2,1)} %get-tuple-element.147.refs_0_, bf16[4,400,800]{2,1,0:T(8,128)(2,1)} %bitcast.68, bf16[4,200,1600]{2,1,0:T(8,128)(2,1)} %bitcast.71), custom_call_target="tpu_custom_call" | custom-call | tf_op jit(solution)/shard_map/exchange_4/pallas_call | solution.py:472
  392.7 4.1 fusion.38.do_ref
  396.7 17.5 %attn_bwd.1 = (bf16[1024,256]{1,0:T(8,128)(2,1)}, bf16[1024,256]{1,0:T(8,128)(2,1)}, bf16[1024,256]{1,0:T(8,128)(2,1)}) custom-call(s32[1024,1]{1,0:T(8,128)} %copy.46.qp_ref, s32[1,1024]{1,0:T(1,128)} %bitcast.84, bf16[1024,256]{1,0:T(8,128)(2,1)} %get-tuple-element.160.q_ref, bf16[1024,256]{1,0:T(8,128)(2,1)} %slice.155.k_ref, ...), custom_call_target="tpu_custom_call" | custom-call | flops 2684354560 | bytes 6291456 | tf_op jit(solution)/shard_map/attn_bwd/pallas_call | solution.py:126
  414.3 1.2 convert_reduce_fusion.5
  415.6 0.5 slice_dynamic-update-slice_fusion.1
  416.2 1.2 convert_reduce_fusion.4
  417.8 2.6 pad_maximum_fusion.refs_0_.refs_3_
  420.4 42.2 %product_5.1 = (f32[128,1600]{1,0:T(8,128)}, bf16[1600,768]{1,0:T(8,128)(2,1)}, bf16[256,1600]{1,0:T(8,128)(2,1)}) custom-call(bf16[1024,768]{1,0:T(8,128)(2,1)} %pad_maximum_fusion.refs_0_.refs_3_, bf16[1600,768]{1,0:T(8,128)(2,1)} %bitcast.75, bf16[1024,1600]{1,0:T(8,128)(2,1)} %fusion.3.refs_2_, bf16[1024,768]{1,0:T(8,128)(2,1)} %pad_maximum_fusion.refs_0_.refs_3_, ...), custom_call_target="tpu_custom_call" | custom-call | tf_op jit(solution)/shard_map/product_5/pallas_call | solution.py:681
  462.6 1.6 fusion.23
  464.4 1.8 fusion.22
  466.2 1.2 copy.54
  467.6 0.6 copy.59
  468.2 1.2 copy.53
  469.4 202.8 %exchange_6.1 = (bf16[8,200,1600]{2,1,0:T(8,128)(2,1)}, bf16[8,400,1568]{2,1,0:T(8,128)(2,1)}, bf16[8,64,1600]{2,1,0:T(8,128)(2,1)}, f32[8,40,128]{2,1,0:T(8,128)}, bf16[400,1600]{1,0:T(8,128)(2,1)}) custom-call(bf16[200,1600]{1,0:T(8,128)(2,1)} %get-tuple-element.74.refs_0_, bf16[4,400,768]{2,1,0:T(8,128)(2,1)} %bitcast.74, bf16[4,64,1600]{2,1,0:T(8,128)(2,1)} %bitcast.77, ...), custom_call_target="tpu_custom_call" | custom-call | tf_op jit(solution)/shard_map/exchange_6/pallas_call | solution.py:472
  672.2 0.9 reduce_sum.212
  673.2 0.7 slice.128
  673.8 0.7 slice.132
  674.5 0.7 fusion.35
  675.2 17.5 %lay_out.1 = (f32[1600,1600]{1,0:T(8,128)}, f32[400,1600]{1,0:T(8,128)}, f32[400,6400]{1,0:T(8,128)}, f32[400,4800]{1,0:T(8,128)}) custom-call(bf16[8,400,1568]{2,1,0:T(8,128)(2,1)} %get-tuple-element.79.joint_ref, bf16[1600,1600]{1,0:T(8,128)(2,1)} %bitcast.59, bf16[400,1600]{1,0:T(8,128)(2,1)} %get-tuple-element.81.out_ref), custom_call_target="tpu_custom_call" | custom-call | bytes 46080000 | tf_op jit(solution)/shard_map/lay_out/pallas_call | solution.py:724
  (86 shorter events, 4.0 us)
Async XLA Ops:
  0.6 12.1 %copy-start.3 = (bf16[400,1600]{1,0:T(8,128)(2,1)S(1)}, bf16[400,1600]{1,0:T(8,128)(2,1)}, u32[]{:S(2)}) copy-start(bf16[400,1600]{1,0:T(8,128)(2,1)} %param.20) | copy-start | bytes 3840004
  0.7 10.0 %copy-start.10 = (bf16[1,128,1600]{1,2,0:T(8,128)(2,1)S(1)}, bf16[1,128,1600]{1,2,0:T(8,128)(2,1)}, u32[]{:S(2)}) copy-start(bf16[1,128,1600]{1,2,0:T(8,128)(2,1)} %param.29) | copy-start | bytes 1228804
  2.2 11.7 %copy-start.11 = (s32[8,128]{1,0:T(8,128)}, s32[8,128]{1,0:T(8,128)S(1)}, u32[]{:S(2)}) copy-start(s32[8,128]{1,0:T(8,128)S(1)} %multiply_add_fusion) | copy-start | bytes 12292
  10.5 6.3 copy-start.1
  68.8 3.0 copy-start
  88.5 1.7 copy-start.9
  149.0 85.5 %copy-start.7 = (bf16[4,400,800]{2,1,0:T(8,128)(2,1)S(1)}, bf16[4,400,800]{2,1,0:T(8,128)(2,1)}, u32[]{:S(2)}) copy-start(bf16[4,400,800]{2,1,0:T(8,128)(2,1)} %get-tuple-element.62) | copy-start | bytes 7680004
  234.5 6.0 copy-start.5
  234.5 6.0 copy-start.8
  342.9 49.8 %copy-start.6 = (bf16[256,1600]{1,0:T(8,128)(2,1)S(1)}, bf16[256,1600]{1,0:T(8,128)(2,1)}, u32[]{:S(2)}) copy-start(bf16[256,1600]{1,0:T(8,128)(2,1)} %reduce_sum.194.refs_1_) | copy-start | bytes 2457604
  420.4 42.2 %copy-start.2 = (bf16[1,128,1600]{2,1,0:T(8,128)(2,1)S(1)}, bf16[1,128,1600]{2,1,0:T(8,128)(2,1)}, u32[]{:S(2)}) copy-start(bf16[1,128,1600]{2,1,0:T(8,128)(2,1)} %copy-done.1) | copy-start | bytes 1228804
  462.6 5.6 copy-start.4

commit v7 on v6

--- a/solution.py
+++ b/solution.py
@@ -41,101 +41,72 @@
     return (dn - first - normed * second) * rstd
 
 
-def attn_fwd_body(slots, qp_ref, kp_ref, q_ref, k_ref, v_ref, attn_ref, o_ref, l_ref):
-    allowed = kp_ref[...] <= qp_ref[...]
+def query_rows(rows):
+    return 256
+
+
+def forward_step(slots, step, ins, outs, scratch):
+    qp_ref, kp_ref, q_ref, k_ref, v_ref = ins
+    attn_ref, o_ref, l_ref = outs
+    size = query_rows(q_ref.shape[0])
+    rows = slice(step * size, (step + 1) * size)
+    allowed = kp_ref[...] <= qp_ref[rows, :]
     for h in range(slots):
         cols = slice(h * HEAD_DIM, (h + 1) * HEAD_DIM)
-        raw = dot_t(q_ref[:, cols], k_ref[:, cols])
+        raw = dot_t(q_ref[rows, cols], k_ref[:, cols])
         e = jnp.where(allowed, jnp.exp(raw * SCALE), 0.0)
         total = jnp.sum(e, axis=1, keepdims=True)
         numer = dot(e.astype(BF16), v_ref[:, cols])
         o = numer / total
-        o_ref[:, cols] = o
-        attn_ref[:, cols] = o.astype(BF16)
-        l_ref[:, h : h + 1] = total
-
-
-def attn_bwd_body(
-    slots, qp_ref, kp_ref, q_ref, k_ref, v_ref, do_ref, o_ref, l_ref, dq_ref, dk_ref, dv_ref, dk_acc, dv_acc
-):
-    step = pl.program_id(0)
-
-    @pl.when(step == 0)
-    def _():
-        dk_acc[...] = jnp.zeros_like(dk_acc)
-        dv_acc[...] = jnp.zeros_like(dv_acc)
-
-    allowed = kp_ref[...] <= qp_ref[...]
+        o_ref[rows, cols] = o
+        attn_ref[rows, cols] = o.astype(BF16)
+        l_ref[rows, h : h + 1] = total
+
+
+def backward_step(slots, step, ins, outs, scratch):
+    qp_ref, kp_ref, q_ref, k_ref, v_ref, do_ref, o_ref, l_ref = ins
+    dq_ref, dk_ref, dv_ref = outs
+    dk_acc, dv_acc = scratch
+    size = query_rows(q_ref.shape[0])
+    steps = q_ref.shape[0] // size
+    rows = slice(step * size, (step + 1) * size)
+    allowed = kp_ref[...] <= qp_ref[rows, :]
     for h in range(slots):
         cols = slice(h * HEAD_DIM, (h + 1) * HEAD_DIM)
-        q = q_ref[:, cols]
-        k = k_ref[:, cols]
-        v = v_ref[:, cols]
-        do = do_ref[:, cols]
-        total = l_ref[:, h : h + 1]
+        q, k, v, do = q_ref[rows, cols], k_ref[:, cols], v_ref[:, cols], do_ref[rows, cols]
+        total = l_ref[rows, h : h + 1]
         w = (do / total).astype(BF16)
-        corr = jnp.sum(do * o_ref[:, cols], axis=1, keepdims=True) / total
+        corr = jnp.sum(do * o_ref[rows, cols], axis=1, keepdims=True) / total
         e = jnp.where(allowed, jnp.exp(dot_t(q, k) * SCALE), 0.0)
         de = dot_t(w, v)
         ds = (e * (de - corr)).astype(BF16)
-        dq_ref[:, cols] = (dot(ds, k) * SCALE).astype(BF16)
-        dk_acc[:, cols] += t_dot(ds, q)
-        dv_acc[:, cols] += t_dot(e.astype(BF16), w)
-
-    @pl.when(step == pl.num_programs(0) - 1)
-    def _():
-        dk_ref[...] = (dk_acc[...] * SCALE).astype(BF16)
-        dv_ref[...] = dv_acc[...].astype(BF16)
-
-
-def attn_specs(rows, wide, slots):
-    qb = 256 if rows <= 1024 else 128
-    q_spec = pl.BlockSpec((qb, wide), lambda i: (i, 0))
-    l_spec = pl.BlockSpec((qb, slots), lambda i: (i, 0))
-    all_spec = pl.BlockSpec((rows, wide), lambda i: (0, 0))
-    qp_spec = pl.BlockSpec((qb, 1), lambda i: (i, 0))
-    kp_spec = pl.BlockSpec((1, rows), lambda i: (0, 0))
-    return rows // qb, q_spec, l_spec, all_spec, qp_spec, kp_spec
-
-
-def attention_fwd(place, q, k, v, slots):
+        dq_ref[rows, cols] = (dot(ds, k) * SCALE).astype(BF16)
+        dk, dv = t_dot(ds, q), t_dot(e.astype(BF16), w)
+        if step:
+            dk, dv = dk + dk_acc[:, cols], dv + dv_acc[:, cols]
+        if step < steps - 1:
+            dk_acc[:, cols] = dk
+            dv_acc[:, cols] = dv
+        else:
+            dk_ref[:, cols] = (dk * SCALE).astype(BF16)
+            dv_ref[:, cols] = dv.astype(BF16)
+
+
+def forward_work(place, q, k, v, slots):
     rows, wide = q.shape
-    steps, q_spec, l_spec, all_spec, qp_spec, kp_spec = attn_specs(rows, wide, slots)
-    return pl.pallas_call(
-        functools.partial(attn_fwd_body, slots),
-        grid=(steps,),
-        in_specs=[qp_spec, kp_spec, q_spec, all_spec, all_spec],
-        out_specs=[q_spec, q_spec, l_spec],
-        out_shape=[
-            jax.ShapeDtypeStruct((rows, wide), BF16),
-            jax.ShapeDtypeStruct((rows, wide), F32),
-            jax.ShapeDtypeStruct((rows, slots), F32),
-        ],
-        name="attn_fwd",
-        cost_estimate=pl.CostEstimate(
-            flops=4 * rows * rows * wide, bytes_accessed=16 * rows * wide, transcendentals=rows * rows * slots
-        ),
-        compiler_params=pltpu.CompilerParams(vmem_limit_bytes=60 * 2**20),
-    )(place.reshape(rows, 1), place.reshape(1, rows), q, k, v)
-
-
-def attention_bwd(place, q, k, v, do, o, total, slots):
+    shape = jax.ShapeDtypeStruct
+    outs = (shape((rows, wide), BF16), shape((rows, wide), F32), shape((rows, slots), F32))
+    steps = rows // query_rows(rows)
+    ins = (place.reshape(rows, 1), place.reshape(1, rows), q, k, v)
+    return steps, functools.partial(forward_step, slots), ins, outs, ()
+
+
+def backward_work(place, q, k, v, do, o, total, slots):
     rows, wide = q.shape
-    steps, q_spec, l_spec, all_spec, qp_spec, kp_spec = attn_specs(rows, wide, slots)
-    shape = jax.ShapeDtypeStruct((rows, wide), BF16)
-    return pl.pallas_call(
-        functools.partial(attn_bwd_body, slots),
-        grid=(steps,),
-        in_specs=[qp_spec, kp_spec, q_spec, all_spec, all_spec, q_spec, q_spec, l_spec],
-        out_specs=[q_spec, all_spec, all_spec],
-        out_shape=[shape, shape, shape],
-        scratch_shapes=[pltpu.VMEM((rows, wide), F32), pltpu.VMEM((rows, wide), F32)],
-        name="attn_bwd",
-        cost_estimate=pl.CostEstimate(
-            flops=10 * rows * rows * wide, bytes_accessed=24 * rows * wide, transcendentals=rows * rows * slots
-        ),
-        compiler_params=pltpu.CompilerParams(vmem_limit_bytes=60 * 2**20),
-    )(place.reshape(rows, 1), place.reshape(1, rows), q, k, v, do, o, total)
+    outs = (jax.ShapeDtypeStruct((rows, wide), BF16),) * 3
+    steps = rows // query_rows(rows)
+    ins = (place.reshape(rows, 1), place.reshape(1, rows), q, k, v, do, o, total)
+    return steps, functools.partial(backward_step, slots), ins, outs, (pltpu.VMEM((rows, wide), F32),) * 2
 
 
 def split_axis(n):
@@ -265,12 +236,12 @@
                 self.to_far(j, y, self.pair).wait_send()
 
 
-def exchange_body(n, nf, counts, firsts, moves, *refs):
-    n_ctx, n_fsdp, n_own, n_red, n_pack = counts
+def exchange_body(n, nf, counts, firsts, moves, work, *refs):
+    n_ctx, n_fsdp, n_own, n_red, n_pack, n_work_in, n_work_out, n_work_scratch = counts
     bounds = [0]
-    for size in counts:
+    for size in counts[:6]:
         bounds.append(bounds[-1] + size)
-    ctx_in, fsdp_in, own_in, red_in, pack_in = (refs[i:j] for i, j in zip(bounds, bounds[1:]))
+    ctx_in, fsdp_in, own_in, red_in, pack_in, work_in = (refs[i:j] for i, j in zip(bounds, bounds[1:]))
     refs = refs[bounds[-1] :]
     n_joint = len(firsts) - n_pack
     n_sums = n_red - n_joint + (1 if n_pack else 0)
@@ -279,6 +250,8 @@
     red_out, refs = refs[:n_sums], refs[n_sums:]
     if moves:
         placed, refs = refs[0], refs[1:]
+    work_out, refs = refs[:n_work_out], refs[n_work_out:]
+    work_scratch, refs = refs[:n_work_scratch], refs[n_work_scratch:]
     sums, scratch = refs[:n_sums], refs[n_sums:]
     copy_sem, send_sem, recv_sem, place_send, place_recv = scratch[:5]
     goals = [(out, 0) for out in own_out]
@@ -289,7 +262,7 @@
     lines, across = split_axis(n)
     me = lax.axis_index("ctx")
     a, b, near = place_of(me, lines, across)
-    pieces = [(src, out, 0, out.shape[1]) for src, out in zip(ctx_in, ctx_out)]
+    pieces = [(src, out, first, rows) for src, out in zip(ctx_in, ctx_out) for first, rows in cut(out.shape[1])]
     late = len(pieces)
     for src, out in reversed(list(zip(sums, red_out))):
         pieces += [(src, out, first, rows) for first, rows in cut(out.shape[1])]
@@ -359,8 +332,19 @@
             each_own(i, start)
             keep(i).start()
 
+    work_steps, work_fn = work
+    points = 1 + (lines - 1) * len(pieces)
+    passed = [0]
+
+    def do_work():
+        at = passed[0]
+        passed[0] += 1
+        for step in range(at * work_steps // points, (at + 1) * work_steps // points):
+            work_fn(step, work_in, work_out, work_scratch)
+
     begin(range(late))
     fs.middle()
+    do_work()
     for j in range(n_pack):
         first = firsts[n_joint + j]
         sums[0][:, first : first + pack_in[j].shape[1]] = pack_in[j][...]
@@ -368,6 +352,7 @@
         if late:
             each_twin(0, True, start)
             each_relay(0, 1, True, start)
+            do_work()
         fs.end()
         begin(range(late, len(pieces)))
     for d in range(1, lines):
@@ -377,6 +362,9 @@
                     continue
                 each_twin(i, True, start)
             each_relay(i, d, True, start)
+            do_work()
+    if not n_sums:
+        fs.end()
 
     def crossed(i):
         for d in range(1, across):
@@ -427,8 +415,6 @@
             keep(i).wait()
     for k in range(len(moves)):
         place(k, wait_copy, wait_send)
-    if not n_sums:
-        fs.end()
 
     for i in range(len(pieces)):
         each_own(i, wait_send)
@@ -447,13 +433,13 @@
 
 
 def cut(rows):
-    if rows < 400:
+    if rows < 200:
         return [(0, rows)]
     half = rows // 32 * 16
     return [(0, rows - half), (rows - half, half)]
 
 
-def exchange(call, n, nf, ctx=(), fsdp=(), own=(), red=(), pack=(), firsts=(), moves=(), kept=0):
+def exchange(call, n, nf, ctx=(), fsdp=(), own=(), red=(), pack=(), firsts=(), moves=(), kept=0, work=None):
     shape = jax.ShapeDtypeStruct
     sums = [shape(x.shape[1:], x.dtype) for x in red]
     if pack:
@@ -465,20 +451,22 @@
     outs += [shape(x.shape[1:], x.dtype) for x in own]
     outs += [shape((n, *x.shape), x.dtype) for x in sums]
     outs += [shape((kept, sums[1].shape[1]), sums[1].dtype)] if moves else []
-    gathered = max(len(ctx) + sum(len(cut(x.shape[0])) for x in sums), 1)
+    steps, work_fn, work_in, work_out, work_scratch = work or (0, None, (), (), ())
+    gathered = max(sum(len(cut(x.shape[0])) for x in [*ctx, *sums]), 1)
     any_spec, vmem_spec = pl.BlockSpec(memory_space=pl.ANY), pl.BlockSpec(memory_space=pltpu.VMEM)
-    inputs = (*ctx, *fsdp, *own, *red, *pack)
+    inputs = (*ctx, *fsdp, *own, *red, *pack, *work_in)
+    counts = [len(x) for x in (ctx, fsdp, own, red, pack, work_in, work_out, work_scratch)]
     dma = pltpu.SemaphoreType.DMA
     return pl.pallas_call(
-        functools.partial(
-            exchange_body, n, nf, (len(ctx), len(fsdp), len(own), len(red), len(pack)), tuple(firsts), tuple(moves)
-        ),
+        functools.partial(exchange_body, n, nf, tuple(counts), tuple(firsts), tuple(moves), (steps, work_fn)),
         in_specs=[vmem_spec] * len(inputs),
         out_specs=[any_spec] * (len(ctx) + len(fsdp))
         + [vmem_spec] * len(own)
-        + [any_spec] * (len(sums) + (1 if moves else 0)),
-        out_shape=outs,
-        scratch_shapes=[pltpu.VMEM(x.shape, x.dtype) for x in sums]
+        + [any_spec] * (len(sums) + (1 if moves else 0))
+        + [vmem_spec] * len(work_out),
+        out_shape=[*outs, *work_out],
+        scratch_shapes=list(work_scratch)
+        + [pltpu.VMEM(x.shape, x.dtype) for x in sums]
         + [dma((gathered,)), dma((gathered, 4, n, 2)), dma((gathered, 4, n, 2))]
         + [dma((max(len(moves), 1),))] * 2
         + Fsdp.scratch(nf, fsdp, [*own, *red]),
@@ -648,10 +636,16 @@
             job.compute(line)
     fs.start()
     steps = [(job, line) for job in jobs for line in order[:-1]]
+    bits = []
+    for j in range(n_sides):
+        size = side_in[2 * j].shape[1]
+        width = -(-size // 3 // 128) * 128
+        bits += [(j, first, min(width, size - first)) for first in range(0, size, width)]
     for step, (job, line) in enumerate(steps):
         job.pass_on(line)
-        for j in range(step * n_sides // len(steps), (step + 1) * n_sides // len(steps)):
-            side_out[j][...] = t_dot(side_in[2 * j][...], side_in[2 * j + 1][...]).astype(BF16)
+        for j, first, size in bits[step * len(bits) // len(steps) : (step + 1) * len(bits) // len(steps)]:
+            part = side_in[2 * j][:, first : first + size]
+            side_out[j][first : first + size, :] = t_dot(part, side_in[2 * j + 1][...]).astype(BF16)
         if step == len(order) - 2:
             fs.end()
     for job in jobs:
@@ -828,10 +822,10 @@
     k_w = head_columns(qkv_weight[:, width : 2 * width], width, c, n)
     v_w = head_columns(qkv_weight[:, 2 * width :], width, c, n)
     w_mine = jnp.concatenate([q_w, k_w, v_w], axis=1)
-    out_mine = head_rows(out_weight, heads, c, f, n)
-    x_all, packed, w_qkv, w_out = exchange(0, n, nf, ctx=[tokens[0]], fsdp=[flat, w_mine, out_mine])
-    up_weight, down_weight, packed = lax.optimization_barrier((up_weight, down_weight, packed))
-    w_out = jnp.sum(w_out.astype(F32), axis=0).astype(BF16)
+    x_all, packed, w_qkv = exchange(0, n, nf, ctx=[tokens[0]], fsdp=[flat, w_mine])
+    out_weight, up_weight, down_weight, packed = lax.optimization_barrier(
+        (out_weight, up_weight, down_weight, packed)
+    )
     x_all = x_all.reshape(n * rows, width)
     w_qkv = w_qkv.reshape(width, 3 * wide)
     full = [packed[:, i, : v.shape[0]].reshape(-1).astype(F32) for i, v in enumerate(vectors)]
@@ -847,19 +841,27 @@
     q = (proj[:, :wide] + bq).astype(BF16)
     k = proj[:, wide : 2 * wide].astype(BF16)
     v = (proj[:, 2 * wide :] + bv).astype(BF16)
-    attn, o, total = attention_fwd(place, q, k, v, slots)
+    g2_all, w_out, attn, o, total = exchange(
+        1,
+        n,
+        nf,
+        ctx=[cotangent[0]],
+        fsdp=[head_rows(out_weight, heads, c, f, n)],
+        work=forward_work(place, q, k, v, slots),
+    )
+    w_out = jnp.sum(w_out.astype(F32), axis=0).astype(BF16)
     up_mine = [lax.dynamic_slice_in_dim(up_weight, i * ff_local + c * ff_part, ff_part, axis=1) for i in range(nf)]
-    mixed, w_up = product(1, n, nf, [(attn, w_out, False)], fsdp=[jnp.concatenate(up_mine, axis=1)])
+    mixed, w_up = product(7, n, nf, [(attn, w_out, False)], fsdp=[jnp.concatenate(up_mine, axis=1)])
     w_up = w_up.reshape(width, nf * ff_part)
     x = tokens[0].astype(F32)
     mid = x + mixed + b_out
 
     n2, rstd2 = ln_stats(mid)
-    act2, g2_all, w_down = exchange(
+    act2, w_down = exchange(
         2,
         n,
         nf,
-        ctx=[(n2 * gain2 + shift2).astype(BF16), cotangent[0]],
+        ctx=[(n2 * gain2 + shift2).astype(BF16)],
         fsdp=[lax.dynamic_slice_in_dim(down_weight, c * ff_part, ff_part, axis=0)],
     )
     act2 = act2.reshape(n * rows, width)
@@ -888,7 +890,9 @@
     g1_all, d_up, d_down = exchange(4, n, nf, ctx=[g1], own=[d_up, d_down])
     g1_all = g1_all.reshape(n * rows, width)
     d_attn = dot_t(g1_all, w_out)
-    gq, gk, gv = attention_bwd(place, q, k, v, d_attn, o, total, slots)
+    d_down, gq, gk, gv = exchange(
+        8, n, nf, ctx=[d_down], work=backward_work(place, q, k, v, d_attn, o, total, slots)
+    )
     g_qkv = jnp.concatenate([gq, gk, gv], axis=1)
     da1, d_qkv, d_out = product(5, n, nf, [(g_qkv, w_qkv, True)], sides=[(act1, g_qkv), (attn, g1_all)])
     d_qkv = d_qkv.reshape(nf, local, 3 * wide)
@@ -917,11 +921,10 @@
     packed = jnp.concatenate([s.reshape(nf, -1) for s in smalls], axis=1)
     packed = jnp.pad(packed, ((0, 0), (0, -packed.shape[1] % 1024))).reshape(nf, -1, 128)
     at_up = 3 * wide
-    d_down, joint, _, packed, d_out = exchange(
+    joint, _, packed, d_out = exchange(
         6,
         n,
         nf,
-        ctx=[d_down],
         red=[d_qkv, d_out, packed],
         pack=[d_up],
         firsts=(0, at_up),

time: 697 us -> 713 us (1.023)
  Pallas kernels: 606 us -> 616 us
    pallas_call x6, Pallas kernels: 412 us -> 423 us  [exchange(): pl.pallas_call(functools.partial(exchange_body, n, nf, tuple(counts), tup...]
where the time goes in v7:
time: 713 us; the launch traced here: 704 us
  Pallas kernels  616 us (86%)
  other arithmetic  37.6 us (5%)
  local copies, waits for them, and re-layouts  29.1 us (4%)
  matrix products  20.3 us (3%)
    pallas_call x6, Pallas kernels, exchange(): pl.pallas_call(functools.partial(exchange_body, n, nf, tuple(counts), tup...  423 us
    pallas_call x3, Pallas kernels, product(): pl.pallas_call(functools.partial(product_body, n, nf, (len(products), len...  175 us
    pallas_call x1, Pallas kernels, lay_out(): pl.pallas_call(functools.partial(layout_body, tuple((tuple(m) for m in mo...  17.5 us

profile of v7, /device:TPU:0, one launch (start us, length us, event | category | flops | bytes accessed | tf_op | source)
XLA Modules:
  0.0 704.1 jit_solution(13532567700343261964)
XLA Ops:
  0.7 0.7 broadcast_subtract_fusion
  1.3 0.7 multiply_add_fusion
  2.1 0.7 pad.31
  2.8 0.7 pad.32
  3.5 0.7 pad.33
  4.2 0.7 pad.34
  4.9 0.7 pad.35
  5.5 0.7 pad.36
  6.2 0.7 pad.37
  6.9 0.7 stack.41
  7.6 1.4 stack.43.refs_1_
  9.0 1.2 copy.45
  10.4 2.0 copy.46
  12.4 1.0 copy.47.refs_2_.refs_1_
  13.5 2.8 fusion.34
  16.9 1.1 concatenate.29.refs_2_
  18.0 46.7 %exchange_0.1 = (bf16[8,128,1600]{2,1,0:T(8,128)(2,1)}, bf16[4,16,1600]{2,1,0:T(8,128)(2,1)}, bf16[4,400,768]{2,1,0:T(8,128)(2,1)}) custom-call(bf16[128,1600]{1,0:T(8,128)(2,1)} %bitcast.58, bf16[16,1600]{1,0:T(8,128)(2,1)} %stack.43.refs_1_, bf16[400,768]{1,0:T(8,128)(2,1)} %concatenate.29.refs_2_), custom_call_target="tpu_custom_call" | custom-call | tf_op jit(solution)/shard_map/exchange_0/pallas_call | solution.py:460
  64.7 2.6 convert_reduce_fusion
  67.3 0.3 copy-done
  67.7 1.0 multiply_reduce_fusion
  68.7 0.8 slice_convert_fusion.1
  70.2 1.0 convert_reduce_fusion.7
  71.2 1.2 convert_reduce_fusion.8
  73.3 1.3 pad_dynamic-slice_fusion.1
  74.6 1.0 pad_maximum_fusion.1.refs_1_
  75.6 2.0 constant_dynamic-slice_fusion.refs_1_
  77.5 1.6 constant_dynamic-slice_fusion.4
  79.1 1.2 pad_maximum_fusion.2.refs_2_
  80.4 2.7 fusion.3.refs_2_
  83.1 1.5 add_convert_fusion
  84.6 0.2 copy-done.7
  84.8 3.0 fusion.36
  87.8 0.9 slice.155.refs_5_.refs_4_
  88.7 1.2 fusion.11
  89.9 46.9 %exchange_1.1 = (bf16[8,128,1600]{2,1,0:T(8,128)(2,1)}, bf16[4,256,1600]{2,1,0:T(8,128)(2,1)}, bf16[1024,256]{1,0:T(8,128)(2,1)}, f32[1024,256]{1,0:T(8,128)}, f32[1024,4]{1,0:T(8,128)}) custom-call(bf16[128,1600]{1,0:T(8,128)(2,1)} %bitcast.60, bf16[256,1600]{1,0:T(8,128)(2,1)} %pad_maximum_fusion.1.refs_1_, s32[1024,1]{1,0:T(8,128)} %copy.47.refs_2_.refs_1_, ...), custom_call_target="tpu_custom_call" | custom-call | tf_op jit(solution)/shard_map/exchange_1/pallas_call | solution.py:460
  136.8 3.6 reduce_sum.194.refs_1_
  140.5 43.1 %product_7.1 = (f32[128,1600]{1,0:T(8,128)}, bf16[4,400,800]{2,1,0:T(8,128)(2,1)}) custom-call(bf16[1024,256]{1,0:T(8,128)(2,1)} %get-tuple-element.56.refs_0_.refs_4_, bf16[256,1600]{1,0:T(8,128)(2,1)} %reduce_sum.194.refs_1_, bf16[400,800]{1,0:T(8,128)(2,1)} %pad_maximum_fusion.2.refs_2_), custom_call_target="tpu_custom_call" | custom-call | tf_op jit(solution)/shard_map/product_7/pallas_call | solution.py:675
  183.6 1.8 fusion.32
  185.3 0.2 multiply_reduce_fusion.3
  185.6 1.0 add_convert_fusion.1.refs_0_
  186.6 45.2 %exchange_2.1 = (bf16[8,128,1600]{2,1,0:T(8,128)(2,1)}, bf16[4,200,1600]{2,1,0:T(8,128)(2,1)}) custom-call(bf16[128,1600]{1,0:T(8,128)(2,1)} %add_convert_fusion.1.refs_0_, bf16[200,1600]{1,0:T(8,128)(2,1)} %constant_dynamic-slice_fusion.refs_1_), custom_call_target="tpu_custom_call" | custom-call | tf_op jit(solution)/shard_map/exchange_2/pallas_call | solution.py:460
  231.8 6.0 fusion.37
  237.8 7.2 %convert_reduce_fusion.1 = (f32[800]{0:T(1024)S(1)}, bf16[1024,800]{1,0:T(8,128)(2,1)}, bf16[1024,800]{1,0:T(8,128)(2,1)}) fusion(f32[1024,800]{1,0:T(8,128)S(1)} %fusion.37, f32[800]{0:T(1024)S(1)} %add.260, bf16[1024,1600]{1,0:T(8,128)(2,1)S(1)} %bitcast.64, bf16[800,1600]{1,0:T(8,128)(2,1)S(1)} %bitcast.73), kind=kOutput, calls=%fused_computation.17 | convolution fusion | flops 2641919232 | bytes 12396800 | tf_op jit(solution)/shard_map/dot_general | solution.py:23
  245.0 88.6 %product_3.1 = (f32[128,1600]{1,0:T(8,128)}, f32[128,1600]{1,0:T(8,128)}, bf16[1600,800]{1,0:T(8,128)(2,1)}, bf16[800,1600]{1,0:T(8,128)(2,1)}) custom-call(bf16[1024,800]{1,0:T(8,128)(2,1)} %get-tuple-element.147.refs_0_.refs_5_, bf16[1600,800]{1,0:T(8,128)(2,1)} %bitcast.69, bf16[1024,800]{1,0:T(8,128)(2,1)} %get-tuple-element.160.refs_2_.refs_6_, ...), custom_call_target="tpu_custom_call" | custom-call | tf_op jit(solution)/shard_map/product_3/pallas_call | solution.py:675
  333.9 1.5 multiply_reduce_fusion.1
  335.5 3.2 convert_reduce_fusion.6
  338.7 47.3 %exchange_4.1 = (bf16[8,128,1600]{2,1,0:T(8,128)(2,1)}, bf16[400,800]{1,0:T(8,128)(2,1)}, bf16[200,1600]{1,0:T(8,128)(2,1)}) custom-call(bf16[128,1600]{1,0:T(8,128)(2,1)} %get-tuple-element.149.refs_0_, bf16[4,400,800]{2,1,0:T(8,128)(2,1)} %bitcast.68, bf16[4,200,1600]{2,1,0:T(8,128)(2,1)} %bitcast.71), custom_call_target="tpu_custom_call" | custom-call | tf_op jit(solution)/shard_map/exchange_4/pallas_call | solution.py:460
  386.3 4.1 fusion.38.refs_6_
  390.4 1.2 copy.53
  391.5 61.2 %exchange_8.1 = (bf16[8,200,1600]{2,1,0:T(8,128)(2,1)}, bf16[1024,256]{1,0:T(8,128)(2,1)}, bf16[1024,256]{1,0:T(8,128)(2,1)}, bf16[1024,256]{1,0:T(8,128)(2,1)}) custom-call(bf16[200,1600]{1,0:T(8,128)(2,1)} %get-tuple-element.69.refs_0_, s32[1024,1]{1,0:T(8,128)} %copy.47.refs_2_.refs_1_, s32[1,1024]{1,0:T(1,128)} %bitcast.84, ...), custom_call_target="tpu_custom_call" | custom-call | tf_op jit(solution)/shard_map/exchange_8/pallas_call | solution.py:460
  452.8 1.2 convert_reduce_fusion.5
  454.3 1.2 convert_reduce_fusion.4
  455.9 2.6 pad_maximum_fusion.refs_0_.refs_3_
  458.5 43.0 %product_5.1 = (f32[128,1600]{1,0:T(8,128)}, bf16[1600,768]{1,0:T(8,128)(2,1)}, bf16[256,1600]{1,0:T(8,128)(2,1)}) custom-call(bf16[1024,768]{1,0:T(8,128)(2,1)} %pad_maximum_fusion.refs_0_.refs_3_, bf16[1600,768]{1,0:T(8,128)(2,1)} %bitcast.74, bf16[1024,1600]{1,0:T(8,128)(2,1)} %fusion.3.refs_2_, bf16[1024,768]{1,0:T(8,128)(2,1)} %pad_maximum_fusion.refs_0_.refs_3_, ...), custom_call_target="tpu_custom_call" | custom-call | tf_op jit(solution)/shard_map/product_5/pallas_call | solution.py:675
  501.5 1.6 fusion.23
  503.2 1.8 fusion.22
  505.0 1.2 copy.54
  506.4 0.6 copy.59
  507.1 176.1 %exchange_6.1 = (bf16[8,400,1568]{2,1,0:T(8,128)(2,1)}, bf16[8,64,1600]{2,1,0:T(8,128)(2,1)}, f32[8,40,128]{2,1,0:T(8,128)}, bf16[400,1600]{1,0:T(8,128)(2,1)}) custom-call(bf16[4,400,768]{2,1,0:T(8,128)(2,1)} %bitcast.76, bf16[4,64,1600]{2,1,0:T(8,128)(2,1)} %bitcast.77, f32[4,40,128]{2,1,0:T(8,128)} %bitcast.78, bf16[400,800]{1,0:T(8,128)(2,1)} %get-tuple-element.79.refs_3_), custom_call_target="tpu_custom_call" | custom-call | tf_op jit(solution)/shard_map/exchange_6/pallas_call | solution.py:460
  683.2 0.9 reduce_sum.212
  684.2 0.7 slice.128
  684.8 0.7 slice.132
  685.5 0.7 fusion.35
  686.2 17.5 %lay_out.1 = (f32[1600,1600]{1,0:T(8,128)}, f32[400,1600]{1,0:T(8,128)}, f32[400,6400]{1,0:T(8,128)}, f32[400,4800]{1,0:T(8,128)}) custom-call(bf16[8,400,1568]{2,1,0:T(8,128)(2,1)} %get-tuple-element.81.joint_ref, bf16[1600,1600]{1,0:T(8,128)(2,1)} %bitcast.59, bf16[400,1600]{1,0:T(8,128)(2,1)} %get-tuple-element.83.out_ref), custom_call_target="tpu_custom_call" | custom-call | bytes 46080000 | tf_op jit(solution)/shard_map/lay_out/pallas_call | solution.py:718
  (80 shorter events, 3.9 us)
Async XLA Ops:
  2.1 14.2 %copy-start.8 = (s32[8,128]{1,0:T(8,128)}, s32[8,128]{1,0:T(8,128)S(1)}, u32[]{:S(2)}) copy-start(s32[8,128]{1,0:T(8,128)S(1)} %multiply_add_fusion) | copy-start | bytes 12292
  10.3 6.0 copy-start.1
  64.7 3.0 copy-start
  83.1 1.7 copy-start.7
  183.5 48.2 %copy-start.5 = (bf16[4,400,800]{2,1,0:T(8,128)(2,1)S(1)}, bf16[4,400,800]{2,1,0:T(8,128)(2,1)}, u32[]{:S(2)}) copy-start(bf16[4,400,800]{2,1,0:T(8,128)(2,1)} %get-tuple-element.64) | copy-start | bytes 7680004
  231.8 6.0 copy-start.3
  231.8 6.0 copy-start.6
  338.7 47.6 %copy-start.4 = (bf16[256,1600]{1,0:T(8,128)(2,1)S(1)}, bf16[256,1600]{1,0:T(8,128)(2,1)}, u32[]{:S(2)}) copy-start(bf16[256,1600]{1,0:T(8,128)(2,1)} %reduce_sum.194.refs_1_) | copy-start | bytes 2457604
  458.5 43.0 %copy-start.2 = (bf16[1,128,1600]{2,1,0:T(8,128)(2,1)S(1)}, bf16[1,128,1600]{2,1,0:T(8,128)(2,1)}, u32[]{:S(2)}) copy-start(bf16[1,128,1600]{2,1,0:T(8,128)(2,1)} %copy-done.1) | copy-start | bytes 1228804

commit v8 on v7

--- a/solution.py
+++ b/solution.py
@@ -120,9 +120,9 @@
     return a, b, near
 
 
-def turned_rows(rows, dtype, across):
+def turned_rows(rows, dtype, across, many=False):
     tile = 16 if dtype == BF16 else 8
-    share = 4 if rows <= 128 else 5
+    share = 4 if rows <= 128 and not many else 5
     return rows // share // tile * tile if across == 2 else 0
 
 
@@ -271,7 +271,7 @@
     fs.start()
 
     def turned_part(i):
-        return turned_rows(pieces[i][3], pieces[i][1].dtype, across)
+        return turned_rows(pieces[i][3], pieces[i][1].dtype, across, len(pieces) > 1)
 
     def hop(i, block, way, turned=False, own=False):
         source, out, first, size = pieces[i]
@@ -459,7 +459,7 @@
     dma = pltpu.SemaphoreType.DMA
     return pl.pallas_call(
         functools.partial(exchange_body, n, nf, tuple(counts), tuple(firsts), tuple(moves), (steps, work_fn)),
-        in_specs=[vmem_spec] * len(inputs),
+        in_specs=[any_spec] * (len(ctx) + len(fsdp)) + [vmem_spec] * (len(inputs) - len(ctx) - len(fsdp)),
         out_specs=[any_spec] * (len(ctx) + len(fsdp))
         + [vmem_spec] * len(own)
         + [any_spec] * (len(sums) + (1 if moves else 0))
@@ -476,7 +476,7 @@
 
 
 class Scatter:
-    def __init__(self, n, transposed, left, right, out, scratch):
+    def __init__(self, n, many, transposed, left, right, out, scratch):
         self.left, self.right, self.out, self.transposed = left, right, out, transposed
         self.part, self.acc, self.acc_t, self.over_in, self.sums, self.sums_t = scratch[:6]
         self.line_in, self.line_in_t, self.twin_in = scratch[6:9]
@@ -486,14 +486,14 @@
         self.me = lax.axis_index("ctx")
         self.a, self.b, self.near = place_of(self.me, self.lines, self.across)
         self.rows = out.shape[0]
-        self.last = turned_rows(self.rows, BF16, self.across)
+        self.last = turned_rows(self.rows, BF16, self.across, many)
         self.head, self.tail = pl.ds(0, self.rows - self.last), pl.ds(self.rows - self.last, self.last)
         self.peers = [self.me - self.b + lax.rem(self.b + k, self.across) for k in range(1, self.across)]
 
     @staticmethod
-    def scratch(n, rows, width):
+    def scratch(n, many, rows, width):
         lines, across = split_axis(n)
-        last = turned_rows(rows, BF16, across)
+        last = turned_rows(rows, BF16, across, many)
         some = max(last, 16)
         vmem, dma = pltpu.VMEM, pltpu.SemaphoreType.DMA
         return [
@@ -617,7 +617,7 @@
     scratch = refs[n_prod + n_sides + n_fsdp :]
     each = 17
     jobs = [
-        Scatter(n, transposed[p], pairs[2 * p], pairs[2 * p + 1], outs[p], scratch[each * p : each * (p + 1)])
+        Scatter(n, n_prod > 1, transposed[p], pairs[2 * p], pairs[2 * p + 1], outs[p], scratch[each * p : each * (p + 1)])
         for p in range(n_prod)
     ]
     fs = Fsdp(nf, fsdp_in, fsdp_out, [], [], scratch[each * n_prod :])
@@ -683,7 +683,7 @@
         in_specs=[vmem_spec] * (len(inputs) + len(fsdp)),
         out_specs=[vmem_spec] * (len(outs) - len(fsdp)) + [any_spec] * len(fsdp),
         out_shape=outs,
-        scratch_shapes=[s for width in widths for s in Scatter.scratch(n, rows, width)] + Fsdp.scratch(nf, fsdp, ()),
+        scratch_shapes=[s for width in widths for s in Scatter.scratch(n, len(widths) > 1, rows, width)] + Fsdp.scratch(nf, fsdp, ()),
         name=f"product_{call}",
         compiler_params=pltpu.CompilerParams(collective_id=call, has_side_effects=True, vmem_limit_bytes=63 * 2**20),
     )(*inputs, *fsdp)
@@ -702,32 +702,38 @@
     return moves
 
 
-def layout_body(moves, joint_ref, down_ref, out_ref, down_out, out_out, *outs):
-    for ref, per_out in zip(outs, moves):
+def layout_body(moves, *refs):
+    ins, outs = refs[: len(refs) // 2], refs[len(refs) // 2 :]
+    for in_ref, out_ref, per_out in zip(ins, outs, moves):
+        if per_out is None:
+            out_ref[...] = in_ref[...].astype(F32)
+            continue
         for block, start, goal, size in per_out:
-            ref[:, goal : goal + size] = joint_ref[block, :, start : start + size].astype(F32)
-    down_out[...] = down_ref[...].astype(F32)
-    out_out[...] = out_ref[...].astype(F32)
-
-
-def lay_out(joint, down, out, widths, moves):
-    n, rows, part = joint.shape
+            out_ref[:, goal : goal + size] = in_ref[block, :, start : start + size].astype(F32)
+
+
+def lay_out(arrays, widths, moves):
+    rows = next(x.shape[1] for x in arrays if x.ndim == 3)
     step = next(s for s in (80, 16, rows) if rows % s == 0)
     grid = rows // step
-    plain = [pl.BlockSpec((x.shape[0] // grid, x.shape[1]), lambda i: (i, 0)) for x in (down, out)]
+    in_specs, out_specs, outs = [], [], []
+    for x, width in zip(arrays, widths):
+        flat = pl.BlockSpec((x.shape[-2] // grid, width), lambda i: (i, 0))
+        in_specs.append(pl.BlockSpec((x.shape[0], step, x.shape[2]), lambda i: (0, i, 0)) if x.ndim == 3 else flat)
+        out_specs.append(flat)
+        outs.append(jax.ShapeDtypeStruct((x.shape[-2], width), F32))
     return pl.pallas_call(
-        functools.partial(layout_body, tuple(tuple(m) for m in moves)),
+        functools.partial(layout_body, tuple(m and tuple(m) for m in moves)),
         grid=(grid,),
-        in_specs=[pl.BlockSpec((n, step, part), lambda i: (0, i, 0)), *plain],
-        out_specs=plain + [pl.BlockSpec((step, width), lambda i: (i, 0)) for width in widths],
-        out_shape=[jax.ShapeDtypeStruct(x.shape, F32) for x in (down, out)]
-        + [jax.ShapeDtypeStruct((rows, width), F32) for width in widths],
+        in_specs=in_specs,
+        out_specs=out_specs,
+        out_shape=outs,
         name="lay_out",
         cost_estimate=pl.CostEstimate(
-            flops=0, bytes_accessed=6 * (rows * sum(widths) + down.size + out.size), transcendentals=0
+            flops=0, bytes_accessed=6 * sum(x.shape[0] * x.shape[1] for x in outs), transcendentals=0
         ),
         compiler_params=pltpu.CompilerParams(vmem_limit_bytes=60 * 2**20),
-    )(joint, down, out)
+    )(*arrays)
 
 
 def head_moves(n, heads, offset, goal):
@@ -817,7 +823,9 @@
 
     vectors = (ln1_gain, ln1_shift, qv_bias, out_bias, ln2_gain, ln2_shift, up_bias, down_bias)
     longest = max(v.shape[0] for v in vectors)
-    flat = jnp.stack([jnp.pad(v, (0, longest - v.shape[0])) for v in vectors] * (-(-16 // len(vectors))))
+    flat = sum(
+        jnp.pad(v.astype(F32)[None, :], ((i, 15 - i), (0, longest - v.shape[0]))) for i, v in enumerate(vectors)
+    ).astype(BF16)
     q_w = head_columns(qkv_weight[:, :width], width, c, n)
     k_w = head_columns(qkv_weight[:, width : 2 * width], width, c, n)
     v_w = head_columns(qkv_weight[:, 2 * width :], width, c, n)
@@ -890,8 +898,8 @@
     g1_all, d_up, d_down = exchange(4, n, nf, ctx=[g1], own=[d_up, d_down])
     g1_all = g1_all.reshape(n * rows, width)
     d_attn = dot_t(g1_all, w_out)
-    d_down, gq, gk, gv = exchange(
-        8, n, nf, ctx=[d_down], work=backward_work(place, q, k, v, d_attn, o, total, slots)
+    d_up, gq, gk, gv = exchange(
+        8, n, nf, ctx=[d_up], work=backward_work(place, q, k, v, d_attn, o, total, slots)
     )
     g_qkv = jnp.concatenate([gq, gk, gv], axis=1)
     da1, d_qkv, d_out = product(5, n, nf, [(g_qkv, w_qkv, True)], sides=[(act1, g_qkv), (attn, g1_all)])
@@ -920,22 +928,16 @@
     )
     packed = jnp.concatenate([s.reshape(nf, -1) for s in smalls], axis=1)
     packed = jnp.pad(packed, ((0, 0), (0, -packed.shape[1] % 1024))).reshape(nf, -1, 128)
-    at_up = 3 * wide
-    joint, _, packed, d_out = exchange(
-        6,
-        n,
-        nf,
-        red=[d_qkv, d_out, packed],
-        pack=[d_up],
-        firsts=(0, at_up),
-        moves=row_moves(n, nf, heads),
-        kept=local,
+    d_down, d_qkv, _, packed, d_out = exchange(
+        6, n, nf, ctx=[d_down], red=[d_qkv, d_out, packed], moves=row_moves(n, nf, heads), kept=local
     )
     mine = jnp.sum(packed, axis=0).reshape(-1)
-    up_moves = [(i, at_up + j * ff_part, j * ff_local + i * ff_part, ff_part) for i in range(n) for j in range(nf)]
+    up_moves = [(i, j * ff_part, j * ff_local + i * ff_part, ff_part) for i in range(n) for j in range(nf)]
     qkv_moves = [m for i in range(3) for m in head_moves(n, heads, i * wide, i * width)]
     d_down_full, d_out_full, d_up_full, d_qkv_full = lay_out(
-        joint, d_down.reshape(ff_local, width), d_out, (ff, 3 * width), (up_moves, qkv_moves)
+        (d_down.reshape(ff_local, width), d_out, d_up, d_qkv),
+        (width, width, ff, 3 * width),
+        (None, None, up_moves, qkv_moves),
     )
     out, at = [], 0
     for s in smalls:

time: 713 us -> 684 us (0.959)
  Pallas kernels: 616 us -> 588 us
    pallas_call x6, Pallas kernels: 423 us -> 403 us  [exchange(): pl.pallas_call(functools.partial(exchange_body, n, nf, tuple(counts), tup...]
    pallas_call x3, Pallas kernels: 175 us -> 167 us  [product(): pl.pallas_call(functools.partial(product_body, n, nf, (len(products), len...]
where the time goes in v8:
time: 684 us; the launch traced here: 676 us
  Pallas kernels  588 us (86%)
  other arithmetic  38.5 us (6%)
  local copies, waits for them, and re-layouts  27.7 us (4%)
  matrix products  20.3 us (3%)
    pallas_call x6, Pallas kernels, exchange(): pl.pallas_call(functools.partial(exchange_body, n, nf, tuple(counts), tup...  403 us
    pallas_call x3, Pallas kernels, product(): pl.pallas_call(functools.partial(product_body, n, nf, (len(products), len...  167 us
    pallas_call x1, Pallas kernels, lay_out(): pl.pallas_call(functools.partial(layout_body, tuple((m and tuple(m) for m...  17.6 us

profile of v8, /device:TPU:0, one launch (start us, length us, event | category | flops | bytes accessed | tf_op | source)
XLA Modules:
  0.0 675.6 jit_solution(3196188095455597010)
XLA Ops:
  0.7 0.7 broadcast_subtract_fusion
  1.3 0.7 broadcast_in_dim.95
  2.0 0.7 broadcast_in_dim.96
  2.7 0.7 broadcast_in_dim.98
  3.4 0.7 broadcast_in_dim.99
  4.1 0.7 broadcast_in_dim.100
  4.7 0.7 broadcast_in_dim.102
  5.4 0.7 multiply_add_fusion
  6.2 0.7 broadcast_in_dim.97
  6.9 0.7 broadcast_in_dim.101
  7.5 0.7 add_convert_fusion.2.refs_1_
  8.2 1.2 copy.45
  9.6 2.0 copy.46
  11.6 1.1 copy.47.refs_2_.refs_1_
  12.7 2.8 fusion.34
  16.2 1.1 concatenate.29.refs_2_
  17.3 45.7 %exchange_0.1 = (bf16[8,128,1600]{2,1,0:T(8,128)(2,1)}, bf16[4,16,1600]{2,1,0:T(8,128)(2,1)}, bf16[4,400,768]{2,1,0:T(8,128)(2,1)}) custom-call(bf16[128,1600]{1,0:T(8,128)(2,1)} %bitcast.58, bf16[16,1600]{1,0:T(8,128)(2,1)} %add_convert_fusion.2.refs_1_, bf16[400,768]{1,0:T(8,128)(2,1)} %concatenate.29.refs_2_), custom_call_target="tpu_custom_call" | custom-call | tf_op jit(solution)/shard_map/exchange_0/pallas_call | solution.py:460
  63.0 2.6 convert_reduce_fusion
  65.6 0.3 copy-done
  65.9 1.0 multiply_reduce_fusion
  67.0 0.8 slice_convert_fusion.1
  68.5 1.0 convert_reduce_fusion.7
  69.5 1.4 convert_reduce_fusion.8
  71.8 1.3 pad_dynamic-slice_fusion.1
  73.1 1.0 pad_maximum_fusion.1.refs_1_
  74.1 2.0 constant_dynamic-slice_fusion.refs_1_
  76.0 1.6 constant_dynamic-slice_fusion.4
  77.6 1.2 pad_maximum_fusion.2.refs_2_
  78.9 2.7 fusion.3.refs_2_
  81.6 1.5 add_convert_fusion
  83.1 0.2 copy-done.7
  83.3 3.0 fusion.36
  86.3 0.9 slice.155.refs_5_.refs_4_
  87.2 1.3 fusion.11
  88.4 46.8 %exchange_1.1 = (bf16[8,128,1600]{2,1,0:T(8,128)(2,1)}, bf16[4,256,1600]{2,1,0:T(8,128)(2,1)}, bf16[1024,256]{1,0:T(8,128)(2,1)}, f32[1024,256]{1,0:T(8,128)}, f32[1024,4]{1,0:T(8,128)}) custom-call(bf16[128,1600]{1,0:T(8,128)(2,1)} %bitcast.60, bf16[256,1600]{1,0:T(8,128)(2,1)} %pad_maximum_fusion.1.refs_1_, s32[1024,1]{1,0:T(8,128)} %copy.47.refs_2_.refs_1_, ...), custom_call_target="tpu_custom_call" | custom-call | tf_op jit(solution)/shard_map/exchange_1/pallas_call | solution.py:460
  135.3 3.6 reduce_sum.194.refs_1_
  138.9 43.1 %product_7.1 = (f32[128,1600]{1,0:T(8,128)}, bf16[4,400,800]{2,1,0:T(8,128)(2,1)}) custom-call(bf16[1024,256]{1,0:T(8,128)(2,1)} %get-tuple-element.57.refs_0_.refs_4_, bf16[256,1600]{1,0:T(8,128)(2,1)} %reduce_sum.194.refs_1_, bf16[400,800]{1,0:T(8,128)(2,1)} %pad_maximum_fusion.2.refs_2_), custom_call_target="tpu_custom_call" | custom-call | tf_op jit(solution)/shard_map/product_7/pallas_call | solution.py:675
  181.9 1.8 fusion.32
  183.7 0.2 multiply_reduce_fusion.3
  184.0 1.0 add_convert_fusion.1.refs_0_
  184.9 44.2 %exchange_2.1 = (bf16[8,128,1600]{2,1,0:T(8,128)(2,1)}, bf16[4,200,1600]{2,1,0:T(8,128)(2,1)}) custom-call(bf16[128,1600]{1,0:T(8,128)(2,1)} %add_convert_fusion.1.refs_0_, bf16[200,1600]{1,0:T(8,128)(2,1)} %constant_dynamic-slice_fusion.refs_1_), custom_call_target="tpu_custom_call" | custom-call | tf_op jit(solution)/shard_map/exchange_2/pallas_call | solution.py:460
  229.2 6.0 fusion.37
  235.2 7.2 %convert_reduce_fusion.1 = (f32[800]{0:T(1024)S(1)}, bf16[1024,800]{1,0:T(8,128)(2,1)}, bf16[1024,800]{1,0:T(8,128)(2,1)}) fusion(f32[1024,800]{1,0:T(8,128)S(1)} %fusion.37, f32[800]{0:T(1024)S(1)} %add.290, bf16[1024,1600]{1,0:T(8,128)(2,1)S(1)} %bitcast.64, bf16[800,1600]{1,0:T(8,128)(2,1)S(1)} %bitcast.73), kind=kOutput, calls=%fused_computation.17 | convolution fusion | flops 2641919232 | bytes 12396800 | tf_op jit(solution)/shard_map/dot_general | solution.py:23
  242.4 82.4 %product_3.1 = (f32[128,1600]{1,0:T(8,128)}, f32[128,1600]{1,0:T(8,128)}, bf16[1600,800]{1,0:T(8,128)(2,1)}, bf16[800,1600]{1,0:T(8,128)(2,1)}) custom-call(bf16[1024,800]{1,0:T(8,128)(2,1)} %get-tuple-element.149.refs_0_.refs_5_, bf16[1600,800]{1,0:T(8,128)(2,1)} %bitcast.69, bf16[1024,800]{1,0:T(8,128)(2,1)} %get-tuple-element.162.refs_2_.refs_6_, ...), custom_call_target="tpu_custom_call" | custom-call | tf_op jit(solution)/shard_map/product_3/pallas_call | solution.py:675
  325.0 1.5 multiply_reduce_fusion.1
  326.7 3.2 convert_reduce_fusion.6
  329.8 47.1 %exchange_4.1 = (bf16[8,128,1600]{2,1,0:T(8,128)(2,1)}, bf16[400,800]{1,0:T(8,128)(2,1)}, bf16[200,1600]{1,0:T(8,128)(2,1)}) custom-call(bf16[128,1600]{1,0:T(8,128)(2,1)} %get-tuple-element.151.refs_0_, bf16[4,400,800]{2,1,0:T(8,128)(2,1)} %bitcast.68, bf16[4,200,1600]{2,1,0:T(8,128)(2,1)} %bitcast.71), custom_call_target="tpu_custom_call" | custom-call | tf_op jit(solution)/shard_map/exchange_4/pallas_call | solution.py:460
  377.2 4.1 fusion.38.refs_6_
  381.3 1.2 copy.53
  382.4 66.1 %exchange_8.1 = (bf16[8,400,800]{2,1,0:T(8,128)(2,1)}, bf16[1024,256]{1,0:T(8,128)(2,1)}, bf16[1024,256]{1,0:T(8,128)(2,1)}, bf16[1024,256]{1,0:T(8,128)(2,1)}) custom-call(bf16[400,800]{1,0:T(8,128)(2,1)} %get-tuple-element.70.refs_0_, s32[1024,1]{1,0:T(8,128)} %copy.47.refs_2_.refs_1_, s32[1,1024]{1,0:T(1,128)} %bitcast.84, ...), custom_call_target="tpu_custom_call" | custom-call | tf_op jit(solution)/shard_map/exchange_8/pallas_call | solution.py:460
  448.5 1.2 convert_reduce_fusion.5
  450.1 1.2 convert_reduce_fusion.4
  451.7 2.6 pad_maximum_fusion.refs_0_.refs_3_
  454.3 41.9 %product_5.1 = (f32[128,1600]{1,0:T(8,128)}, bf16[1600,768]{1,0:T(8,128)(2,1)}, bf16[256,1600]{1,0:T(8,128)(2,1)}) custom-call(bf16[1024,768]{1,0:T(8,128)(2,1)} %pad_maximum_fusion.refs_0_.refs_3_, bf16[1600,768]{1,0:T(8,128)(2,1)} %bitcast.75, bf16[1024,1600]{1,0:T(8,128)(2,1)} %fusion.3.refs_2_, bf16[1024,768]{1,0:T(8,128)(2,1)} %pad_maximum_fusion.refs_0_.refs_3_, ...), custom_call_target="tpu_custom_call" | custom-call | tf_op jit(solution)/shard_map/product_5/pallas_call | solution.py:675
  496.2 1.6 fusion.23
  497.8 1.8 fusion.22
  499.6 1.2 copy.54
  501.1 0.6 copy.59
  501.7 152.8 %exchange_6.1 = (bf16[8,200,1600]{2,1,0:T(8,128)(2,1)}, bf16[8,400,768]{2,1,0:T(8,128)(2,1)}, bf16[8,64,1600]{2,1,0:T(8,128)(2,1)}, f32[8,40,128]{2,1,0:T(8,128)}, bf16[400,1600]{1,0:T(8,128)(2,1)}) custom-call(bf16[200,1600]{1,0:T(8,128)(2,1)} %get-tuple-element.78.refs_0_, bf16[4,400,768]{2,1,0:T(8,128)(2,1)} %bitcast.74, bf16[4,64,1600]{2,1,0:T(8,128)(2,1)} %bitcast.77, ...), custom_call_target="tpu_custom_call" | custom-call | tf_op jit(solution)/shard_map/exchange_6/pallas_call | solution.py:460
  654.6 0.9 reduce_sum.212
  655.5 0.7 slice.128
  656.2 0.7 slice.132
  656.8 0.7 fusion.35
  657.5 17.6 %lay_out.1 = (f32[1600,1600]{1,0:T(8,128)}, f32[400,1600]{1,0:T(8,128)}, f32[400,6400]{1,0:T(8,128)}, f32[400,4800]{1,0:T(8,128)}) custom-call(bf16[1600,1600]{1,0:T(8,128)(2,1)} %bitcast.59, bf16[400,1600]{1,0:T(8,128)(2,1)} %get-tuple-element.83.refs_1_, bf16[8,400,800]{2,1,0:T(8,128)(2,1)} %get-tuple-element.84.refs_2_, ...), custom_call_target="tpu_custom_call" | custom-call | bytes 46080000 | tf_op jit(solution)/shard_map/lay_out/pallas_call | solution.py:725
  (73 shorter events, 3.8 us)
Async XLA Ops:
  6.2 9.4 %copy-start.8 = (s32[8,128]{1,0:T(8,128)}, s32[8,128]{1,0:T(8,128)S(1)}, u32[]{:S(2)}) copy-start(s32[8,128]{1,0:T(8,128)S(1)} %multiply_add_fusion) | copy-start | bytes 12292
  9.5 6.1 copy-start.1
  63.0 3.0 copy-start
  81.6 1.7 copy-start.7
  181.9 47.2 %copy-start.5 = (bf16[4,400,800]{2,1,0:T(8,128)(2,1)S(1)}, bf16[4,400,800]{2,1,0:T(8,128)(2,1)}, u32[]{:S(2)}) copy-start(bf16[4,400,800]{2,1,0:T(8,128)(2,1)} %get-tuple-element.65) | copy-start | bytes 7680004
  229.2 6.0 copy-start.3
  229.2 6.0 copy-start.6
  329.8 47.3 %copy-start.4 = (bf16[256,1600]{1,0:T(8,128)(2,1)S(1)}, bf16[256,1600]{1,0:T(8,128)(2,1)}, u32[]{:S(2)}) copy-start(bf16[256,1600]{1,0:T(8,128)(2,1)} %reduce_sum.194.refs_1_) | copy-start | bytes 2457604
  454.3 41.9 %copy-start.2 = (bf16[1,128,1600]{2,1,0:T(8,128)(2,1)S(1)}, bf16[1,128,1600]{2,1,0:T(8,128)(2,1)}, u32[]{:S(2)}) copy-start(bf16[1,128,1600]{2,1,0:T(8,128)(2,1)} %copy-done.1) | copy-start | bytes 1228804

commit v9 on v8

--- a/solution.py
+++ b/solution.py
@@ -45,7 +45,7 @@
     return 256
 
 
-def forward_step(slots, step, ins, outs, scratch):
+def forward_step(slots, step, ins, outs, scratch, gathered):
     qp_ref, kp_ref, q_ref, k_ref, v_ref = ins
     attn_ref, o_ref, l_ref = outs
     size = query_rows(q_ref.shape[0])
@@ -63,10 +63,17 @@
         l_ref[rows, h : h + 1] = total
 
 
-def backward_step(slots, step, ins, outs, scratch):
-    qp_ref, kp_ref, q_ref, k_ref, v_ref, do_ref, o_ref, l_ref = ins
+def backward_step(slots, step, ins, outs, scratch, gathered):
+    qp_ref, kp_ref, q_ref, k_ref, v_ref, w_ref, o_ref, l_ref = ins
     dq_ref, dk_ref, dv_ref = outs
-    dk_acc, dv_acc = scratch
+    dk_acc, dv_acc, do_ref, g_ref, sem = scratch
+    if step == 0:
+        copy = pltpu.make_async_copy(gathered[0], g_ref, sem)
+        copy.start()
+        copy.wait()
+        each = g_ref.shape[1]
+        for j in range(g_ref.shape[0]):
+            do_ref[j * each : (j + 1) * each, :] = dot_t(g_ref[j], w_ref[...])
     size = query_rows(q_ref.shape[0])
     steps = q_ref.shape[0] // size
     rows = slice(step * size, (step + 1) * size)
@@ -98,15 +105,34 @@
     outs = (shape((rows, wide), BF16), shape((rows, wide), F32), shape((rows, slots), F32))
     steps = rows // query_rows(rows)
     ins = (place.reshape(rows, 1), place.reshape(1, rows), q, k, v)
-    return steps, functools.partial(forward_step, slots), ins, outs, ()
-
-
-def backward_work(place, q, k, v, do, o, total, slots):
+    return steps, functools.partial(forward_step, slots), False, ins, outs, ()
+
+
+def backward_work(place, q, k, v, weight, o, total, slots, g):
     rows, wide = q.shape
     outs = (jax.ShapeDtypeStruct((rows, wide), BF16),) * 3
     steps = rows // query_rows(rows)
-    ins = (place.reshape(rows, 1), place.reshape(1, rows), q, k, v, do, o, total)
-    return steps, functools.partial(backward_step, slots), ins, outs, (pltpu.VMEM((rows, wide), F32),) * 2
+    ins = (place.reshape(rows, 1), place.reshape(1, rows), q, k, v, weight, o, total)
+    scratch = (pltpu.VMEM((rows, wide), F32),) * 3
+    scratch += (pltpu.VMEM((rows // g.shape[0], *g.shape), g.dtype), pltpu.SemaphoreType.DMA)
+    return steps, functools.partial(backward_step, slots), True, ins, outs, scratch
+
+
+def stack_body(*refs):
+    out = refs[-1]
+    out[...] = jnp.zeros_like(out)
+    for i, ref in enumerate(refs[:-1]):
+        out[i : i + 1, : ref.shape[0]] = ref[...].reshape(1, ref.shape[0])
+
+
+def stack_rows(vectors, longest):
+    return pl.pallas_call(
+        stack_body,
+        in_specs=[pl.BlockSpec(memory_space=pltpu.VMEM)] * len(vectors),
+        out_specs=pl.BlockSpec(memory_space=pltpu.VMEM),
+        out_shape=jax.ShapeDtypeStruct((16, longest), vectors[0].dtype),
+        name="stack_rows",
+    )(*vectors)
 
 
 def split_axis(n):
@@ -206,13 +232,15 @@
                 self.stage[j][y] = value.astype(self.stage[j].dtype)
                 self.to_far(j, y, self.pair).start()
 
-    def end(self):
-        for j in range(len(self.red_in)):
+    def end(self, first, last):
+        for j in range(first, last):
             value = self.red_in[j][self.f].astype(F32) + self.near_in[j][self.pair].astype(F32)
             for y in self.other:
                 self.to_far(j, y, y).wait_recv()
                 value = value + self.far_in[j][y].astype(F32)
             self.write(j, value)
+
+    def forward(self):
         for i in range(len(self.gather_in)):
             for y in self.other:
                 source = 2 * y + self.core
@@ -254,10 +282,10 @@
     work_scratch, refs = refs[:n_work_scratch], refs[n_work_scratch:]
     sums, scratch = refs[:n_sums], refs[n_sums:]
     copy_sem, send_sem, recv_sem, place_send, place_recv = scratch[:5]
-    goals = [(out, 0) for out in own_out]
-    goals += [(sums[0], firsts[j]) for j in range(n_joint)]
+    goals = [(sums[0], firsts[j]) for j in range(n_joint)]
     goals += [(out, 0) for out in sums[1 if n_pack else 0 :]]
-    fs = Fsdp(nf, fsdp_in, fsdp_out, own_in + red_in, goals, scratch[5:])
+    goals += [(out, 0) for out in own_out]
+    fs = Fsdp(nf, fsdp_in, fsdp_out, red_in + own_in, goals, scratch[5:])
 
     lines, across = split_axis(n)
     me = lax.axis_index("ctx")
@@ -332,40 +360,6 @@
             each_own(i, start)
             keep(i).start()
 
-    work_steps, work_fn = work
-    points = 1 + (lines - 1) * len(pieces)
-    passed = [0]
-
-    def do_work():
-        at = passed[0]
-        passed[0] += 1
-        for step in range(at * work_steps // points, (at + 1) * work_steps // points):
-            work_fn(step, work_in, work_out, work_scratch)
-
-    begin(range(late))
-    fs.middle()
-    do_work()
-    for j in range(n_pack):
-        first = firsts[n_joint + j]
-        sums[0][:, first : first + pack_in[j].shape[1]] = pack_in[j][...]
-    if n_sums:
-        if late:
-            each_twin(0, True, start)
-            each_relay(0, 1, True, start)
-            do_work()
-        fs.end()
-        begin(range(late, len(pieces)))
-    for d in range(1, lines):
-        for i in range(len(pieces)):
-            if d == 1:
-                if i == 0 and late and n_sums:
-                    continue
-                each_twin(i, True, start)
-            each_relay(i, d, True, start)
-            do_work()
-    if not n_sums:
-        fs.end()
-
     def crossed(i):
         for d in range(1, across):
             for step in range(lines):
@@ -378,6 +372,59 @@
                             hop(i, source, way).wait_recv()
                             if d < across - 1:
                                 pl.when(near[way][0])(lambda: hop(i, source, way).start())
+
+    work_steps, work_fn, gated = work
+    plan = []
+
+    def add(act, *args, then_work=True):
+        plan.append((functools.partial(act, *args), then_work))
+
+    def hops(i, d):
+        if d == 1:
+            each_twin(i, True, start)
+        each_relay(i, d, True, start)
+
+    def complete(i):
+        crossed(i)
+        keep(i).wait()
+
+    begin(range(late))
+    fs.middle()
+    for j in range(n_pack):
+        first = firsts[n_joint + j]
+        sums[0][:, first : first + pack_in[j].shape[1]] = pack_in[j][...]
+    early = set()
+    if n_sums:
+        early = {(i, 1) for i in range(late)} | ({(i, 2) for i in range(late)} if gated else set())
+        for d in (1, 2):
+            for i in range(late):
+                if (i, d) in early:
+                    add(hops, i, d, then_work=not gated)
+        add(fs.end, 0, n_red, then_work=False)
+        add(begin, range(late, len(pieces)), then_work=False)
+    if gated:
+        for i in range(late):
+            for d in range(3, lines):
+                add(hops, i, d, then_work=False)
+                early.add((i, d))
+        for i in range(late):
+            add(complete, i, then_work=i == late - 1)
+        add(fs.end, n_red, n_red + n_own)
+    for d in range(1, lines):
+        for i in range(len(pieces)):
+            if (i, d) not in early:
+                add(hops, i, d)
+    if not gated:
+        add(fs.end, n_red, n_red + n_own)
+    add(fs.forward, then_work=False)
+    points = sum(then_work for _, then_work in plan)
+    at = 0
+    for act, then_work in plan:
+        act()
+        if then_work:
+            for step in range(at * work_steps // points, (at + 1) * work_steps // points):
+                work_fn(step, work_in, work_out, work_scratch, ctx_out)
+            at += 1
 
     def place(k, act_local, act_send):
         block, row, src, dst, goal, size = moves[k]
@@ -402,17 +449,17 @@
 
     if moves:
         ready = [i for i in range(len(pieces)) if pieces[i][1] is red_out[1]]
+        assert not gated
         for i in ready:
             crossed(i)
             keep(i).wait()
         for k in range(len(moves)):
             place(k, start, start)
     else:
-        ready = []
+        ready = range(late) if gated else []
     for i in range(len(pieces)):
         if i not in ready:
-            crossed(i)
-            keep(i).wait()
+            complete(i)
     for k in range(len(moves)):
         place(k, wait_copy, wait_send)
 
@@ -451,14 +498,14 @@
     outs += [shape(x.shape[1:], x.dtype) for x in own]
     outs += [shape((n, *x.shape), x.dtype) for x in sums]
     outs += [shape((kept, sums[1].shape[1]), sums[1].dtype)] if moves else []
-    steps, work_fn, work_in, work_out, work_scratch = work or (0, None, (), (), ())
+    steps, work_fn, gated, work_in, work_out, work_scratch = work or (0, None, False, (), (), ())
     gathered = max(sum(len(cut(x.shape[0])) for x in [*ctx, *sums]), 1)
     any_spec, vmem_spec = pl.BlockSpec(memory_space=pl.ANY), pl.BlockSpec(memory_space=pltpu.VMEM)
     inputs = (*ctx, *fsdp, *own, *red, *pack, *work_in)
     counts = [len(x) for x in (ctx, fsdp, own, red, pack, work_in, work_out, work_scratch)]
     dma = pltpu.SemaphoreType.DMA
     return pl.pallas_call(
-        functools.partial(exchange_body, n, nf, tuple(counts), tuple(firsts), tuple(moves), (steps, work_fn)),
+        functools.partial(exchange_body, n, nf, tuple(counts), tuple(firsts), tuple(moves), (steps, work_fn, gated)),
         in_specs=[any_spec] * (len(ctx) + len(fsdp)) + [vmem_spec] * (len(inputs) - len(ctx) - len(fsdp)),
         out_specs=[any_spec] * (len(ctx) + len(fsdp))
         + [vmem_spec] * len(own)
@@ -469,7 +516,7 @@
         + [pltpu.VMEM(x.shape, x.dtype) for x in sums]
         + [dma((gathered,)), dma((gathered, 4, n, 2)), dma((gathered, 4, n, 2))]
         + [dma((max(len(moves), 1),))] * 2
-        + Fsdp.scratch(nf, fsdp, [*own, *red]),
+        + Fsdp.scratch(nf, fsdp, [*red, *own]),
         name=f"exchange_{call}",
         compiler_params=pltpu.CompilerParams(collective_id=call, has_side_effects=True, vmem_limit_bytes=60 * 2**20),
     )(*inputs)
@@ -615,6 +662,8 @@
     fsdp_in, refs = refs[:n_fsdp], refs[n_fsdp:]
     outs, side_out, fsdp_out = refs[:n_prod], refs[n_prod : n_prod + n_sides], refs[n_prod + n_sides : n_prod + n_sides + n_fsdp]
     scratch = refs[n_prod + n_sides + n_fsdp :]
+    side_at, side_sem, scratch = scratch[: 2 * n_sides], scratch[2 * n_sides], scratch[2 * n_sides + 1 :]
+    fetches = [pltpu.make_async_copy(side_in[j], side_at[j], side_sem.at[j]) for j in range(2 * n_sides)]
     each = 17
     jobs = [
         Scatter(n, n_prod > 1, transposed[p], pairs[2 * p], pairs[2 * p + 1], outs[p], scratch[each * p : each * (p + 1)])
@@ -631,6 +680,8 @@
             line = jnp.where(a == av, sorted(range(lines), key=lambda j: (-abs(j - av), j))[k], line)
         order.append(line)
 
+    for fetch in fetches:
+        fetch.start()
     for job in jobs:
         for line in order:
             job.compute(line)
@@ -644,10 +695,13 @@
     for step, (job, line) in enumerate(steps):
         job.pass_on(line)
         for j, first, size in bits[step * len(bits) // len(steps) : (step + 1) * len(bits) // len(steps)]:
-            part = side_in[2 * j][:, first : first + size]
-            side_out[j][first : first + size, :] = t_dot(part, side_in[2 * j + 1][...]).astype(BF16)
+            if first == 0:
+                fetches[2 * j].wait()
+                fetches[2 * j + 1].wait()
+            part = side_at[2 * j][:, first : first + size]
+            side_out[j][first : first + size, :] = t_dot(part, side_at[2 * j + 1][...]).astype(BF16)
         if step == len(order) - 2:
-            fs.end()
+            fs.forward()
     for job in jobs:
         job.own()
     for job in jobs:
@@ -680,10 +734,12 @@
             (len(products), len(sides), len(fsdp)),
             tuple(turned for _, _, turned in products),
         ),
-        in_specs=[vmem_spec] * (len(inputs) + len(fsdp)),
+        in_specs=[vmem_spec] * (2 * len(products)) + [any_spec] * (2 * len(sides) + len(fsdp)),
         out_specs=[vmem_spec] * (len(outs) - len(fsdp)) + [any_spec] * len(fsdp),
         out_shape=outs,
-        scratch_shapes=[s for width in widths for s in Scatter.scratch(n, len(widths) > 1, rows, width)] + Fsdp.scratch(nf, fsdp, ()),
+        scratch_shapes=[pltpu.VMEM(z.shape, z.dtype) for side in sides for z in side]
+        + [pltpu.SemaphoreType.DMA((max(2 * len(sides), 1),))]
+        + [s for width in widths for s in Scatter.scratch(n, len(widths) > 1, rows, width)] + Fsdp.scratch(nf, fsdp, ()),
         name=f"product_{call}",
         compiler_params=pltpu.CompilerParams(collective_id=call, has_side_effects=True, vmem_limit_bytes=63 * 2**20),
     )(*inputs, *fsdp)
@@ -823,9 +879,7 @@
 
     vectors = (ln1_gain, ln1_shift, qv_bias, out_bias, ln2_gain, ln2_shift, up_bias, down_bias)
     longest = max(v.shape[0] for v in vectors)
-    flat = sum(
-        jnp.pad(v.astype(F32)[None, :], ((i, 15 - i), (0, longest - v.shape[0]))) for i, v in enumerate(vectors)
-    ).astype(BF16)
+    flat = stack_rows(vectors, longest)
     q_w = head_columns(qkv_weight[:, :width], width, c, n)
     k_w = head_columns(qkv_weight[:, width : 2 * width], width, c, n)
     v_w = head_columns(qkv_weight[:, 2 * width :], width, c, n)
@@ -857,8 +911,8 @@
         fsdp=[head_rows(out_weight, heads, c, f, n)],
         work=forward_work(place, q, k, v, slots),
     )
-    w_out = jnp.sum(w_out.astype(F32), axis=0).astype(BF16)
     up_mine = [lax.dynamic_slice_in_dim(up_weight, i * ff_local + c * ff_part, ff_part, axis=1) for i in range(nf)]
+    w_out = functools.reduce(jnp.add, [w_out[i] for i in range(nf)])
     mixed, w_up = product(7, n, nf, [(attn, w_out, False)], fsdp=[jnp.concatenate(up_mine, axis=1)])
     w_up = w_up.reshape(width, nf * ff_part)
     x = tokens[0].astype(F32)
@@ -895,12 +949,10 @@
     d_mid = grad_out + ln_back(da2, n2, rstd2, gain2)
     g1 = d_mid.astype(BF16)
     d_out_bias = jnp.sum(g1.astype(F32), axis=0)
-    g1_all, d_up, d_down = exchange(4, n, nf, ctx=[g1], own=[d_up, d_down])
+    g1_all, d_down, d_up, gq, gk, gv = exchange(
+        4, n, nf, ctx=[g1], own=[d_down], red=[d_up], work=backward_work(place, q, k, v, w_out, o, total, slots, g1)
+    )
     g1_all = g1_all.reshape(n * rows, width)
-    d_attn = dot_t(g1_all, w_out)
-    d_up, gq, gk, gv = exchange(
-        8, n, nf, ctx=[d_up], work=backward_work(place, q, k, v, d_attn, o, total, slots)
-    )
     g_qkv = jnp.concatenate([gq, gk, gv], axis=1)
     da1, d_qkv, d_out = product(5, n, nf, [(g_qkv, w_qkv, True)], sides=[(act1, g_qkv), (attn, g1_all)])
     d_qkv = d_qkv.reshape(nf, local, 3 * wide)

time: 684 us -> 666 us (0.974)
  Pallas kernels: 588 us -> 581 us
    pallas_call x6 -> x5, Pallas kernels: 403 us -> 400 us  [exchange(): pl.pallas_call(functools.partial(exchange_body, n, nf, tuple(counts), tup...]
where the time goes in v9:
time: 666 us; the launch traced here: 657 us
  Pallas kernels  581 us (87%)
  other arithmetic  36.9 us (6%)
  local copies, waits for them, and re-layouts  22.1 us (3%)
  matrix products  16.2 us (2%)
    pallas_call x5, Pallas kernels, exchange(): pl.pallas_call(functools.partial(exchange_body, n, nf, tuple(counts), tup...  400 us
    pallas_call x3, Pallas kernels, product(): pl.pallas_call(functools.partial(product_body, n, nf, (len(products), len...  161 us
    pallas_call x1, Pallas kernels, lay_out(): pl.pallas_call(functools.partial(layout_body, tuple((m and tuple(m) for m...  17.6 us

profile of v9, /device:TPU:0, one launch (start us, length us, event | category | flops | bytes accessed | tf_op | source)
XLA Modules:
  0.0 657.3 jit_solution(1344502201150183174)
XLA Ops:
  0.7 0.7 broadcast_subtract_fusion
  1.3 0.7 multiply_add_fusion
  2.1 1.5 stack_rows.1.refs_1_
  3.5 1.2 copy.45
  4.8 0.1 convert_reduce_fusion.2
  4.9 2.0 copy.46
  6.9 1.0 copy.47.refs_2_.refs_3_
  8.0 2.8 fusion.34
  10.8 0.1 dynamic-slice_select_fusion.2
  10.9 0.1 constant_dynamic-slice_fusion.7
  11.1 0.1 dynamic-slice_select_fusion
  11.2 0.2 constant_dynamic-slice_fusion.5
  11.4 1.1 concatenate.29.refs_2_
  12.5 45.7 %exchange_0.1 = (bf16[8,128,1600]{2,1,0:T(8,128)(2,1)}, bf16[4,16,1600]{2,1,0:T(8,128)(2,1)}, bf16[4,400,768]{2,1,0:T(8,128)(2,1)}) custom-call(bf16[128,1600]{1,0:T(8,128)(2,1)} %bitcast.58, bf16[16,1600]{1,0:T(8,128)(2,1)} %stack_rows.1.refs_1_, bf16[400,768]{1,0:T(8,128)(2,1)} %concatenate.29.refs_2_), custom_call_target="tpu_custom_call" | custom-call | tf_op jit(solution)/shard_map/exchange_0/pallas_call | solution.py:507
  58.2 2.6 convert_reduce_fusion
  60.9 0.3 copy-done
  61.2 1.0 multiply_reduce_fusion
  62.3 0.8 slice_convert_fusion.1
  63.8 1.0 convert_reduce_fusion.7
  64.8 1.2 convert_reduce_fusion.8
  66.7 0.1 fusion.26
  66.8 1.3 pad_dynamic-slice_fusion.1
  68.1 1.0 pad_maximum_fusion.1.refs_1_
  69.1 2.0 constant_dynamic-slice_fusion.refs_1_
  71.1 1.6 constant_dynamic-slice_fusion.4
  72.7 1.2 pad_maximum_fusion.2.refs_2_
  73.9 2.7 fusion.3.refs_2_
  76.6 1.5 add_convert_fusion
  78.1 0.2 copy-done.6
  78.3 3.0 fusion.36
  81.3 0.9 slice.175.refs_5_.refs_6_
  82.2 1.2 fusion.11
  83.4 47.9 %exchange_1.1 = (bf16[8,128,1600]{2,1,0:T(8,128)(2,1)}, bf16[4,256,1600]{2,1,0:T(8,128)(2,1)}, bf16[1024,256]{1,0:T(8,128)(2,1)}, f32[1024,256]{1,0:T(8,128)}, f32[1024,4]{1,0:T(8,128)}) custom-call(bf16[128,1600]{1,0:T(8,128)(2,1)} %bitcast.60, bf16[256,1600]{1,0:T(8,128)(2,1)} %pad_maximum_fusion.1.refs_1_, s32[1024,1]{1,0:T(8,128)} %copy.47.refs_2_.refs_3_, ...), custom_call_target="tpu_custom_call" | custom-call | tf_op jit(solution)/shard_map/exchange_1/pallas_call | solution.py:507
  131.3 3.0 add_bitcast_fusion.1.refs_1_.refs_8_
  134.2 42.9 %product_7.1 = (f32[128,1600]{1,0:T(8,128)}, bf16[4,400,800]{2,1,0:T(8,128)(2,1)}) custom-call(bf16[1024,256]{1,0:T(8,128)(2,1)} %get-tuple-element.56.refs_0_.refs_4_, bf16[256,1600]{1,0:T(8,128)(2,1)} %add_bitcast_fusion.1.refs_1_.refs_8_, bf16[400,800]{1,0:T(8,128)(2,1)} %pad_maximum_fusion.2.refs_2_), custom_call_target="tpu_custom_call" | custom-call | tf_op jit(solution)/shard_map/product_7/pallas_call | solution.py:729
  177.1 1.8 fusion.32
  178.9 0.2 multiply_reduce_fusion.3
  179.1 1.0 add_convert_fusion.1.refs_0_
  180.1 44.4 %exchange_2.1 = (bf16[8,128,1600]{2,1,0:T(8,128)(2,1)}, bf16[4,200,1600]{2,1,0:T(8,128)(2,1)}) custom-call(bf16[128,1600]{1,0:T(8,128)(2,1)} %add_convert_fusion.1.refs_0_, bf16[200,1600]{1,0:T(8,128)(2,1)} %constant_dynamic-slice_fusion.refs_1_), custom_call_target="tpu_custom_call" | custom-call | tf_op jit(solution)/shard_map/exchange_2/pallas_call | solution.py:507
  224.5 6.0 fusion.37
  230.5 7.2 %convert_reduce_fusion.1 = (f32[800]{0:T(1024)S(1)}, bf16[1024,800]{1,0:T(8,128)(2,1)}, bf16[1024,800]{1,0:T(8,128)(2,1)}) fusion(f32[1024,800]{1,0:T(8,128)S(1)} %fusion.37, f32[800]{0:T(1024)S(1)} %add.263, bf16[1024,1600]{1,0:T(8,128)(2,1)S(1)} %bitcast.63, bf16[800,1600]{1,0:T(8,128)(2,1)S(1)} %bitcast.72), kind=kOutput, calls=%fused_computation.17 | convolution fusion | flops 2641919232 | bytes 12396800 | tf_op jit(solution)/shard_map/dot_general | solution.py:23
  237.8 79.2 %product_3.1 = (f32[128,1600]{1,0:T(8,128)}, f32[128,1600]{1,0:T(8,128)}, bf16[1600,800]{1,0:T(8,128)(2,1)}, bf16[800,1600]{1,0:T(8,128)(2,1)}) custom-call(bf16[1024,800]{1,0:T(8,128)(2,1)} %get-tuple-element.147.refs_0_.refs_5_, bf16[1600,800]{1,0:T(8,128)(2,1)} %bitcast.68, bf16[1024,800]{1,0:T(8,128)(2,1)} %get-tuple-element.160.refs_2_.refs_6_, ...), custom_call_target="tpu_custom_call" | custom-call | tf_op jit(solution)/shard_map/product_3/pallas_call | solution.py:729
  317.1 0.1 reshape_reshape.2
  317.2 1.5 multiply_reduce_fusion.1
  318.9 3.2 convert_reduce_fusion.6
  322.3 1.2 copy.53
  323.5 113.9 %exchange_4.1 = (bf16[8,128,1600]{2,1,0:T(8,128)(2,1)}, bf16[200,1600]{1,0:T(8,128)(2,1)}, bf16[8,400,800]{2,1,0:T(8,128)(2,1)}, bf16[1024,256]{1,0:T(8,128)(2,1...) custom-call(bf16[128,1600]{1,0:T(8,128)(2,1)} %get-tuple-element.149.refs_0_, bf16[4,200,1600]{2,1,0:T(8,128)(2,1)} %bitcast.70, ...), custom_call_target="tpu_custom_call" | custom-call | tf_op jit(solution)/shard_map/exchange_4/pallas_call | solution.py:507
  437.4 1.2 convert_reduce_fusion.5
  438.6 0.2 fusion.27
  438.9 1.2 convert_reduce_fusion.4
  440.1 0.2 fusion.28
  440.5 2.6 pad_maximum_fusion.refs_0_.refs_3_
  443.1 39.0 %product_5.1 = (f32[128,1600]{1,0:T(8,128)}, bf16[1600,768]{1,0:T(8,128)(2,1)}, bf16[256,1600]{1,0:T(8,128)(2,1)}) custom-call(bf16[1024,768]{1,0:T(8,128)(2,1)} %pad_maximum_fusion.refs_0_.refs_3_, bf16[1600,768]{1,0:T(8,128)(2,1)} %bitcast.74, bf16[1024,1600]{1,0:T(8,128)(2,1)} %fusion.3.refs_2_, bf16[1024,768]{1,0:T(8,128)(2,1)} %pad_maximum_fusion.refs_0_.refs_3_, ...), custom_call_target="tpu_custom_call" | custom-call | tf_op jit(solution)/shard_map/product_5/pallas_call | solution.py:729
  482.1 1.6 fusion.23
  483.8 1.8 fusion.22
  485.6 1.2 copy.54
  486.8 0.1 concatenate.38
  487.0 0.6 copy.59
  487.6 148.6 %exchange_6.1 = (bf16[8,200,1600]{2,1,0:T(8,128)(2,1)}, bf16[8,400,768]{2,1,0:T(8,128)(2,1)}, bf16[8,64,1600]{2,1,0:T(8,128)(2,1)}, f32[8,40,128]{2,1,0:T(8,128)}, bf16[400,1600]{1,0:T(8,128)(2,1)}) custom-call(bf16[200,1600]{1,0:T(8,128)(2,1)} %get-tuple-element.76.refs_0_, bf16[4,400,768]{2,1,0:T(8,128)(2,1)} %bitcast.73, bf16[4,64,1600]{2,1,0:T(8,128)(2,1)} %bitcast.76, ...), custom_call_target="tpu_custom_call" | custom-call | tf_op jit(solution)/shard_map/exchange_6/pallas_call | solution.py:507
  636.3 0.9 reduce_sum.199
  637.2 0.7 slice.144
  637.9 0.7 slice.148
  638.6 0.7 fusion.35
  639.2 17.6 %lay_out.1 = (f32[1600,1600]{1,0:T(8,128)}, f32[400,1600]{1,0:T(8,128)}, f32[400,6400]{1,0:T(8,128)}, f32[400,4800]{1,0:T(8,128)}) custom-call(bf16[1600,1600]{1,0:T(8,128)(2,1)} %bitcast.59, bf16[400,1600]{1,0:T(8,128)(2,1)} %get-tuple-element.81.refs_1_, bf16[8,400,800]{2,1,0:T(8,128)(2,1)} %get-tuple-element.82.refs_2_, ...), custom_call_target="tpu_custom_call" | custom-call | bytes 46080000 | tf_op jit(solution)/shard_map/lay_out/pallas_call | solution.py:781
  (61 shorter events, 2.4 us)
Async XLA Ops:
  2.1 8.7 %copy-start.7 = (s32[8,128]{1,0:T(8,128)}, s32[8,128]{1,0:T(8,128)S(1)}, u32[]{:S(2)}) copy-start(s32[8,128]{1,0:T(8,128)S(1)} %multiply_add_fusion) | copy-start | bytes 12292
  4.8 6.1 copy-start.1
  58.2 3.0 copy-start
  76.6 1.7 copy-start.6
  177.1 47.4 %copy-start.4 = (bf16[4,400,800]{2,1,0:T(8,128)(2,1)S(1)}, bf16[4,400,800]{2,1,0:T(8,128)(2,1)}, u32[]{:S(2)}) copy-start(bf16[4,400,800]{2,1,0:T(8,128)(2,1)} %get-tuple-element.64) | copy-start | bytes 7680004
  224.5 6.0 copy-start.3
  224.5 6.0 copy-start.5
  443.1 39.0 %copy-start.2 = (bf16[1,128,1600]{2,1,0:T(8,128)(2,1)S(1)}, bf16[1,128,1600]{2,1,0:T(8,128)(2,1)}, u32[]{:S(2)}) copy-start(bf16[1,128,1600]{2,1,0:T(8,128)(2,1)} %copy-done.1) | copy-start | bytes 1228804

commit v10 on v9

--- a/solution.py
+++ b/solution.py
@@ -45,13 +45,19 @@
     return 256
 
 
+def head_groups(slots):
+    return [range(h, min(h + 2, slots)) for h in range(0, slots, 2)]
+
+
 def forward_step(slots, step, ins, outs, scratch, gathered):
     qp_ref, kp_ref, q_ref, k_ref, v_ref = ins
     attn_ref, o_ref, l_ref = outs
     size = query_rows(q_ref.shape[0])
-    rows = slice(step * size, (step + 1) * size)
+    groups = head_groups(slots)
+    block, group = divmod(step, len(groups))
+    rows = slice(block * size, (block + 1) * size)
     allowed = kp_ref[...] <= qp_ref[rows, :]
-    for h in range(slots):
+    for h in groups[group]:
         cols = slice(h * HEAD_DIM, (h + 1) * HEAD_DIM)
         raw = dot_t(q_ref[rows, cols], k_ref[:, cols])
         e = jnp.where(allowed, jnp.exp(raw * SCALE), 0.0)
@@ -75,10 +81,12 @@
         for j in range(g_ref.shape[0]):
             do_ref[j * each : (j + 1) * each, :] = dot_t(g_ref[j], w_ref[...])
     size = query_rows(q_ref.shape[0])
-    steps = q_ref.shape[0] // size
-    rows = slice(step * size, (step + 1) * size)
+    blocks = q_ref.shape[0] // size
+    groups = head_groups(slots)
+    block, group = divmod(step, len(groups))
+    rows = slice(block * size, (block + 1) * size)
     allowed = kp_ref[...] <= qp_ref[rows, :]
-    for h in range(slots):
+    for h in groups[group]:
         cols = slice(h * HEAD_DIM, (h + 1) * HEAD_DIM)
         q, k, v, do = q_ref[rows, cols], k_ref[:, cols], v_ref[:, cols], do_ref[rows, cols]
         total = l_ref[rows, h : h + 1]
@@ -89,9 +97,9 @@
         ds = (e * (de - corr)).astype(BF16)
         dq_ref[rows, cols] = (dot(ds, k) * SCALE).astype(BF16)
         dk, dv = t_dot(ds, q), t_dot(e.astype(BF16), w)
-        if step:
+        if block:
             dk, dv = dk + dk_acc[:, cols], dv + dv_acc[:, cols]
-        if step < steps - 1:
+        if block < blocks - 1:
             dk_acc[:, cols] = dk
             dv_acc[:, cols] = dv
         else:
@@ -103,7 +111,7 @@
     rows, wide = q.shape
     shape = jax.ShapeDtypeStruct
     outs = (shape((rows, wide), BF16), shape((rows, wide), F32), shape((rows, slots), F32))
-    steps = rows // query_rows(rows)
+    steps = rows // query_rows(rows) * len(head_groups(slots))
     ins = (place.reshape(rows, 1), place.reshape(1, rows), q, k, v)
     return steps, functools.partial(forward_step, slots), False, ins, outs, ()
 
@@ -111,7 +119,7 @@
 def backward_work(place, q, k, v, weight, o, total, slots, g):
     rows, wide = q.shape
     outs = (jax.ShapeDtypeStruct((rows, wide), BF16),) * 3
-    steps = rows // query_rows(rows)
+    steps = rows // query_rows(rows) * len(head_groups(slots))
     ins = (place.reshape(rows, 1), place.reshape(1, rows), q, k, v, weight, o, total)
     scratch = (pltpu.VMEM((rows, wide), F32),) * 3
     scratch += (pltpu.VMEM((rows // g.shape[0], *g.shape), g.dtype), pltpu.SemaphoreType.DMA)
@@ -210,10 +218,6 @@
         send, recv = self.r_send.at[j, 1, y], self.r_recv.at[j, 1, source]
         return self.copy(self.stage[j].at[y], self.far_in[j].at[source], send, recv, 2 * y + self.core)
 
-    def write(self, j, value):
-        out, first = self.red_out[j]
-        out[:, first : first + value.shape[1]] = value.astype(out.dtype)
-
     def start(self):
         for j in range(len(self.red_in)):
             for y in range(self.pairs):
@@ -238,7 +242,7 @@
             for y in self.other:
                 self.to_far(j, y, y).wait_recv()
                 value = value + self.far_in[j][y].astype(F32)
-            self.write(j, value)
+            self.red_out[j][...] = value.astype(self.red_out[j].dtype)
 
     def forward(self):
         for i in range(len(self.gather_in)):
@@ -264,39 +268,35 @@
                 self.to_far(j, y, self.pair).wait_send()
 
 
-def exchange_body(n, nf, counts, firsts, moves, work, *refs):
-    n_ctx, n_fsdp, n_own, n_red, n_pack, n_work_in, n_work_out, n_work_scratch = counts
+def exchange_body(n, nf, counts, moves, work, *refs):
+    n_ctx, n_fsdp, n_own, n_red, n_work_in, n_work_out, n_work_scratch = counts
     bounds = [0]
-    for size in counts[:6]:
+    for size in counts[:5]:
         bounds.append(bounds[-1] + size)
-    ctx_in, fsdp_in, own_in, red_in, pack_in, work_in = (refs[i:j] for i, j in zip(bounds, bounds[1:]))
+    ctx_in, fsdp_in, own_in, red_in, work_in = (refs[i:j] for i, j in zip(bounds, bounds[1:]))
     refs = refs[bounds[-1] :]
-    n_joint = len(firsts) - n_pack
-    n_sums = n_red - n_joint + (1 if n_pack else 0)
     ctx_out, fsdp_out, own_out = refs[:n_ctx], refs[n_ctx : n_ctx + n_fsdp], refs[n_ctx + n_fsdp : n_ctx + n_fsdp + n_own]
     refs = refs[n_ctx + n_fsdp + n_own :]
-    red_out, refs = refs[:n_sums], refs[n_sums:]
+    red_out, refs = refs[:n_red], refs[n_red:]
     if moves:
         placed, refs = refs[0], refs[1:]
     work_out, refs = refs[:n_work_out], refs[n_work_out:]
     work_scratch, refs = refs[:n_work_scratch], refs[n_work_scratch:]
-    sums, scratch = refs[:n_sums], refs[n_sums:]
+    sums, scratch = refs[:n_red], refs[n_red:]
     copy_sem, send_sem, recv_sem, place_send, place_recv = scratch[:5]
-    goals = [(sums[0], firsts[j]) for j in range(n_joint)]
-    goals += [(out, 0) for out in sums[1 if n_pack else 0 :]]
-    goals += [(out, 0) for out in own_out]
-    fs = Fsdp(nf, fsdp_in, fsdp_out, red_in + own_in, goals, scratch[5:])
+    fs = Fsdp(nf, fsdp_in, fsdp_out, red_in + own_in, sums + own_out, scratch[5:])
 
     lines, across = split_axis(n)
     me = lax.axis_index("ctx")
     a, b, near = place_of(me, lines, across)
     pieces = [(src, out, first, rows) for src, out in zip(ctx_in, ctx_out) for first, rows in cut(out.shape[1])]
     late = len(pieces)
-    for src, out in reversed(list(zip(sums, red_out))):
+    second = late
+    for src, out in zip(sums, red_out):
+        second = len(pieces)
         pieces += [(src, out, first, rows) for first, rows in cut(out.shape[1])]
     peers = [lax.rem(fs.f + k, nf) for k in range(1, nf)] if moves else fs.peers
     meet(near if pieces else [], [("fsdp", peer) for peer in peers])
-    fs.start()
 
     def turned_part(i):
         return turned_rows(pieces[i][3], pieces[i][1].dtype, across, len(pieces) > 1)
@@ -373,62 +373,9 @@
                             if d < across - 1:
                                 pl.when(near[way][0])(lambda: hop(i, source, way).start())
 
-    work_steps, work_fn, gated = work
-    plan = []
-
-    def add(act, *args, then_work=True):
-        plan.append((functools.partial(act, *args), then_work))
-
-    def hops(i, d):
-        if d == 1:
-            each_twin(i, True, start)
-        each_relay(i, d, True, start)
-
-    def complete(i):
-        crossed(i)
-        keep(i).wait()
-
-    begin(range(late))
-    fs.middle()
-    for j in range(n_pack):
-        first = firsts[n_joint + j]
-        sums[0][:, first : first + pack_in[j].shape[1]] = pack_in[j][...]
-    early = set()
-    if n_sums:
-        early = {(i, 1) for i in range(late)} | ({(i, 2) for i in range(late)} if gated else set())
-        for d in (1, 2):
-            for i in range(late):
-                if (i, d) in early:
-                    add(hops, i, d, then_work=not gated)
-        add(fs.end, 0, n_red, then_work=False)
-        add(begin, range(late, len(pieces)), then_work=False)
-    if gated:
-        for i in range(late):
-            for d in range(3, lines):
-                add(hops, i, d, then_work=False)
-                early.add((i, d))
-        for i in range(late):
-            add(complete, i, then_work=i == late - 1)
-        add(fs.end, n_red, n_red + n_own)
-    for d in range(1, lines):
-        for i in range(len(pieces)):
-            if (i, d) not in early:
-                add(hops, i, d)
-    if not gated:
-        add(fs.end, n_red, n_red + n_own)
-    add(fs.forward, then_work=False)
-    points = sum(then_work for _, then_work in plan)
-    at = 0
-    for act, then_work in plan:
-        act()
-        if then_work:
-            for step in range(at * work_steps // points, (at + 1) * work_steps // points):
-                work_fn(step, work_in, work_out, work_scratch, ctx_out)
-            at += 1
-
     def place(k, act_local, act_send):
         block, row, src, dst, goal, size = moves[k]
-        source, goal = red_out[1].at[block, pl.ds(row, size)], placed.at[pl.ds(goal, size)]
+        source, goal = red_out[0].at[block, pl.ds(row, size)], placed.at[pl.ds(goal, size)]
         if src == dst:
             pl.when(fs.f == src)(lambda: act_local(pltpu.make_async_copy(source, goal, place_send.at[k])))
             return
@@ -447,16 +394,79 @@
     def wait_copy(copy):
         copy.wait()
 
-    if moves:
-        ready = [i for i in range(len(pieces)) if pieces[i][1] is red_out[1]]
-        assert not gated
+    work_steps, work_fn, gated = work
+    plan = []
+
+    def add(act, *args, then_work=True):
+        plan.append((functools.partial(act, *args), then_work))
+
+    def hops(i, d):
+        if d == 1:
+            each_twin(i, True, start)
+        each_relay(i, d, True, start)
+
+    def complete(i):
+        crossed(i)
+        keep(i).wait()
+
+    begin(range(late))
+    fs.start()
+    fs.middle()
+    if not gated:
+        add(lambda: None)
+    before, after = range(second), range(second, len(pieces))
+    ready = []
+    if gated:
+        for d in range(1, lines):
+            for i in range(late):
+                add(hops, i, d, then_work=False)
+            if d == 2:
+                add(fs.end, 0, n_red, then_work=False)
+                add(begin, range(late, len(pieces)), then_work=False)
+        ready = range(late)
         for i in ready:
-            crossed(i)
-            keep(i).wait()
-        for k in range(len(moves)):
-            place(k, start, start)
+            add(complete, i, then_work=i == late - 1)
+        add(fs.end, n_red, n_red + n_own)
+        for d in range(1, lines):
+            for i in range(late, len(pieces)):
+                add(hops, i, d)
+    elif n_red:
+        add(fs.end, 0, n_red - 1)
+        add(begin, range(late, second))
+        for i in before:
+            add(hops, i, 1)
+        add(fs.end, n_red - 1, n_red)
+        add(begin, after)
+        for d in range(2, lines):
+            for i in before:
+                add(hops, i, d)
+            for i in after if d == 2 else ():
+                add(hops, i, 1)
+        if moves:
+            ready = [i for i in before if pieces[i][1] is red_out[0]]
+            for i in ready:
+                add(complete, i)
+            for k in range(len(moves)):
+                add(place, k, start, start)
+        for d in range(2, lines):
+            for i in after:
+                add(hops, i, d)
     else:
-        ready = range(late) if gated else []
+        for d in range(1, lines):
+            for i in range(len(pieces)):
+                add(hops, i, d)
+            if d == lines - 2:
+                add(fs.forward, then_work=False)
+        add(fs.end, 0, n_own)
+    points = sum(then_work for _, then_work in plan)
+    at = 0
+    for act, then_work in plan:
+        act()
+        if then_work:
+            for step in range(at * work_steps // points, (at + 1) * work_steps // points):
+                work_fn(step, work_in, work_out, work_scratch, ctx_out)
+            at += 1
+
     for i in range(len(pieces)):
         if i not in ready:
             complete(i)
@@ -486,26 +496,22 @@
     return [(0, rows - half), (rows - half, half)]
 
 
-def exchange(call, n, nf, ctx=(), fsdp=(), own=(), red=(), pack=(), firsts=(), moves=(), kept=0, work=None):
+def exchange(call, n, nf, ctx=(), fsdp=(), own=(), red=(), moves=(), kept=0, work=None):
     shape = jax.ShapeDtypeStruct
     sums = [shape(x.shape[1:], x.dtype) for x in red]
-    if pack:
-        joint = len(firsts) - len(pack)
-        width = sum(x.shape[1] for x in [*sums[:joint], *pack])
-        sums = [shape((pack[0].shape[0], width), pack[0].dtype)] + sums[joint:]
     outs = [shape((n, *x.shape), x.dtype) for x in ctx]
     outs += [shape((nf, *x.shape), x.dtype) for x in fsdp]
     outs += [shape(x.shape[1:], x.dtype) for x in own]
     outs += [shape((n, *x.shape), x.dtype) for x in sums]
-    outs += [shape((kept, sums[1].shape[1]), sums[1].dtype)] if moves else []
+    outs += [shape((kept, sums[0].shape[1]), sums[0].dtype)] if moves else []
     steps, work_fn, gated, work_in, work_out, work_scratch = work or (0, None, False, (), (), ())
     gathered = max(sum(len(cut(x.shape[0])) for x in [*ctx, *sums]), 1)
     any_spec, vmem_spec = pl.BlockSpec(memory_space=pl.ANY), pl.BlockSpec(memory_space=pltpu.VMEM)
-    inputs = (*ctx, *fsdp, *own, *red, *pack, *work_in)
-    counts = [len(x) for x in (ctx, fsdp, own, red, pack, work_in, work_out, work_scratch)]
+    inputs = (*ctx, *fsdp, *own, *red, *work_in)
+    counts = [len(x) for x in (ctx, fsdp, own, red, work_in, work_out, work_scratch)]
     dma = pltpu.SemaphoreType.DMA
     return pl.pallas_call(
-        functools.partial(exchange_body, n, nf, tuple(counts), tuple(firsts), tuple(moves), (steps, work_fn, gated)),
+        functools.partial(exchange_body, n, nf, tuple(counts), tuple(moves), (steps, work_fn, gated)),
         in_specs=[any_spec] * (len(ctx) + len(fsdp)) + [vmem_spec] * (len(inputs) - len(ctx) - len(fsdp)),
         out_specs=[any_spec] * (len(ctx) + len(fsdp))
         + [vmem_spec] * len(own)
@@ -700,7 +706,7 @@
                 fetches[2 * j + 1].wait()
             part = side_at[2 * j][:, first : first + size]
             side_out[j][first : first + size, :] = t_dot(part, side_at[2 * j + 1][...]).astype(BF16)
-        if step == len(order) - 2:
+        if step == len(order) - 3:
             fs.forward()
     for job in jobs:
         job.own()
@@ -980,8 +986,8 @@
     )
     packed = jnp.concatenate([s.reshape(nf, -1) for s in smalls], axis=1)
     packed = jnp.pad(packed, ((0, 0), (0, -packed.shape[1] % 1024))).reshape(nf, -1, 128)
-    d_down, d_qkv, _, packed, d_out = exchange(
-        6, n, nf, ctx=[d_down], red=[d_qkv, d_out, packed], moves=row_moves(n, nf, heads), kept=local
+    d_down, _, packed, d_qkv, d_out = exchange(
+        6, n, nf, ctx=[d_down], red=[d_out, packed, d_qkv], moves=row_moves(n, nf, heads), kept=local
     )
     mine = jnp.sum(packed, axis=0).reshape(-1)
     up_moves = [(i, j * ff_part, j * ff_local + i * ff_part, ff_part) for i in range(n) for j in range(nf)]

time: 666 us -> 656 us (0.985)
  Pallas kernels: 581 us -> 570 us
where the time goes in v10:
time: 656 us; the launch traced here: 647 us
  Pallas kernels  570 us (87%)
  other arithmetic  36.9 us (6%)
  local copies, waits for them, and re-layouts  22.1 us (3%)
  matrix products  16.2 us (2%)
    pallas_call x5, Pallas kernels, exchange(): pl.pallas_call(functools.partial(exchange_body, n, nf, tuple(counts), tup...  395 us
    pallas_call x3, Pallas kernels, product(): pl.pallas_call(functools.partial(product_body, n, nf, (len(products), len...  156 us
    pallas_call x1, Pallas kernels, lay_out(): pl.pallas_call(functools.partial(layout_body, tuple((m and tuple(m) for m...  17.6 us

profile of v10, /device:TPU:0, one launch (start us, length us, event | category | flops | bytes accessed | tf_op | source)
XLA Modules:
  0.0 647.1 jit_solution(2694750398473955918)
XLA Ops:
  0.7 0.7 broadcast_subtract_fusion
  1.3 0.7 multiply_add_fusion
  2.1 1.5 stack_rows.1.refs_1_
  3.5 1.2 copy.45
  4.8 0.1 convert_reduce_fusion.2
  4.9 2.0 copy.46
  6.9 1.0 copy.47.refs_2_.refs_3_
  8.0 2.8 fusion.34
  10.8 0.1 dynamic-slice_select_fusion.2
  10.9 0.1 constant_dynamic-slice_fusion.7
  11.1 0.1 dynamic-slice_select_fusion
  11.2 0.2 constant_dynamic-slice_fusion.5
  11.4 1.1 concatenate.29.refs_2_
  12.5 45.7 %exchange_0.1 = (bf16[8,128,1600]{2,1,0:T(8,128)(2,1)}, bf16[4,16,1600]{2,1,0:T(8,128)(2,1)}, bf16[4,400,768]{2,1,0:T(8,128)(2,1)}) custom-call(bf16[128,1600]{1,0:T(8,128)(2,1)} %bitcast.58, bf16[16,1600]{1,0:T(8,128)(2,1)} %stack_rows.1.refs_1_, bf16[400,768]{1,0:T(8,128)(2,1)} %concatenate.29.refs_2_), custom_call_target="tpu_custom_call" | custom-call | tf_op jit(solution)/shard_map/exchange_0/pallas_call | solution.py:513
  58.2 2.6 convert_reduce_fusion
  60.9 0.3 copy-done
  61.2 1.0 multiply_reduce_fusion
  62.2 0.8 slice_convert_fusion.1
  63.8 1.0 convert_reduce_fusion.7
  64.8 1.2 convert_reduce_fusion.8
  66.7 0.1 fusion.26
  66.8 1.3 pad_dynamic-slice_fusion.1
  68.1 1.0 pad_maximum_fusion.1.refs_1_
  69.1 2.0 constant_dynamic-slice_fusion.refs_1_
  71.1 1.6 constant_dynamic-slice_fusion.4
  72.7 1.2 pad_maximum_fusion.2.refs_2_
  73.9 2.7 fusion.3.refs_2_
  76.6 1.5 add_convert_fusion
  78.1 0.2 copy-done.6
  78.3 3.0 fusion.36
  81.3 0.9 slice.175.refs_5_.refs_6_
  82.2 1.2 fusion.11
  83.4 45.6 %exchange_1.1 = (bf16[8,128,1600]{2,1,0:T(8,128)(2,1)}, bf16[4,256,1600]{2,1,0:T(8,128)(2,1)}, bf16[1024,256]{1,0:T(8,128)(2,1)}, f32[1024,256]{1,0:T(8,128)}, f32[1024,4]{1,0:T(8,128)}) custom-call(bf16[128,1600]{1,0:T(8,128)(2,1)} %bitcast.60, bf16[256,1600]{1,0:T(8,128)(2,1)} %pad_maximum_fusion.1.refs_1_, s32[1024,1]{1,0:T(8,128)} %copy.47.refs_2_.refs_3_, ...), custom_call_target="tpu_custom_call" | custom-call | tf_op jit(solution)/shard_map/exchange_1/pallas_call | solution.py:513
  129.0 3.0 add_bitcast_fusion.1.refs_1_.refs_8_
  132.0 41.7 %product_7.1 = (f32[128,1600]{1,0:T(8,128)}, bf16[4,400,800]{2,1,0:T(8,128)(2,1)}) custom-call(bf16[1024,256]{1,0:T(8,128)(2,1)} %get-tuple-element.56.refs_0_.refs_4_, bf16[256,1600]{1,0:T(8,128)(2,1)} %add_bitcast_fusion.1.refs_1_.refs_8_, bf16[400,800]{1,0:T(8,128)(2,1)} %pad_maximum_fusion.2.refs_2_), custom_call_target="tpu_custom_call" | custom-call | tf_op jit(solution)/shard_map/product_7/pallas_call | solution.py:735
  173.7 1.8 fusion.32
  175.5 0.2 multiply_reduce_fusion.3
  175.7 1.0 add_convert_fusion.1.refs_0_
  176.7 44.1 %exchange_2.1 = (bf16[8,128,1600]{2,1,0:T(8,128)(2,1)}, bf16[4,200,1600]{2,1,0:T(8,128)(2,1)}) custom-call(bf16[128,1600]{1,0:T(8,128)(2,1)} %add_convert_fusion.1.refs_0_, bf16[200,1600]{1,0:T(8,128)(2,1)} %constant_dynamic-slice_fusion.refs_1_), custom_call_target="tpu_custom_call" | custom-call | tf_op jit(solution)/shard_map/exchange_2/pallas_call | solution.py:513
  220.8 6.0 fusion.37
  226.8 7.2 %convert_reduce_fusion.1 = (f32[800]{0:T(1024)S(1)}, bf16[1024,800]{1,0:T(8,128)(2,1)}, bf16[1024,800]{1,0:T(8,128)(2,1)}) fusion(f32[1024,800]{1,0:T(8,128)S(1)} %fusion.37, f32[800]{0:T(1024)S(1)} %add.263, bf16[1024,1600]{1,0:T(8,128)(2,1)S(1)} %bitcast.63, bf16[800,1600]{1,0:T(8,128)(2,1)S(1)} %bitcast.72), kind=kOutput, calls=%fused_computation.17 | convolution fusion | flops 2641919232 | bytes 12396800 | tf_op jit(solution)/shard_map/dot_general | solution.py:23
  234.0 76.8 %product_3.1 = (f32[128,1600]{1,0:T(8,128)}, f32[128,1600]{1,0:T(8,128)}, bf16[1600,800]{1,0:T(8,128)(2,1)}, bf16[800,1600]{1,0:T(8,128)(2,1)}) custom-call(bf16[1024,800]{1,0:T(8,128)(2,1)} %get-tuple-element.147.refs_0_.refs_5_, bf16[1600,800]{1,0:T(8,128)(2,1)} %bitcast.68, bf16[1024,800]{1,0:T(8,128)(2,1)} %get-tuple-element.160.refs_2_.refs_6_, ...), custom_call_target="tpu_custom_call" | custom-call | tf_op jit(solution)/shard_map/product_3/pallas_call | solution.py:735
  311.0 0.1 reshape_reshape.2
  311.1 1.5 multiply_reduce_fusion.1
  312.8 3.2 convert_reduce_fusion.6
  316.2 1.2 copy.53
  317.4 114.5 %exchange_4.1 = (bf16[8,128,1600]{2,1,0:T(8,128)(2,1)}, bf16[200,1600]{1,0:T(8,128)(2,1)}, bf16[8,400,800]{2,1,0:T(8,128)(2,1)}, bf16[1024,256]{1,0:T(8,128)(2,1...) custom-call(bf16[128,1600]{1,0:T(8,128)(2,1)} %get-tuple-element.149.refs_0_, bf16[4,200,1600]{2,1,0:T(8,128)(2,1)} %bitcast.70, ...), custom_call_target="tpu_custom_call" | custom-call | tf_op jit(solution)/shard_map/exchange_4/pallas_call | solution.py:513
  431.9 1.2 convert_reduce_fusion.5
  433.1 0.2 fusion.27
  433.4 1.2 convert_reduce_fusion.4
  434.6 0.2 fusion.28
  435.0 2.6 pad_maximum_fusion.refs_0_.refs_3_
  437.6 37.3 %product_5.1 = (f32[128,1600]{1,0:T(8,128)}, bf16[1600,768]{1,0:T(8,128)(2,1)}, bf16[256,1600]{1,0:T(8,128)(2,1)}) custom-call(bf16[1024,768]{1,0:T(8,128)(2,1)} %pad_maximum_fusion.refs_0_.refs_3_, bf16[1600,768]{1,0:T(8,128)(2,1)} %bitcast.74, bf16[1024,1600]{1,0:T(8,128)(2,1)} %fusion.3.refs_2_, bf16[1024,768]{1,0:T(8,128)(2,1)} %pad_maximum_fusion.refs_0_.refs_3_, ...), custom_call_target="tpu_custom_call" | custom-call | tf_op jit(solution)/shard_map/product_5/pallas_call | solution.py:735
  475.0 1.6 fusion.23
  476.6 1.8 fusion.22
  478.4 1.2 copy.54
  479.7 0.1 concatenate.38
  479.9 0.6 copy.59
  480.5 145.5 %exchange_6.1 = (bf16[8,200,1600]{2,1,0:T(8,128)(2,1)}, bf16[8,64,1600]{2,1,0:T(8,128)(2,1)}, f32[8,40,128]{2,1,0:T(8,128)}, bf16[8,400,768]{2,1,0:T(8,128)(2,1)}, bf16[400,1600]{1,0:T(8,128)(2,1)}) custom-call(bf16[200,1600]{1,0:T(8,128)(2,1)} %get-tuple-element.76.refs_0_, bf16[4,64,1600]{2,1,0:T(8,128)(2,1)} %bitcast.76, f32[4,40,128]{2,1,0:T(8,128)} %bitcast.77, ...), custom_call_target="tpu_custom_call" | custom-call | tf_op jit(solution)/shard_map/exchange_6/pallas_call | solution.py:513
  626.0 0.9 reduce_sum.199
  627.0 0.7 slice.144
  627.6 0.7 slice.148
  628.3 0.7 fusion.35
  629.0 17.6 %lay_out.1 = (f32[1600,1600]{1,0:T(8,128)}, f32[400,1600]{1,0:T(8,128)}, f32[400,6400]{1,0:T(8,128)}, f32[400,4800]{1,0:T(8,128)}) custom-call(bf16[1600,1600]{1,0:T(8,128)(2,1)} %bitcast.59, bf16[400,1600]{1,0:T(8,128)(2,1)} %get-tuple-element.81.refs_1_, bf16[8,400,800]{2,1,0:T(8,128)(2,1)} %get-tuple-element.82.refs_2_, ...), custom_call_target="tpu_custom_call" | custom-call | bytes 46080000 | tf_op jit(solution)/shard_map/lay_out/pallas_call | solution.py:787
  (61 shorter events, 2.4 us)
Async XLA Ops:
  2.1 8.7 %copy-start.7 = (s32[8,128]{1,0:T(8,128)}, s32[8,128]{1,0:T(8,128)S(1)}, u32[]{:S(2)}) copy-start(s32[8,128]{1,0:T(8,128)S(1)} %multiply_add_fusion) | copy-start | bytes 12292
  4.8 6.1 copy-start.1
  58.2 3.0 copy-start
  76.6 1.7 copy-start.6
  173.7 47.1 %copy-start.4 = (bf16[4,400,800]{2,1,0:T(8,128)(2,1)S(1)}, bf16[4,400,800]{2,1,0:T(8,128)(2,1)}, u32[]{:S(2)}) copy-start(bf16[4,400,800]{2,1,0:T(8,128)(2,1)} %get-tuple-element.64) | copy-start | bytes 7680004
  220.8 6.0 copy-start.3
  220.8 6.0 copy-start.5
  437.6 37.4 %copy-start.2 = (bf16[1,128,1600]{2,1,0:T(8,128)(2,1)S(1)}, bf16[1,128,1600]{2,1,0:T(8,128)(2,1)}, u32[]{:S(2)}) copy-start(bf16[1,128,1600]{2,1,0:T(8,128)(2,1)} %copy-done.1) | copy-start | bytes 1228804

commit v11 on v10

--- a/solution.py
+++ b/solution.py
@@ -890,11 +890,13 @@
     k_w = head_columns(qkv_weight[:, width : 2 * width], width, c, n)
     v_w = head_columns(qkv_weight[:, 2 * width :], width, c, n)
     w_mine = jnp.concatenate([q_w, k_w, v_w], axis=1)
-    x_all, packed, w_qkv = exchange(0, n, nf, ctx=[tokens[0]], fsdp=[flat, w_mine])
+    x = tokens[0].astype(F32)
+    n1, rstd1 = ln_stats(x)
+    n1_all, packed, w_qkv = exchange(0, n, nf, ctx=[n1.astype(BF16)], fsdp=[flat, w_mine])
     out_weight, up_weight, down_weight, packed = lax.optimization_barrier(
         (out_weight, up_weight, down_weight, packed)
     )
-    x_all = x_all.reshape(n * rows, width)
+    n1_all = n1_all.reshape(n * rows, width)
     w_qkv = w_qkv.reshape(width, 3 * wide)
     full = [packed[:, i, : v.shape[0]].reshape(-1).astype(F32) for i, v in enumerate(vectors)]
     gain1, shift1, b_qv, b_out, gain2, shift2, b_up, b_down = full
@@ -903,8 +905,7 @@
     bq = head_columns(b_qv[:width], width, c, n)
     bv = head_columns(b_qv[width:], width, c, n)
 
-    n1_all, _ = ln_stats(x_all.astype(F32))
-    act1 = (n1_all * gain1 + shift1).astype(BF16)
+    act1 = (n1_all.astype(F32) * gain1 + shift1).astype(BF16)
     proj = dot(act1, w_qkv)
     q = (proj[:, :wide] + bq).astype(BF16)
     k = proj[:, wide : 2 * wide].astype(BF16)
@@ -921,7 +922,6 @@
     w_out = functools.reduce(jnp.add, [w_out[i] for i in range(nf)])
     mixed, w_up = product(7, n, nf, [(attn, w_out, False)], fsdp=[jnp.concatenate(up_mine, axis=1)])
     w_up = w_up.reshape(width, nf * ff_part)
-    x = tokens[0].astype(F32)
     mid = x + mixed + b_out
 
     n2, rstd2 = ln_stats(mid)
@@ -964,7 +964,6 @@
     d_qkv = d_qkv.reshape(nf, local, 3 * wide)
     d_out = d_out.reshape(nf, wide // nf, width)
 
-    n1, rstd1 = ln_stats(x)
     d_gain1 = jnp.sum(da1 * n1, axis=0)
     d_shift1 = jnp.sum(da1, axis=0)
     input_grad = d_mid + ln_back(da1, n1, rstd1, gain1)

time: 656 us -> 651 us (level)
  no operation moved by 1% of the time
where the time goes in v11:
time: 651 us; the launch traced here: 642 us
  Pallas kernels  569 us (87%)
  other arithmetic  33.6 us (5%)
  local copies, waits for them, and re-layouts  21.7 us (3%)
  matrix products  16.2 us (2%)
    pallas_call x5, Pallas kernels, exchange(): pl.pallas_call(functools.partial(exchange_body, n, nf, tuple(counts), tup...  391 us
    pallas_call x3, Pallas kernels, product(): pl.pallas_call(functools.partial(product_body, n, nf, (len(products), len...  159 us
    pallas_call x1, Pallas kernels, lay_out(): pl.pallas_call(functools.partial(layout_body, tuple((m and tuple(m) for m...  17.6 us

profile of v11, /device:TPU:0, one launch (start us, length us, event | category | flops | bytes accessed | tf_op | source)
XLA Modules:
  0.0 642.0 jit_solution(3275418663157632538)
XLA Ops:
  0.7 0.7 broadcast_subtract_fusion
  1.3 0.7 multiply_add_fusion
  2.1 1.5 stack_rows.1.refs_1_
  3.5 1.2 copy.45
  4.8 0.1 convert_reduce_fusion.2
  4.9 0.3 fusion.25
  5.2 2.0 copy.46
  7.2 1.0 fusion.18.refs_0_
  8.2 1.0 copy.47.refs_2_.refs_3_
  9.3 2.8 fusion.33
  12.1 0.1 dynamic-slice_select_fusion.2
  12.3 0.1 constant_dynamic-slice_fusion.7
  12.4 0.1 dynamic-slice_select_fusion
  12.5 0.2 constant_dynamic-slice_fusion.5
  12.7 1.1 concatenate.29.refs_2_
  13.8 45.7 %exchange_0.1 = (bf16[8,128,1600]{2,1,0:T(8,128)(2,1)}, bf16[4,16,1600]{2,1,0:T(8,128)(2,1)}, bf16[4,400,768]{2,1,0:T(8,128)(2,1)}) custom-call(bf16[128,1600]{1,0:T(8,128)(2,1)} %fusion.18.refs_0_, bf16[16,1600]{1,0:T(8,128)(2,1)} %stack_rows.1.refs_1_, bf16[400,768]{1,0:T(8,128)(2,1)} %concatenate.29.refs_2_), custom_call_target="tpu_custom_call" | custom-call | tf_op jit(solution)/shard_map/exchange_0/pallas_call | solution.py:513
  59.5 0.8 slice_convert_fusion.1
  61.0 1.0 convert_reduce_fusion.6
  62.0 1.2 convert_reduce_fusion.7
  64.0 0.1 fusion.27
  64.1 0.3 pad_dynamic-slice_fusion.1
  64.4 1.0 pad_maximum_fusion.1.refs_1_
  65.3 2.3 constant_dynamic-slice_fusion.refs_1_
  67.7 1.6 constant_dynamic-slice_fusion.4
  69.3 1.2 pad_maximum_fusion.2.refs_2_
  70.5 2.6 fusion.1.refs_2_
  73.1 0.8 add_convert_fusion
  74.0 0.8 copy-done.7
  74.8 3.0 fusion.35
  77.8 0.9 slice.175.refs_5_.refs_6_
  78.7 1.2 fusion.11
  79.9 45.5 %exchange_1.1 = (bf16[8,128,1600]{2,1,0:T(8,128)(2,1)}, bf16[4,256,1600]{2,1,0:T(8,128)(2,1)}, bf16[1024,256]{1,0:T(8,128)(2,1)}, f32[1024,256]{1,0:T(8,128)}, f32[1024,4]{1,0:T(8,128)}) custom-call(bf16[128,1600]{1,0:T(8,128)(2,1)} %bitcast.78, bf16[256,1600]{1,0:T(8,128)(2,1)} %pad_maximum_fusion.1.refs_1_, s32[1024,1]{1,0:T(8,128)} %copy.47.refs_2_.refs_3_, ...), custom_call_target="tpu_custom_call" | custom-call | tf_op jit(solution)/shard_map/exchange_1/pallas_call | solution.py:513
  125.4 3.0 add_bitcast_fusion.1.refs_1_.refs_8_
  128.4 41.1 %product_7.1 = (f32[128,1600]{1,0:T(8,128)}, bf16[4,400,800]{2,1,0:T(8,128)(2,1)}) custom-call(bf16[1024,256]{1,0:T(8,128)(2,1)} %get-tuple-element.56.refs_0_.refs_4_, bf16[256,1600]{1,0:T(8,128)(2,1)} %add_bitcast_fusion.1.refs_1_.refs_8_, bf16[400,800]{1,0:T(8,128)(2,1)} %pad_maximum_fusion.2.refs_2_), custom_call_target="tpu_custom_call" | custom-call | tf_op jit(solution)/shard_map/product_7/pallas_call | solution.py:735
  169.6 1.6 fusion.31
  171.2 0.2 multiply_reduce_fusion.2
  171.4 1.0 add_convert_fusion.1.refs_0_
  172.4 44.3 %exchange_2.1 = (bf16[8,128,1600]{2,1,0:T(8,128)(2,1)}, bf16[4,200,1600]{2,1,0:T(8,128)(2,1)}) custom-call(bf16[128,1600]{1,0:T(8,128)(2,1)} %add_convert_fusion.1.refs_0_, bf16[200,1600]{1,0:T(8,128)(2,1)} %constant_dynamic-slice_fusion.refs_1_), custom_call_target="tpu_custom_call" | custom-call | tf_op jit(solution)/shard_map/exchange_2/pallas_call | solution.py:513
  216.7 6.0 fusion.36
  222.7 7.2 %convert_reduce_fusion = (f32[800]{0:T(1024)S(1)}, bf16[1024,800]{1,0:T(8,128)(2,1)}, bf16[1024,800]{1,0:T(8,128)(2,1)}) fusion(f32[1024,800]{1,0:T(8,128)S(1)} %fusion.36, f32[800]{0:T(1024)S(1)} %add.249, bf16[1024,1600]{1,0:T(8,128)(2,1)S(1)} %bitcast.81, bf16[800,1600]{1,0:T(8,128)(2,1)S(1)} %bitcast.90), kind=kOutput, calls=%fused_computation.13 | convolution fusion | flops 2641919232 | bytes 12396800 | tf_op jit(solution)/shard_map/dot_general | solution.py:23
  229.9 77.0 %product_3.1 = (f32[128,1600]{1,0:T(8,128)}, f32[128,1600]{1,0:T(8,128)}, bf16[1600,800]{1,0:T(8,128)(2,1)}, bf16[800,1600]{1,0:T(8,128)(2,1)}) custom-call(bf16[1024,800]{1,0:T(8,128)(2,1)} %get-tuple-element.147.refs_0_.refs_5_, bf16[1600,800]{1,0:T(8,128)(2,1)} %bitcast.86, bf16[1024,800]{1,0:T(8,128)(2,1)} %get-tuple-element.160.refs_2_.refs_6_, ...), custom_call_target="tpu_custom_call" | custom-call | tf_op jit(solution)/shard_map/product_3/pallas_call | solution.py:735
  307.1 0.1 reshape_reshape.2
  307.2 1.5 multiply_reduce_fusion
  308.8 3.2 convert_reduce_fusion.5
  312.3 1.2 copy.53
  313.4 114.1 %exchange_4.1 = (bf16[8,128,1600]{2,1,0:T(8,128)(2,1)}, bf16[200,1600]{1,0:T(8,128)(2,1)}, bf16[8,400,800]{2,1,0:T(8,128)(2,1)}, bf16[1024,256]{1,0:T(8,128)(2,1...) custom-call(bf16[128,1600]{1,0:T(8,128)(2,1)} %get-tuple-element.149.refs_0_, bf16[4,200,1600]{2,1,0:T(8,128)(2,1)} %bitcast.88, ...), custom_call_target="tpu_custom_call" | custom-call | tf_op jit(solution)/shard_map/exchange_4/pallas_call | solution.py:513
  427.5 1.2 convert_reduce_fusion.4
  428.7 0.2 fusion.28
  429.1 1.2 convert_reduce_fusion.3
  430.3 0.2 fusion.29
  430.5 0.1 slice_dynamic-update-slice_fusion
  430.7 2.6 pad_maximum_fusion.refs_0_.refs_3_
  433.3 40.6 %product_5.1 = (f32[128,1600]{1,0:T(8,128)}, bf16[1600,768]{1,0:T(8,128)(2,1)}, bf16[256,1600]{1,0:T(8,128)(2,1)}) custom-call(bf16[1024,768]{1,0:T(8,128)(2,1)} %pad_maximum_fusion.refs_0_.refs_3_, bf16[1600,768]{1,0:T(8,128)(2,1)} %bitcast.92, bf16[1024,1600]{1,0:T(8,128)(2,1)} %fusion.1.refs_2_, bf16[1024,768]{1,0:T(8,128)(2,1)} %pad_maximum_fusion.refs_0_.refs_3_, ...), custom_call_target="tpu_custom_call" | custom-call | tf_op jit(solution)/shard_map/product_5/pallas_call | solution.py:735
  473.8 1.6 fusion.24
  475.5 1.8 fusion.23
  477.3 1.2 copy.54
  478.6 0.1 concatenate.38
  478.7 0.6 copy.59
  479.4 141.8 %exchange_6.1 = (bf16[8,200,1600]{2,1,0:T(8,128)(2,1)}, bf16[8,64,1600]{2,1,0:T(8,128)(2,1)}, f32[8,40,128]{2,1,0:T(8,128)}, bf16[8,400,768]{2,1,0:T(8,128)(2,1)}, bf16[400,1600]{1,0:T(8,128)(2,1)}) custom-call(bf16[200,1600]{1,0:T(8,128)(2,1)} %get-tuple-element.76.refs_0_, bf16[4,64,1600]{2,1,0:T(8,128)(2,1)} %bitcast.94, f32[4,40,128]{2,1,0:T(8,128)} %bitcast.95, ...), custom_call_target="tpu_custom_call" | custom-call | tf_op jit(solution)/shard_map/exchange_6/pallas_call | solution.py:513
  621.2 0.9 reduce_sum.179
  622.1 0.7 slice.144
  622.8 0.7 slice.148
  623.5 0.7 fusion.34
  624.1 17.6 %lay_out.1 = (f32[1600,1600]{1,0:T(8,128)}, f32[400,1600]{1,0:T(8,128)}, f32[400,6400]{1,0:T(8,128)}, f32[400,4800]{1,0:T(8,128)}) custom-call(bf16[1600,1600]{1,0:T(8,128)(2,1)} %bitcast.77, bf16[400,1600]{1,0:T(8,128)(2,1)} %get-tuple-element.81.refs_1_, bf16[8,400,800]{2,1,0:T(8,128)(2,1)} %get-tuple-element.82.refs_2_, ...), custom_call_target="tpu_custom_call" | custom-call | bytes 46080000 | tf_op jit(solution)/shard_map/lay_out/pallas_call | solution.py:787
  (61 shorter events, 2.3 us)
Async XLA Ops:
  2.1 10.0 %copy-start.8 = (s32[8,128]{1,0:T(8,128)}, s32[8,128]{1,0:T(8,128)S(1)}, u32[]{:S(2)}) copy-start(s32[8,128]{1,0:T(8,128)S(1)} %multiply_add_fusion) | copy-start | bytes 12292
  4.8 7.4 %copy-start = (bf16[1,128,1600]{2,1,0:T(8,128)(2,1)}, bf16[1,128,1600]{2,1,0:T(8,128)(2,1)S(1)}, u32[]{:S(2)}) copy-start(bf16[1,128,1600]{2,1,0:T(8,128)(2,1)S(1)} %copy.45) | copy-start | bytes 1228804
  12.1 51.8 %copy-start.3 = (bf16[400,1600]{1,0:T(8,128)(2,1)S(1)}, bf16[400,1600]{1,0:T(8,128)(2,1)}, u32[]{:S(2)}) copy-start(bf16[400,1600]{1,0:T(8,128)(2,1)} %param.20) | copy-start | bytes 3840004
  64.3 6.2 copy-start.2
  73.1 1.7 copy-start.7
  169.5 47.1 %copy-start.5 = (bf16[4,400,800]{2,1,0:T(8,128)(2,1)S(1)}, bf16[4,400,800]{2,1,0:T(8,128)(2,1)}, u32[]{:S(2)}) copy-start(bf16[4,400,800]{2,1,0:T(8,128)(2,1)} %get-tuple-element.64) | copy-start | bytes 7680004
  216.7 6.0 copy-start.4
  216.7 6.0 copy-start.6
  433.3 40.6 %copy-start.1 = (bf16[1,128,1600]{2,1,0:T(8,128)(2,1)S(1)}, bf16[1,128,1600]{2,1,0:T(8,128)(2,1)}, u32[]{:S(2)}) copy-start(bf16[1,128,1600]{2,1,0:T(8,128)(2,1)} %copy-done) | copy-start | bytes 1228804
